TPU v7x, 256 devices: a whole 4x4x8 slice. The times are simulated.
256 devices in a mesh: fsdp: 8 (over x, core), vocab: 32 (over y, z).
Axes of the slice: x: 4, y: 4, z: 8, core: 2. Of those that a mesh axis runs over, the one named last changes fastest.
Arguments:
- hidden_states: bfloat16 [1024, 3072], P('fsdp', 'vocab'), may hold values from -512 to 512
- head: bfloat16 [3072, 65536], P('fsdp', 'vocab'), may hold values from -0.25259074 to 0.25259074
- labels: int32 [1024], P('fsdp'), may hold values from 0 to 65535
Outputs:
- token_loss: float32 [1024], P('fsdp')
- state_grad: bfloat16 [1024, 3072], P('fsdp', 'vocab')
- head_grad: float32 [3072, 65536], P('fsdp', 'vocab')
All inputs are finite; a program needn't handle non-finite values.
Results may differ from a plain program's by a relative error of at most 0.0034.
Values may be sent and summed in bfloat16 or wider, within the bound.
No kernel may reach another device: no remote copies, remote signals or barrier semaphores. Data moves between devices by JAX's collectives and lax.ppermute only.
A program may use at most 128 MiB of HBM per device.

v0:
```python
import jax
import jax.numpy as jnp
from jax import lax
from jax.experimental import pallas as pl
from jax.experimental.pallas import tpu as pltpu
from jax.sharding import Mesh, PartitionSpec as P


BF = jnp.bfloat16
F32 = jnp.float32
NX, NY, NZ = 4, 4, 8
STEPS = 4


def shift(a, axis, n, s):
    return lax.ppermute(a, axis, [(i, (i + s) % n) for i in range(n)])


def swap(a):
    return lax.ppermute(a, "core", [(0, 1), (1, 0)])


def from_everyone(a, axis, n):
    return lax.all_to_all(jnp.broadcast_to(a[None], (n, *a.shape)), axis, 0, 0, tiled=True)


def ordered(parts, index):
    n = len(parts)
    both = jnp.stack(parts + parts[:-1])
    return lax.dynamic_slice_in_dim(both, (n - index) % n, n, 0)


def dot(a, b):
    return lax.dot_general(a, b, (((1,), (0,)), ((), ())), preferred_element_type=F32)


def whole(a):
    zeros = (0,) * a.ndim
    return pl.BlockSpec(a.shape, lambda j, s: zeros)


def early(j):
    return jnp.minimum(j, STEPS // 2 - 1)


def late(j):
    return jnp.maximum(j - STEPS // 2, 0)


def call(kernel, scalars, args, in_specs, out_specs, out_shape, flops, scratch=()):
    return pl.pallas_call(
        kernel,
        grid_spec=pltpu.PrefetchScalarGridSpec(
            num_scalar_prefetch=1,
            grid=(STEPS,),
            in_specs=in_specs,
            out_specs=out_specs,
            scratch_shapes=scratch,
        ),
        out_shape=out_shape,
        cost_estimate=pl.CostEstimate(flops=flops, bytes_accessed=flops // 256, transcendentals=0),
    )(jnp.stack(scalars).astype(jnp.int32), *args)


def near_kernel(who, states, *refs):
    acc = None
    for k, ref in enumerate(refs[:-1]):
        term = dot(states[who[k]], ref[...])
        acc = term if acc is None else acc + term
    refs[-1][...] = acc


def near_logits(states, arrays, who):
    rows, width = arrays[0].shape
    tokens = states.shape[1]
    wide = width // STEPS
    return call(
        near_kernel,
        who,
        [states, *arrays],
        [whole(states)] + [pl.BlockSpec((rows, wide), lambda j, s: (0, j))] * len(arrays),
        pl.BlockSpec((tokens, wide), lambda j, s: (0, j)),
        jax.ShapeDtypeStruct((tokens, width), F32),
        2 * tokens * rows * width * len(arrays),
    )


def far_kernel(who, states, labels, near, left, left_other, right, right_other, powers, stats, logits):
    step = pl.program_id(0)
    first = step < STEPS // 2
    wide = near.shape[1]
    for mine, theirs, here in ((left, left_other, first), (right, right_other, ~first)):

        @pl.when(here)
        def _():
            logits[:, pl.ds(pl.multiple_of(step * wide, wide), wide)] = (
                near[...] + dot(states[who[0]], mine[...]) + dot(states[who[1]], theirs[...])
            )

    @pl.when(step == STEPS - 1)
    def _():
        values = logits[...]
        peak = jnp.max(values, axis=1, keepdims=True)
        shifted = jnp.exp(values - peak)
        columns = who[2] + lax.broadcasted_iota(jnp.int32, values.shape, 1)
        hits = labels[...] == columns
        total = jnp.sum(shifted, axis=1, keepdims=True)
        target = jnp.sum(jnp.where(hits, values, 0.0), axis=1, keepdims=True)
        powers[...] = shifted.astype(BF)
        lanes = lax.broadcasted_iota(jnp.int32, stats.shape, 1)
        stats[...] = jnp.where(lanes == 0, peak, jnp.where(lanes == 1, total, target))


def far_logits(states, labels, near, left, right, who):
    tokens, width = near.shape
    wide = width // STEPS
    rows = left[0].shape[0]
    args = [states, labels, near, *left, *right]
    specs = [whole(states), whole(labels), pl.BlockSpec((tokens, wide), lambda j, s: (0, j))]
    specs += [pl.BlockSpec((rows, wide), lambda j, s: (0, early(j)))] * 2
    specs += [pl.BlockSpec((rows, wide), lambda j, s: (0, late(j)))] * 2
    powers = jax.ShapeDtypeStruct((tokens, width), BF)
    stats = jax.ShapeDtypeStruct((tokens, 128), F32)
    return call(
        far_kernel,
        who,
        args,
        specs,
        [whole(powers), whole(stats)],
        [powers, stats],
        4 * tokens * rows * width,
        [pltpu.VMEM((tokens, width), F32)],
    )


def terms_kernel(starts, powers, labels, *refs):
    *arrays, sums, picks, both = refs
    step = pl.program_id(0)
    width, double = both.shape
    tokens = double // 2

    @pl.when(step == 0)
    def _():
        both[:, :tokens] = powers[...].T
        columns = starts[8] + lax.broadcasted_iota(jnp.int32, (width, tokens), 0)
        both[:, tokens:] = jnp.where(columns == labels[...], 1.0, 0.0).astype(BF)

    def put(k, term):
        rows = term.shape[0]
        at = pl.ds(pl.multiple_of(starts[k] + step * rows, 32), rows)
        sums[at, :] = term[:, :tokens]
        picks[at, :] = term[:, tokens:].astype(BF)

    for k in range(6):
        put(k, dot(arrays[k][...], both[...]))
    half = width // 2
    for k in range(2):
        left, right = arrays[6 + k], arrays[8 + k]
        put(6 + k, dot(left[...], both[:half, :]) + dot(right[...], both[half:, :]))


def state_terms(powers, labels, near, left, right, starts, depth):
    tokens, width = powers.shape
    rows = near[0].shape[0] // STEPS
    args = [powers, labels, *near, *left, *right]
    specs = [whole(powers), whole(labels)]
    specs += [pl.BlockSpec((rows, a.shape[1]), lambda j, s: (j, 0)) for a in args[2:]]
    sums = jax.ShapeDtypeStruct((depth, tokens), F32)
    picks = jax.ShapeDtypeStruct((depth, tokens), BF)
    return call(
        terms_kernel,
        starts,
        args,
        specs,
        [whole(sums), whole(picks)],
        [sums, picks],
        4 * tokens * width * depth,
        [pltpu.VMEM((width, 2 * tokens), BF)],
    )


def grad_kernel(who, states, scales, labels, *refs):
    *arrays, out = refs
    step = pl.program_id(0)
    tokens = states.shape[2]
    wide = out.shape[1]
    columns = who[8] + step * wide + lax.broadcasted_iota(jnp.int32, (tokens, wide), 1)
    blocks = [a[...] for a in arrays[:6]]
    first = step < STEPS // 2
    blocks += [jnp.where(first, arrays[6 + k][...], arrays[8 + k][...]) for k in range(2)]
    acc = None
    for pair in range(4):
        left, right = [], []
        for k in (2 * pair, 2 * pair + 1):
            wanted = labels[pl.ds(pl.multiple_of(who[k] * tokens, tokens), tokens), :]
            hit = jnp.where(wanted == columns, 1.0, 0.0)
            scale = scales[k * tokens : (k + 1) * tokens, :]
            right.append((blocks[k].astype(F32) * scale - hit).astype(BF))
            left.append(states[who[k]])
        term = dot(jnp.concatenate(left, axis=1), jnp.concatenate(right, axis=0))
        acc = term if acc is None else acc + term
    out[...] = acc


def head_grad_of(states, scales, labels, near, left, right, who):
    groups, rows, tokens = states.shape
    width = near[0].shape[1]
    wide = width // STEPS
    args = [states, scales, labels, *near, *left, *right]
    specs = [whole(states), whole(scales), whole(labels)]
    specs += [pl.BlockSpec((tokens, wide), lambda j, s: (0, j))] * 6
    specs += [pl.BlockSpec((tokens, wide), lambda j, s: (0, early(j)))] * 2
    specs += [pl.BlockSpec((tokens, wide), lambda j, s: (0, late(j)))] * 2
    return call(
        grad_kernel,
        who,
        args,
        specs,
        pl.BlockSpec((rows, wide), lambda j, s: (0, j)),
        jax.ShapeDtypeStruct((rows, width), F32),
        2 * groups * tokens * rows * width,
    )


def step(hidden_states, head, labels):
    x, core, y = lax.axis_index("x"), lax.axis_index("core"), lax.axis_index("y")
    vocab = y * NZ + lax.axis_index("z")
    tokens, part = hidden_states.shape
    rows, width = head.shape
    half = width // 2
    depth = NY * NZ * part
    base = vocab * width

    def who(offset):
        chip = ((x + offset) % NX) * 2
        return [chip + core, chip + 1 - core]

    up = shift(head, "x", NX, 1)
    down = shift(head, "x", NX, -1)
    partner = swap(head)
    far_left = shift(up[:, :half], "x", NX, 1)
    far_right = shift(down[:, half:], "x", NX, -1)
    near = [head, partner, up, swap(up), down, swap(down)]
    left = [far_left, swap(far_left)]
    right = [far_right, swap(far_right)]

    features = from_everyone(hidden_states.T, ("y", "z"), NY * NZ)
    flat = jnp.swapaxes(features.reshape(8, rows, tokens), 1, 2)

    wanted = lax.dynamic_index_in_dim(
        features.reshape(8, NY, part, tokens), y, 1, keepdims=False
    )
    digits = jnp.stack([labels // 256, labels % 256]).astype(BF)
    digits = jnp.broadcast_to(jnp.pad(digits, ((0, 14), (0, 0)))[None], (8, 16, tokens))
    wanted = lax.all_to_all(
        jnp.concatenate([wanted, digits], axis=1), ("x", "core"), 0, 0, tiled=True
    )
    digits = wanted[:, part : part + 2].astype(jnp.int32)
    all_labels = (digits[:, 0] * 256 + digits[:, 1]).reshape(8 * tokens, 1)
    wanted = wanted[:, :part]

    logits = near_logits(flat, near, who(0) + who(3) + who(1))
    powers, stats = far_logits(
        flat, labels[:, None], logits, left, right, who(2) + [base]
    )
    stats = stats.T[:3]

    pow_up = shift(powers, "x", NX, 1)
    pow_down = shift(powers, "x", NX, -1)
    pow_left = shift(pow_up[:, :half], "x", NX, 1)
    pow_right = shift(pow_down[:, half:], "x", NX, -1)
    pow_near = [powers, swap(powers), pow_up, swap(pow_up), pow_down, swap(pow_down)]
    pow_left = [pow_left, swap(pow_left)]
    pow_right = [pow_right, swap(pow_right)]

    parts = from_everyone(stats, ("y", "z"), NY * NZ)
    starts = [w * rows for w in who(0) + who(3) + who(1) + who(2)]
    sums, picks = state_terms(
        powers, labels[None], near, left, right, starts + [base], depth
    )
    peak = jnp.max(parts[:, 0], axis=0)
    total = jnp.sum(parts[:, 1] * jnp.exp(parts[:, 0] - peak), axis=0)
    target = jnp.sum(parts[:, 2], axis=0)
    token_loss = jnp.log(total) + peak - target
    scale = jnp.exp(stats[0] - peak) / total

    terms = (sums * scale - picks.astype(F32)).astype(BF)
    arrived = lax.all_to_all(
        terms.reshape(NY * NZ, part, tokens), ("y", "z"), 0, 0, tiled=True
    )
    state_grad = arrived.astype(F32).sum(axis=0).astype(BF).T

    slices = ordered([wanted] + [shift(wanted, "y", NY, -j) for j in (1, 2, 3)], y)
    slices = jnp.swapaxes(slices, 0, 1).reshape(8, rows, tokens)
    scale = jnp.stack([scale, swap(scale)])
    scales = [scale] + [shift(scale, "x", NX, s) for s in (1, -1, 2)]
    scales = jnp.concatenate(scales).reshape(8 * tokens, 1)
    head_grad = head_grad_of(
        slices,
        scales,
        all_labels,
        pow_near,
        pow_left,
        pow_right,
        who(0) + who(3) + who(1) + who(2) + [base],
    )
    return (token_loss, state_grad, head_grad)


def solution(mesh):
    chips = Mesh(mesh.devices.reshape(NX, 2, NY, NZ), ("x", "core", "y", "z"))
    tok, voc = ("x", "core"), ("y", "z")
    in_specs = (P(tok, voc), P(tok, voc), P(tok))
    out_specs = (P(tok), P(tok, voc), P(tok, voc))
    return jax.shard_map(step, mesh=chips, in_specs=in_specs, out_specs=out_specs, check_vma=False)
```

profile of v0, /device:TPU:32, one launch (start us, length us, event | category | flops | bytes accessed | tf_op | source)
XLA Modules:
  0.0 168.9 jit_solution(3133910781053968775)
XLA Ops:
  0.6 1.7 %broadcast_in_dim.10 = bf16[32,96,128]{2,1,0:T(8,128)(2,1)} broadcast(bf16[96,128]{1,0:T(8,128)(2,1)} %bitcast.68), dimensions={1,2} | broadcast | bytes 811008 | tf_op jit(solution)/shard_map/broadcast_in_dim | solution.py:24
  2.4 11.4 %all-to-all-start = ((bf16[32,96,128]{2,1,0:T(8,128)(2,1)}), bf16[32,96,128]{2,1,0:T(8,128)(2,1)}, u32[]{:S(2)}, u32[]{:S(2)}) async-start(bf16[32,96,128]{2,1,0:T(8,128)(2,1)} %broadcast_in_dim.10), calls=%async_computation | async-start | bytes 1572864 | tf_op jit(solution)/shard_map/all_to_all | solution.py:24
  13.8 1.6 collective-permute-start.1
  15.3 1.7 %collective-permute-start.3 = (bf16[384,2048]{1,0:T(8,128)(2,1)}, bf16[384,2048]{1,0:T(8,128)(2,1)S(1)}, u32[]{:S(2)}, u32[]{:S(2)}) collective-permute-start(bf16[384,2048]{1,0:T(8,128)(2,1)} %refs_0_.3), channel_id=1, source_target_pairs={{0,192},{64,0},{128,64},{192,128},{1,193},{65,1},{129,65},{193,129... | collective-permute-start | bytes 4718600 | tf_op jit(solution)/shard_map/ppermute | solution.py:16
  17.1 19.9 %all-to-all-done = bf16[32,96,128]{2,1,0:T(8,128)(2,1)} async-done(((bf16[32,96,128]{2,1,0:T(8,128)(2,1)}), bf16[32,96,128]{2,1,0:T(8,128)(2,1)}, u32[]{:S(2)}, u32[]{:S(2)}) %all-to-all-start) | async-done | bytes 786464 | tf_op jit(solution)/shard_map/all_to_all | solution.py:24
  37.0 0.9 dynamic-slice_bitcast_fusion.1
  38.0 16.3 %all_to_all.20 = bf16[8,112,128]{2,1,0:T(8,128)(2,1)S(1)} all-to-all(bf16[8,112,128]{2,1,0:T(8,128)(2,1)S(1)} %pad_maximum_fusion), channel_id=1, replica_groups=mesh['x'=4,'core'=2,'y'=4,'z'=8] {'x','core'}, dimensions={0} | all-to-all | bytes 458752 | tf_op jit(solution)/shard_map/all_to_all | solution.py:255
  54.3 2.8 %collective-permute-start.9 = (bf16[8,96,128]{2,1,0:T(8,128)(2,1)S(1)}, bf16[8,96,128]{2,1,0:T(8,128)(2,1)S(1)}, u32[]{:S(2)}, u32[]{:S(2)}) collective-permute-start(bf16[8,96,128]{2,1,0:T(8,128)(2,1)S(1)} %slice.61), channel_id=1, source_target_pairs={{0,24},{8,0},{16,8},{24,16},{1,25},{9,1},{17,9},{25,17},{2,26},{10... | collective-permute-start | bytes 589832 | tf_op jit(solution)/shard_map/ppermute | solution.py:16
  57.1 0.8 collective-permute-start.10
  58.6 1.1 slice.54
  59.7 0.9 slice.55
  60.6 4.6 %collective-permute-done.9 = bf16[8,96,128]{2,1,0:T(8,128)(2,1)S(1)} collective-permute-done((bf16[8,96,128]{2,1,0:T(8,128)(2,1)S(1)}, bf16[8,96,128]{2,1,0:T(8,128)(2,1)S(1)}, u32[]{:S(2)}, u32[]{:S(2)}) %collective-permute-start.9) | collective-permute-done | bytes 196640 | tf_op jit(solution)/shard_map/ppermute | solution.py:16
  65.2 0.7 copy-done.5
  65.9 1.1 collective-permute-start.5
  67.0 2.1 %collective-permute-start.7 = (bf16[384,1024]{1,0:T(8,128)(2,1)}, bf16[384,1024]{1,0:T(8,128)(2,1)}, u32[]{:S(2)}, u32[]{:S(2)}) collective-permute-start(bf16[384,1024]{1,0:T(8,128)(2,1)} %slice.55), channel_id=1, source_target_pairs={{0,192},{64,0},{128,64},{192,128},{1,193},{65,1},{129,65},{193,129... | collective-permute-start | bytes 2359304 | tf_op jit(solution)/shard_map/ppermute | solution.py:16
  69.1 0.7 copy.74.labels
  69.9 0.7 stack.120.who
  70.5 0.7 stack.130.who
  71.2 0.7 stack.129.starts
  72.5 2.3 %copy.73 = bf16[8,384,128]{1,2,0:T(8,128)(2,1)} copy(bf16[8,384,128]{2,1,0:T(8,128)(2,1)} %bitcast.4) | data formatting | bytes 1572864 | tf_op jit(solution)/shard_map/reshape | solution.py:248
  74.8 1.1 copy.85.labels
  75.9 7.1 %collective-permute-done.5.left.refs_6_ = bf16[384,1024]{1,0:T(8,128)(2,1)} collective-permute-done((bf16[384,1024]{1,0:T(8,128)(2,1)}, bf16[384,1024]{1,0:T(8,128)(2,1)}, u32[]{:S(2)}, u32[]{:S(2)}) %collective-permute-start.5) | collective-permute-done | bytes 786464 | tf_op jit(solution)/shard_map/ppermute | solution.py:16
  83.5 1.0 bitcast_dynamic-update-slice_fusion.3
  84.4 1.0 bitcast_dynamic-update-slice_fusion.1
  85.4 2.4 %collective-permute-start.11 = (bf16[8,96,128]{2,1,0:T(8,128)(2,1)}, bf16[8,96,128]{2,1,0:T(8,128)(2,1)}, u32[]{:S(2)}, u32[]{:S(2)}) collective-permute-start(bf16[8,96,128]{2,1,0:T(8,128)(2,1)} %copy-done.9), channel_id=1, source_target_pairs={{0,8},{8,16},{16,24},{24,0},{1,9},{9,17},{17,25},{25,1},{2,10},{10... | collective-permute-start | bytes 589832 | tf_op jit(solution)/shard_map/ppermute | solution.py:16
  87.9 7.5 %shard_map.58.near = f32[128,2048]{1,0:T(8,128)} custom-call(s32[6]{0:T(128)} %stack.120.who, bf16[8,128,384]{2,1,0:T(8,128)(2,1)} %bitcast.59, bf16[384,2048]{1,0:T(8,128)(2,1)} %refs_0_.3, bf16[384,2048]{1,0:T(8,128)(2,1)} %collective-permute-done.refs_1_, bf16[384,2048]{1,0:T(8,128)(2,1)} %copy-done, bf16[384,2048]{1,0:T(8,128)(2,1)} %collective-permute-done.2.refs_3_, ...), custom_call_target="tpu_custom_call" | custom-call | flops 1207959552 | bytes 4718592 | tf_op jit(solution)/shard_map/pallas_call | solution.py:51
  95.4 6.0 %shard_map.59 = (bf16[128,2048]{1,0:T(8,128)(2,1)}, f32[128,128]{1,0:T(8,128)}) custom-call(s32[3]{0:T(128)} %pad_add_fusion.who, bf16[8,128,384]{2,1,0:T(8,128)(2,1)} %bitcast.60, s32[128,1]{1,0:T(8,128)} %copy.74.labels, f32[128,2048]{1,0:T(8,128)} %shard_map.58.near, bf16[384,1024]{1,0:T(8,128)(2,1)} %collective-permute-done.5.left.refs_6_, ...), custom_call_target="tpu_custom_call" | custom-call | flops 402653184 | bytes 1572864 | tf_op jit(solution)/shard_map/pallas_call | solution.py:51
  101.4 1.1 collective-permute-start.17
  102.5 2.1 %collective-permute-start.19 = (bf16[128,2048]{1,0:T(8,128)(2,1)}, bf16[128,2048]{1,0:T(8,128)(2,1)S(1)}, u32[]{:S(2)}, u32[]{:S(2)}) collective-permute-start(bf16[128,2048]{1,0:T(8,128)(2,1)} %get-tuple-element.8.powers.refs_0_), channel_id=1, source_target_pairs={{0,192},{64,0},{128,64},{192,128},{1,193},{65,1},{129,65},{193,129... | collective-permute-start | bytes 1572872 | tf_op jit(solution)/shard_map/ppermute | solution.py:16
  104.6 0.9 copy.75
  105.5 0.7 broadcast_in_dim.12
  106.2 9.2 %all-to-all-start.1 = ((f32[32,3,128]{2,1,0:T(4,128)}), f32[32,3,128]{2,1,0:T(4,128)S(1)}, u32[]{:S(2)}, u32[]{:S(2)}) async-start(f32[32,3,128]{2,1,0:T(4,128)} %broadcast_in_dim.12), calls=%async_computation.1 | async-start | bytes 131072 | tf_op jit(solution)/shard_map/all_to_all | solution.py:24
  115.4 11.4 %shard_map.60 = (f32[3072,128]{1,0:T(8,128)}, bf16[3072,128]{1,0:T(8,128)(2,1)}) custom-call(s32[9]{0:T(128)} %stack.129.starts, bf16[128,2048]{1,0:T(8,128)(2,1)} %get-tuple-element.8.powers.refs_0_, s32[1,128]{1,0:T(1,128)} %bitcast.75, bf16[384,2048]{1,0:T(8,128)(2,1)} %refs_0_.3, bf16[384,2048]{1,0:T(8,128)(2,1)} %collective-permute-done.refs_1_, ...), custom_call_target="tpu_custom_call" | custom-call | flops 3221225472 | bytes 12582912 | tf_op jit(solution)/shard_map/pallas_call | solution.py:51
  127.2 2.8 %subtract_convert_fusion = bf16[3072,128]{1,0:T(8,128)(2,1)} fusion(bf16[3072,128]{1,0:T(8,128)(2,1)} %get-tuple-element.10, f32[3072,128]{1,0:T(8,128)} %get-tuple-element.9, f32[128]{0:T(128)S(1)} %get-tuple-element.11), kind=kLoop, calls=%fused_computation | loop fusion | flops 1572864 | bytes 3146240 | tf_op jit(solution)/shard_map/convert_element_type | solution.py:287
  130.0 9.9 %all-to-all-start.2 = ((bf16[32,96,128]{2,1,0:T(8,128)(2,1)}), bf16[32,96,128]{2,1,0:T(8,128)(2,1)S(1)}, u32[]{:S(2)}, u32[]{:S(2)}) async-start(bf16[32,96,128]{2,1,0:T(8,128)(2,1)} %bitcast.29), calls=%async_computation.2 | async-start | bytes 1572864 | tf_op jit(solution)/shard_map/all_to_all | solution.py:288
  140.5 1.6 bitcast_dynamic-update-slice_fusion
  142.3 3.2 %collective-permute-start.14 = (f32[2,128]{1,0:T(2,128)S(1)}, f32[2,128]{1,0:T(2,128)S(1)}, u32[]{:S(2)}, u32[]{:S(2)}) collective-permute-start(f32[2,128]{1,0:T(2,128)S(1)} %pad_maximum_fusion.1), channel_id=1, source_target_pairs={{0,192},{64,0},{128,64},{192,128},{1,193},{65,1},{129,65},{193,129... | collective-permute-start | bytes 3080 | tf_op jit(solution)/shard_map/ppermute | solution.py:16
  145.6 0.9 collective-permute-start.21
  146.5 2.4 %collective-permute-start.23 = (bf16[128,1024]{1,0:T(8,128)(2,1)S(1)}, bf16[128,1024]{1,0:T(8,128)(2,1)}, u32[]{:S(2)}, u32[]{:S(2)}) collective-permute-start(bf16[128,1024]{1,0:T(8,128)(2,1)S(1)} %slice.66), channel_id=1, source_target_pairs={{0,192},{64,0},{128,64},{192,128},{1,193},{65,1},{129,65},{193,129... | collective-permute-start | bytes 786440 | tf_op jit(solution)/shard_map/ppermute | solution.py:16
  149.0 0.7 bitcast_dynamic-update-slice_fusion.6
  150.6 0.7 bitcast_dynamic-update-slice_fusion.4
  151.3 3.8 %collective-permute-done.21.refs_6_ = bf16[128,1024]{1,0:T(8,128)(2,1)} collective-permute-done((bf16[128,1024]{1,0:T(8,128)(2,1)S(1)}, bf16[128,1024]{1,0:T(8,128)(2,1)}, u32[]{:S(2)}, u32[]{:S(2)}) %collective-permute-start.21) | collective-permute-done | bytes 262176 | tf_op jit(solution)/shard_map/ppermute | solution.py:16
  155.6 1.6 bitcast_dynamic-update-slice_fusion.2
  157.3 1.2 dynamic-slice_bitcast_fusion
  158.5 0.9 copy.81
  159.5 1.0 copy.84.scales
  160.5 7.6 %shard_map.61 = f32[384,2048]{1,0:T(8,128)} custom-call(s32[9]{0:T(128)} %stack.130.who, bf16[8,384,128]{2,1,0:T(8,128)(2,1)} %bitcast.61, f32[1024,1]{1,0:T(8,128)} %copy.84.scales, s32[1024,1]{1,0:T(8,128)} %copy.85.labels, bf16[128,2048]{1,0:T(8,128)(2,1)} %get-tuple-element.8.powers.refs_0_, bf16[128,2048]{1,0:T(8,128)(2,1)} %collective-permute-done.16.refs_1_, ...), custom_call_target="tpu_custom_call" | custom-call | flops 1610612736 | bytes 6291456 | tf_op jit(solution)/shard_map/pallas_call | solution.py:51
  168.1 0.7 reduce_sum.35
  (80 shorter events, 4.5 us)
Async XLA Ops:
  0.6 16.5 %copy-start.10 = (s32[128]{0:T(128)S(1)}, s32[128]{0:T(128)}, u32[]{:S(2)}) copy-start(s32[128]{0:T(128)} %param.5) | copy-start | bytes 1540
  2.4 34.6 %all-to-all-start = ((bf16[32,96,128]{2,1,0:T(8,128)(2,1)}), bf16[32,96,128]{2,1,0:T(8,128)(2,1)}, u32[]{:S(2)}, u32[]{:S(2)}) async-start(bf16[32,96,128]{2,1,0:T(8,128)(2,1)} %broadcast_in_dim.10), calls=%async_computation | async-start | bytes 1572864 | tf_op jit(solution)/shard_map/all_to_all | solution.py:24
  13.8 44.2 %collective-permute-start.1 = (bf16[384,2048]{1,0:T(8,128)(2,1)}, bf16[384,2048]{1,0:T(8,128)(2,1)S(1)}, u32[]{:S(2)}, u32[]{:S(2)}) collective-permute-start(bf16[384,2048]{1,0:T(8,128)(2,1)} %refs_0_.3), channel_id=1, source_target_pairs={{0,64},{64,128},{128,192},{192,0},{1,65},{65,129},{129,193},{193,1... | collective-permute-start | bytes 4718600 | tf_op jit(solution)/shard_map/ppermute | solution.py:16
  15.3 43.1 %collective-permute-start.3 = (bf16[384,2048]{1,0:T(8,128)(2,1)}, bf16[384,2048]{1,0:T(8,128)(2,1)S(1)}, u32[]{:S(2)}, u32[]{:S(2)}) collective-permute-start(bf16[384,2048]{1,0:T(8,128)(2,1)} %refs_0_.3), channel_id=1, source_target_pairs={{0,192},{64,0},{128,64},{192,128},{1,193},{65,1},{129,65},{193,129... | collective-permute-start | bytes 4718600 | tf_op jit(solution)/shard_map/ppermute | solution.py:16
  54.3 12.7 %copy-start.9 = (bf16[8,96,128]{2,1,0:T(8,128)(2,1)}, bf16[8,96,128]{2,1,0:T(8,128)(2,1)S(1)}, u32[]{:S(2)}) copy-start(bf16[8,96,128]{2,1,0:T(8,128)(2,1)S(1)} %slice.61) | copy-start | bytes 589828
  54.3 10.9 %collective-permute-start.9 = (bf16[8,96,128]{2,1,0:T(8,128)(2,1)S(1)}, bf16[8,96,128]{2,1,0:T(8,128)(2,1)S(1)}, u32[]{:S(2)}, u32[]{:S(2)}) collective-permute-start(bf16[8,96,128]{2,1,0:T(8,128)(2,1)S(1)} %slice.61), channel_id=1, source_target_pairs={{0,24},{8,0},{16,8},{24,16},{1,25},{9,1},{17,9},{25,17},{2,26},{10... | collective-permute-start | bytes 589832 | tf_op jit(solution)/shard_map/ppermute | solution.py:16
  57.1 9.9 %collective-permute-start.10 = (bf16[8,96,128]{2,1,0:T(8,128)(2,1)S(1)}, bf16[8,96,128]{2,1,0:T(8,128)(2,1)}, u32[]{:S(2)}, u32[]{:S(2)}) collective-permute-start(bf16[8,96,128]{2,1,0:T(8,128)(2,1)S(1)} %slice.61), channel_id=1, source_target_pairs={{0,16},{8,24},{16,0},{24,8},{1,17},{9,25},{17,1},{25,9},{2,18},{10... | collective-permute-start | bytes 589832 | tf_op jit(solution)/shard_map/ppermute | solution.py:16
  57.9 27.5 %collective-permute-start = (bf16[384,2048]{1,0:T(8,128)(2,1)}, bf16[384,2048]{1,0:T(8,128)(2,1)}, u32[]{:S(2)}, u32[]{:S(2)}) collective-permute-start(bf16[384,2048]{1,0:T(8,128)(2,1)} %refs_0_.3), channel_id=1, source_target_pairs={{0,32},{32,0},{1,33},{33,1},{2,34},{34,2},{3,35},{35,3},{4,36},{36... | collective-permute-start | bytes 4718600 | tf_op jit(solution)/shard_map/ppermute | solution.py:20
  57.9 2.7 %copy-start = (bf16[384,2048]{1,0:T(8,128)(2,1)}, bf16[384,2048]{1,0:T(8,128)(2,1)S(1)}, u32[]{:S(2)}) copy-start(bf16[384,2048]{1,0:T(8,128)(2,1)S(1)} %collective-permute-done.1.refs_2_) | copy-start | bytes 4718596
  57.9 29.9 %collective-permute-start.2 = (bf16[384,2048]{1,0:T(8,128)(2,1)S(1)}, bf16[384,2048]{1,0:T(8,128)(2,1)}, u32[]{:S(2)}, u32[]{:S(2)}) collective-permute-start(bf16[384,2048]{1,0:T(8,128)(2,1)S(1)} %collective-permute-done.1.refs_2_), channel_id=1, source_target_pairs={{0,32},{32,0},{1,33},{33,1},{2,34},{34,2},{3,35},{35,3},{4,36},{36... | collective-permute-start | bytes 4718600 | tf_op jit(solution)/shard_map/ppermute | solution.py:20
  58.5 2.2 %copy-start.1 = (bf16[384,2048]{1,0:T(8,128)(2,1)}, bf16[384,2048]{1,0:T(8,128)(2,1)S(1)}, u32[]{:S(2)}) copy-start(bf16[384,2048]{1,0:T(8,128)(2,1)S(1)} %collective-permute-done.3.refs_4_) | copy-start | bytes 4718596
  58.5 29.4 %collective-permute-start.4 = (bf16[384,2048]{1,0:T(8,128)(2,1)S(1)}, bf16[384,2048]{1,0:T(8,128)(2,1)}, u32[]{:S(2)}, u32[]{:S(2)}) collective-permute-start(bf16[384,2048]{1,0:T(8,128)(2,1)S(1)} %collective-permute-done.3.refs_4_), channel_id=1, source_target_pairs={{0,32},{32,0},{1,33},{33,1},{2,34},{34,2},{3,35},{35,3},{4,36},{36... | collective-permute-start | bytes 4718600 | tf_op jit(solution)/shard_map/ppermute | solution.py:20
  65.2 0.7 copy-start.5
  65.9 17.1 %collective-permute-start.5 = (bf16[384,1024]{1,0:T(8,128)(2,1)}, bf16[384,1024]{1,0:T(8,128)(2,1)}, u32[]{:S(2)}, u32[]{:S(2)}) collective-permute-start(bf16[384,1024]{1,0:T(8,128)(2,1)} %slice.54), channel_id=1, source_target_pairs={{0,64},{64,128},{128,192},{192,0},{1,65},{65,129},{129,193},{193,1... | collective-permute-start | bytes 2359304 | tf_op jit(solution)/shard_map/ppermute | solution.py:16
  67.0 15.9 %collective-permute-start.7 = (bf16[384,1024]{1,0:T(8,128)(2,1)}, bf16[384,1024]{1,0:T(8,128)(2,1)}, u32[]{:S(2)}, u32[]{:S(2)}) collective-permute-start(bf16[384,1024]{1,0:T(8,128)(2,1)} %slice.55), channel_id=1, source_target_pairs={{0,192},{64,0},{128,64},{192,128},{1,193},{65,1},{129,65},{193,129... | collective-permute-start | bytes 2359304 | tf_op jit(solution)/shard_map/ppermute | solution.py:16
  83.0 12.4 %collective-permute-start.6 = (bf16[384,1024]{1,0:T(8,128)(2,1)}, bf16[384,1024]{1,0:T(8,128)(2,1)}, u32[]{:S(2)}, u32[]{:S(2)}) collective-permute-start(bf16[384,1024]{1,0:T(8,128)(2,1)} %collective-permute-done.5.left.refs_6_), channel_id=1, source_target_pairs={{0,32},{32,0},{1,33},{33,1},{2,34},{34,2},{3,35},{35,3},{4,36},{36... | collective-permute-start | bytes 2359304 | tf_op jit(solution)/shard_map/ppermute | solution.py:20
  83.0 12.4 %collective-permute-start.8 = (bf16[384,1024]{1,0:T(8,128)(2,1)}, bf16[384,1024]{1,0:T(8,128)(2,1)}, u32[]{:S(2)}, u32[]{:S(2)}) collective-permute-start(bf16[384,1024]{1,0:T(8,128)(2,1)} %collective-permute-done.7.right.refs_8_), channel_id=1, source_target_pairs={{0,32},{32,0},{1,33},{33,1},{2,34},{34,2},{3,35},{35,3},{4,36},{36... | collective-permute-start | bytes 2359304 | tf_op jit(solution)/shard_map/ppermute | solution.py:20
  85.4 2.5 %copy-start.7 = (bf16[7,8,96,128]{3,2,1,0:T(8,128)(2,1)}, bf16[7,8,96,128]{3,2,1,0:T(8,128)(2,1)S(1)}, u32[]{:S(2)}) copy-start(bf16[7,8,96,128]{3,2,1,0:T(8,128)(2,1)S(1)} %bitcast_dynamic-update-slice_fusion.1) | copy-start | bytes 4128772
  85.4 55.1 %collective-permute-start.11 = (bf16[8,96,128]{2,1,0:T(8,128)(2,1)}, bf16[8,96,128]{2,1,0:T(8,128)(2,1)}, u32[]{:S(2)}, u32[]{:S(2)}) collective-permute-start(bf16[8,96,128]{2,1,0:T(8,128)(2,1)} %copy-done.9), channel_id=1, source_target_pairs={{0,8},{8,16},{16,24},{24,0},{1,9},{9,17},{17,25},{25,1},{2,10},{10... | collective-permute-start | bytes 589832 | tf_op jit(solution)/shard_map/ppermute | solution.py:16
  101.4 44.1 %collective-permute-start.17 = (bf16[128,2048]{1,0:T(8,128)(2,1)}, bf16[128,2048]{1,0:T(8,128)(2,1)S(1)}, u32[]{:S(2)}, u32[]{:S(2)}) collective-permute-start(bf16[128,2048]{1,0:T(8,128)(2,1)} %get-tuple-element.8.powers.refs_0_), channel_id=1, source_target_pairs={{0,64},{64,128},{128,192},{192,0},{1,65},{65,129},{129,193},{193,1... | collective-permute-start | bytes 1572872 | tf_op jit(solution)/shard_map/ppermute | solution.py:16
  102.5 44.0 %collective-permute-start.19 = (bf16[128,2048]{1,0:T(8,128)(2,1)}, bf16[128,2048]{1,0:T(8,128)(2,1)S(1)}, u32[]{:S(2)}, u32[]{:S(2)}) collective-permute-start(bf16[128,2048]{1,0:T(8,128)(2,1)} %get-tuple-element.8.powers.refs_0_), channel_id=1, source_target_pairs={{0,192},{64,0},{128,64},{192,128},{1,193},{65,1},{129,65},{193,129... | collective-permute-start | bytes 1572872 | tf_op jit(solution)/shard_map/ppermute | solution.py:16
  106.2 20.6 %all-to-all-start.1 = ((f32[32,3,128]{2,1,0:T(4,128)}), f32[32,3,128]{2,1,0:T(4,128)S(1)}, u32[]{:S(2)}, u32[]{:S(2)}) async-start(f32[32,3,128]{2,1,0:T(4,128)} %broadcast_in_dim.12), calls=%async_computation.1 | async-start | bytes 131072 | tf_op jit(solution)/shard_map/all_to_all | solution.py:24
  115.4 11.7 %copy-start.8 = (f32[128,128]{1,0:T(8,128)S(1)}, f32[128,128]{1,0:T(8,128)}, u32[]{:S(2)}) copy-start(f32[128,128]{1,0:T(8,128)} %get-tuple-element.7) | copy-start | bytes 196612
  130.0 19.7 %copy-start.2 = (bf16[128,2048]{1,0:T(8,128)(2,1)S(1)}, bf16[128,2048]{1,0:T(8,128)(2,1)}, u32[]{:S(2)}) copy-start(bf16[128,2048]{1,0:T(8,128)(2,1)} %get-tuple-element.8.powers.refs_0_) | copy-start | bytes 1572868
  130.0 20.6 %copy-start.6 = (bf16[8,96,128]{2,1,0:T(8,128)(2,1)S(1)}, bf16[8,96,128]{2,1,0:T(8,128)(2,1)}, u32[]{:S(2)}) copy-start(bf16[8,96,128]{2,1,0:T(8,128)(2,1)} %copy-done.5) | copy-start | bytes 589828
  130.0 38.1 %all-to-all-start.2 = ((bf16[32,96,128]{2,1,0:T(8,128)(2,1)}), bf16[32,96,128]{2,1,0:T(8,128)(2,1)S(1)}, u32[]{:S(2)}, u32[]{:S(2)}) async-start(bf16[32,96,128]{2,1,0:T(8,128)(2,1)} %bitcast.29), calls=%async_computation.2 | async-start | bytes 1572864 | tf_op jit(solution)/shard_map/all_to_all | solution.py:288
  140.5 1.7 collective-permute-start.12
  142.2 7.5 %collective-permute-start.13 = (f32[2,128]{1,0:T(2,128)S(1)}, f32[2,128]{1,0:T(2,128)S(1)}, u32[]{:S(2)}, u32[]{:S(2)}) collective-permute-start(f32[2,128]{1,0:T(2,128)S(1)} %pad_maximum_fusion.1), channel_id=1, source_target_pairs={{0,64},{64,128},{128,192},{192,0},{1,65},{65,129},{129,193},{193,1... | collective-permute-start | bytes 3080 | tf_op jit(solution)/shard_map/ppermute | solution.py:16
  142.3 7.4 %collective-permute-start.14 = (f32[2,128]{1,0:T(2,128)S(1)}, f32[2,128]{1,0:T(2,128)S(1)}, u32[]{:S(2)}, u32[]{:S(2)}) collective-permute-start(f32[2,128]{1,0:T(2,128)S(1)} %pad_maximum_fusion.1), channel_id=1, source_target_pairs={{0,192},{64,0},{128,64},{192,128},{1,193},{65,1},{129,65},{193,129... | collective-permute-start | bytes 3080 | tf_op jit(solution)/shard_map/ppermute | solution.py:16
  145.5 5.1 %collective-permute-start.15 = (f32[2,128]{1,0:T(2,128)S(1)}, f32[2,128]{1,0:T(2,128)S(1)}, u32[]{:S(2)}, u32[]{:S(2)}) collective-permute-start(f32[2,128]{1,0:T(2,128)S(1)} %pad_maximum_fusion.1), channel_id=1, source_target_pairs={{0,128},{64,192},{128,0},{192,64},{1,129},{65,193},{129,1},{193,65... | collective-permute-start | bytes 3080 | tf_op jit(solution)/shard_map/ppermute | solution.py:16
  145.5 12.9 %copy-start.3 = (bf16[128,2048]{1,0:T(8,128)(2,1)}, bf16[128,2048]{1,0:T(8,128)(2,1)S(1)}, u32[]{:S(2)}) copy-start(bf16[128,2048]{1,0:T(8,128)(2,1)S(1)} %collective-permute-done.17.refs_2_) | copy-start | bytes 1572868
  145.6 9.6 %collective-permute-start.21 = (bf16[128,1024]{1,0:T(8,128)(2,1)S(1)}, bf16[128,1024]{1,0:T(8,128)(2,1)}, u32[]{:S(2)}, u32[]{:S(2)}) collective-permute-start(bf16[128,1024]{1,0:T(8,128)(2,1)S(1)} %slice.65), channel_id=1, source_target_pairs={{0,64},{64,128},{128,192},{192,0},{1,65},{65,129},{129,193},{193,1... | collective-permute-start | bytes 786440 | tf_op jit(solution)/shard_map/ppermute | solution.py:16
  146.5 12.0 %copy-start.4 = (bf16[128,2048]{1,0:T(8,128)(2,1)}, bf16[128,2048]{1,0:T(8,128)(2,1)S(1)}, u32[]{:S(2)}) copy-start(bf16[128,2048]{1,0:T(8,128)(2,1)S(1)} %collective-permute-done.19.refs_4_) | copy-start | bytes 1572868
  146.5 8.7 %collective-permute-start.23 = (bf16[128,1024]{1,0:T(8,128)(2,1)S(1)}, bf16[128,1024]{1,0:T(8,128)(2,1)}, u32[]{:S(2)}, u32[]{:S(2)}) collective-permute-start(bf16[128,1024]{1,0:T(8,128)(2,1)S(1)} %slice.66), channel_id=1, source_target_pairs={{0,192},{64,0},{128,64},{192,128},{1,193},{65,1},{129,65},{193,129... | collective-permute-start | bytes 786440 | tf_op jit(solution)/shard_map/ppermute | solution.py:16
  149.7 10.8 %collective-permute-start.16 = (bf16[128,2048]{1,0:T(8,128)(2,1)S(1)}, bf16[128,2048]{1,0:T(8,128)(2,1)}, u32[]{:S(2)}, u32[]{:S(2)}) collective-permute-start(bf16[128,2048]{1,0:T(8,128)(2,1)S(1)} %copy-done.2), channel_id=1, source_target_pairs={{0,32},{32,0},{1,33},{33,1},{2,34},{34,2},{3,35},{35,3},{4,36},{36... | collective-permute-start | bytes 1572872 | tf_op jit(solution)/shard_map/ppermute | solution.py:20
  149.7 10.8 %collective-permute-start.18 = (bf16[128,2048]{1,0:T(8,128)(2,1)S(1)}, bf16[128,2048]{1,0:T(8,128)(2,1)}, u32[]{:S(2)}, u32[]{:S(2)}) collective-permute-start(bf16[128,2048]{1,0:T(8,128)(2,1)S(1)} %collective-permute-done.17.refs_2_), channel_id=1, source_target_pairs={{0,32},{32,0},{1,33},{33,1},{2,34},{34,2},{3,35},{35,3},{4,36},{36... | collective-permute-start | bytes 1572872 | tf_op jit(solution)/shard_map/ppermute | solution.py:20
  150.6 9.9 %collective-permute-start.20 = (bf16[128,2048]{1,0:T(8,128)(2,1)S(1)}, bf16[128,2048]{1,0:T(8,128)(2,1)}, u32[]{:S(2)}, u32[]{:S(2)}) collective-permute-start(bf16[128,2048]{1,0:T(8,128)(2,1)S(1)} %collective-permute-done.19.refs_4_), channel_id=1, source_target_pairs={{0,32},{32,0},{1,33},{33,1},{2,34},{34,2},{3,35},{35,3},{4,36},{36... | collective-permute-start | bytes 1572872 | tf_op jit(solution)/shard_map/ppermute | solution.py:20
  155.1 5.4 %collective-permute-start.22 = (bf16[128,1024]{1,0:T(8,128)(2,1)}, bf16[128,1024]{1,0:T(8,128)(2,1)}, u32[]{:S(2)}, u32[]{:S(2)}) collective-permute-start(bf16[128,1024]{1,0:T(8,128)(2,1)} %collective-permute-done.21.refs_6_), channel_id=1, source_target_pairs={{0,32},{32,0},{1,33},{33,1},{2,34},{34,2},{3,35},{35,3},{4,36},{36... | collective-permute-start | bytes 786440 | tf_op jit(solution)/shard_map/ppermute | solution.py:20
  155.2 5.3 %collective-permute-start.24 = (bf16[128,1024]{1,0:T(8,128)(2,1)}, bf16[128,1024]{1,0:T(8,128)(2,1)}, u32[]{:S(2)}, u32[]{:S(2)}) collective-permute-start(bf16[128,1024]{1,0:T(8,128)(2,1)} %collective-permute-done.23.refs_8_), channel_id=1, source_target_pairs={{0,32},{32,0},{1,33},{33,1},{2,34},{34,2},{3,35},{35,3},{4,36},{36... | collective-permute-start | bytes 786440 | tf_op jit(solution)/shard_map/ppermute | solution.py:20
where the time goes:
time: 171 us; the launch traced here: 169 us
  starting transfers between devices  55.1 us (32%)
  waiting for transfers between devices  35.9 us (21%)
  Pallas kernels  32.5 us (19%)
  local copies, waits for them, and re-layouts  23.3 us (14%)
  blocking collectives  16.3 us (10%)
  other arithmetic  4.89 us (3%)
    pallas_call x4, Pallas kernels, call(): pl.pallas_call(kernel, grid_spec=pltpu.PrefetchScalarGridSpec(num_scalar_...  32.5 us
    ppermute x14, starting transfers between devices, shift(): return lax.ppermute(a, axis, [(i, (i + s) % n) for i in range(n)])  22.5 us
    all_to_all x2, starting transfers between devices, from_everyone(): lax.all_to_all(jnp.broadcast_to(a[None], (n, *a.shape)), axis, 0, 0, tile...  20.6 us
    all_to_all x2, waiting for transfers between devices, from_everyone(): lax.all_to_all(jnp.broadcast_to(a[None], (n, *a.shape)), axis, 0, 0, tile...  19.9 us
    all_to_all x1, blocking collectives, step(): lax.all_to_all(jnp.concatenate([wanted, digits], axis=1), ('x', 'core'),...  16.3 us
    ppermute x14, waiting for transfers between devices, shift(): return lax.ppermute(a, axis, [(i, (i + s) % n) for i in range(n)])  16 us
    all_to_all x1, starting transfers between devices, step(): lax.all_to_all(terms.reshape(NY * NZ, part, tokens), ('y', 'z'), 0, 0, ti...  9.92 us
    unnamed x28, local copies, waits for them, and re-layouts  5.65 us
  transfers between devices with their start and end apart: 28, of which 6 were waited for; matrix products, arithmetic and copies ran while one was open for 15% of the time, Pallas kernels for 19%

commit v1 on v0

--- a/solution.py
+++ b/solution.py
@@ -63,29 +63,44 @@
 
 
 def near_kernel(who, states, *refs):
-    acc = None
-    for k, ref in enumerate(refs[:-1]):
-        term = dot(states[who[k]], ref[...])
-        acc = term if acc is None else acc + term
-    refs[-1][...] = acc
-
-
-def near_logits(states, arrays, who):
-    rows, width = arrays[0].shape
+    *arrays, out = refs
+    first = pl.program_id(0) < STEPS // 2
+
+    def total(chosen):
+        acc = None
+        for k, ref in enumerate(chosen):
+            term = dot(states[who[k]], ref[...])
+            acc = term if acc is None else acc + term
+        return acc
+
+    @pl.when(first)
+    def _():
+        out[...] = total(arrays[:6])
+
+    @pl.when(~first)
+    def _():
+        out[...] = total(arrays[:2] + arrays[6:])
+
+
+def near_logits(states, own, left, right, who):
+    rows, width = own[0].shape
     tokens = states.shape[1]
     wide = width // STEPS
+    specs = [whole(states)] + [pl.BlockSpec((rows, wide), lambda j, s: (0, j))] * 2
+    specs += [pl.BlockSpec((rows, wide), lambda j, s: (0, early(j)))] * 4
+    specs += [pl.BlockSpec((rows, wide), lambda j, s: (0, late(j)))] * 4
     return call(
         near_kernel,
         who,
-        [states, *arrays],
-        [whole(states)] + [pl.BlockSpec((rows, wide), lambda j, s: (0, j))] * len(arrays),
+        [states, *own, *left, *right],
+        specs,
         pl.BlockSpec((tokens, wide), lambda j, s: (0, j)),
         jax.ShapeDtypeStruct((tokens, width), F32),
-        2 * tokens * rows * width * len(arrays),
-    )
-
-
-def far_kernel(who, states, labels, near, left, left_other, right, right_other, powers, stats, logits):
+        12 * tokens * rows * width,
+    )
+
+
+def far_kernel(who, mine_states, other_states, labels, near, left, left_other, right, right_other, powers, stats, logits):
     step = pl.program_id(0)
     first = step < STEPS // 2
     wide = near.shape[1]
@@ -94,7 +109,7 @@
         @pl.when(here)
         def _():
             logits[:, pl.ds(pl.multiple_of(step * wide, wide), wide)] = (
-                near[...] + dot(states[who[0]], mine[...]) + dot(states[who[1]], theirs[...])
+                near[...] + dot(mine_states[0], mine[...]) + dot(other_states[0], theirs[...])
             )
 
     @pl.when(step == STEPS - 1)
@@ -107,20 +122,23 @@
         total = jnp.sum(shifted, axis=1, keepdims=True)
         target = jnp.sum(jnp.where(hits, values, 0.0), axis=1, keepdims=True)
         powers[...] = shifted.astype(BF)
-        lanes = lax.broadcasted_iota(jnp.int32, stats.shape, 1)
-        stats[...] = jnp.where(lanes == 0, peak, jnp.where(lanes == 1, total, target))
+        tokens = values.shape[0]
+        lanes = lax.broadcasted_iota(jnp.int32, (tokens, 128), 1)
+        both = jnp.where(lanes == 0, peak, jnp.where(lanes == 1, total, target))
+        stats[...] = both.T[:8]
 
 
 def far_logits(states, labels, near, left, right, who):
     tokens, width = near.shape
     wide = width // STEPS
     rows = left[0].shape[0]
-    args = [states, labels, near, *left, *right]
-    specs = [whole(states), whole(labels), pl.BlockSpec((tokens, wide), lambda j, s: (0, j))]
+    args = [states, states, labels, near, *left, *right]
+    specs = [pl.BlockSpec((1, tokens, rows), lambda j, s, k=k: (s[k], 0, 0)) for k in (0, 1)]
+    specs += [whole(labels), pl.BlockSpec((tokens, wide), lambda j, s: (0, j))]
     specs += [pl.BlockSpec((rows, wide), lambda j, s: (0, early(j)))] * 2
     specs += [pl.BlockSpec((rows, wide), lambda j, s: (0, late(j)))] * 2
     powers = jax.ShapeDtypeStruct((tokens, width), BF)
-    stats = jax.ShapeDtypeStruct((tokens, 128), F32)
+    stats = jax.ShapeDtypeStruct((8, 128), F32)
     return call(
         far_kernel,
         who,
@@ -145,24 +163,22 @@
         columns = starts[8] + lax.broadcasted_iota(jnp.int32, (width, tokens), 0)
         both[:, tokens:] = jnp.where(columns == labels[...], 1.0, 0.0).astype(BF)
 
-    def put(k, term):
-        rows = term.shape[0]
+    half = width // 2
+    own, left, right = arrays[:2], arrays[2:8], arrays[8:]
+    lefts = jnp.concatenate([a[:, :half] for a in own] + [a[...] for a in left], axis=0)
+    rights = jnp.concatenate([a[:, half:] for a in own] + [a[...] for a in right], axis=0)
+    term = dot(lefts, both[:half, :]) + dot(rights, both[half:, :])
+    rows = own[0].shape[0]
+    for k in range(8):
         at = pl.ds(pl.multiple_of(starts[k] + step * rows, 32), rows)
-        sums[at, :] = term[:, :tokens]
-        picks[at, :] = term[:, tokens:].astype(BF)
-
-    for k in range(6):
-        put(k, dot(arrays[k][...], both[...]))
-    half = width // 2
-    for k in range(2):
-        left, right = arrays[6 + k], arrays[8 + k]
-        put(6 + k, dot(left[...], both[:half, :]) + dot(right[...], both[half:, :]))
-
-
-def state_terms(powers, labels, near, left, right, starts, depth):
+        sums[at, :] = term[k * rows : (k + 1) * rows, :tokens]
+        picks[at, :] = term[k * rows : (k + 1) * rows, tokens:].astype(BF)
+
+
+def state_terms(powers, labels, own, left, right, starts, depth):
     tokens, width = powers.shape
-    rows = near[0].shape[0] // STEPS
-    args = [powers, labels, *near, *left, *right]
+    rows = own[0].shape[0] // STEPS
+    args = [powers, labels, *own, *left, *right]
     specs = [whole(powers), whole(labels)]
     specs += [pl.BlockSpec((rows, a.shape[1]), lambda j, s: (j, 0)) for a in args[2:]]
     sums = jax.ShapeDtypeStruct((depth, tokens), F32)
@@ -179,11 +195,19 @@
     )
 
 
-def grad_kernel(who, states, scales, labels, *refs):
-    *arrays, out = refs
+def grad_kernel(who, p0, p1, p2, p3, scales, labels, *refs):
+    *arrays, out, states = refs
     step = pl.program_id(0)
-    tokens = states.shape[2]
+    groups, part, tokens = p0.shape
     wide = out.shape[1]
+
+    @pl.when(step == 0)
+    def _():
+        for j, parts in enumerate((p0, p1, p2, p3)):
+            at = pl.multiple_of(((who[9] + j) % NY) * part, 32)
+            for k in range(groups):
+                states[k, pl.ds(at, part), :] = parts[k]
+
     columns = who[8] + step * wide + lax.broadcasted_iota(jnp.int32, (tokens, wide), 1)
     blocks = [a[...] for a in arrays[:6]]
     first = step < STEPS // 2
@@ -202,12 +226,13 @@
     out[...] = acc
 
 
-def head_grad_of(states, scales, labels, near, left, right, who):
-    groups, rows, tokens = states.shape
+def head_grad_of(parts, scales, labels, near, left, right, who):
+    groups, part, tokens = parts[0].shape
+    rows = NY * part
     width = near[0].shape[1]
     wide = width // STEPS
-    args = [states, scales, labels, *near, *left, *right]
-    specs = [whole(states), whole(scales), whole(labels)]
+    args = [*parts, scales, labels, *near, *left, *right]
+    specs = [whole(a) for a in args[:6]]
     specs += [pl.BlockSpec((tokens, wide), lambda j, s: (0, j))] * 6
     specs += [pl.BlockSpec((tokens, wide), lambda j, s: (0, early(j)))] * 2
     specs += [pl.BlockSpec((tokens, wide), lambda j, s: (0, late(j)))] * 2
@@ -219,6 +244,7 @@
         pl.BlockSpec((rows, wide), lambda j, s: (0, j)),
         jax.ShapeDtypeStruct((rows, width), F32),
         2 * groups * tokens * rows * width,
+        [pltpu.VMEM((groups, rows, tokens), BF)],
     )
 
 
@@ -235,35 +261,46 @@
         chip = ((x + offset) % NX) * 2
         return [chip + core, chip + 1 - core]
 
-    up = shift(head, "x", NX, 1)
-    down = shift(head, "x", NX, -1)
-    partner = swap(head)
-    far_left = shift(up[:, :half], "x", NX, 1)
-    far_right = shift(down[:, half:], "x", NX, -1)
-    near = [head, partner, up, swap(up), down, swap(down)]
-    left = [far_left, swap(far_left)]
-    right = [far_right, swap(far_right)]
-
-    features = from_everyone(hidden_states.T, ("y", "z"), NY * NZ)
-    flat = jnp.swapaxes(features.reshape(8, rows, tokens), 1, 2)
-
-    wanted = lax.dynamic_index_in_dim(
-        features.reshape(8, NY, part, tokens), y, 1, keepdims=False
-    )
+    up_left = shift(head[:, :half], "x", NX, 1)
+    down_right = shift(head[:, half:], "x", NX, -1)
+    up_right = shift(head[:, half:], "x", NX, 1)
+    down_left = shift(head[:, :half], "x", NX, -1)
+    own = [head, swap(head)]
+    far_left = shift(up_left, "x", NX, 1)
+    far_right = shift(down_right, "x", NX, -1)
+    left = [up_left, swap(up_left), down_left, swap(down_left)]
+    right = [up_right, swap(up_right), down_right, swap(down_right)]
+    away_left = [far_left, swap(far_left)]
+    away_right = [far_right, swap(far_right)]
+
+    row = from_everyone(hidden_states.T, "z", NZ)
+    parts = [row] + [shift(row, "y", NY, -j) for j in (1, 2, 3)]
+    flat = jnp.stack(parts).reshape(8, rows, tokens)
+    flat = jnp.swapaxes(flat, 1, 2)
+
+    def block(offset):
+        chip = ((x + offset - y) % NY) * 2
+        return [chip + core, chip + 1 - core]
+
+    picked = [
+        lax.dynamic_index_in_dim(p.reshape(2, NY, part, tokens), y, 1, keepdims=False)
+        for p in parts
+    ]
+    wanted = ordered(picked, y).reshape(8, part, tokens)
     digits = jnp.stack([labels // 256, labels % 256]).astype(BF)
     digits = jnp.broadcast_to(jnp.pad(digits, ((0, 14), (0, 0)))[None], (8, 16, tokens))
     wanted = lax.all_to_all(
         jnp.concatenate([wanted, digits], axis=1), ("x", "core"), 0, 0, tiled=True
     )
+    far_states, wanted = lax.optimization_barrier((flat, wanted))
     digits = wanted[:, part : part + 2].astype(jnp.int32)
     all_labels = (digits[:, 0] * 256 + digits[:, 1]).reshape(8 * tokens, 1)
     wanted = wanted[:, :part]
 
-    logits = near_logits(flat, near, who(0) + who(3) + who(1))
+    logits = near_logits(flat, own, left, right, block(0) + block(3) + block(1))
     powers, stats = far_logits(
-        flat, labels[:, None], logits, left, right, who(2) + [base]
-    )
-    stats = stats.T[:3]
+        far_states, labels[:, None], logits, away_left, away_right, block(2) + [base]
+    )
 
     pow_up = shift(powers, "x", NX, 1)
     pow_down = shift(powers, "x", NX, -1)
@@ -273,10 +310,10 @@
     pow_left = [pow_left, swap(pow_left)]
     pow_right = [pow_right, swap(pow_right)]
 
-    parts = from_everyone(stats, ("y", "z"), NY * NZ)
+    parts = from_everyone(stats[:3], ("y", "z"), NY * NZ)
     starts = [w * rows for w in who(0) + who(3) + who(1) + who(2)]
     sums, picks = state_terms(
-        powers, labels[None], near, left, right, starts + [base], depth
+        powers, labels[None], own, left + away_left, right + away_right, starts + [base], depth
     )
     peak = jnp.max(parts[:, 0], axis=0)
     total = jnp.sum(parts[:, 1] * jnp.exp(parts[:, 0] - peak), axis=0)
@@ -290,8 +327,7 @@
     )
     state_grad = arrived.astype(F32).sum(axis=0).astype(BF).T
 
-    slices = ordered([wanted] + [shift(wanted, "y", NY, -j) for j in (1, 2, 3)], y)
-    slices = jnp.swapaxes(slices, 0, 1).reshape(8, rows, tokens)
+    slices = [wanted] + [shift(wanted, "y", NY, -j) for j in (1, 2, 3)]
     scale = jnp.stack([scale, swap(scale)])
     scales = [scale] + [shift(scale, "x", NX, s) for s in (1, -1, 2)]
     scales = jnp.concatenate(scales).reshape(8 * tokens, 1)
@@ -302,7 +338,7 @@
         pow_near,
         pow_left,
         pow_right,
-        who(0) + who(3) + who(1) + who(2) + [base],
+        who(0) + who(3) + who(1) + who(2) + [base, y],
     )
     return (token_loss, state_grad, head_grad)
 

time: 171 us -> 184 us (1.076); the launches traced: 169 us -> 180 us
  blocking collectives: 16.3 us -> 0 us
  waiting for transfers between devices: 35.9 us -> 51.7 us
  starting transfers between devices: 55.1 us -> 67.6 us
  other arithmetic: 4.89 us -> 8.72 us
  local copies, waits for them, and re-layouts: 23.3 us -> 19.9 us
    ppermute x14 -> x19, waiting for transfers between devices: 16 us -> 46.2 us  [shift(): return lax.ppermute(a, axis, [(i, (i + s) % n) for i in range(n)])]
    all_to_all x2, waiting for transfers between devices: 19.9 us -> 1.46 us  [from_everyone(): lax.all_to_all(jnp.broadcast_to(a[None], (n, *a.shape)), axis, 0, 0, tile...]
    all_to_all x1 -> x0, blocking collectives: 16.3 us -> none  [step(): lax.all_to_all(jnp.concatenate([wanted, digits], axis=1), ('x', 'core'),...]
    ppermute x14 -> x19, starting transfers between devices: 22.5 us -> 31 us  [shift(): return lax.ppermute(a, axis, [(i, (i + s) % n) for i in range(n)])]
    all_to_all x0 -> x1, starting transfers between devices: none -> 4.21 us  [step(): lax.all_to_all(jnp.concatenate([wanted, digits], axis=1), ('x', 'core'),...]
    all_to_all x0 -> x1, waiting for transfers between devices: none -> 4.01 us  [step(): lax.all_to_all(jnp.concatenate([wanted, digits], axis=1), ('x', 'core'),...]
    transpose x2 -> x0, local copies, waits for them, and re-layouts: 2.14 us -> none  [step(): slices = jnp.swapaxes(slices, 0, 1).reshape(8, rows, tokens)]
    unnamed x28 -> x34, local copies, waits for them, and re-layouts: 5.65 us -> 5.22 us
  transfers between devices with their start and end apart: 28 -> 36, of which waited for: 6 -> 14; matrix products, arithmetic and copies ran while one was open for 15% -> 10% of each run, Pallas kernels for 19% -> 14%
where the time goes in v1:
time: 184 us; the launch traced here: 180 us
  starting transfers between devices  67.6 us (37%)
  waiting for transfers between devices  51.7 us (28%)
  Pallas kernels  30.9 us (17%)
  local copies, waits for them, and re-layouts  19.9 us (11%)
  other arithmetic  8.72 us (5%)
    ppermute x19, waiting for transfers between devices, shift(): return lax.ppermute(a, axis, [(i, (i + s) % n) for i in range(n)])  46.2 us
    ppermute x19, starting transfers between devices, shift(): return lax.ppermute(a, axis, [(i, (i + s) % n) for i in range(n)])  31 us
    pallas_call x4, Pallas kernels, call(): pl.pallas_call(kernel, grid_spec=pltpu.PrefetchScalarGridSpec(num_scalar_...  30.9 us
    all_to_all x2, starting transfers between devices, from_everyone(): lax.all_to_all(jnp.broadcast_to(a[None], (n, *a.shape)), axis, 0, 0, tile...  20.3 us
    all_to_all x1, starting transfers between devices, step(): lax.all_to_all(terms.reshape(NY * NZ, part, tokens), ('y', 'z'), 0, 0, ti...  9.92 us
    unnamed x34, local copies, waits for them, and re-layouts  5.22 us
    all_to_all x1, starting transfers between devices, step(): lax.all_to_all(jnp.concatenate([wanted, digits], axis=1), ('x', 'core'),...  4.21 us
    all_to_all x1, waiting for transfers between devices, step(): lax.all_to_all(jnp.concatenate([wanted, digits], axis=1), ('x', 'core'),...  4.01 us
  transfers between devices with their start and end apart: 36, of which 14 were waited for; matrix products, arithmetic and copies ran while one was open for 10% of the time, Pallas kernels for 14%

profile of v1, /device:TPU:32, one launch (start us, length us, event | category | flops | bytes accessed | tf_op | source)
XLA Modules:
  0.0 179.9 jit_solution(13497611180568284262)
XLA Ops:
  0.6 1.4 broadcast_in_dim.10
  2.1 8.6 %all-to-all-start = ((bf16[8,96,128]{2,1,0:T(8,128)(2,1)}), bf16[8,96,128]{2,1,0:T(8,128)(2,1)S(1)}, u32[]{:S(2)}, u32[]{:S(2)}) async-start(bf16[8,96,128]{2,1,0:T(8,128)(2,1)} %broadcast_in_dim.10), calls=%async_computation | async-start | bytes 393216 | tf_op jit(solution)/shard_map/all_to_all | solution.py:24
  10.7 2.8 %fusion.9 = (bf16[384,1024]{1,0:T(8,128)(2,1)}, bf16[384,1024]{1,0:T(8,128)(2,1)}) fusion(bf16[384,2048]{1,0:T(8,128)(2,1)} %refs_0_.3), kind=kLoop, calls=%fused_computation.37 | loop fusion | bytes 3145728 | tf_op jit(solution)/shard_map/slice | solution.py:266
  13.4 1.5 collective-permute-start.4
  14.9 1.7 collective-permute-start.6
  16.7 1.5 collective-permute-start.10
  18.2 1.5 all-to-all-done
  19.7 1.6 collective-permute-start.2
  21.2 5.7 %collective-permute-done.2 = bf16[8,96,128]{2,1,0:T(8,128)(2,1)} collective-permute-done((bf16[8,96,128]{2,1,0:T(8,128)(2,1)S(1)}, bf16[8,96,128]{2,1,0:T(8,128)(2,1)}, u32[]{:S(2)}, u32[]{:S(2)}) %collective-permute-start.2) | collective-permute-done | bytes 196640 | tf_op jit(solution)/shard_map/ppermute | solution.py:16
  26.9 1.9 %collective-permute-start.1 = (bf16[8,96,128]{2,1,0:T(8,128)(2,1)S(1)}, bf16[8,96,128]{2,1,0:T(8,128)(2,1)S(1)}, u32[]{:S(2)}, u32[]{:S(2)}) collective-permute-start(bf16[8,96,128]{2,1,0:T(8,128)(2,1)S(1)} %all-to-all-done), channel_id=1, source_target_pairs={{0,16},{8,24},{16,0},{24,8},{1,17},{9,25},{17,1},{25,9},{2,18},{10... | collective-permute-start | bytes 589832 | tf_op jit(solution)/shard_map/ppermute | solution.py:16
  28.8 5.3 %collective-permute-done.1 = bf16[8,96,128]{2,1,0:T(8,128)(2,1)S(1)} collective-permute-done((bf16[8,96,128]{2,1,0:T(8,128)(2,1)S(1)}, bf16[8,96,128]{2,1,0:T(8,128)(2,1)S(1)}, u32[]{:S(2)}, u32[]{:S(2)}) %collective-permute-start.1) | collective-permute-done | bytes 196640 | tf_op jit(solution)/shard_map/ppermute | solution.py:16
  34.1 1.7 collective-permute-start
  35.8 3.9 %collective-permute-done = bf16[8,96,128]{2,1,0:T(8,128)(2,1)S(1)} collective-permute-done((bf16[8,96,128]{2,1,0:T(8,128)(2,1)S(1)}, bf16[8,96,128]{2,1,0:T(8,128)(2,1)S(1)}, u32[]{:S(2)}, u32[]{:S(2)}) %collective-permute-start) | collective-permute-done | bytes 196640 | tf_op jit(solution)/shard_map/ppermute | solution.py:16
  40.4 1.4 collective-permute-start.8
  41.8 2.2 %collective-permute-start.12 = (bf16[384,1024]{1,0:T(8,128)(2,1)}, bf16[384,1024]{1,0:T(8,128)(2,1)}, u32[]{:S(2)}, u32[]{:S(2)}) collective-permute-start(bf16[384,1024]{1,0:T(8,128)(2,1)} %collective-permute-done.4.refs_2_), channel_id=1, source_target_pairs={{0,64},{64,128},{128,192},{192,0},{1,65},{65,129},{129,193},{193,1... | collective-permute-start | bytes 2359304 | tf_op jit(solution)/shard_map/ppermute | solution.py:16
  44.0 6.5 %collective-permute-done.10.refs_8_.refs_10_ = bf16[384,1024]{1,0:T(8,128)(2,1)} collective-permute-done((bf16[384,1024]{1,0:T(8,128)(2,1)}, bf16[384,1024]{1,0:T(8,128)(2,1)}, u32[]{:S(2)}, u32[]{:S(2)}) %collective-permute-start.10) | collective-permute-done | bytes 786464 | tf_op jit(solution)/shard_map/ppermute | solution.py:16
  50.5 3.0 %collective-permute-start.14 = (bf16[384,1024]{1,0:T(8,128)(2,1)}, bf16[384,1024]{1,0:T(8,128)(2,1)}, u32[]{:S(2)}, u32[]{:S(2)}) collective-permute-start(bf16[384,1024]{1,0:T(8,128)(2,1)} %collective-permute-done.10.refs_8_.refs_10_), channel_id=1, source_target_pairs={{0,192},{64,0},{128,64},{192,128},{1,193},{65,1},{129,65},{193,129... | collective-permute-start | bytes 2359304 | tf_op jit(solution)/shard_map/ppermute | solution.py:16
  55.7 0.8 bitcast_dynamic-update-slice_fusion.3
  56.5 0.8 bitcast_dynamic-update-slice_fusion
  57.4 5.0 %collective-permute-done.8.refs_6_.refs_8_ = bf16[384,1024]{1,0:T(8,128)(2,1)} collective-permute-done((bf16[384,1024]{1,0:T(8,128)(2,1)}, bf16[384,1024]{1,0:T(8,128)(2,1)}, u32[]{:S(2)}, u32[]{:S(2)}) %collective-permute-start.8) | collective-permute-done | bytes 786464 | tf_op jit(solution)/shard_map/ppermute | solution.py:16
  63.0 11.6 %collective-permute-done.12.left.refs_6_ = bf16[384,1024]{1,0:T(8,128)(2,1)} collective-permute-done((bf16[384,1024]{1,0:T(8,128)(2,1)}, bf16[384,1024]{1,0:T(8,128)(2,1)}, u32[]{:S(2)}, u32[]{:S(2)}) %collective-permute-start.12) | collective-permute-done | bytes 786464 | tf_op jit(solution)/shard_map/ppermute | solution.py:16
  75.1 0.8 bitcast_dynamic-update-slice_fusion.4
  76.7 4.2 %all-to-all-start.1 = ((bf16[8,112,128]{2,1,0:T(8,128)(2,1)}), bf16[8,112,128]{2,1,0:T(8,128)(2,1)}, u32[]{:S(2)}, u32[]{:S(2)}) async-start(bf16[8,112,128]{2,1,0:T(8,128)(2,1)} %pad_maximum_fusion.1), calls=%async_computation.1 | async-start | bytes 458752 | tf_op jit(solution)/shard_map/all_to_all | solution.py:292
  81.6 1.1 pad_maximum_fusion
  82.7 1.2 copy.17
  83.9 4.0 %all-to-all-done.1 = bf16[8,112,128]{2,1,0:T(8,128)(2,1)} async-done(((bf16[8,112,128]{2,1,0:T(8,128)(2,1)}), bf16[8,112,128]{2,1,0:T(8,128)(2,1)}, u32[]{:S(2)}, u32[]{:S(2)}) %all-to-all-start.1) | async-done | bytes 229408 | tf_op jit(solution)/shard_map/all_to_all | solution.py:292
  87.9 0.9 copy-done.2
  88.8 7.8 %shard_map.58.near = f32[128,2048]{1,0:T(8,128)} custom-call(s32[6]{0:T(128)} %stack.167.who, bf16[8,128,384]{2,1,0:T(8,128)(2,1)} %bitcast.82, bf16[384,2048]{1,0:T(8,128)(2,1)} %refs_0_.3, bf16[384,2048]{1,0:T(8,128)(2,1)} %copy-done.1, bf16[384,1024]{1,0:T(8,128)(2,1)} %collective-permute-done.4.refs_2_, ...), custom_call_target="tpu_custom_call" | custom-call | flops 1207959552 | bytes 4718592 | tf_op jit(solution)/shard_map/pallas_call | solution.py:51
  96.7 5.9 %shard_map.59 = (bf16[128,2048]{1,0:T(8,128)(2,1)}, f32[8,128]{1,0:T(8,128)}) custom-call(s32[3]{0:T(128)} %pad_add_fusion.who, bf16[8,128,384]{2,1,0:T(8,128)(2,1)} %bitcast.83, bf16[8,128,384]{2,1,0:T(8,128)(2,1)} %bitcast.84, s32[128,1]{1,0:T(8,128)} %copy.18.labels, f32[128,2048]{1,0:T(8,128)} %shard_map.58.near, ...), custom_call_target="tpu_custom_call" | custom-call | flops 402653184 | bytes 1572864 | tf_op jit(solution)/shard_map/pallas_call | solution.py:51
  103.8 11.7 %all-to-all-start.2 = ((f32[32,3,128]{2,1,0:T(4,128)}), f32[32,3,128]{2,1,0:T(4,128)S(1)}, u32[]{:S(2)}, u32[]{:S(2)}) async-start(f32[32,3,128]{2,1,0:T(4,128)} %broadcast_in_dim.13), calls=%async_computation.2 | async-start | bytes 131072 | tf_op jit(solution)/shard_map/all_to_all | solution.py:24
  115.5 9.7 %shard_map.60 = (f32[3072,128]{1,0:T(8,128)}, bf16[3072,128]{1,0:T(8,128)(2,1)}) custom-call(s32[9]{0:T(128)} %stack.176.starts, bf16[128,2048]{1,0:T(8,128)(2,1)} %get-tuple-element.11.powers.refs_0_, s32[1,128]{1,0:T(1,128)} %bitcast.106, bf16[384,2048]{1,0:T(8,128)(2,1)} %refs_0_.3, bf16[384,2048]{1,0:T(8,128)(2,1)} %copy-done.1, ...), custom_call_target="tpu_custom_call" | custom-call | flops 3221225472 | bytes 12582912 | tf_op jit(solution)/shard_map/pallas_call | solution.py:51
  126.0 2.8 %subtract_convert_fusion = bf16[3072,128]{1,0:T(8,128)(2,1)} fusion(bf16[3072,128]{1,0:T(8,128)(2,1)} %get-tuple-element.13, f32[3072,128]{1,0:T(8,128)} %get-tuple-element.12, f32[128]{0:T(128)S(1)} %bitcast.103), kind=kLoop, calls=%fused_computation | loop fusion | flops 1572864 | bytes 3146240 | tf_op jit(solution)/shard_map/convert_element_type | solution.py:324
  128.7 9.9 %all-to-all-start.3 = ((bf16[32,96,128]{2,1,0:T(8,128)(2,1)}), bf16[32,96,128]{2,1,0:T(8,128)(2,1)S(1)}, u32[]{:S(2)}, u32[]{:S(2)}) async-start(bf16[32,96,128]{2,1,0:T(8,128)(2,1)} %bitcast.44), calls=%async_computation.3 | async-start | bytes 1572864 | tf_op jit(solution)/shard_map/all_to_all | solution.py:325
  139.3 2.7 %collective-permute-start.26 = (bf16[128,2048]{1,0:T(8,128)(2,1)S(1)}, bf16[128,2048]{1,0:T(8,128)(2,1)S(1)}, u32[]{:S(2)}, u32[]{:S(2)}) collective-permute-start(bf16[128,2048]{1,0:T(8,128)(2,1)S(1)} %copy-done.3), channel_id=1, source_target_pairs={{0,192},{64,0},{128,64},{192,128},{1,193},{65,1},{129,65},{193,129... | collective-permute-start | bytes 1572872 | tf_op jit(solution)/shard_map/ppermute | solution.py:16
  142.0 0.9 slice.49.p0
  142.9 2.8 %collective-permute-start.16 = (bf16[8,96,128]{2,1,0:T(8,128)(2,1)S(1)}, bf16[8,96,128]{2,1,0:T(8,128)(2,1)S(1)}, u32[]{:S(2)}, u32[]{:S(2)}) collective-permute-start(bf16[8,96,128]{2,1,0:T(8,128)(2,1)S(1)} %slice.49.p0), channel_id=1, source_target_pairs={{0,24},{8,0},{16,8},{24,16},{1,25},{9,1},{17,9},{25,17},{2,26},{10... | collective-permute-start | bytes 589832 | tf_op jit(solution)/shard_map/ppermute | solution.py:16
  145.7 0.8 collective-permute-start.17
  146.6 0.9 collective-permute-start.18
  147.4 1.2 fusion.7
  148.6 3.5 %collective-permute-done.24.refs_2_ = bf16[128,2048]{1,0:T(8,128)(2,1)S(1)} collective-permute-done((bf16[128,2048]{1,0:T(8,128)(2,1)S(1)}, bf16[128,2048]{1,0:T(8,128)(2,1)S(1)}, u32[]{:S(2)}, u32[]{:S(2)}) %collective-permute-start.24) | collective-permute-done | bytes 524320 | tf_op jit(solution)/shard_map/ppermute | solution.py:16
  152.2 0.8 slice.60
  153.8 3.2 %collective-permute-start.30 = (bf16[128,1024]{1,0:T(8,128)(2,1)}, bf16[128,1024]{1,0:T(8,128)(2,1)}, u32[]{:S(2)}, u32[]{:S(2)}) collective-permute-start(bf16[128,1024]{1,0:T(8,128)(2,1)} %slice.61), channel_id=1, source_target_pairs={{0,192},{64,0},{128,64},{192,128},{1,193},{65,1},{129,65},{193,129... | collective-permute-start | bytes 786440 | tf_op jit(solution)/shard_map/ppermute | solution.py:16
  157.5 3.2 %collective-permute-start.21 = (f32[2,128]{1,0:T(2,128)S(1)}, f32[2,128]{1,0:T(2,128)}, u32[]{:S(2)}, u32[]{:S(2)}) collective-permute-start(f32[2,128]{1,0:T(2,128)S(1)} %pad_maximum_fusion.2), channel_id=1, source_target_pairs={{0,192},{64,0},{128,64},{192,128},{1,193},{65,1},{129,65},{193,129... | collective-permute-start | bytes 3080 | tf_op jit(solution)/shard_map/ppermute | solution.py:16
  161.6 1.6 collective-permute-done.20
  163.6 2.4 %collective-permute-done.22 = f32[2,128]{1,0:T(2,128)} collective-permute-done((f32[2,128]{1,0:T(2,128)S(1)}, f32[2,128]{1,0:T(2,128)}, u32[]{:S(2)}, u32[]{:S(2)}) %collective-permute-start.22) | collective-permute-done | bytes 1056 | tf_op jit(solution)/shard_map/ppermute | solution.py:16
  168.0 1.0 copy.23.labels
  169.7 1.0 copy.22.scales
  171.6 7.6 %shard_map.61 = f32[384,2048]{1,0:T(8,128)} custom-call(s32[10]{0:T(128)} %stack.186.who, bf16[8,96,128]{2,1,0:T(8,128)(2,1)} %copy-done.6, bf16[8,96,128]{2,1,0:T(8,128)(2,1)} %copy-done.10, bf16[8,96,128]{2,1,0:T(8,128)(2,1)} %copy-done.11, bf16[8,96,128]{2,1,0:T(8,128)(2,1)} %copy-done.12, f32[1024,1]{1,0:T(8,128)} %copy.22.scales, ...), custom_call_target="tpu_custom_call" | custom-call | flops 1610612736 | bytes 6291456 | tf_op jit(solution)/shard_map/pallas_call | solution.py:51
  (96 shorter events, 14.9 us)
Async XLA Ops:
  2.1 17.6 %all-to-all-start = ((bf16[8,96,128]{2,1,0:T(8,128)(2,1)}), bf16[8,96,128]{2,1,0:T(8,128)(2,1)S(1)}, u32[]{:S(2)}, u32[]{:S(2)}) async-start(bf16[8,96,128]{2,1,0:T(8,128)(2,1)} %broadcast_in_dim.10), calls=%async_computation | async-start | bytes 393216 | tf_op jit(solution)/shard_map/all_to_all | solution.py:24
  10.6 7.6 %copy-start = (bf16[384,2048]{1,0:T(8,128)(2,1)S(1)}, bf16[384,2048]{1,0:T(8,128)(2,1)}, u32[]{:S(2)}) copy-start(bf16[384,2048]{1,0:T(8,128)(2,1)} %refs_0_.3) | copy-start | bytes 4718596
  10.7 42.8 %copy-start.13 = (s32[128]{0:T(128)S(1)}, s32[128]{0:T(128)}, u32[]{:S(2)}) copy-start(s32[128]{0:T(128)} %param.5) | copy-start | bytes 1540
  13.4 28.4 %collective-permute-start.4 = (bf16[384,1024]{1,0:T(8,128)(2,1)}, bf16[384,1024]{1,0:T(8,128)(2,1)}, u32[]{:S(2)}, u32[]{:S(2)}) collective-permute-start(bf16[384,1024]{1,0:T(8,128)(2,1)} %get-tuple-element.16), channel_id=1, source_target_pairs={{0,64},{64,128},{128,192},{192,0},{1,65},{65,129},{129,193},{193,1... | collective-permute-start | bytes 2359304 | tf_op jit(solution)/shard_map/ppermute | solution.py:16
  14.9 26.9 %collective-permute-start.6 = (bf16[384,1024]{1,0:T(8,128)(2,1)}, bf16[384,1024]{1,0:T(8,128)(2,1)}, u32[]{:S(2)}, u32[]{:S(2)}) collective-permute-start(bf16[384,1024]{1,0:T(8,128)(2,1)} %get-tuple-element.16), channel_id=1, source_target_pairs={{0,192},{64,0},{128,64},{192,128},{1,193},{65,1},{129,65},{193,129... | collective-permute-start | bytes 2359304 | tf_op jit(solution)/shard_map/ppermute | solution.py:16
  16.7 33.9 %collective-permute-start.10 = (bf16[384,1024]{1,0:T(8,128)(2,1)}, bf16[384,1024]{1,0:T(8,128)(2,1)}, u32[]{:S(2)}, u32[]{:S(2)}) collective-permute-start(bf16[384,1024]{1,0:T(8,128)(2,1)} %get-tuple-element.15), channel_id=1, source_target_pairs={{0,192},{64,0},{128,64},{192,128},{1,193},{65,1},{129,65},{193,129... | collective-permute-start | bytes 2359304 | tf_op jit(solution)/shard_map/ppermute | solution.py:16
  18.2 44.2 %collective-permute-start.3 = (bf16[384,2048]{1,0:T(8,128)(2,1)S(1)}, bf16[384,2048]{1,0:T(8,128)(2,1)S(1)}, u32[]{:S(2)}, u32[]{:S(2)}) collective-permute-start(bf16[384,2048]{1,0:T(8,128)(2,1)S(1)} %copy-done), channel_id=1, source_target_pairs={{0,32},{32,0},{1,33},{33,1},{2,34},{34,2},{3,35},{35,3},{4,36},{36... | collective-permute-start | bytes 4718600 | tf_op jit(solution)/shard_map/ppermute | solution.py:20
  19.7 7.2 %collective-permute-start.2 = (bf16[8,96,128]{2,1,0:T(8,128)(2,1)S(1)}, bf16[8,96,128]{2,1,0:T(8,128)(2,1)}, u32[]{:S(2)}, u32[]{:S(2)}) collective-permute-start(bf16[8,96,128]{2,1,0:T(8,128)(2,1)S(1)} %all-to-all-done), channel_id=1, source_target_pairs={{0,8},{8,16},{16,24},{24,0},{1,9},{9,17},{17,25},{25,1},{2,10},{10... | collective-permute-start | bytes 589832 | tf_op jit(solution)/shard_map/ppermute | solution.py:16
  26.9 7.2 %collective-permute-start.1 = (bf16[8,96,128]{2,1,0:T(8,128)(2,1)S(1)}, bf16[8,96,128]{2,1,0:T(8,128)(2,1)S(1)}, u32[]{:S(2)}, u32[]{:S(2)}) collective-permute-start(bf16[8,96,128]{2,1,0:T(8,128)(2,1)S(1)} %all-to-all-done), channel_id=1, source_target_pairs={{0,16},{8,24},{16,0},{24,8},{1,17},{9,25},{17,1},{25,9},{2,18},{10... | collective-permute-start | bytes 589832 | tf_op jit(solution)/shard_map/ppermute | solution.py:16
  34.1 5.7 %collective-permute-start = (bf16[8,96,128]{2,1,0:T(8,128)(2,1)S(1)}, bf16[8,96,128]{2,1,0:T(8,128)(2,1)S(1)}, u32[]{:S(2)}, u32[]{:S(2)}) collective-permute-start(bf16[8,96,128]{2,1,0:T(8,128)(2,1)S(1)} %all-to-all-done), channel_id=1, source_target_pairs={{0,24},{8,0},{16,8},{24,16},{1,25},{9,1},{17,9},{25,17},{2,26},{10... | collective-permute-start | bytes 589832 | tf_op jit(solution)/shard_map/ppermute | solution.py:16
  40.4 21.9 %collective-permute-start.8 = (bf16[384,1024]{1,0:T(8,128)(2,1)}, bf16[384,1024]{1,0:T(8,128)(2,1)}, u32[]{:S(2)}, u32[]{:S(2)}) collective-permute-start(bf16[384,1024]{1,0:T(8,128)(2,1)} %get-tuple-element.15), channel_id=1, source_target_pairs={{0,64},{64,128},{128,192},{192,0},{1,65},{65,129},{129,193},{193,1... | collective-permute-start | bytes 2359304 | tf_op jit(solution)/shard_map/ppermute | solution.py:16
  41.8 21.1 %collective-permute-start.5 = (bf16[384,1024]{1,0:T(8,128)(2,1)}, bf16[384,1024]{1,0:T(8,128)(2,1)}, u32[]{:S(2)}, u32[]{:S(2)}) collective-permute-start(bf16[384,1024]{1,0:T(8,128)(2,1)} %collective-permute-done.4.refs_2_), channel_id=1, source_target_pairs={{0,32},{32,0},{1,33},{33,1},{2,34},{34,2},{3,35},{35,3},{4,36},{36... | collective-permute-start | bytes 2359304 | tf_op jit(solution)/shard_map/ppermute | solution.py:20
  41.8 32.8 %collective-permute-start.12 = (bf16[384,1024]{1,0:T(8,128)(2,1)}, bf16[384,1024]{1,0:T(8,128)(2,1)}, u32[]{:S(2)}, u32[]{:S(2)}) collective-permute-start(bf16[384,1024]{1,0:T(8,128)(2,1)} %collective-permute-done.4.refs_2_), channel_id=1, source_target_pairs={{0,64},{64,128},{128,192},{192,0},{1,65},{65,129},{129,193},{193,1... | collective-permute-start | bytes 2359304 | tf_op jit(solution)/shard_map/ppermute | solution.py:16
  50.5 24.1 %collective-permute-start.14 = (bf16[384,1024]{1,0:T(8,128)(2,1)}, bf16[384,1024]{1,0:T(8,128)(2,1)}, u32[]{:S(2)}, u32[]{:S(2)}) collective-permute-start(bf16[384,1024]{1,0:T(8,128)(2,1)} %collective-permute-done.10.refs_8_.refs_10_), channel_id=1, source_target_pairs={{0,192},{64,0},{128,64},{192,128},{1,193},{65,1},{129,65},{193,129... | collective-permute-start | bytes 2359304 | tf_op jit(solution)/shard_map/ppermute | solution.py:16
  62.4 25.6 %collective-permute-start.11 = (bf16[384,1024]{1,0:T(8,128)(2,1)}, bf16[384,1024]{1,0:T(8,128)(2,1)}, u32[]{:S(2)}, u32[]{:S(2)}) collective-permute-start(bf16[384,1024]{1,0:T(8,128)(2,1)} %collective-permute-done.10.refs_8_.refs_10_), channel_id=1, source_target_pairs={{0,32},{32,0},{1,33},{33,1},{2,34},{34,2},{3,35},{35,3},{4,36},{36... | collective-permute-start | bytes 2359304 | tf_op jit(solution)/shard_map/ppermute | solution.py:20
  62.4 20.3 %copy-start.1 = (bf16[384,2048]{1,0:T(8,128)(2,1)}, bf16[384,2048]{1,0:T(8,128)(2,1)S(1)}, u32[]{:S(2)}) copy-start(bf16[384,2048]{1,0:T(8,128)(2,1)S(1)} %collective-permute-done.3.refs_1_) | copy-start | bytes 4718596
  62.4 25.5 %collective-permute-start.7 = (bf16[384,1024]{1,0:T(8,128)(2,1)}, bf16[384,1024]{1,0:T(8,128)(2,1)S(1)}, u32[]{:S(2)}, u32[]{:S(2)}) collective-permute-start(bf16[384,1024]{1,0:T(8,128)(2,1)} %collective-permute-done.6.refs_4_), channel_id=1, source_target_pairs={{0,32},{32,0},{1,33},{33,1},{2,34},{34,2},{3,35},{35,3},{4,36},{36... | collective-permute-start | bytes 2359304 | tf_op jit(solution)/shard_map/ppermute | solution.py:20
  62.9 25.0 %collective-permute-start.9 = (bf16[384,1024]{1,0:T(8,128)(2,1)}, bf16[384,1024]{1,0:T(8,128)(2,1)}, u32[]{:S(2)}, u32[]{:S(2)}) collective-permute-start(bf16[384,1024]{1,0:T(8,128)(2,1)} %collective-permute-done.8.refs_6_.refs_8_), channel_id=1, source_target_pairs={{0,32},{32,0},{1,33},{33,1},{2,34},{34,2},{3,35},{35,3},{4,36},{36... | collective-permute-start | bytes 2359304 | tf_op jit(solution)/shard_map/ppermute | solution.py:20
  74.6 22.0 %collective-permute-start.13 = (bf16[384,1024]{1,0:T(8,128)(2,1)}, bf16[384,1024]{1,0:T(8,128)(2,1)}, u32[]{:S(2)}, u32[]{:S(2)}) collective-permute-start(bf16[384,1024]{1,0:T(8,128)(2,1)} %collective-permute-done.12.left.refs_6_), channel_id=1, source_target_pairs={{0,32},{32,0},{1,33},{33,1},{2,34},{34,2},{3,35},{35,3},{4,36},{36... | collective-permute-start | bytes 2359304 | tf_op jit(solution)/shard_map/ppermute | solution.py:20
  74.6 22.0 %collective-permute-start.15 = (bf16[384,1024]{1,0:T(8,128)(2,1)}, bf16[384,1024]{1,0:T(8,128)(2,1)}, u32[]{:S(2)}, u32[]{:S(2)}) collective-permute-start(bf16[384,1024]{1,0:T(8,128)(2,1)} %collective-permute-done.14.right.refs_12_), channel_id=1, source_target_pairs={{0,32},{32,0},{1,33},{33,1},{2,34},{34,2},{3,35},{35,3},{4,36},{36... | collective-permute-start | bytes 2359304 | tf_op jit(solution)/shard_map/ppermute | solution.py:20
  76.7 11.2 %all-to-all-start.1 = ((bf16[8,112,128]{2,1,0:T(8,128)(2,1)}), bf16[8,112,128]{2,1,0:T(8,128)(2,1)}, u32[]{:S(2)}, u32[]{:S(2)}) async-start(bf16[8,112,128]{2,1,0:T(8,128)(2,1)} %pad_maximum_fusion.1), calls=%async_computation.1 | async-start | bytes 458752 | tf_op jit(solution)/shard_map/all_to_all | solution.py:292
  87.9 0.9 copy-start.2
  103.8 21.4 %all-to-all-start.2 = ((f32[32,3,128]{2,1,0:T(4,128)}), f32[32,3,128]{2,1,0:T(4,128)S(1)}, u32[]{:S(2)}, u32[]{:S(2)}) async-start(f32[32,3,128]{2,1,0:T(4,128)} %broadcast_in_dim.13), calls=%async_computation.2 | async-start | bytes 131072 | tf_op jit(solution)/shard_map/all_to_all | solution.py:24
  128.7 9.9 %copy-start.3 = (bf16[128,2048]{1,0:T(8,128)(2,1)S(1)}, bf16[128,2048]{1,0:T(8,128)(2,1)}, u32[]{:S(2)}) copy-start(bf16[128,2048]{1,0:T(8,128)(2,1)} %get-tuple-element.11.powers.refs_0_) | copy-start | bytes 1572868
  128.7 50.5 %all-to-all-start.3 = ((bf16[32,96,128]{2,1,0:T(8,128)(2,1)}), bf16[32,96,128]{2,1,0:T(8,128)(2,1)S(1)}, u32[]{:S(2)}, u32[]{:S(2)}) async-start(bf16[32,96,128]{2,1,0:T(8,128)(2,1)} %bitcast.44), calls=%async_computation.3 | async-start | bytes 1572864 | tf_op jit(solution)/shard_map/all_to_all | solution.py:325
  138.7 13.5 %collective-permute-start.24 = (bf16[128,2048]{1,0:T(8,128)(2,1)S(1)}, bf16[128,2048]{1,0:T(8,128)(2,1)S(1)}, u32[]{:S(2)}, u32[]{:S(2)}) collective-permute-start(bf16[128,2048]{1,0:T(8,128)(2,1)S(1)} %copy-done.3), channel_id=1, source_target_pairs={{0,64},{64,128},{128,192},{192,0},{1,65},{65,129},{129,193},{193,1... | collective-permute-start | bytes 1572872 | tf_op jit(solution)/shard_map/ppermute | solution.py:16
  139.3 13.7 %collective-permute-start.26 = (bf16[128,2048]{1,0:T(8,128)(2,1)S(1)}, bf16[128,2048]{1,0:T(8,128)(2,1)S(1)}, u32[]{:S(2)}, u32[]{:S(2)}) collective-permute-start(bf16[128,2048]{1,0:T(8,128)(2,1)S(1)} %copy-done.3), channel_id=1, source_target_pairs={{0,192},{64,0},{128,64},{192,128},{1,193},{65,1},{129,65},{193,129... | collective-permute-start | bytes 1572872 | tf_op jit(solution)/shard_map/ppermute | solution.py:16
  142.9 27.9 %copy-start.6 = (bf16[8,96,128]{2,1,0:T(8,128)(2,1)}, bf16[8,96,128]{2,1,0:T(8,128)(2,1)S(1)}, u32[]{:S(2)}) copy-start(bf16[8,96,128]{2,1,0:T(8,128)(2,1)S(1)} %slice.49.p0) | copy-start | bytes 589828
  142.9 14.6 %collective-permute-start.16 = (bf16[8,96,128]{2,1,0:T(8,128)(2,1)S(1)}, bf16[8,96,128]{2,1,0:T(8,128)(2,1)S(1)}, u32[]{:S(2)}, u32[]{:S(2)}) collective-permute-start(bf16[8,96,128]{2,1,0:T(8,128)(2,1)S(1)} %slice.49.p0), channel_id=1, source_target_pairs={{0,24},{8,0},{16,8},{24,16},{1,25},{9,1},{17,9},{25,17},{2,26},{10... | collective-permute-start | bytes 589832 | tf_op jit(solution)/shard_map/ppermute | solution.py:16
  145.7 11.8 %collective-permute-start.17 = (bf16[8,96,128]{2,1,0:T(8,128)(2,1)S(1)}, bf16[8,96,128]{2,1,0:T(8,128)(2,1)S(1)}, u32[]{:S(2)}, u32[]{:S(2)}) collective-permute-start(bf16[8,96,128]{2,1,0:T(8,128)(2,1)S(1)} %slice.49.p0), channel_id=1, source_target_pairs={{0,16},{8,24},{16,0},{24,8},{1,17},{9,25},{17,1},{25,9},{2,18},{10... | collective-permute-start | bytes 589832 | tf_op jit(solution)/shard_map/ppermute | solution.py:16
  146.6 14.3 %collective-permute-start.18 = (bf16[8,96,128]{2,1,0:T(8,128)(2,1)S(1)}, bf16[8,96,128]{2,1,0:T(8,128)(2,1)S(1)}, u32[]{:S(2)}, u32[]{:S(2)}) collective-permute-start(bf16[8,96,128]{2,1,0:T(8,128)(2,1)S(1)} %slice.49.p0), channel_id=1, source_target_pairs={{0,8},{8,16},{16,24},{24,0},{1,9},{9,17},{17,25},{25,1},{2,10},{10... | collective-permute-start | bytes 589832 | tf_op jit(solution)/shard_map/ppermute | solution.py:16
  152.2 18.6 %copy-start.4 = (bf16[128,2048]{1,0:T(8,128)(2,1)}, bf16[128,2048]{1,0:T(8,128)(2,1)S(1)}, u32[]{:S(2)}) copy-start(bf16[128,2048]{1,0:T(8,128)(2,1)S(1)} %collective-permute-done.24.refs_2_) | copy-start | bytes 1572868
  152.2 1.6 collective-permute-start.19
  153.0 17.8 %copy-start.5 = (bf16[128,2048]{1,0:T(8,128)(2,1)}, bf16[128,2048]{1,0:T(8,128)(2,1)S(1)}, u32[]{:S(2)}) copy-start(bf16[128,2048]{1,0:T(8,128)(2,1)S(1)} %collective-permute-done.26.refs_4_) | copy-start | bytes 1572868
  153.0 13.6 %collective-permute-start.28 = (bf16[128,1024]{1,0:T(8,128)(2,1)}, bf16[128,1024]{1,0:T(8,128)(2,1)S(1)}, u32[]{:S(2)}, u32[]{:S(2)}) collective-permute-start(bf16[128,1024]{1,0:T(8,128)(2,1)} %slice.60), channel_id=1, source_target_pairs={{0,64},{64,128},{128,192},{192,0},{1,65},{65,129},{129,193},{193,1... | collective-permute-start | bytes 786440 | tf_op jit(solution)/shard_map/ppermute | solution.py:16
  153.8 13.4 %collective-permute-start.30 = (bf16[128,1024]{1,0:T(8,128)(2,1)}, bf16[128,1024]{1,0:T(8,128)(2,1)}, u32[]{:S(2)}, u32[]{:S(2)}) collective-permute-start(bf16[128,1024]{1,0:T(8,128)(2,1)} %slice.61), channel_id=1, source_target_pairs={{0,192},{64,0},{128,64},{192,128},{1,193},{65,1},{129,65},{193,129... | collective-permute-start | bytes 786440 | tf_op jit(solution)/shard_map/ppermute | solution.py:16
  157.5 13.3 %copy-start.10 = (bf16[8,96,128]{2,1,0:T(8,128)(2,1)}, bf16[8,96,128]{2,1,0:T(8,128)(2,1)S(1)}, u32[]{:S(2)}) copy-start(bf16[8,96,128]{2,1,0:T(8,128)(2,1)S(1)} %collective-permute-done.16.p1) | copy-start | bytes 589828
  157.5 5.6 %collective-permute-start.20 = (f32[2,128]{1,0:T(2,128)S(1)}, f32[2,128]{1,0:T(2,128)S(1)}, u32[]{:S(2)}, u32[]{:S(2)}) collective-permute-start(f32[2,128]{1,0:T(2,128)S(1)} %pad_maximum_fusion.2), channel_id=1, source_target_pairs={{0,64},{64,128},{128,192},{192,0},{1,65},{65,129},{129,193},{193,1... | collective-permute-start | bytes 3080 | tf_op jit(solution)/shard_map/ppermute | solution.py:16
  157.5 3.6 %copy-start.11 = (bf16[8,96,128]{2,1,0:T(8,128)(2,1)}, bf16[8,96,128]{2,1,0:T(8,128)(2,1)S(1)}, u32[]{:S(2)}) copy-start(bf16[8,96,128]{2,1,0:T(8,128)(2,1)S(1)} %collective-permute-done.17.p2) | copy-start | bytes 589828
  157.5 5.7 %collective-permute-start.21 = (f32[2,128]{1,0:T(2,128)S(1)}, f32[2,128]{1,0:T(2,128)}, u32[]{:S(2)}, u32[]{:S(2)}) collective-permute-start(f32[2,128]{1,0:T(2,128)S(1)} %pad_maximum_fusion.2), channel_id=1, source_target_pairs={{0,192},{64,0},{128,64},{192,128},{1,193},{65,1},{129,65},{193,129... | collective-permute-start | bytes 3080 | tf_op jit(solution)/shard_map/ppermute | solution.py:16
  160.8 5.2 %collective-permute-start.22 = (f32[2,128]{1,0:T(2,128)S(1)}, f32[2,128]{1,0:T(2,128)}, u32[]{:S(2)}, u32[]{:S(2)}) collective-permute-start(f32[2,128]{1,0:T(2,128)S(1)} %pad_maximum_fusion.2), channel_id=1, source_target_pairs={{0,128},{64,192},{128,0},{192,64},{1,129},{65,193},{129,1},{193,65... | collective-permute-start | bytes 3080 | tf_op jit(solution)/shard_map/ppermute | solution.py:16
  163.1 7.6 %collective-permute-start.23 = (bf16[128,2048]{1,0:T(8,128)(2,1)S(1)}, bf16[128,2048]{1,0:T(8,128)(2,1)S(1)}, u32[]{:S(2)}, u32[]{:S(2)}) collective-permute-start(bf16[128,2048]{1,0:T(8,128)(2,1)S(1)} %copy-done.3), channel_id=1, source_target_pairs={{0,32},{32,0},{1,33},{33,1},{2,34},{34,2},{3,35},{35,3},{4,36},{36... | collective-permute-start | bytes 1572872 | tf_op jit(solution)/shard_map/ppermute | solution.py:20
  163.2 7.6 %collective-permute-start.25 = (bf16[128,2048]{1,0:T(8,128)(2,1)S(1)}, bf16[128,2048]{1,0:T(8,128)(2,1)}, u32[]{:S(2)}, u32[]{:S(2)}) collective-permute-start(bf16[128,2048]{1,0:T(8,128)(2,1)S(1)} %collective-permute-done.24.refs_2_), channel_id=1, source_target_pairs={{0,32},{32,0},{1,33},{33,1},{2,34},{34,2},{3,35},{35,3},{4,36},{36... | collective-permute-start | bytes 1572872 | tf_op jit(solution)/shard_map/ppermute | solution.py:20
  166.0 4.7 %collective-permute-start.27 = (bf16[128,2048]{1,0:T(8,128)(2,1)S(1)}, bf16[128,2048]{1,0:T(8,128)(2,1)}, u32[]{:S(2)}, u32[]{:S(2)}) collective-permute-start(bf16[128,2048]{1,0:T(8,128)(2,1)S(1)} %collective-permute-done.26.refs_4_), channel_id=1, source_target_pairs={{0,32},{32,0},{1,33},{33,1},{2,34},{34,2},{3,35},{35,3},{4,36},{36... | collective-permute-start | bytes 1572872 | tf_op jit(solution)/shard_map/ppermute | solution.py:20
  166.6 4.2 %copy-start.9 = (bf16[128,1024]{1,0:T(8,128)(2,1)}, bf16[128,1024]{1,0:T(8,128)(2,1)S(1)}, u32[]{:S(2)}) copy-start(bf16[128,1024]{1,0:T(8,128)(2,1)S(1)} %collective-permute-done.28.refs_6_) | copy-start | bytes 786436
  166.6 4.1 %collective-permute-start.29 = (bf16[128,1024]{1,0:T(8,128)(2,1)S(1)}, bf16[128,1024]{1,0:T(8,128)(2,1)}, u32[]{:S(2)}, u32[]{:S(2)}) collective-permute-start(bf16[128,1024]{1,0:T(8,128)(2,1)S(1)} %collective-permute-done.28.refs_6_), channel_id=1, source_target_pairs={{0,32},{32,0},{1,33},{33,1},{2,34},{34,2},{3,35},{35,3},{4,36},{36... | collective-permute-start | bytes 786440 | tf_op jit(solution)/shard_map/ppermute | solution.py:20
  167.2 3.6 %collective-permute-start.31 = (bf16[128,1024]{1,0:T(8,128)(2,1)}, bf16[128,1024]{1,0:T(8,128)(2,1)}, u32[]{:S(2)}, u32[]{:S(2)}) collective-permute-start(bf16[128,1024]{1,0:T(8,128)(2,1)} %collective-permute-done.30.refs_8_), channel_id=1, source_target_pairs={{0,32},{32,0},{1,33},{33,1},{2,34},{34,2},{3,35},{35,3},{4,36},{36... | collective-permute-start | bytes 786440 | tf_op jit(solution)/shard_map/ppermute | solution.py:20
  170.8 0.8 copy-start.7
  (2 other events, 1.4 us)

commit v2 on v1

--- a/solution.py
+++ b/solution.py
@@ -24,12 +24,6 @@
     return lax.all_to_all(jnp.broadcast_to(a[None], (n, *a.shape)), axis, 0, 0, tiled=True)
 
 
-def ordered(parts, index):
-    n = len(parts)
-    both = jnp.stack(parts + parts[:-1])
-    return lax.dynamic_slice_in_dim(both, (n - index) % n, n, 0)
-
-
 def dot(a, b):
     return lax.dot_general(a, b, (((1,), (0,)), ((), ())), preferred_element_type=F32)
 
@@ -47,12 +41,12 @@
     return jnp.maximum(j - STEPS // 2, 0)
 
 
-def call(kernel, scalars, args, in_specs, out_specs, out_shape, flops, scratch=()):
+def call(kernel, scalars, args, in_specs, out_specs, out_shape, flops, scratch=(), steps=STEPS):
     return pl.pallas_call(
         kernel,
         grid_spec=pltpu.PrefetchScalarGridSpec(
             num_scalar_prefetch=1,
-            grid=(STEPS,),
+            grid=(steps,),
             in_specs=in_specs,
             out_specs=out_specs,
             scratch_shapes=scratch,
@@ -60,6 +54,34 @@
         out_shape=out_shape,
         cost_estimate=pl.CostEstimate(flops=flops, bytes_accessed=flops // 256, transcendentals=0),
     )(jnp.stack(scalars).astype(jnp.int32), *args)
+
+
+def prepare_kernel(who, p0, p1, p2, p3, digits, states, wanted):
+    part = p0.shape[1]
+    for j, parts in enumerate((p0, p1, p2, p3)):
+        chip = (who[0] + j) % NY
+        for c in range(2):
+            rows = parts[4 * c : 4 * c + 4].reshape(4 * part, -1)
+            states[2 * chip + c] = rows.T
+            wanted[2 * chip + c, :part, :] = parts[4 * c + who[0]]
+            wanted[2 * chip + c, part:, :] = digits[...]
+
+
+def prepared(parts, digits, y):
+    _, part, tokens = parts[0].shape
+    states = jax.ShapeDtypeStruct((8, tokens, 4 * part), BF)
+    wanted = jax.ShapeDtypeStruct((8, part + 16, tokens), BF)
+    args = [*parts, digits]
+    return call(
+        prepare_kernel,
+        [y, y],
+        args,
+        [whole(a) for a in args],
+        [whole(states), whole(wanted)],
+        [states, wanted],
+        1 << 20,
+        steps=1,
+    )
 
 
 def near_kernel(who, states, *refs):
@@ -195,10 +217,11 @@
     )
 
 
-def grad_kernel(who, p0, p1, p2, p3, scales, labels, *refs):
-    *arrays, out, states = refs
+def grad_kernel(who, p0, p1, p2, p3, scales, *refs):
+    *arrays, out, states, turned = refs
     step = pl.program_id(0)
-    groups, part, tokens = p0.shape
+    groups, padded, tokens = p0.shape
+    part = padded - 16
     wide = out.shape[1]
 
     @pl.when(step == 0)
@@ -206,9 +229,15 @@
         for j, parts in enumerate((p0, p1, p2, p3)):
             at = pl.multiple_of(((who[9] + j) % NY) * part, 32)
             for k in range(groups):
-                states[k, pl.ds(at, part), :] = parts[k]
+                states[k, pl.ds(at, part), :] = parts[k, :part, :]
+        for k in range(groups):
+            digits = p0[who[k], part:, :].astype(F32)
+            number = digits[0:1] * 256.0 + digits[1:2]
+            both = jnp.concatenate([number, scales[k : k + 1, :], digits[:6]], axis=0)
+            turned[k] = both.T
 
     columns = who[8] + step * wide + lax.broadcasted_iota(jnp.int32, (tokens, wide), 1)
+    columns = columns.astype(F32)
     blocks = [a[...] for a in arrays[:6]]
     first = step < STEPS // 2
     blocks += [jnp.where(first, arrays[6 + k][...], arrays[8 + k][...]) for k in range(2)]
@@ -216,23 +245,21 @@
     for pair in range(4):
         left, right = [], []
         for k in (2 * pair, 2 * pair + 1):
-            wanted = labels[pl.ds(pl.multiple_of(who[k] * tokens, tokens), tokens), :]
-            hit = jnp.where(wanted == columns, 1.0, 0.0)
-            scale = scales[k * tokens : (k + 1) * tokens, :]
-            right.append((blocks[k].astype(F32) * scale - hit).astype(BF))
+            hit = jnp.where(turned[k][:, 0:1] == columns, 1.0, 0.0)
+            right.append((blocks[k].astype(F32) * turned[k][:, 1:2] - hit).astype(BF))
             left.append(states[who[k]])
         term = dot(jnp.concatenate(left, axis=1), jnp.concatenate(right, axis=0))
         acc = term if acc is None else acc + term
     out[...] = acc
 
 
-def head_grad_of(parts, scales, labels, near, left, right, who):
-    groups, part, tokens = parts[0].shape
-    rows = NY * part
+def head_grad_of(parts, scales, near, left, right, who):
+    groups, padded, tokens = parts[0].shape
+    rows = NY * (padded - 16)
     width = near[0].shape[1]
     wide = width // STEPS
-    args = [*parts, scales, labels, *near, *left, *right]
-    specs = [whole(a) for a in args[:6]]
+    args = [*parts, scales, *near, *left, *right]
+    specs = [whole(a) for a in args[:5]]
     specs += [pl.BlockSpec((tokens, wide), lambda j, s: (0, j))] * 6
     specs += [pl.BlockSpec((tokens, wide), lambda j, s: (0, early(j)))] * 2
     specs += [pl.BlockSpec((tokens, wide), lambda j, s: (0, late(j)))] * 2
@@ -244,7 +271,7 @@
         pl.BlockSpec((rows, wide), lambda j, s: (0, j)),
         jax.ShapeDtypeStruct((rows, width), F32),
         2 * groups * tokens * rows * width,
-        [pltpu.VMEM((groups, rows, tokens), BF)],
+        [pltpu.VMEM((groups, rows, tokens), BF), pltpu.VMEM((groups, tokens, 8), F32)],
     )
 
 
@@ -268,38 +295,24 @@
     own = [head, swap(head)]
     far_left = shift(up_left, "x", NX, 1)
     far_right = shift(down_right, "x", NX, -1)
-    left = [up_left, swap(up_left), down_left, swap(down_left)]
-    right = [up_right, swap(up_right), down_right, swap(down_right)]
+    up_left_other, down_right_other = swap(up_left), swap(down_right)
+    left = [up_left, up_left_other, down_left, swap(down_left)]
+    right = [up_right, swap(up_right), down_right, down_right_other]
     away_left = [far_left, swap(far_left)]
     away_right = [far_right, swap(far_right)]
 
     row = from_everyone(hidden_states.T, "z", NZ)
     parts = [row] + [shift(row, "y", NY, -j) for j in (1, 2, 3)]
-    flat = jnp.stack(parts).reshape(8, rows, tokens)
-    flat = jnp.swapaxes(flat, 1, 2)
-
-    def block(offset):
-        chip = ((x + offset - y) % NY) * 2
-        return [chip + core, chip + 1 - core]
-
-    picked = [
-        lax.dynamic_index_in_dim(p.reshape(2, NY, part, tokens), y, 1, keepdims=False)
-        for p in parts
-    ]
-    wanted = ordered(picked, y).reshape(8, part, tokens)
     digits = jnp.stack([labels // 256, labels % 256]).astype(BF)
-    digits = jnp.broadcast_to(jnp.pad(digits, ((0, 14), (0, 0)))[None], (8, 16, tokens))
-    wanted = lax.all_to_all(
-        jnp.concatenate([wanted, digits], axis=1), ("x", "core"), 0, 0, tiled=True
-    )
-    far_states, wanted = lax.optimization_barrier((flat, wanted))
-    digits = wanted[:, part : part + 2].astype(jnp.int32)
-    all_labels = (digits[:, 0] * 256 + digits[:, 1]).reshape(8 * tokens, 1)
-    wanted = wanted[:, :part]
-
-    logits = near_logits(flat, own, left, right, block(0) + block(3) + block(1))
+    digits = jnp.pad(digits, ((0, 14), (0, 0)))
+    states, wanted = prepared(parts, digits, y)
+    wanted = lax.all_to_all(wanted, ("x", "core"), 0, 0, tiled=True)
+    far_states, wanted = lax.optimization_barrier((states, wanted))
+
+    slices = [wanted] + [shift(wanted, "y", NY, -j) for j in (1, 2, 3)]
+    logits = near_logits(states, own, left, right, who(0) + who(3) + who(1))
     powers, stats = far_logits(
-        far_states, labels[:, None], logits, away_left, away_right, block(2) + [base]
+        far_states, labels[:, None], logits, away_left, away_right, who(2) + [base]
     )
 
     pow_up = shift(powers, "x", NX, 1)
@@ -327,14 +340,12 @@
     )
     state_grad = arrived.astype(F32).sum(axis=0).astype(BF).T
 
-    slices = [wanted] + [shift(wanted, "y", NY, -j) for j in (1, 2, 3)]
     scale = jnp.stack([scale, swap(scale)])
     scales = [scale] + [shift(scale, "x", NX, s) for s in (1, -1, 2)]
-    scales = jnp.concatenate(scales).reshape(8 * tokens, 1)
+    scales = jnp.concatenate(scales)
     head_grad = head_grad_of(
         slices,
         scales,
-        all_labels,
         pow_near,
         pow_left,
         pow_right,

time: 184 us -> 185 us (level)
  waiting for transfers between devices: 51.7 us -> 65.7 us
  local copies, waits for them, and re-layouts: 19.9 us -> 9.91 us
  starting transfers between devices: 67.6 us -> 64.6 us
  Pallas kernels: 30.9 us -> 33.8 us
    ppermute x19, waiting for transfers between devices: 46.2 us -> 59 us  [shift(): return lax.ppermute(a, axis, [(i, (i + s) % n) for i in range(n)])]
    unnamed x34, local copies, waits for them, and re-layouts: 5.22 us -> 1.22 us
    pallas_call x4 -> x5, Pallas kernels: 30.9 us -> 33.8 us  [call(): pl.pallas_call(kernel, grid_spec=pltpu.PrefetchScalarGridSpec(num_scalar_...]
    reshape x2 -> x0, local copies, waits for them, and re-layouts: 2.21 us -> none  [the longest x1 1.18 us: step(): flat = jnp.stack(parts).reshape(8, rows, tokens)]
    all_to_all x2, starting transfers between devices: 20.3 us -> 18.2 us  [from_everyone(): lax.all_to_all(jnp.broadcast_to(a[None], (n, *a.shape)), axis, 0, 0, tile...]
  transfers between devices with their start and end apart: 36 -> 36, of which waited for: 14 -> 16; matrix products, arithmetic and copies ran while one was open for 10% -> 5% of each run, Pallas kernels for 14% -> 15%
where the time goes in v2:
time: 185 us; the launch traced here: 182 us
  waiting for transfers between devices  65.7 us (36%)
  starting transfers between devices  64.6 us (35%)
  Pallas kernels  33.8 us (18%)
  local copies, waits for them, and re-layouts  9.91 us (5%)
  other arithmetic  7.25 us (4%)
    ppermute x19, waiting for transfers between devices, shift(): return lax.ppermute(a, axis, [(i, (i + s) % n) for i in range(n)])  59 us
    pallas_call x5, Pallas kernels, call(): pl.pallas_call(kernel, grid_spec=pltpu.PrefetchScalarGridSpec(num_scalar_...  33.8 us
    ppermute x19, starting transfers between devices, shift(): return lax.ppermute(a, axis, [(i, (i + s) % n) for i in range(n)])  30.6 us
    all_to_all x2, starting transfers between devices, from_everyone(): lax.all_to_all(jnp.broadcast_to(a[None], (n, *a.shape)), axis, 0, 0, tile...  18.2 us
    all_to_all x1, starting transfers between devices, step(): lax.all_to_all(terms.reshape(NY * NZ, part, tokens), ('y', 'z'), 0, 0, ti...  9.91 us
    all_to_all x1, waiting for transfers between devices, step(): wanted = lax.all_to_all(wanted, ('x', 'core'), 0, 0, tiled=True)  4.34 us
  transfers between devices with their start and end apart: 36, of which 16 were waited for; matrix products, arithmetic and copies ran while one was open for 5% of the time, Pallas kernels for 15%

profile of v2, /device:TPU:32, one launch (start us, length us, event | category | flops | bytes accessed | tf_op | source)
XLA Modules:
  0.0 182.2 jit_solution(16564890140390683991)
XLA Ops:
  0.6 1.5 broadcast_in_dim.8
  2.1 8.6 %all-to-all-start = ((bf16[8,96,128]{2,1,0:T(8,128)(2,1)}), bf16[8,96,128]{2,1,0:T(8,128)(2,1)S(1)}, u32[]{:S(2)}, u32[]{:S(2)}) async-start(bf16[8,96,128]{2,1,0:T(8,128)(2,1)} %broadcast_in_dim.8), calls=%async_computation | async-start | bytes 393216 | tf_op jit(solution)/shard_map/all_to_all | solution.py:24
  10.7 2.7 %fusion.8 = (bf16[384,1024]{1,0:T(8,128)(2,1)}, bf16[384,1024]{1,0:T(8,128)(2,1)}) fusion(bf16[384,2048]{1,0:T(8,128)(2,1)} %refs_0_.3), kind=kLoop, calls=%fused_computation.24 | loop fusion | bytes 3145728 | tf_op jit(solution)/shard_map/slice | solution.py:293
  13.3 1.5 collective-permute-start.4
  14.8 1.7 collective-permute-start.6
  16.5 1.5 collective-permute-start.10
  18.1 1.6 all-to-all-done.p0
  19.7 3.0 %collective-permute-start = (bf16[8,96,128]{2,1,0:T(8,128)(2,1)S(1)}, bf16[8,96,128]{2,1,0:T(8,128)(2,1)S(1)}, u32[]{:S(2)}, u32[]{:S(2)}) collective-permute-start(bf16[8,96,128]{2,1,0:T(8,128)(2,1)S(1)} %all-to-all-done.p0), channel_id=1, source_target_pairs={{0,24},{8,0},{16,8},{24,16},{1,25},{9,1},{17,9},{25,17},{2,26},{10... | collective-permute-start | bytes 589832 | tf_op jit(solution)/shard_map/ppermute | solution.py:16
  22.7 3.2 %collective-permute-done.p1 = bf16[8,96,128]{2,1,0:T(8,128)(2,1)S(1)} collective-permute-done((bf16[8,96,128]{2,1,0:T(8,128)(2,1)S(1)}, bf16[8,96,128]{2,1,0:T(8,128)(2,1)S(1)}, u32[]{:S(2)}, u32[]{:S(2)}) %collective-permute-start) | collective-permute-done | bytes 196640 | tf_op jit(solution)/shard_map/ppermute | solution.py:16
  25.9 2.7 %collective-permute-start.1 = (bf16[8,96,128]{2,1,0:T(8,128)(2,1)S(1)}, bf16[8,96,128]{2,1,0:T(8,128)(2,1)S(1)}, u32[]{:S(2)}, u32[]{:S(2)}) collective-permute-start(bf16[8,96,128]{2,1,0:T(8,128)(2,1)S(1)} %all-to-all-done.p0), channel_id=1, source_target_pairs={{0,16},{8,24},{16,0},{24,8},{1,17},{9,25},{17,1},{25,9},{2,18},{10... | collective-permute-start | bytes 589832 | tf_op jit(solution)/shard_map/ppermute | solution.py:16
  28.5 4.5 %collective-permute-done.1.p2 = bf16[8,96,128]{2,1,0:T(8,128)(2,1)S(1)} collective-permute-done((bf16[8,96,128]{2,1,0:T(8,128)(2,1)S(1)}, bf16[8,96,128]{2,1,0:T(8,128)(2,1)S(1)}, u32[]{:S(2)}, u32[]{:S(2)}) %collective-permute-start.1) | collective-permute-done | bytes 196640 | tf_op jit(solution)/shard_map/ppermute | solution.py:16
  33.1 1.0 collective-permute-start.2
  34.1 6.3 %collective-permute-done.2.p3 = bf16[8,96,128]{2,1,0:T(8,128)(2,1)S(1)} collective-permute-done((bf16[8,96,128]{2,1,0:T(8,128)(2,1)S(1)}, bf16[8,96,128]{2,1,0:T(8,128)(2,1)S(1)}, u32[]{:S(2)}, u32[]{:S(2)}) %collective-permute-start.2) | collective-permute-done | bytes 196640 | tf_op jit(solution)/shard_map/ppermute | solution.py:16
  40.4 1.5 collective-permute-start.8
  42.0 1.6 collective-permute-start.12
  43.6 8.0 %collective-permute-done.10.refs_8_.refs_10_ = bf16[384,1024]{1,0:T(8,128)(2,1)} collective-permute-done((bf16[384,1024]{1,0:T(8,128)(2,1)}, bf16[384,1024]{1,0:T(8,128)(2,1)}, u32[]{:S(2)}, u32[]{:S(2)}) %collective-permute-start.10) | collective-permute-done | bytes 786464 | tf_op jit(solution)/shard_map/ppermute | solution.py:16
  51.6 3.0 %collective-permute-start.14 = (bf16[384,1024]{1,0:T(8,128)(2,1)}, bf16[384,1024]{1,0:T(8,128)(2,1)}, u32[]{:S(2)}, u32[]{:S(2)}) collective-permute-start(bf16[384,1024]{1,0:T(8,128)(2,1)} %collective-permute-done.10.refs_8_.refs_10_), channel_id=1, source_target_pairs={{0,192},{64,0},{128,64},{192,128},{1,193},{65,1},{129,65},{193,129... | collective-permute-start | bytes 2359304 | tf_op jit(solution)/shard_map/ppermute | solution.py:16
  54.6 7.7 %collective-permute-done.8.refs_6_.refs_8_ = bf16[384,1024]{1,0:T(8,128)(2,1)} collective-permute-done((bf16[384,1024]{1,0:T(8,128)(2,1)}, bf16[384,1024]{1,0:T(8,128)(2,1)}, u32[]{:S(2)}, u32[]{:S(2)}) %collective-permute-start.8) | collective-permute-done | bytes 786464 | tf_op jit(solution)/shard_map/ppermute | solution.py:16
  63.0 10.5 %collective-permute-done.12.left.refs_6_ = bf16[384,1024]{1,0:T(8,128)(2,1)} collective-permute-done((bf16[384,1024]{1,0:T(8,128)(2,1)S(1)}, bf16[384,1024]{1,0:T(8,128)(2,1)}, u32[]{:S(2)}, u32[]{:S(2)}) %collective-permute-start.12) | collective-permute-done | bytes 786464 | tf_op jit(solution)/shard_map/ppermute | solution.py:16
  74.6 0.6 fusion.2.digits
  75.2 3.1 %shard_map.58 = (bf16[8,128,384]{2,1,0:T(8,128)(2,1)}, bf16[8,112,128]{2,1,0:T(8,128)(2,1)}) custom-call(s32[2]{0:T(128)} %pad_add_fusion.1.who, bf16[8,96,128]{2,1,0:T(8,128)(2,1)} %copy-done.8, bf16[8,96,128]{2,1,0:T(8,128)(2,1)} %copy-done.13, bf16[8,96,128]{2,1,0:T(8,128)(2,1)} %copy-done.14, bf16[8,96,128]{2,1,0:T(8,128)(2,1)} %copy-done.15, ...), custom_call_target="tpu_custom_call" | custom-call | flops 1048576 | bytes 4096 | tf_op jit(solution)/shard_map/pallas_call | solution.py:45
  78.2 3.6 %all-to-all-start.1 = ((bf16[8,112,128]{2,1,0:T(8,128)(2,1)}), bf16[8,112,128]{2,1,0:T(8,128)(2,1)S(1)}, u32[]{:S(2)}, u32[]{:S(2)}) async-start(bf16[8,112,128]{2,1,0:T(8,128)(2,1)} %get-tuple-element.12), calls=%async_computation.1 | async-start | bytes 458752 | tf_op jit(solution)/shard_map/all_to_all | solution.py:309
  81.9 0.7 copy.9.labels
  84.4 4.3 %all-to-all-done.1.p0 = bf16[8,112,128]{2,1,0:T(8,128)(2,1)S(1)} async-done(((bf16[8,112,128]{2,1,0:T(8,128)(2,1)}), bf16[8,112,128]{2,1,0:T(8,128)(2,1)S(1)}, u32[]{:S(2)}, u32[]{:S(2)}) %all-to-all-start.1) | async-done | bytes 229408 | tf_op jit(solution)/shard_map/all_to_all | solution.py:309
  88.8 7.8 %shard_map.59.near = f32[128,2048]{1,0:T(8,128)} custom-call(s32[6]{0:T(128)} %stack.115.who, bf16[8,128,384]{2,1,0:T(8,128)(2,1)} %get-tuple-element.13.states.mine_states.other_states, bf16[384,2048]{1,0:T(8,128)(2,1)} %refs_0_.3, bf16[384,2048]{1,0:T(8,128)(2,1)} %copy-done, bf16[384,1024]{1,0:T(8,128)(2,1)} %copy-done.1, bf16[384,1024]{1,0:T(8,128)(2,1)} %copy-done.3, ...), custom_call_target="tpu_custom_call" | custom-call | flops 1207959552 | bytes 4718592 | tf_op jit(solution)/shard_map/pallas_call | solution.py:45
  96.6 5.8 %shard_map.60 = (bf16[128,2048]{1,0:T(8,128)(2,1)}, f32[8,128]{1,0:T(8,128)}) custom-call(s32[3]{0:T(128)} %pad_add_fusion.who, bf16[8,128,384]{2,1,0:T(8,128)(2,1)} %get-tuple-element.13.states.mine_states.other_states, bf16[8,128,384]{2,1,0:T(8,128)(2,1)} %get-tuple-element.13.states.mine_states.other_states, s32[128,1]{1,0:T(8,128)} %copy.9.labels, ...), custom_call_target="tpu_custom_call" | custom-call | flops 402653184 | bytes 1572864 | tf_op jit(solution)/shard_map/pallas_call | solution.py:45
  102.5 0.7 slice.32
  103.2 0.6 broadcast_in_dim.10
  103.8 9.6 %all-to-all-start.2 = ((f32[32,3,128]{2,1,0:T(4,128)}), f32[32,3,128]{2,1,0:T(4,128)S(1)}, u32[]{:S(2)}, u32[]{:S(2)}) async-start(f32[32,3,128]{2,1,0:T(4,128)} %broadcast_in_dim.10), calls=%async_computation.2 | async-start | bytes 131072 | tf_op jit(solution)/shard_map/all_to_all | solution.py:24
  113.4 9.6 %shard_map.61 = (f32[3072,128]{1,0:T(8,128)}, bf16[3072,128]{1,0:T(8,128)(2,1)}) custom-call(s32[9]{0:T(128)} %stack.124.starts, bf16[128,2048]{1,0:T(8,128)(2,1)} %get-tuple-element.15.powers.refs_0_, s32[1,128]{1,0:T(1,128)} %bitcast.58, bf16[384,2048]{1,0:T(8,128)(2,1)} %refs_0_.3, bf16[384,2048]{1,0:T(8,128)(2,1)} %copy-done, ...), custom_call_target="tpu_custom_call" | custom-call | flops 3221225472 | bytes 12582912 | tf_op jit(solution)/shard_map/pallas_call | solution.py:45
  123.2 0.7 bitcast_divide_fusion
  123.9 2.7 %subtract_convert_fusion = bf16[3072,128]{1,0:T(8,128)(2,1)} fusion(bf16[3072,128]{1,0:T(8,128)(2,1)} %get-tuple-element.17, f32[3072,128]{1,0:T(8,128)} %get-tuple-element.16, f32[128]{0:T(128)S(1)} %bitcast.55), kind=kLoop, calls=%fused_computation | loop fusion | flops 1572864 | bytes 3146240 | tf_op jit(solution)/shard_map/convert_element_type | solution.py:337
  126.6 9.9 %all-to-all-start.3 = ((bf16[32,96,128]{2,1,0:T(8,128)(2,1)}), bf16[32,96,128]{2,1,0:T(8,128)(2,1)S(1)}, u32[]{:S(2)}, u32[]{:S(2)}) async-start(bf16[32,96,128]{2,1,0:T(8,128)(2,1)} %bitcast.30), calls=%async_computation.3 | async-start | bytes 1572864 | tf_op jit(solution)/shard_map/all_to_all | solution.py:338
  136.6 0.7 collective-permute-start.24
  137.2 2.7 %collective-permute-start.26 = (bf16[128,2048]{1,0:T(8,128)(2,1)S(1)}, bf16[128,2048]{1,0:T(8,128)(2,1)S(1)}, u32[]{:S(2)}, u32[]{:S(2)}) collective-permute-start(bf16[128,2048]{1,0:T(8,128)(2,1)S(1)} %copy-done.4), channel_id=1, source_target_pairs={{0,192},{64,0},{128,64},{192,128},{1,193},{65,1},{129,65},{193,129... | collective-permute-start | bytes 1572872 | tf_op jit(solution)/shard_map/ppermute | solution.py:16
  139.9 2.7 %collective-permute-start.16 = (bf16[8,112,128]{2,1,0:T(8,128)(2,1)S(1)}, bf16[8,112,128]{2,1,0:T(8,128)(2,1)S(1)}, u32[]{:S(2)}, u32[]{:S(2)}) collective-permute-start(bf16[8,112,128]{2,1,0:T(8,128)(2,1)S(1)} %all-to-all-done.1.p0), channel_id=1, source_target_pairs={{0,24},{8,0},{16,8},{24,16},{1,25},{9,1},{17,9},{25,17},{2,26},{10... | collective-permute-start | bytes 688136 | tf_op jit(solution)/shard_map/ppermute | solution.py:16
  142.6 1.2 fusion.6
  143.8 0.8 collective-permute-start.17
  145.5 9.2 %collective-permute-done.16.p1 = bf16[8,112,128]{2,1,0:T(8,128)(2,1)S(1)} collective-permute-done((bf16[8,112,128]{2,1,0:T(8,128)(2,1)S(1)}, bf16[8,112,128]{2,1,0:T(8,128)(2,1)S(1)}, u32[]{:S(2)}, u32[]{:S(2)}) %collective-permute-start.16) | collective-permute-done | bytes 229408 | tf_op jit(solution)/shard_map/ppermute | solution.py:16
  154.7 3.2 %collective-permute-start.21 = (f32[2,128]{1,0:T(2,128)S(1)}, f32[2,128]{1,0:T(2,128)S(1)}, u32[]{:S(2)}, u32[]{:S(2)}) collective-permute-start(f32[2,128]{1,0:T(2,128)S(1)} %pad_maximum_fusion), channel_id=1, source_target_pairs={{0,192},{64,0},{128,64},{192,128},{1,193},{65,1},{129,65},{193,129... | collective-permute-start | bytes 3080 | tf_op jit(solution)/shard_map/ppermute | solution.py:16
  158.1 3.6 %collective-permute-done.18.p3 = bf16[8,112,128]{2,1,0:T(8,128)(2,1)S(1)} collective-permute-done((bf16[8,112,128]{2,1,0:T(8,128)(2,1)S(1)}, bf16[8,112,128]{2,1,0:T(8,128)(2,1)S(1)}, u32[]{:S(2)}, u32[]{:S(2)}) %collective-permute-start.18) | collective-permute-done | bytes 229408 | tf_op jit(solution)/shard_map/ppermute | solution.py:16
  161.7 0.7 copy-done.12
  163.0 2.4 %collective-permute-start.30 = (bf16[128,1024]{1,0:T(8,128)(2,1)S(1)}, bf16[128,1024]{1,0:T(8,128)(2,1)}, u32[]{:S(2)}, u32[]{:S(2)}) collective-permute-start(bf16[128,1024]{1,0:T(8,128)(2,1)S(1)} %slice.43), channel_id=1, source_target_pairs={{0,192},{64,0},{128,64},{192,128},{1,193},{65,1},{129,65},{193,129... | collective-permute-start | bytes 786440 | tf_op jit(solution)/shard_map/ppermute | solution.py:16
  165.4 5.8 %collective-permute-done.28.refs_6_ = bf16[128,1024]{1,0:T(8,128)(2,1)} collective-permute-done((bf16[128,1024]{1,0:T(8,128)(2,1)S(1)}, bf16[128,1024]{1,0:T(8,128)(2,1)}, u32[]{:S(2)}, u32[]{:S(2)}) %collective-permute-start.28) | collective-permute-done | bytes 262176 | tf_op jit(solution)/shard_map/ppermute | solution.py:16
  171.8 0.7 stack.125.who
  172.4 0.6 concatenate.4.scales
  174.0 7.4 %shard_map.62 = f32[384,2048]{1,0:T(8,128)} custom-call(s32[10]{0:T(128)} %stack.125.who, bf16[8,112,128]{2,1,0:T(8,128)(2,1)} %copy-done.7, bf16[8,112,128]{2,1,0:T(8,128)(2,1)} %copy-done.11, bf16[8,112,128]{2,1,0:T(8,128)(2,1)} %collective-permute-done.17.p2, bf16[8,112,128]{2,1,0:T(8,128)(2,1)} %copy-done.12, f32[8,128]{1,0:T(8,128)} %concatenate.4.scales, ...), custom_call_target="tpu_custom_call" | custom-call | flops 1610612736 | bytes 6291456 | tf_op jit(solution)/shard_map/pallas_call | solution.py:45
  181.5 0.7 reduce_sum.35
  (87 shorter events, 6.9 us)
Async XLA Ops:
  2.1 17.6 %all-to-all-start = ((bf16[8,96,128]{2,1,0:T(8,128)(2,1)}), bf16[8,96,128]{2,1,0:T(8,128)(2,1)S(1)}, u32[]{:S(2)}, u32[]{:S(2)}) async-start(bf16[8,96,128]{2,1,0:T(8,128)(2,1)} %broadcast_in_dim.8), calls=%async_computation | async-start | bytes 393216 | tf_op jit(solution)/shard_map/all_to_all | solution.py:24
  10.7 63.9 %copy-start.16 = (s32[128]{0:T(128)S(1)}, s32[128]{0:T(128)}, u32[]{:S(2)}) copy-start(s32[128]{0:T(128)} %param.5) | copy-start | bytes 1540
  10.7 51.7 %collective-permute-start.3 = (bf16[384,2048]{1,0:T(8,128)(2,1)}, bf16[384,2048]{1,0:T(8,128)(2,1)S(1)}, u32[]{:S(2)}, u32[]{:S(2)}) collective-permute-start(bf16[384,2048]{1,0:T(8,128)(2,1)} %refs_0_.3), channel_id=1, source_target_pairs={{0,32},{32,0},{1,33},{33,1},{2,34},{34,2},{3,35},{35,3},{4,36},{36... | collective-permute-start | bytes 4718600 | tf_op jit(solution)/shard_map/ppermute | solution.py:20
  13.3 28.6 %collective-permute-start.4 = (bf16[384,1024]{1,0:T(8,128)(2,1)}, bf16[384,1024]{1,0:T(8,128)(2,1)S(1)}, u32[]{:S(2)}, u32[]{:S(2)}) collective-permute-start(bf16[384,1024]{1,0:T(8,128)(2,1)} %get-tuple-element.20), channel_id=1, source_target_pairs={{0,64},{64,128},{128,192},{192,0},{1,65},{65,129},{129,193},{193,1... | collective-permute-start | bytes 2359304 | tf_op jit(solution)/shard_map/ppermute | solution.py:16
  14.8 27.2 %collective-permute-start.6 = (bf16[384,1024]{1,0:T(8,128)(2,1)}, bf16[384,1024]{1,0:T(8,128)(2,1)S(1)}, u32[]{:S(2)}, u32[]{:S(2)}) collective-permute-start(bf16[384,1024]{1,0:T(8,128)(2,1)} %get-tuple-element.20), channel_id=1, source_target_pairs={{0,192},{64,0},{128,64},{192,128},{1,193},{65,1},{129,65},{193,129... | collective-permute-start | bytes 2359304 | tf_op jit(solution)/shard_map/ppermute | solution.py:16
  16.5 35.1 %collective-permute-start.10 = (bf16[384,1024]{1,0:T(8,128)(2,1)}, bf16[384,1024]{1,0:T(8,128)(2,1)}, u32[]{:S(2)}, u32[]{:S(2)}) collective-permute-start(bf16[384,1024]{1,0:T(8,128)(2,1)} %get-tuple-element.19), channel_id=1, source_target_pairs={{0,192},{64,0},{128,64},{192,128},{1,193},{65,1},{129,65},{193,129... | collective-permute-start | bytes 2359304 | tf_op jit(solution)/shard_map/ppermute | solution.py:16
  19.7 55.5 %copy-start.8 = (bf16[8,96,128]{2,1,0:T(8,128)(2,1)}, bf16[8,96,128]{2,1,0:T(8,128)(2,1)S(1)}, u32[]{:S(2)}) copy-start(bf16[8,96,128]{2,1,0:T(8,128)(2,1)S(1)} %all-to-all-done.p0) | copy-start | bytes 589828
  19.7 6.2 %collective-permute-start = (bf16[8,96,128]{2,1,0:T(8,128)(2,1)S(1)}, bf16[8,96,128]{2,1,0:T(8,128)(2,1)S(1)}, u32[]{:S(2)}, u32[]{:S(2)}) collective-permute-start(bf16[8,96,128]{2,1,0:T(8,128)(2,1)S(1)} %all-to-all-done.p0), channel_id=1, source_target_pairs={{0,24},{8,0},{16,8},{24,16},{1,25},{9,1},{17,9},{25,17},{2,26},{10... | collective-permute-start | bytes 589832 | tf_op jit(solution)/shard_map/ppermute | solution.py:16
  25.9 49.3 %copy-start.13 = (bf16[8,96,128]{2,1,0:T(8,128)(2,1)}, bf16[8,96,128]{2,1,0:T(8,128)(2,1)S(1)}, u32[]{:S(2)}) copy-start(bf16[8,96,128]{2,1,0:T(8,128)(2,1)S(1)} %collective-permute-done.p1) | copy-start | bytes 589828
  25.9 7.2 %collective-permute-start.1 = (bf16[8,96,128]{2,1,0:T(8,128)(2,1)S(1)}, bf16[8,96,128]{2,1,0:T(8,128)(2,1)S(1)}, u32[]{:S(2)}, u32[]{:S(2)}) collective-permute-start(bf16[8,96,128]{2,1,0:T(8,128)(2,1)S(1)} %all-to-all-done.p0), channel_id=1, source_target_pairs={{0,16},{8,24},{16,0},{24,8},{1,17},{9,25},{17,1},{25,9},{2,18},{10... | collective-permute-start | bytes 589832 | tf_op jit(solution)/shard_map/ppermute | solution.py:16
  33.0 8.8 %copy-start.14 = (bf16[8,96,128]{2,1,0:T(8,128)(2,1)}, bf16[8,96,128]{2,1,0:T(8,128)(2,1)S(1)}, u32[]{:S(2)}) copy-start(bf16[8,96,128]{2,1,0:T(8,128)(2,1)S(1)} %collective-permute-done.1.p2) | copy-start | bytes 589828
  33.1 7.3 %collective-permute-start.2 = (bf16[8,96,128]{2,1,0:T(8,128)(2,1)S(1)}, bf16[8,96,128]{2,1,0:T(8,128)(2,1)S(1)}, u32[]{:S(2)}, u32[]{:S(2)}) collective-permute-start(bf16[8,96,128]{2,1,0:T(8,128)(2,1)S(1)} %all-to-all-done.p0), channel_id=1, source_target_pairs={{0,8},{8,16},{16,24},{24,0},{1,9},{9,17},{17,25},{25,1},{2,10},{10... | collective-permute-start | bytes 589832 | tf_op jit(solution)/shard_map/ppermute | solution.py:16
  40.4 21.9 %collective-permute-start.8 = (bf16[384,1024]{1,0:T(8,128)(2,1)}, bf16[384,1024]{1,0:T(8,128)(2,1)}, u32[]{:S(2)}, u32[]{:S(2)}) collective-permute-start(bf16[384,1024]{1,0:T(8,128)(2,1)} %get-tuple-element.19), channel_id=1, source_target_pairs={{0,64},{64,128},{128,192},{192,0},{1,65},{65,129},{129,193},{193,1... | collective-permute-start | bytes 2359304 | tf_op jit(solution)/shard_map/ppermute | solution.py:16
  41.9 46.9 %copy-start.1 = (bf16[384,1024]{1,0:T(8,128)(2,1)}, bf16[384,1024]{1,0:T(8,128)(2,1)S(1)}, u32[]{:S(2)}) copy-start(bf16[384,1024]{1,0:T(8,128)(2,1)S(1)} %collective-permute-done.4.refs_2_) | copy-start | bytes 2359300
  41.9 20.9 %collective-permute-start.5 = (bf16[384,1024]{1,0:T(8,128)(2,1)S(1)}, bf16[384,1024]{1,0:T(8,128)(2,1)S(1)}, u32[]{:S(2)}, u32[]{:S(2)}) collective-permute-start(bf16[384,1024]{1,0:T(8,128)(2,1)S(1)} %collective-permute-done.4.refs_2_), channel_id=1, source_target_pairs={{0,32},{32,0},{1,33},{33,1},{2,34},{34,2},{3,35},{35,3},{4,36},{36... | collective-permute-start | bytes 2359304 | tf_op jit(solution)/shard_map/ppermute | solution.py:20
  42.0 46.7 %copy-start.2 = (bf16[384,1024]{1,0:T(8,128)(2,1)}, bf16[384,1024]{1,0:T(8,128)(2,1)S(1)}, u32[]{:S(2)}) copy-start(bf16[384,1024]{1,0:T(8,128)(2,1)S(1)} %collective-permute-done.6.refs_4_) | copy-start | bytes 2359300
  42.0 31.4 %collective-permute-start.12 = (bf16[384,1024]{1,0:T(8,128)(2,1)S(1)}, bf16[384,1024]{1,0:T(8,128)(2,1)}, u32[]{:S(2)}, u32[]{:S(2)}) collective-permute-start(bf16[384,1024]{1,0:T(8,128)(2,1)S(1)} %collective-permute-done.4.refs_2_), channel_id=1, source_target_pairs={{0,64},{64,128},{128,192},{192,0},{1,65},{65,129},{129,193},{193,1... | collective-permute-start | bytes 2359304 | tf_op jit(solution)/shard_map/ppermute | solution.py:16
  51.6 21.8 %collective-permute-start.14 = (bf16[384,1024]{1,0:T(8,128)(2,1)}, bf16[384,1024]{1,0:T(8,128)(2,1)}, u32[]{:S(2)}, u32[]{:S(2)}) collective-permute-start(bf16[384,1024]{1,0:T(8,128)(2,1)} %collective-permute-done.10.refs_8_.refs_10_), channel_id=1, source_target_pairs={{0,192},{64,0},{128,64},{192,128},{1,193},{65,1},{129,65},{193,129... | collective-permute-start | bytes 2359304 | tf_op jit(solution)/shard_map/ppermute | solution.py:16
  62.3 26.4 %collective-permute-start.7 = (bf16[384,1024]{1,0:T(8,128)(2,1)S(1)}, bf16[384,1024]{1,0:T(8,128)(2,1)}, u32[]{:S(2)}, u32[]{:S(2)}) collective-permute-start(bf16[384,1024]{1,0:T(8,128)(2,1)S(1)} %collective-permute-done.6.refs_4_), channel_id=1, source_target_pairs={{0,32},{32,0},{1,33},{33,1},{2,34},{34,2},{3,35},{35,3},{4,36},{36... | collective-permute-start | bytes 2359304 | tf_op jit(solution)/shard_map/ppermute | solution.py:20
  62.3 26.4 %copy-start = (bf16[384,2048]{1,0:T(8,128)(2,1)}, bf16[384,2048]{1,0:T(8,128)(2,1)S(1)}, u32[]{:S(2)}) copy-start(bf16[384,2048]{1,0:T(8,128)(2,1)S(1)} %collective-permute-done.3.refs_1_) | copy-start | bytes 4718596
  62.3 26.4 %collective-permute-start.9 = (bf16[384,1024]{1,0:T(8,128)(2,1)}, bf16[384,1024]{1,0:T(8,128)(2,1)}, u32[]{:S(2)}, u32[]{:S(2)}) collective-permute-start(bf16[384,1024]{1,0:T(8,128)(2,1)} %collective-permute-done.8.refs_6_.refs_8_), channel_id=1, source_target_pairs={{0,32},{32,0},{1,33},{33,1},{2,34},{34,2},{3,35},{35,3},{4,36},{36... | collective-permute-start | bytes 2359304 | tf_op jit(solution)/shard_map/ppermute | solution.py:20
  62.9 10.6 %copy-start.3 = (bf16[384,1024]{1,0:T(8,128)(2,1)}, bf16[384,1024]{1,0:T(8,128)(2,1)S(1)}, u32[]{:S(2)}) copy-start(bf16[384,1024]{1,0:T(8,128)(2,1)S(1)} %collective-permute-done.5.refs_3_) | copy-start | bytes 2359300
  62.9 25.9 %collective-permute-start.11 = (bf16[384,1024]{1,0:T(8,128)(2,1)}, bf16[384,1024]{1,0:T(8,128)(2,1)}, u32[]{:S(2)}, u32[]{:S(2)}) collective-permute-start(bf16[384,1024]{1,0:T(8,128)(2,1)} %collective-permute-done.10.refs_8_.refs_10_), channel_id=1, source_target_pairs={{0,32},{32,0},{1,33},{33,1},{2,34},{34,2},{3,35},{35,3},{4,36},{36... | collective-permute-start | bytes 2359304 | tf_op jit(solution)/shard_map/ppermute | solution.py:20
  73.4 23.2 %collective-permute-start.13 = (bf16[384,1024]{1,0:T(8,128)(2,1)}, bf16[384,1024]{1,0:T(8,128)(2,1)}, u32[]{:S(2)}, u32[]{:S(2)}) collective-permute-start(bf16[384,1024]{1,0:T(8,128)(2,1)} %collective-permute-done.12.left.refs_6_), channel_id=1, source_target_pairs={{0,32},{32,0},{1,33},{33,1},{2,34},{34,2},{3,35},{35,3},{4,36},{36... | collective-permute-start | bytes 2359304 | tf_op jit(solution)/shard_map/ppermute | solution.py:20
  73.5 23.2 %collective-permute-start.15 = (bf16[384,1024]{1,0:T(8,128)(2,1)}, bf16[384,1024]{1,0:T(8,128)(2,1)}, u32[]{:S(2)}, u32[]{:S(2)}) collective-permute-start(bf16[384,1024]{1,0:T(8,128)(2,1)} %collective-permute-done.14.right.refs_12_), channel_id=1, source_target_pairs={{0,32},{32,0},{1,33},{33,1},{2,34},{34,2},{3,35},{35,3},{4,36},{36... | collective-permute-start | bytes 2359304 | tf_op jit(solution)/shard_map/ppermute | solution.py:20
  78.2 10.5 %all-to-all-start.1 = ((bf16[8,112,128]{2,1,0:T(8,128)(2,1)}), bf16[8,112,128]{2,1,0:T(8,128)(2,1)S(1)}, u32[]{:S(2)}, u32[]{:S(2)}) async-start(bf16[8,112,128]{2,1,0:T(8,128)(2,1)} %get-tuple-element.12), calls=%async_computation.1 | async-start | bytes 458752 | tf_op jit(solution)/shard_map/all_to_all | solution.py:309
  88.7 56.3 %copy-start.7 = (bf16[8,112,128]{2,1,0:T(8,128)(2,1)}, bf16[8,112,128]{2,1,0:T(8,128)(2,1)S(1)}, u32[]{:S(2)}) copy-start(bf16[8,112,128]{2,1,0:T(8,128)(2,1)S(1)} %all-to-all-done.1.p0) | copy-start | bytes 688132
  103.8 19.3 %all-to-all-start.2 = ((f32[32,3,128]{2,1,0:T(4,128)}), f32[32,3,128]{2,1,0:T(4,128)S(1)}, u32[]{:S(2)}, u32[]{:S(2)}) async-start(f32[32,3,128]{2,1,0:T(4,128)} %broadcast_in_dim.10), calls=%async_computation.2 | async-start | bytes 131072 | tf_op jit(solution)/shard_map/all_to_all | solution.py:24
  126.6 9.9 %copy-start.4 = (bf16[128,2048]{1,0:T(8,128)(2,1)S(1)}, bf16[128,2048]{1,0:T(8,128)(2,1)}, u32[]{:S(2)}) copy-start(bf16[128,2048]{1,0:T(8,128)(2,1)} %get-tuple-element.15.powers.refs_0_) | copy-start | bytes 1572868
  126.6 54.8 %all-to-all-start.3 = ((bf16[32,96,128]{2,1,0:T(8,128)(2,1)}), bf16[32,96,128]{2,1,0:T(8,128)(2,1)S(1)}, u32[]{:S(2)}, u32[]{:S(2)}) async-start(bf16[32,96,128]{2,1,0:T(8,128)(2,1)} %bitcast.30), calls=%async_computation.3 | async-start | bytes 1572864 | tf_op jit(solution)/shard_map/all_to_all | solution.py:338
  136.6 18.1 %collective-permute-start.24 = (bf16[128,2048]{1,0:T(8,128)(2,1)S(1)}, bf16[128,2048]{1,0:T(8,128)(2,1)S(1)}, u32[]{:S(2)}, u32[]{:S(2)}) collective-permute-start(bf16[128,2048]{1,0:T(8,128)(2,1)S(1)} %copy-done.4), channel_id=1, source_target_pairs={{0,64},{64,128},{128,192},{192,0},{1,65},{65,129},{129,193},{193,1... | collective-permute-start | bytes 1572872 | tf_op jit(solution)/shard_map/ppermute | solution.py:16
  137.2 20.7 %collective-permute-start.26 = (bf16[128,2048]{1,0:T(8,128)(2,1)S(1)}, bf16[128,2048]{1,0:T(8,128)(2,1)S(1)}, u32[]{:S(2)}, u32[]{:S(2)}) collective-permute-start(bf16[128,2048]{1,0:T(8,128)(2,1)S(1)} %copy-done.4), channel_id=1, source_target_pairs={{0,192},{64,0},{128,64},{192,128},{1,193},{65,1},{129,65},{193,129... | collective-permute-start | bytes 1572872 | tf_op jit(solution)/shard_map/ppermute | solution.py:16
  139.9 14.8 %collective-permute-start.16 = (bf16[8,112,128]{2,1,0:T(8,128)(2,1)S(1)}, bf16[8,112,128]{2,1,0:T(8,128)(2,1)S(1)}, u32[]{:S(2)}, u32[]{:S(2)}) collective-permute-start(bf16[8,112,128]{2,1,0:T(8,128)(2,1)S(1)} %all-to-all-done.1.p0), channel_id=1, source_target_pairs={{0,24},{8,0},{16,8},{24,16},{1,25},{9,1},{17,9},{25,17},{2,26},{10... | collective-permute-start | bytes 688136 | tf_op jit(solution)/shard_map/ppermute | solution.py:16
  143.8 1.2 collective-permute-start.19
  143.8 14.2 %collective-permute-start.17 = (bf16[8,112,128]{2,1,0:T(8,128)(2,1)S(1)}, bf16[8,112,128]{2,1,0:T(8,128)(2,1)}, u32[]{:S(2)}, u32[]{:S(2)}) collective-permute-start(bf16[8,112,128]{2,1,0:T(8,128)(2,1)S(1)} %all-to-all-done.1.p0), channel_id=1, source_target_pairs={{0,16},{8,24},{16,0},{24,8},{1,17},{9,25},{17,1},{25,9},{2,18},{10... | collective-permute-start | bytes 688136 | tf_op jit(solution)/shard_map/ppermute | solution.py:16
  145.0 16.7 %collective-permute-start.18 = (bf16[8,112,128]{2,1,0:T(8,128)(2,1)S(1)}, bf16[8,112,128]{2,1,0:T(8,128)(2,1)S(1)}, u32[]{:S(2)}, u32[]{:S(2)}) collective-permute-start(bf16[8,112,128]{2,1,0:T(8,128)(2,1)S(1)} %all-to-all-done.1.p0), channel_id=1, source_target_pairs={{0,8},{8,16},{16,24},{24,0},{1,9},{9,17},{17,25},{25,1},{2,10},{10... | collective-permute-start | bytes 688136 | tf_op jit(solution)/shard_map/ppermute | solution.py:16
  154.7 7.7 %collective-permute-start.20 = (f32[2,128]{1,0:T(2,128)S(1)}, f32[2,128]{1,0:T(2,128)S(1)}, u32[]{:S(2)}, u32[]{:S(2)}) collective-permute-start(f32[2,128]{1,0:T(2,128)S(1)} %pad_maximum_fusion), channel_id=1, source_target_pairs={{0,64},{64,128},{128,192},{192,0},{1,65},{65,129},{129,193},{193,1... | collective-permute-start | bytes 3080 | tf_op jit(solution)/shard_map/ppermute | solution.py:16
  154.7 18.8 %copy-start.5 = (bf16[128,2048]{1,0:T(8,128)(2,1)}, bf16[128,2048]{1,0:T(8,128)(2,1)S(1)}, u32[]{:S(2)}) copy-start(bf16[128,2048]{1,0:T(8,128)(2,1)S(1)} %collective-permute-done.24.refs_2_) | copy-start | bytes 1572868
  154.7 7.7 %collective-permute-start.21 = (f32[2,128]{1,0:T(2,128)S(1)}, f32[2,128]{1,0:T(2,128)S(1)}, u32[]{:S(2)}, u32[]{:S(2)}) collective-permute-start(f32[2,128]{1,0:T(2,128)S(1)} %pad_maximum_fusion), channel_id=1, source_target_pairs={{0,192},{64,0},{128,64},{192,128},{1,193},{65,1},{129,65},{193,129... | collective-permute-start | bytes 3080 | tf_op jit(solution)/shard_map/ppermute | solution.py:16
  157.9 15.6 %copy-start.6 = (bf16[128,2048]{1,0:T(8,128)(2,1)}, bf16[128,2048]{1,0:T(8,128)(2,1)S(1)}, u32[]{:S(2)}) copy-start(bf16[128,2048]{1,0:T(8,128)(2,1)S(1)} %collective-permute-done.26.refs_4_) | copy-start | bytes 1572868
  157.9 5.1 %collective-permute-start.22 = (f32[2,128]{1,0:T(2,128)S(1)}, f32[2,128]{1,0:T(2,128)S(1)}, u32[]{:S(2)}, u32[]{:S(2)}) collective-permute-start(f32[2,128]{1,0:T(2,128)S(1)} %pad_maximum_fusion), channel_id=1, source_target_pairs={{0,128},{64,192},{128,0},{192,64},{1,129},{65,193},{129,1},{193,65... | collective-permute-start | bytes 3080 | tf_op jit(solution)/shard_map/ppermute | solution.py:16
  158.0 15.0 %collective-permute-start.23 = (bf16[128,2048]{1,0:T(8,128)(2,1)S(1)}, bf16[128,2048]{1,0:T(8,128)(2,1)S(1)}, u32[]{:S(2)}, u32[]{:S(2)}) collective-permute-start(bf16[128,2048]{1,0:T(8,128)(2,1)S(1)} %copy-done.4), channel_id=1, source_target_pairs={{0,32},{32,0},{1,33},{33,1},{2,34},{34,2},{3,35},{35,3},{4,36},{36... | collective-permute-start | bytes 1572872 | tf_op jit(solution)/shard_map/ppermute | solution.py:20
  161.7 9.6 %collective-permute-start.28 = (bf16[128,1024]{1,0:T(8,128)(2,1)S(1)}, bf16[128,1024]{1,0:T(8,128)(2,1)}, u32[]{:S(2)}, u32[]{:S(2)}) collective-permute-start(bf16[128,1024]{1,0:T(8,128)(2,1)S(1)} %slice.42), channel_id=1, source_target_pairs={{0,64},{64,128},{128,192},{192,0},{1,65},{65,129},{129,193},{193,1... | collective-permute-start | bytes 786440 | tf_op jit(solution)/shard_map/ppermute | solution.py:16
  162.4 10.6 %collective-permute-start.25 = (bf16[128,2048]{1,0:T(8,128)(2,1)S(1)}, bf16[128,2048]{1,0:T(8,128)(2,1)S(1)}, u32[]{:S(2)}, u32[]{:S(2)}) collective-permute-start(bf16[128,2048]{1,0:T(8,128)(2,1)S(1)} %collective-permute-done.24.refs_2_), channel_id=1, source_target_pairs={{0,32},{32,0},{1,33},{33,1},{2,34},{34,2},{3,35},{35,3},{4,36},{36... | collective-permute-start | bytes 1572872 | tf_op jit(solution)/shard_map/ppermute | solution.py:20
  162.4 10.6 %collective-permute-start.27 = (bf16[128,2048]{1,0:T(8,128)(2,1)S(1)}, bf16[128,2048]{1,0:T(8,128)(2,1)}, u32[]{:S(2)}, u32[]{:S(2)}) collective-permute-start(bf16[128,2048]{1,0:T(8,128)(2,1)S(1)} %collective-permute-done.26.refs_4_), channel_id=1, source_target_pairs={{0,32},{32,0},{1,33},{33,1},{2,34},{34,2},{3,35},{35,3},{4,36},{36... | collective-permute-start | bytes 1572872 | tf_op jit(solution)/shard_map/ppermute | solution.py:20
  163.0 8.3 %collective-permute-start.30 = (bf16[128,1024]{1,0:T(8,128)(2,1)S(1)}, bf16[128,1024]{1,0:T(8,128)(2,1)}, u32[]{:S(2)}, u32[]{:S(2)}) collective-permute-start(bf16[128,1024]{1,0:T(8,128)(2,1)S(1)} %slice.43), channel_id=1, source_target_pairs={{0,192},{64,0},{128,64},{192,128},{1,193},{65,1},{129,65},{193,129... | collective-permute-start | bytes 786440 | tf_op jit(solution)/shard_map/ppermute | solution.py:16
  171.2 1.9 %collective-permute-start.29 = (bf16[128,1024]{1,0:T(8,128)(2,1)}, bf16[128,1024]{1,0:T(8,128)(2,1)}, u32[]{:S(2)}, u32[]{:S(2)}) collective-permute-start(bf16[128,1024]{1,0:T(8,128)(2,1)} %collective-permute-done.28.refs_6_), channel_id=1, source_target_pairs={{0,32},{32,0},{1,33},{33,1},{2,34},{34,2},{3,35},{35,3},{4,36},{36... | collective-permute-start | bytes 786440 | tf_op jit(solution)/shard_map/ppermute | solution.py:20
  171.3 2.2 %collective-permute-start.31 = (bf16[128,1024]{1,0:T(8,128)(2,1)}, bf16[128,1024]{1,0:T(8,128)(2,1)}, u32[]{:S(2)}, u32[]{:S(2)}) collective-permute-start(bf16[128,1024]{1,0:T(8,128)(2,1)} %collective-permute-done.30.refs_8_), channel_id=1, source_target_pairs={{0,32},{32,0},{1,33},{33,1},{2,34},{34,2},{3,35},{35,3},{4,36},{36... | collective-permute-start | bytes 786440 | tf_op jit(solution)/shard_map/ppermute | solution.py:20
  (5 other events, 7.3 us)

commit v3 on v2

--- a/solution.py
+++ b/solution.py
@@ -1,3 +1,5 @@
+import functools
+
 import jax
 import jax.numpy as jnp
 from jax import lax
@@ -84,41 +86,44 @@
     )
 
 
-def near_kernel(who, states, *refs):
+def part_kernel(who, states, *refs, own, halves, more):
     *arrays, out = refs
     first = pl.program_id(0) < STEPS // 2
 
-    def total(chosen):
-        acc = None
-        for k, ref in enumerate(chosen):
+    def total(chosen, at):
+        acc = arrays[-1][...] if more else None
+        for k, ref in list(enumerate(arrays[:own])) + list(enumerate(chosen, at)):
             term = dot(states[who[k]], ref[...])
             acc = term if acc is None else acc + term
-        return acc
+        out[...] = acc
 
     @pl.when(first)
     def _():
-        out[...] = total(arrays[:6])
+        total(arrays[own : own + halves], own)
 
     @pl.when(~first)
     def _():
-        out[...] = total(arrays[:2] + arrays[6:])
-
-
-def near_logits(states, own, left, right, who):
-    rows, width = own[0].shape
+        total(arrays[own + halves : own + 2 * halves], own + halves)
+
+
+def logits_part(states, own, left, right, who, acc=None):
+    rows, half = left[0].shape
+    width = 2 * half
     tokens = states.shape[1]
     wide = width // STEPS
-    specs = [whole(states)] + [pl.BlockSpec((rows, wide), lambda j, s: (0, j))] * 2
-    specs += [pl.BlockSpec((rows, wide), lambda j, s: (0, early(j)))] * 4
-    specs += [pl.BlockSpec((rows, wide), lambda j, s: (0, late(j)))] * 4
-    return call(
-        near_kernel,
+    tail = [] if acc is None else [acc]
+    specs = [whole(states)] + [pl.BlockSpec((rows, wide), lambda j, s: (0, j))] * len(own)
+    specs += [pl.BlockSpec((rows, wide), lambda j, s: (0, early(j)))] * len(left)
+    specs += [pl.BlockSpec((rows, wide), lambda j, s: (0, late(j)))] * len(right)
+    specs += [pl.BlockSpec((tokens, wide), lambda j, s: (0, j))] * len(tail)
+    return call(
+        functools.partial(part_kernel, own=len(own), halves=len(left), more=bool(tail)),
         who,
-        [states, *own, *left, *right],
+        [states, *own, *left, *right, *tail],
         specs,
         pl.BlockSpec((tokens, wide), lambda j, s: (0, j)),
         jax.ShapeDtypeStruct((tokens, width), F32),
-        12 * tokens * rows * width,
+        2 * (len(own) + len(left)) * tokens * rows * width,
     )
 
 
@@ -173,47 +178,52 @@
     )
 
 
-def terms_kernel(starts, powers, labels, *refs):
-    *arrays, sums, picks, both = refs
+def terms_kernel(starts, powers, labels, parts, stats, *refs):
+    *arrays, out, rows_out, errors = refs
     step = pl.program_id(0)
-    width, double = both.shape
-    tokens = double // 2
+    width, tokens = errors.shape
 
     @pl.when(step == 0)
     def _():
-        both[:, :tokens] = powers[...].T
+        peaks = parts[:, 0, :]
+        peak = jnp.max(peaks, axis=0, keepdims=True)
+        total = jnp.sum(parts[:, 1, :] * jnp.exp(peaks - peak), axis=0, keepdims=True)
+        target = jnp.sum(parts[:, 2, :], axis=0, keepdims=True)
+        scale = jnp.exp(stats[0:1, :] - peak) / total
+        loss = jnp.log(total) + peak - target
+        rows_out[...] = jnp.concatenate([scale, loss] + [scale] * 6, axis=0)
         columns = starts[8] + lax.broadcasted_iota(jnp.int32, (width, tokens), 0)
-        both[:, tokens:] = jnp.where(columns == labels[...], 1.0, 0.0).astype(BF)
+        hit = jnp.where(columns == labels[...], 1.0, 0.0)
+        errors[...] = (powers[...].T.astype(F32) * scale - hit).astype(BF)
 
     half = width // 2
     own, left, right = arrays[:2], arrays[2:8], arrays[8:]
     lefts = jnp.concatenate([a[:, :half] for a in own] + [a[...] for a in left], axis=0)
     rights = jnp.concatenate([a[:, half:] for a in own] + [a[...] for a in right], axis=0)
-    term = dot(lefts, both[:half, :]) + dot(rights, both[half:, :])
+    term = dot(lefts, errors[:half, :]) + dot(rights, errors[half:, :])
     rows = own[0].shape[0]
     for k in range(8):
         at = pl.ds(pl.multiple_of(starts[k] + step * rows, 32), rows)
-        sums[at, :] = term[k * rows : (k + 1) * rows, :tokens]
-        picks[at, :] = term[k * rows : (k + 1) * rows, tokens:].astype(BF)
-
-
-def state_terms(powers, labels, own, left, right, starts, depth):
+        out[at, :] = term[k * rows : (k + 1) * rows].astype(BF)
+
+
+def state_terms(powers, labels, parts, stats, own, left, right, starts, depth):
     tokens, width = powers.shape
     rows = own[0].shape[0] // STEPS
-    args = [powers, labels, *own, *left, *right]
-    specs = [whole(powers), whole(labels)]
-    specs += [pl.BlockSpec((rows, a.shape[1]), lambda j, s: (j, 0)) for a in args[2:]]
-    sums = jax.ShapeDtypeStruct((depth, tokens), F32)
-    picks = jax.ShapeDtypeStruct((depth, tokens), BF)
+    args = [powers, labels, parts, stats, *own, *left, *right]
+    specs = [whole(a) for a in args[:4]]
+    specs += [pl.BlockSpec((rows, a.shape[1]), lambda j, s: (j, 0)) for a in args[4:]]
+    terms = jax.ShapeDtypeStruct((depth, tokens), BF)
+    rows_out = jax.ShapeDtypeStruct((8, tokens), F32)
     return call(
         terms_kernel,
         starts,
         args,
         specs,
-        [whole(sums), whole(picks)],
-        [sums, picks],
-        4 * tokens * width * depth,
-        [pltpu.VMEM((width, 2 * tokens), BF)],
+        [whole(terms), whole(rows_out)],
+        [terms, rows_out],
+        2 * tokens * width * depth,
+        [pltpu.VMEM((width, tokens), BF)],
     )
 
 
@@ -296,8 +306,8 @@
     far_left = shift(up_left, "x", NX, 1)
     far_right = shift(down_right, "x", NX, -1)
     up_left_other, down_right_other = swap(up_left), swap(down_right)
-    left = [up_left, up_left_other, down_left, swap(down_left)]
-    right = [up_right, swap(up_right), down_right, down_right_other]
+    left = [down_left, swap(down_left)]
+    right = [up_right, swap(up_right)]
     away_left = [far_left, swap(far_left)]
     away_right = [far_right, swap(far_right)]
 
@@ -310,7 +320,14 @@
     far_states, wanted = lax.optimization_barrier((states, wanted))
 
     slices = [wanted] + [shift(wanted, "y", NY, -j) for j in (1, 2, 3)]
-    logits = near_logits(states, own, left, right, who(0) + who(3) + who(1))
+    logits = logits_part(
+        states,
+        own,
+        [up_left, up_left_other],
+        [down_right, down_right_other],
+        who(0) + who(3) + who(1),
+    )
+    logits = logits_part(states, [], left, right, who(1) + who(3), logits)
     powers, stats = far_logits(
         far_states, labels[:, None], logits, away_left, away_right, who(2) + [base]
     )
@@ -325,16 +342,13 @@
 
     parts = from_everyone(stats[:3], ("y", "z"), NY * NZ)
     starts = [w * rows for w in who(0) + who(3) + who(1) + who(2)]
-    sums, picks = state_terms(
-        powers, labels[None], own, left + away_left, right + away_right, starts + [base], depth
-    )
-    peak = jnp.max(parts[:, 0], axis=0)
-    total = jnp.sum(parts[:, 1] * jnp.exp(parts[:, 0] - peak), axis=0)
-    target = jnp.sum(parts[:, 2], axis=0)
-    token_loss = jnp.log(total) + peak - target
-    scale = jnp.exp(stats[0] - peak) / total
-
-    terms = (sums * scale - picks.astype(F32)).astype(BF)
+    all_left = [up_left, up_left_other, *left, *away_left]
+    all_right = [*right, down_right, down_right_other, *away_right]
+    terms, lines = state_terms(
+        powers, labels[None], parts, stats, own, all_left, all_right, starts + [base], depth
+    )
+    scale, token_loss = lines[0], lines[1]
+
     arrived = lax.all_to_all(
         terms.reshape(NY * NZ, part, tokens), ("y", "z"), 0, 0, tiled=True
     )

time: 185 us -> 189 us (1.022)
  waiting for transfers between devices: 65.7 us -> 73.9 us
  starting transfers between devices: 64.6 us -> 57.2 us
  Pallas kernels: 33.8 us -> 38 us
  other arithmetic: 7.25 us -> 3.11 us
  local copies, waits for them, and re-layouts: 9.91 us -> 12.6 us
    all_to_all x2, waiting for transfers between devices: 1.57 us -> 8.69 us  [from_everyone(): lax.all_to_all(jnp.broadcast_to(a[None], (n, *a.shape)), axis, 0, 0, tile...]
    all_to_all x1, starting transfers between devices: 9.91 us -> 4.85 us  [step(): lax.all_to_all(terms.reshape(NY * NZ, part, tokens), ('y', 'z'), 0, 0, ti...]
    pallas_call x5 -> x6, Pallas kernels: 33.8 us -> 38 us  [call(): pl.pallas_call(kernel, grid_spec=pltpu.PrefetchScalarGridSpec(num_scalar_...]
    convert_element_type x1 -> x0, other arithmetic: 2.75 us -> none  [step(): terms = (sums * scale - picks.astype(F32)).astype(BF)]
    ppermute x19, starting transfers between devices: 30.6 us -> 28 us  [shift(): return lax.ppermute(a, axis, [(i, (i + s) % n) for i in range(n)])]
    div x2 -> x0, other arithmetic: 1.9 us -> none  [step(): scale = jnp.exp(stats[0] - peak) / total]
  transfers between devices with their start and end apart: 36 -> 36, of which waited for: 16 -> 15; matrix products, arithmetic and copies ran while one was open for 5% -> 5% of each run, Pallas kernels for 15% -> 12%
where the time goes in v3:
time: 189 us; the launch traced here: 186 us
  waiting for transfers between devices  73.9 us (39%)
  starting transfers between devices  57.2 us (30%)
  Pallas kernels  38 us (20%)
  local copies, waits for them, and re-layouts  12.6 us (7%)
  other arithmetic  3.11 us (2%)
    ppermute x19, waiting for transfers between devices, shift(): return lax.ppermute(a, axis, [(i, (i + s) % n) for i in range(n)])  58.9 us
    pallas_call x6, Pallas kernels, call(): pl.pallas_call(kernel, grid_spec=pltpu.PrefetchScalarGridSpec(num_scalar_...  38 us
    ppermute x19, starting transfers between devices, shift(): return lax.ppermute(a, axis, [(i, (i + s) % n) for i in range(n)])  28 us
    all_to_all x2, starting transfers between devices, from_everyone(): lax.all_to_all(jnp.broadcast_to(a[None], (n, *a.shape)), axis, 0, 0, tile...  18.6 us
    all_to_all x2, waiting for transfers between devices, from_everyone(): lax.all_to_all(jnp.broadcast_to(a[None], (n, *a.shape)), axis, 0, 0, tile...  8.69 us
    all_to_all x1, waiting for transfers between devices, step(): wanted = lax.all_to_all(wanted, ('x', 'core'), 0, 0, tiled=True)  5.72 us
    all_to_all x1, starting transfers between devices, step(): lax.all_to_all(terms.reshape(NY * NZ, part, tokens), ('y', 'z'), 0, 0, ti...  4.85 us
  transfers between devices with their start and end apart: 36, of which 15 were waited for; matrix products, arithmetic and copies ran while one was open for 5% of the time, Pallas kernels for 12%

profile of v3, /device:TPU:32, one launch (start us, length us, event | category | flops | bytes accessed | tf_op | source)
XLA Modules:
  0.0 185.7 jit_solution(17815799030359526546)
XLA Ops:
  0.6 1.4 broadcast_in_dim.8
  2.1 8.6 %all-to-all-start = ((bf16[8,96,128]{2,1,0:T(8,128)(2,1)}), bf16[8,96,128]{2,1,0:T(8,128)(2,1)S(1)}, u32[]{:S(2)}, u32[]{:S(2)}) async-start(bf16[8,96,128]{2,1,0:T(8,128)(2,1)} %broadcast_in_dim.8), calls=%async_computation | async-start | bytes 393216 | tf_op jit(solution)/shard_map/all_to_all | solution.py:26
  10.6 2.8 %fusion.5 = (bf16[384,1024]{1,0:T(8,128)(2,1)}, bf16[384,1024]{1,0:T(8,128)(2,1)}) fusion(bf16[384,2048]{1,0:T(8,128)(2,1)} %refs_0_.3), kind=kLoop, calls=%fused_computation.18 | loop fusion | bytes 3145728 | tf_op jit(solution)/shard_map/slice | solution.py:303
  13.4 2.8 %collective-permute-start.10 = (bf16[384,1024]{1,0:T(8,128)(2,1)}, bf16[384,1024]{1,0:T(8,128)(2,1)}, u32[]{:S(2)}, u32[]{:S(2)}) collective-permute-start(bf16[384,1024]{1,0:T(8,128)(2,1)} %get-tuple-element.19), channel_id=1, source_target_pairs={{0,192},{64,0},{128,64},{192,128},{1,193},{65,1},{129,65},{193,129... | collective-permute-start | bytes 2359304 | tf_op jit(solution)/shard_map/ppermute | solution.py:18
  16.2 3.2 %collective-permute-start.3 = (bf16[384,1024]{1,0:T(8,128)(2,1)}, bf16[384,1024]{1,0:T(8,128)(2,1)}, u32[]{:S(2)}, u32[]{:S(2)}) collective-permute-start(bf16[384,1024]{1,0:T(8,128)(2,1)} %get-tuple-element.20), channel_id=1, source_target_pairs={{0,192},{64,0},{128,64},{192,128},{1,193},{65,1},{129,65},{193,129... | collective-permute-start | bytes 2359304 | tf_op jit(solution)/shard_map/ppermute | solution.py:18
  19.6 3.0 %collective-permute-start = (bf16[8,96,128]{2,1,0:T(8,128)(2,1)S(1)}, bf16[8,96,128]{2,1,0:T(8,128)(2,1)S(1)}, u32[]{:S(2)}, u32[]{:S(2)}) collective-permute-start(bf16[8,96,128]{2,1,0:T(8,128)(2,1)S(1)} %all-to-all-done.p0), channel_id=1, source_target_pairs={{0,24},{8,0},{16,8},{24,16},{1,25},{9,1},{17,9},{25,17},{2,26},{10... | collective-permute-start | bytes 589832 | tf_op jit(solution)/shard_map/ppermute | solution.py:18
  22.7 3.2 %collective-permute-done.p1 = bf16[8,96,128]{2,1,0:T(8,128)(2,1)S(1)} collective-permute-done((bf16[8,96,128]{2,1,0:T(8,128)(2,1)S(1)}, bf16[8,96,128]{2,1,0:T(8,128)(2,1)S(1)}, u32[]{:S(2)}, u32[]{:S(2)}) %collective-permute-start) | collective-permute-done | bytes 196640 | tf_op jit(solution)/shard_map/ppermute | solution.py:18
  25.9 2.7 %collective-permute-start.1 = (bf16[8,96,128]{2,1,0:T(8,128)(2,1)S(1)}, bf16[8,96,128]{2,1,0:T(8,128)(2,1)S(1)}, u32[]{:S(2)}, u32[]{:S(2)}) collective-permute-start(bf16[8,96,128]{2,1,0:T(8,128)(2,1)S(1)} %all-to-all-done.p0), channel_id=1, source_target_pairs={{0,16},{8,24},{16,0},{24,8},{1,17},{9,25},{17,1},{25,9},{2,18},{10... | collective-permute-start | bytes 589832 | tf_op jit(solution)/shard_map/ppermute | solution.py:18
  28.5 4.5 %collective-permute-done.1.p2 = bf16[8,96,128]{2,1,0:T(8,128)(2,1)S(1)} collective-permute-done((bf16[8,96,128]{2,1,0:T(8,128)(2,1)S(1)}, bf16[8,96,128]{2,1,0:T(8,128)(2,1)S(1)}, u32[]{:S(2)}, u32[]{:S(2)}) %collective-permute-start.1) | collective-permute-done | bytes 196640 | tf_op jit(solution)/shard_map/ppermute | solution.py:18
  33.0 1.0 collective-permute-start.2
  34.1 6.4 %collective-permute-done.2.p3 = bf16[8,96,128]{2,1,0:T(8,128)(2,1)} collective-permute-done((bf16[8,96,128]{2,1,0:T(8,128)(2,1)S(1)}, bf16[8,96,128]{2,1,0:T(8,128)(2,1)}, u32[]{:S(2)}, u32[]{:S(2)}) %collective-permute-start.2) | collective-permute-done | bytes 196640 | tf_op jit(solution)/shard_map/ppermute | solution.py:18
  41.1 8.5 %collective-permute-done.3.refs_0_.refs_4_ = bf16[384,1024]{1,0:T(8,128)(2,1)} collective-permute-done((bf16[384,1024]{1,0:T(8,128)(2,1)}, bf16[384,1024]{1,0:T(8,128)(2,1)}, u32[]{:S(2)}, u32[]{:S(2)}) %collective-permute-start.3) | collective-permute-done | bytes 786464 | tf_op jit(solution)/shard_map/ppermute | solution.py:18
  49.6 1.2 collective-permute-start.12
  50.8 2.3 %collective-permute-done.5.refs_2_.refs_8_ = bf16[384,1024]{1,0:T(8,128)(2,1)} collective-permute-done((bf16[384,1024]{1,0:T(8,128)(2,1)}, bf16[384,1024]{1,0:T(8,128)(2,1)}, u32[]{:S(2)}, u32[]{:S(2)}) %collective-permute-start.5) | collective-permute-done | bytes 786464 | tf_op jit(solution)/shard_map/ppermute | solution.py:18
  53.8 0.7 copy.6.labels
  54.5 0.7 stack.131.who
  55.2 14.6 %collective-permute-done.12.left.refs_6_ = bf16[384,1024]{1,0:T(8,128)(2,1)} collective-permute-done((bf16[384,1024]{1,0:T(8,128)(2,1)}, bf16[384,1024]{1,0:T(8,128)(2,1)}, u32[]{:S(2)}, u32[]{:S(2)}) %collective-permute-start.12) | collective-permute-done | bytes 786464 | tf_op jit(solution)/shard_map/ppermute | solution.py:18
  69.8 1.0 collective-permute-done.14.right.refs_12_
  71.5 0.6 fusion.2.digits
  72.1 3.1 %shard_map.58 = (bf16[8,128,384]{2,1,0:T(8,128)(2,1)}, bf16[8,112,128]{2,1,0:T(8,128)(2,1)}) custom-call(s32[2]{0:T(128)} %pad_add_fusion.1.who, bf16[8,96,128]{2,1,0:T(8,128)(2,1)} %copy-done.6, bf16[8,96,128]{2,1,0:T(8,128)(2,1)} %copy-done.13, bf16[8,96,128]{2,1,0:T(8,128)(2,1)} %copy-done.14, bf16[8,96,128]{2,1,0:T(8,128)(2,1)} %collective-permute-done.2.p3, ...), custom_call_target="tpu_custom_call" | custom-call | flops 1048576 | bytes 4096 | tf_op jit(solution)/shard_map/pallas_call | solution.py:47
  75.2 3.6 %all-to-all-start.1 = ((bf16[8,112,128]{2,1,0:T(8,128)(2,1)}), bf16[8,112,128]{2,1,0:T(8,128)(2,1)S(1)}, u32[]{:S(2)}, u32[]{:S(2)}) async-start(bf16[8,112,128]{2,1,0:T(8,128)(2,1)} %get-tuple-element.12), calls=%async_computation.1 | async-start | bytes 458752 | tf_op jit(solution)/shard_map/all_to_all | solution.py:319
  79.9 5.7 %all-to-all-done.1.p0 = bf16[8,112,128]{2,1,0:T(8,128)(2,1)S(1)} async-done(((bf16[8,112,128]{2,1,0:T(8,128)(2,1)}), bf16[8,112,128]{2,1,0:T(8,128)(2,1)S(1)}, u32[]{:S(2)}, u32[]{:S(2)}) %all-to-all-start.1) | async-done | bytes 229408 | tf_op jit(solution)/shard_map/all_to_all | solution.py:319
  85.7 1.2 copy-done.1
  86.8 6.8 %shard_map.59.refs_4_ = f32[128,2048]{1,0:T(8,128)} custom-call(s32[6]{0:T(128)} %stack.131.who, bf16[8,128,384]{2,1,0:T(8,128)(2,1)} %get-tuple-element.13.states.mine_states.other_states, bf16[384,2048]{1,0:T(8,128)(2,1)} %refs_0_.3, bf16[384,2048]{1,0:T(8,128)(2,1)} %copy-done.1, bf16[384,1024]{1,0:T(8,128)(2,1)} %collective-permute-done.8.refs_2_, ...), custom_call_target="tpu_custom_call" | custom-call | flops 805306368 | bytes 3145728 | tf_op jit(solution)/shard_map/pallas_call | solution.py:47
  93.6 5.9 %shard_map.60.near = f32[128,2048]{1,0:T(8,128)} custom-call(s32[4]{0:T(128)} %pad_add_fusion.2.who, bf16[8,128,384]{2,1,0:T(8,128)(2,1)} %get-tuple-element.13.states.mine_states.other_states, bf16[384,1024]{1,0:T(8,128)(2,1)} %collective-permute-done.3.refs_0_.refs_4_, bf16[384,1024]{1,0:T(8,128)(2,1)} %collective-permute-done.4.refs_1_.refs_5_, ...), custom_call_target="tpu_custom_call" | custom-call | flops 402653184 | bytes 1572864 | tf_op jit(solution)/shard_map/pallas_call | solution.py:47
  99.6 5.8 %shard_map.61 = (bf16[128,2048]{1,0:T(8,128)(2,1)}, f32[8,128]{1,0:T(8,128)}) custom-call(s32[3]{0:T(128)} %pad_add_fusion.who, bf16[8,128,384]{2,1,0:T(8,128)(2,1)} %get-tuple-element.13.states.mine_states.other_states, bf16[8,128,384]{2,1,0:T(8,128)(2,1)} %get-tuple-element.13.states.mine_states.other_states, s32[128,1]{1,0:T(8,128)} %copy.6.labels, ...), custom_call_target="tpu_custom_call" | custom-call | flops 402653184 | bytes 1572864 | tf_op jit(solution)/shard_map/pallas_call | solution.py:47
  105.4 0.7 slice.25
  106.1 0.6 broadcast_in_dim.21
  106.7 10.0 %all-to-all-start.2 = ((f32[32,3,128]{2,1,0:T(4,128)}), f32[32,3,128]{2,1,0:T(4,128)S(1)}, u32[]{:S(2)}, u32[]{:S(2)}) async-start(f32[32,3,128]{2,1,0:T(4,128)} %broadcast_in_dim.21), calls=%async_computation.2 | async-start | bytes 131072 | tf_op jit(solution)/shard_map/all_to_all | solution.py:26
  116.7 0.6 stack.115.starts
  117.3 8.5 %all-to-all-done.2.parts = f32[32,3,128]{2,1,0:T(4,128)S(1)} async-done(((f32[32,3,128]{2,1,0:T(4,128)}), f32[32,3,128]{2,1,0:T(4,128)S(1)}, u32[]{:S(2)}, u32[]{:S(2)}) %all-to-all-start.2) | async-done | bytes 49184 | tf_op jit(solution)/shard_map/all_to_all | solution.py:26
  125.8 0.6 copy-done.8
  126.4 9.0 %shard_map.62 = (bf16[3072,128]{1,0:T(8,128)(2,1)}, f32[8,128]{1,0:T(8,128)}) custom-call(s32[9]{0:T(128)} %stack.115.starts, bf16[128,2048]{1,0:T(8,128)(2,1)} %get-tuple-element.14.powers.refs_0_, s32[1,128]{1,0:T(1,128)} %bitcast.35, f32[32,3,128]{2,1,0:T(4,128)} %copy-done.8, f32[8,128]{1,0:T(8,128)} %get-tuple-element.15.stats, ...), custom_call_target="tpu_custom_call" | custom-call | flops 1610612736 | bytes 6291456 | tf_op jit(solution)/shard_map/pallas_call | solution.py:47
  135.4 4.9 %all-to-all-start.3 = ((bf16[32,96,128]{2,1,0:T(8,128)(2,1)}), bf16[32,96,128]{2,1,0:T(8,128)(2,1)S(1)}, u32[]{:S(2)}, u32[]{:S(2)}) async-start(bf16[32,96,128]{2,1,0:T(8,128)(2,1)} %bitcast.32), calls=%async_computation.3 | async-start | bytes 1572864 | tf_op jit(solution)/shard_map/all_to_all | solution.py:352
  140.3 0.7 collective-permute-start.24
  141.0 2.6 %collective-permute-start.26 = (bf16[128,2048]{1,0:T(8,128)(2,1)S(1)}, bf16[128,2048]{1,0:T(8,128)(2,1)S(1)}, u32[]{:S(2)}, u32[]{:S(2)}) collective-permute-start(bf16[128,2048]{1,0:T(8,128)(2,1)S(1)} %copy-done.2), channel_id=1, source_target_pairs={{0,192},{64,0},{128,64},{192,128},{1,193},{65,1},{129,65},{193,129... | collective-permute-start | bytes 1572872 | tf_op jit(solution)/shard_map/ppermute | solution.py:18
  143.6 2.8 %collective-permute-start.16 = (bf16[8,112,128]{2,1,0:T(8,128)(2,1)S(1)}, bf16[8,112,128]{2,1,0:T(8,128)(2,1)S(1)}, u32[]{:S(2)}, u32[]{:S(2)}) collective-permute-start(bf16[8,112,128]{2,1,0:T(8,128)(2,1)S(1)} %all-to-all-done.1.p0), channel_id=1, source_target_pairs={{0,24},{8,0},{16,8},{24,16},{1,25},{9,1},{17,9},{25,17},{2,26},{10... | collective-permute-start | bytes 688136 | tf_op jit(solution)/shard_map/ppermute | solution.py:18
  146.4 1.3 slice_bitcast_fusion.1
  147.7 0.7 collective-permute-start.17
  149.4 10.1 %collective-permute-done.16.p1 = bf16[8,112,128]{2,1,0:T(8,128)(2,1)S(1)} collective-permute-done((bf16[8,112,128]{2,1,0:T(8,128)(2,1)S(1)}, bf16[8,112,128]{2,1,0:T(8,128)(2,1)S(1)}, u32[]{:S(2)}, u32[]{:S(2)}) %collective-permute-start.16) | collective-permute-done | bytes 229408 | tf_op jit(solution)/shard_map/ppermute | solution.py:18
  159.5 3.2 %collective-permute-start.21 = (f32[2,128]{1,0:T(2,128)S(1)}, f32[2,128]{1,0:T(2,128)S(1)}, u32[]{:S(2)}, u32[]{:S(2)}) collective-permute-start(f32[2,128]{1,0:T(2,128)S(1)} %pad_maximum_fusion), channel_id=1, source_target_pairs={{0,192},{64,0},{128,64},{192,128},{1,193},{65,1},{129,65},{193,129... | collective-permute-start | bytes 3080 | tf_op jit(solution)/shard_map/ppermute | solution.py:18
  162.9 2.5 %collective-permute-done.18.p3 = bf16[8,112,128]{2,1,0:T(8,128)(2,1)S(1)} collective-permute-done((bf16[8,112,128]{2,1,0:T(8,128)(2,1)S(1)}, bf16[8,112,128]{2,1,0:T(8,128)(2,1)S(1)}, u32[]{:S(2)}, u32[]{:S(2)}) %collective-permute-start.18) | collective-permute-done | bytes 229408 | tf_op jit(solution)/shard_map/ppermute | solution.py:18
  165.4 3.2 %collective-permute-start.30 = (bf16[128,1024]{1,0:T(8,128)(2,1)S(1)}, bf16[128,1024]{1,0:T(8,128)(2,1)}, u32[]{:S(2)}, u32[]{:S(2)}) collective-permute-start(bf16[128,1024]{1,0:T(8,128)(2,1)S(1)} %slice.31), channel_id=1, source_target_pairs={{0,192},{64,0},{128,64},{192,128},{1,193},{65,1},{129,65},{193,129... | collective-permute-start | bytes 786440 | tf_op jit(solution)/shard_map/ppermute | solution.py:18
  169.2 5.7 %collective-permute-done.28.refs_6_ = bf16[128,1024]{1,0:T(8,128)(2,1)S(1)} collective-permute-done((bf16[128,1024]{1,0:T(8,128)(2,1)S(1)}, bf16[128,1024]{1,0:T(8,128)(2,1)S(1)}, u32[]{:S(2)}, u32[]{:S(2)}) %collective-permute-start.28) | collective-permute-done | bytes 262176 | tf_op jit(solution)/shard_map/ppermute | solution.py:18
  175.4 0.6 stack.132.who
  176.0 0.6 concatenate.4.scales
  177.5 7.4 %shard_map.63 = f32[384,2048]{1,0:T(8,128)} custom-call(s32[10]{0:T(128)} %stack.132.who, bf16[8,112,128]{2,1,0:T(8,128)(2,1)} %copy-done.5, bf16[8,112,128]{2,1,0:T(8,128)(2,1)} %copy-done.11, bf16[8,112,128]{2,1,0:T(8,128)(2,1)} %collective-permute-done.17.p2, bf16[8,112,128]{2,1,0:T(8,128)(2,1)} %copy-done.12, f32[8,128]{1,0:T(8,128)} %concatenate.4.scales, ...), custom_call_target="tpu_custom_call" | custom-call | flops 1610612736 | bytes 6291456 | tf_op jit(solution)/shard_map/pallas_call | solution.py:47
  184.9 0.7 reduce_sum.12
  (81 shorter events, 6.3 us)
Async XLA Ops:
  2.1 17.6 %all-to-all-start = ((bf16[8,96,128]{2,1,0:T(8,128)(2,1)}), bf16[8,96,128]{2,1,0:T(8,128)(2,1)S(1)}, u32[]{:S(2)}, u32[]{:S(2)}) async-start(bf16[8,96,128]{2,1,0:T(8,128)(2,1)} %broadcast_in_dim.8), calls=%async_computation | async-start | bytes 393216 | tf_op jit(solution)/shard_map/all_to_all | solution.py:26
  10.6 29.8 %copy-start = (bf16[384,2048]{1,0:T(8,128)(2,1)S(1)}, bf16[384,2048]{1,0:T(8,128)(2,1)}, u32[]{:S(2)}) copy-start(bf16[384,2048]{1,0:T(8,128)(2,1)} %refs_0_.3) | copy-start | bytes 4718596
  10.6 43.2 %copy-start.15 = (s32[128]{0:T(128)S(1)}, s32[128]{0:T(128)}, u32[]{:S(2)}) copy-start(s32[128]{0:T(128)} %param.5) | copy-start | bytes 1540
  13.4 27.1 %collective-permute-start.10 = (bf16[384,1024]{1,0:T(8,128)(2,1)}, bf16[384,1024]{1,0:T(8,128)(2,1)}, u32[]{:S(2)}, u32[]{:S(2)}) collective-permute-start(bf16[384,1024]{1,0:T(8,128)(2,1)} %get-tuple-element.19), channel_id=1, source_target_pairs={{0,192},{64,0},{128,64},{192,128},{1,193},{65,1},{129,65},{193,129... | collective-permute-start | bytes 2359304 | tf_op jit(solution)/shard_map/ppermute | solution.py:18
  16.2 24.8 %collective-permute-start.8 = (bf16[384,1024]{1,0:T(8,128)(2,1)}, bf16[384,1024]{1,0:T(8,128)(2,1)}, u32[]{:S(2)}, u32[]{:S(2)}) collective-permute-start(bf16[384,1024]{1,0:T(8,128)(2,1)} %get-tuple-element.20), channel_id=1, source_target_pairs={{0,64},{64,128},{128,192},{192,0},{1,65},{65,129},{129,193},{193,1... | collective-permute-start | bytes 2359304 | tf_op jit(solution)/shard_map/ppermute | solution.py:18
  16.2 33.4 %collective-permute-start.3 = (bf16[384,1024]{1,0:T(8,128)(2,1)}, bf16[384,1024]{1,0:T(8,128)(2,1)}, u32[]{:S(2)}, u32[]{:S(2)}) collective-permute-start(bf16[384,1024]{1,0:T(8,128)(2,1)} %get-tuple-element.20), channel_id=1, source_target_pairs={{0,192},{64,0},{128,64},{192,128},{1,193},{65,1},{129,65},{193,129... | collective-permute-start | bytes 2359304 | tf_op jit(solution)/shard_map/ppermute | solution.py:18
  19.4 33.7 %collective-permute-start.5 = (bf16[384,1024]{1,0:T(8,128)(2,1)}, bf16[384,1024]{1,0:T(8,128)(2,1)}, u32[]{:S(2)}, u32[]{:S(2)}) collective-permute-start(bf16[384,1024]{1,0:T(8,128)(2,1)} %get-tuple-element.19), channel_id=1, source_target_pairs={{0,64},{64,128},{128,192},{192,0},{1,65},{65,129},{129,193},{193,1... | collective-permute-start | bytes 2359304 | tf_op jit(solution)/shard_map/ppermute | solution.py:18
  19.6 52.5 %copy-start.6 = (bf16[8,96,128]{2,1,0:T(8,128)(2,1)}, bf16[8,96,128]{2,1,0:T(8,128)(2,1)S(1)}, u32[]{:S(2)}) copy-start(bf16[8,96,128]{2,1,0:T(8,128)(2,1)S(1)} %all-to-all-done.p0) | copy-start | bytes 589828
  19.6 6.2 %collective-permute-start = (bf16[8,96,128]{2,1,0:T(8,128)(2,1)S(1)}, bf16[8,96,128]{2,1,0:T(8,128)(2,1)S(1)}, u32[]{:S(2)}, u32[]{:S(2)}) collective-permute-start(bf16[8,96,128]{2,1,0:T(8,128)(2,1)S(1)} %all-to-all-done.p0), channel_id=1, source_target_pairs={{0,24},{8,0},{16,8},{24,16},{1,25},{9,1},{17,9},{25,17},{2,26},{10... | collective-permute-start | bytes 589832 | tf_op jit(solution)/shard_map/ppermute | solution.py:18
  25.8 46.2 %copy-start.13 = (bf16[8,96,128]{2,1,0:T(8,128)(2,1)}, bf16[8,96,128]{2,1,0:T(8,128)(2,1)S(1)}, u32[]{:S(2)}) copy-start(bf16[8,96,128]{2,1,0:T(8,128)(2,1)S(1)} %collective-permute-done.p1) | copy-start | bytes 589828
  25.9 7.2 %collective-permute-start.1 = (bf16[8,96,128]{2,1,0:T(8,128)(2,1)S(1)}, bf16[8,96,128]{2,1,0:T(8,128)(2,1)S(1)}, u32[]{:S(2)}, u32[]{:S(2)}) collective-permute-start(bf16[8,96,128]{2,1,0:T(8,128)(2,1)S(1)} %all-to-all-done.p0), channel_id=1, source_target_pairs={{0,16},{8,24},{16,0},{24,8},{1,17},{9,25},{17,1},{25,9},{2,18},{10... | collective-permute-start | bytes 589832 | tf_op jit(solution)/shard_map/ppermute | solution.py:18
  33.0 7.4 %collective-permute-start.2 = (bf16[8,96,128]{2,1,0:T(8,128)(2,1)S(1)}, bf16[8,96,128]{2,1,0:T(8,128)(2,1)}, u32[]{:S(2)}, u32[]{:S(2)}) collective-permute-start(bf16[8,96,128]{2,1,0:T(8,128)(2,1)S(1)} %all-to-all-done.p0), channel_id=1, source_target_pairs={{0,8},{8,16},{16,24},{24,0},{1,9},{9,17},{17,25},{25,1},{2,10},{10... | collective-permute-start | bytes 589832 | tf_op jit(solution)/shard_map/ppermute | solution.py:18
  40.5 45.2 %collective-permute-start.7 = (bf16[384,2048]{1,0:T(8,128)(2,1)S(1)}, bf16[384,2048]{1,0:T(8,128)(2,1)S(1)}, u32[]{:S(2)}, u32[]{:S(2)}) collective-permute-start(bf16[384,2048]{1,0:T(8,128)(2,1)S(1)} %copy-done), channel_id=1, source_target_pairs={{0,32},{32,0},{1,33},{33,1},{2,34},{34,2},{3,35},{35,3},{4,36},{36... | collective-permute-start | bytes 4718600 | tf_op jit(solution)/shard_map/ppermute | solution.py:22
  40.5 12.8 %collective-permute-start.11 = (bf16[384,1024]{1,0:T(8,128)(2,1)}, bf16[384,1024]{1,0:T(8,128)(2,1)}, u32[]{:S(2)}, u32[]{:S(2)}) collective-permute-start(bf16[384,1024]{1,0:T(8,128)(2,1)} %collective-permute-done.10.refs_4_.refs_10_), channel_id=1, source_target_pairs={{0,32},{32,0},{1,33},{33,1},{2,34},{34,2},{3,35},{35,3},{4,36},{36... | collective-permute-start | bytes 2359304 | tf_op jit(solution)/shard_map/ppermute | solution.py:22
  41.0 12.3 %collective-permute-start.9 = (bf16[384,1024]{1,0:T(8,128)(2,1)}, bf16[384,1024]{1,0:T(8,128)(2,1)}, u32[]{:S(2)}, u32[]{:S(2)}) collective-permute-start(bf16[384,1024]{1,0:T(8,128)(2,1)} %collective-permute-done.8.refs_2_), channel_id=1, source_target_pairs={{0,32},{32,0},{1,33},{33,1},{2,34},{34,2},{3,35},{35,3},{4,36},{36... | collective-permute-start | bytes 2359304 | tf_op jit(solution)/shard_map/ppermute | solution.py:22
  49.6 20.3 %collective-permute-start.12 = (bf16[384,1024]{1,0:T(8,128)(2,1)}, bf16[384,1024]{1,0:T(8,128)(2,1)}, u32[]{:S(2)}, u32[]{:S(2)}) collective-permute-start(bf16[384,1024]{1,0:T(8,128)(2,1)} %collective-permute-done.8.refs_2_), channel_id=1, source_target_pairs={{0,64},{64,128},{128,192},{192,0},{1,65},{65,129},{129,193},{193,1... | collective-permute-start | bytes 2359304 | tf_op jit(solution)/shard_map/ppermute | solution.py:18
  53.1 17.8 %collective-permute-start.14 = (bf16[384,1024]{1,0:T(8,128)(2,1)}, bf16[384,1024]{1,0:T(8,128)(2,1)}, u32[]{:S(2)}, u32[]{:S(2)}) collective-permute-start(bf16[384,1024]{1,0:T(8,128)(2,1)} %collective-permute-done.10.refs_4_.refs_10_), channel_id=1, source_target_pairs={{0,192},{64,0},{128,64},{192,128},{1,193},{65,1},{129,65},{193,129... | collective-permute-start | bytes 2359304 | tf_op jit(solution)/shard_map/ppermute | solution.py:18
  53.3 40.3 %collective-permute-start.4 = (bf16[384,1024]{1,0:T(8,128)(2,1)}, bf16[384,1024]{1,0:T(8,128)(2,1)}, u32[]{:S(2)}, u32[]{:S(2)}) collective-permute-start(bf16[384,1024]{1,0:T(8,128)(2,1)} %collective-permute-done.3.refs_0_.refs_4_), channel_id=1, source_target_pairs={{0,32},{32,0},{1,33},{33,1},{2,34},{34,2},{3,35},{35,3},{4,36},{36... | collective-permute-start | bytes 2359304 | tf_op jit(solution)/shard_map/ppermute | solution.py:22
  53.3 40.3 %collective-permute-start.6 = (bf16[384,1024]{1,0:T(8,128)(2,1)}, bf16[384,1024]{1,0:T(8,128)(2,1)}, u32[]{:S(2)}, u32[]{:S(2)}) collective-permute-start(bf16[384,1024]{1,0:T(8,128)(2,1)} %collective-permute-done.5.refs_2_.refs_8_), channel_id=1, source_target_pairs={{0,32},{32,0},{1,33},{33,1},{2,34},{34,2},{3,35},{35,3},{4,36},{36... | collective-permute-start | bytes 2359304 | tf_op jit(solution)/shard_map/ppermute | solution.py:22
  69.8 29.7 %collective-permute-start.13 = (bf16[384,1024]{1,0:T(8,128)(2,1)}, bf16[384,1024]{1,0:T(8,128)(2,1)}, u32[]{:S(2)}, u32[]{:S(2)}) collective-permute-start(bf16[384,1024]{1,0:T(8,128)(2,1)} %collective-permute-done.12.left.refs_6_), channel_id=1, source_target_pairs={{0,32},{32,0},{1,33},{33,1},{2,34},{34,2},{3,35},{35,3},{4,36},{36... | collective-permute-start | bytes 2359304 | tf_op jit(solution)/shard_map/ppermute | solution.py:22
  70.9 28.7 %collective-permute-start.15 = (bf16[384,1024]{1,0:T(8,128)(2,1)}, bf16[384,1024]{1,0:T(8,128)(2,1)}, u32[]{:S(2)}, u32[]{:S(2)}) collective-permute-start(bf16[384,1024]{1,0:T(8,128)(2,1)} %collective-permute-done.14.right.refs_12_), channel_id=1, source_target_pairs={{0,32},{32,0},{1,33},{33,1},{2,34},{34,2},{3,35},{35,3},{4,36},{36... | collective-permute-start | bytes 2359304 | tf_op jit(solution)/shard_map/ppermute | solution.py:22
  75.2 10.5 %all-to-all-start.1 = ((bf16[8,112,128]{2,1,0:T(8,128)(2,1)}), bf16[8,112,128]{2,1,0:T(8,128)(2,1)S(1)}, u32[]{:S(2)}, u32[]{:S(2)}) async-start(bf16[8,112,128]{2,1,0:T(8,128)(2,1)} %get-tuple-element.12), calls=%async_computation.1 | async-start | bytes 458752 | tf_op jit(solution)/shard_map/all_to_all | solution.py:319
  85.7 63.2 %copy-start.5 = (bf16[8,112,128]{2,1,0:T(8,128)(2,1)}, bf16[8,112,128]{2,1,0:T(8,128)(2,1)S(1)}, u32[]{:S(2)}) copy-start(bf16[8,112,128]{2,1,0:T(8,128)(2,1)S(1)} %all-to-all-done.1.p0) | copy-start | bytes 688132
  85.7 1.2 copy-start.1
  106.7 19.1 %all-to-all-start.2 = ((f32[32,3,128]{2,1,0:T(4,128)}), f32[32,3,128]{2,1,0:T(4,128)S(1)}, u32[]{:S(2)}, u32[]{:S(2)}) async-start(f32[32,3,128]{2,1,0:T(4,128)} %broadcast_in_dim.21), calls=%async_computation.2 | async-start | bytes 131072 | tf_op jit(solution)/shard_map/all_to_all | solution.py:26
  135.4 4.9 %copy-start.2 = (bf16[128,2048]{1,0:T(8,128)(2,1)S(1)}, bf16[128,2048]{1,0:T(8,128)(2,1)}, u32[]{:S(2)}) copy-start(bf16[128,2048]{1,0:T(8,128)(2,1)} %get-tuple-element.14.powers.refs_0_) | copy-start | bytes 1572868
  135.4 49.5 %all-to-all-start.3 = ((bf16[32,96,128]{2,1,0:T(8,128)(2,1)}), bf16[32,96,128]{2,1,0:T(8,128)(2,1)S(1)}, u32[]{:S(2)}, u32[]{:S(2)}) async-start(bf16[32,96,128]{2,1,0:T(8,128)(2,1)} %bitcast.32), calls=%async_computation.3 | async-start | bytes 1572864 | tf_op jit(solution)/shard_map/all_to_all | solution.py:352
  140.3 19.2 %collective-permute-start.24 = (bf16[128,2048]{1,0:T(8,128)(2,1)S(1)}, bf16[128,2048]{1,0:T(8,128)(2,1)S(1)}, u32[]{:S(2)}, u32[]{:S(2)}) collective-permute-start(bf16[128,2048]{1,0:T(8,128)(2,1)S(1)} %copy-done.2), channel_id=1, source_target_pairs={{0,64},{64,128},{128,192},{192,0},{1,65},{65,129},{129,193},{193,1... | collective-permute-start | bytes 1572872 | tf_op jit(solution)/shard_map/ppermute | solution.py:18
  141.0 21.8 %collective-permute-start.26 = (bf16[128,2048]{1,0:T(8,128)(2,1)S(1)}, bf16[128,2048]{1,0:T(8,128)(2,1)S(1)}, u32[]{:S(2)}, u32[]{:S(2)}) collective-permute-start(bf16[128,2048]{1,0:T(8,128)(2,1)S(1)} %copy-done.2), channel_id=1, source_target_pairs={{0,192},{64,0},{128,64},{192,128},{1,193},{65,1},{129,65},{193,129... | collective-permute-start | bytes 1572872 | tf_op jit(solution)/shard_map/ppermute | solution.py:18
  143.6 15.9 %collective-permute-start.16 = (bf16[8,112,128]{2,1,0:T(8,128)(2,1)S(1)}, bf16[8,112,128]{2,1,0:T(8,128)(2,1)S(1)}, u32[]{:S(2)}, u32[]{:S(2)}) collective-permute-start(bf16[8,112,128]{2,1,0:T(8,128)(2,1)S(1)} %all-to-all-done.1.p0), channel_id=1, source_target_pairs={{0,24},{8,0},{16,8},{24,16},{1,25},{9,1},{17,9},{25,17},{2,26},{10... | collective-permute-start | bytes 688136 | tf_op jit(solution)/shard_map/ppermute | solution.py:18
  147.7 1.2 collective-permute-start.19
  147.7 15.1 %collective-permute-start.17 = (bf16[8,112,128]{2,1,0:T(8,128)(2,1)S(1)}, bf16[8,112,128]{2,1,0:T(8,128)(2,1)}, u32[]{:S(2)}, u32[]{:S(2)}) collective-permute-start(bf16[8,112,128]{2,1,0:T(8,128)(2,1)S(1)} %all-to-all-done.1.p0), channel_id=1, source_target_pairs={{0,16},{8,24},{16,0},{24,8},{1,17},{9,25},{17,1},{25,9},{2,18},{10... | collective-permute-start | bytes 688136 | tf_op jit(solution)/shard_map/ppermute | solution.py:18
  148.9 16.5 %collective-permute-start.18 = (bf16[8,112,128]{2,1,0:T(8,128)(2,1)S(1)}, bf16[8,112,128]{2,1,0:T(8,128)(2,1)S(1)}, u32[]{:S(2)}, u32[]{:S(2)}) collective-permute-start(bf16[8,112,128]{2,1,0:T(8,128)(2,1)S(1)} %all-to-all-done.1.p0), channel_id=1, source_target_pairs={{0,8},{8,16},{16,24},{24,0},{1,9},{9,17},{17,25},{25,1},{2,10},{10... | collective-permute-start | bytes 688136 | tf_op jit(solution)/shard_map/ppermute | solution.py:18
  159.5 3.3 %copy-start.11 = (bf16[8,112,128]{2,1,0:T(8,128)(2,1)}, bf16[8,112,128]{2,1,0:T(8,128)(2,1)S(1)}, u32[]{:S(2)}) copy-start(bf16[8,112,128]{2,1,0:T(8,128)(2,1)S(1)} %collective-permute-done.16.p1) | copy-start | bytes 688132
  159.5 5.9 %collective-permute-start.20 = (f32[2,128]{1,0:T(2,128)S(1)}, f32[2,128]{1,0:T(2,128)S(1)}, u32[]{:S(2)}, u32[]{:S(2)}) collective-permute-start(f32[2,128]{1,0:T(2,128)S(1)} %pad_maximum_fusion), channel_id=1, source_target_pairs={{0,64},{64,128},{128,192},{192,0},{1,65},{65,129},{129,193},{193,1... | collective-permute-start | bytes 3080 | tf_op jit(solution)/shard_map/ppermute | solution.py:18
  159.5 17.3 %copy-start.3 = (bf16[128,2048]{1,0:T(8,128)(2,1)}, bf16[128,2048]{1,0:T(8,128)(2,1)S(1)}, u32[]{:S(2)}) copy-start(bf16[128,2048]{1,0:T(8,128)(2,1)S(1)} %collective-permute-done.24.refs_2_) | copy-start | bytes 1572868
  159.5 9.2 %collective-permute-start.21 = (f32[2,128]{1,0:T(2,128)S(1)}, f32[2,128]{1,0:T(2,128)S(1)}, u32[]{:S(2)}, u32[]{:S(2)}) collective-permute-start(f32[2,128]{1,0:T(2,128)S(1)} %pad_maximum_fusion), channel_id=1, source_target_pairs={{0,192},{64,0},{128,64},{192,128},{1,193},{65,1},{129,65},{193,129... | collective-permute-start | bytes 3080 | tf_op jit(solution)/shard_map/ppermute | solution.py:18
  162.7 14.1 %copy-start.4 = (bf16[128,2048]{1,0:T(8,128)(2,1)}, bf16[128,2048]{1,0:T(8,128)(2,1)S(1)}, u32[]{:S(2)}) copy-start(bf16[128,2048]{1,0:T(8,128)(2,1)S(1)} %collective-permute-done.26.refs_4_) | copy-start | bytes 1572868
  162.7 5.9 %collective-permute-start.22 = (f32[2,128]{1,0:T(2,128)S(1)}, f32[2,128]{1,0:T(2,128)S(1)}, u32[]{:S(2)}, u32[]{:S(2)}) collective-permute-start(f32[2,128]{1,0:T(2,128)S(1)} %pad_maximum_fusion), channel_id=1, source_target_pairs={{0,128},{64,192},{128,0},{192,64},{1,129},{65,193},{129,1},{193,65... | collective-permute-start | bytes 3080 | tf_op jit(solution)/shard_map/ppermute | solution.py:18
  162.8 13.8 %collective-permute-start.23 = (bf16[128,2048]{1,0:T(8,128)(2,1)S(1)}, bf16[128,2048]{1,0:T(8,128)(2,1)S(1)}, u32[]{:S(2)}, u32[]{:S(2)}) collective-permute-start(bf16[128,2048]{1,0:T(8,128)(2,1)S(1)} %copy-done.2), channel_id=1, source_target_pairs={{0,32},{32,0},{1,33},{33,1},{2,34},{34,2},{3,35},{35,3},{4,36},{36... | collective-permute-start | bytes 1572872 | tf_op jit(solution)/shard_map/ppermute | solution.py:22
  165.4 9.5 %copy-start.12 = (bf16[8,112,128]{2,1,0:T(8,128)(2,1)}, bf16[8,112,128]{2,1,0:T(8,128)(2,1)S(1)}, u32[]{:S(2)}) copy-start(bf16[8,112,128]{2,1,0:T(8,128)(2,1)S(1)} %collective-permute-done.18.p3) | copy-start | bytes 688132
  165.4 9.5 %collective-permute-start.28 = (bf16[128,1024]{1,0:T(8,128)(2,1)S(1)}, bf16[128,1024]{1,0:T(8,128)(2,1)S(1)}, u32[]{:S(2)}, u32[]{:S(2)}) collective-permute-start(bf16[128,1024]{1,0:T(8,128)(2,1)S(1)} %slice.30), channel_id=1, source_target_pairs={{0,64},{64,128},{128,192},{192,0},{1,65},{65,129},{129,193},{193,1... | collective-permute-start | bytes 786440 | tf_op jit(solution)/shard_map/ppermute | solution.py:18
  165.4 9.5 %collective-permute-start.30 = (bf16[128,1024]{1,0:T(8,128)(2,1)S(1)}, bf16[128,1024]{1,0:T(8,128)(2,1)}, u32[]{:S(2)}, u32[]{:S(2)}) collective-permute-start(bf16[128,1024]{1,0:T(8,128)(2,1)S(1)} %slice.31), channel_id=1, source_target_pairs={{0,192},{64,0},{128,64},{192,128},{1,193},{65,1},{129,65},{193,129... | collective-permute-start | bytes 786440 | tf_op jit(solution)/shard_map/ppermute | solution.py:18
  168.6 8.1 %collective-permute-start.25 = (bf16[128,2048]{1,0:T(8,128)(2,1)S(1)}, bf16[128,2048]{1,0:T(8,128)(2,1)}, u32[]{:S(2)}, u32[]{:S(2)}) collective-permute-start(bf16[128,2048]{1,0:T(8,128)(2,1)S(1)} %collective-permute-done.24.refs_2_), channel_id=1, source_target_pairs={{0,32},{32,0},{1,33},{33,1},{2,34},{34,2},{3,35},{35,3},{4,36},{36... | collective-permute-start | bytes 1572872 | tf_op jit(solution)/shard_map/ppermute | solution.py:22
  168.7 8.1 %collective-permute-start.27 = (bf16[128,2048]{1,0:T(8,128)(2,1)S(1)}, bf16[128,2048]{1,0:T(8,128)(2,1)}, u32[]{:S(2)}, u32[]{:S(2)}) collective-permute-start(bf16[128,2048]{1,0:T(8,128)(2,1)S(1)} %collective-permute-done.26.refs_4_), channel_id=1, source_target_pairs={{0,32},{32,0},{1,33},{33,1},{2,34},{34,2},{3,35},{35,3},{4,36},{36... | collective-permute-start | bytes 1572872 | tf_op jit(solution)/shard_map/ppermute | solution.py:22
  174.9 1.9 %copy-start.9 = (bf16[128,1024]{1,0:T(8,128)(2,1)}, bf16[128,1024]{1,0:T(8,128)(2,1)S(1)}, u32[]{:S(2)}) copy-start(bf16[128,1024]{1,0:T(8,128)(2,1)S(1)} %collective-permute-done.28.refs_6_) | copy-start | bytes 786436
  174.9 1.7 collective-permute-start.29
  174.9 1.9 %collective-permute-start.31 = (bf16[128,1024]{1,0:T(8,128)(2,1)}, bf16[128,1024]{1,0:T(8,128)(2,1)S(1)}, u32[]{:S(2)}, u32[]{:S(2)}) collective-permute-start(bf16[128,1024]{1,0:T(8,128)(2,1)} %collective-permute-done.30.refs_8_), channel_id=1, source_target_pairs={{0,32},{32,0},{1,33},{33,1},{2,34},{34,2},{3,35},{35,3},{4,36},{36... | collective-permute-start | bytes 786440 | tf_op jit(solution)/shard_map/ppermute | solution.py:22
  (4 other events, 3.2 us)

commit v4 on v3

--- a/solution.py
+++ b/solution.py
@@ -11,7 +11,8 @@
 BF = jnp.bfloat16
 F32 = jnp.float32
 NX, NY, NZ = 4, 4, 8
-STEPS = 4
+STEPS = 2
+ROOM = 65000 << 10
 
 
 def shift(a, axis, n, s):
@@ -43,7 +44,7 @@
     return jnp.maximum(j - STEPS // 2, 0)
 
 
-def call(kernel, scalars, args, in_specs, out_specs, out_shape, flops, scratch=(), steps=STEPS):
+def call(kernel, scalars, args, in_specs, out_specs, out_shape, flops, scratch=(), steps=STEPS, room=None):
     return pl.pallas_call(
         kernel,
         grid_spec=pltpu.PrefetchScalarGridSpec(
@@ -54,6 +55,7 @@
             scratch_shapes=scratch,
         ),
         out_shape=out_shape,
+        compiler_params=pltpu.CompilerParams(vmem_limit_bytes=room),
         cost_estimate=pl.CostEstimate(flops=flops, bytes_accessed=flops // 256, transcendentals=0),
     )(jnp.stack(scalars).astype(jnp.int32), *args)
 
@@ -127,59 +129,65 @@
     )
 
 
-def far_kernel(who, mine_states, other_states, labels, near, left, left_other, right, right_other, powers, stats, logits):
-    step = pl.program_id(0)
-    first = step < STEPS // 2
-    wide = near.shape[1]
-    for mine, theirs, here in ((left, left_other, first), (right, right_other, ~first)):
-
-        @pl.when(here)
-        def _():
-            logits[:, pl.ds(pl.multiple_of(step * wide, wide), wide)] = (
-                near[...] + dot(mine_states[0], mine[...]) + dot(other_states[0], theirs[...])
-            )
-
-    @pl.when(step == STEPS - 1)
-    def _():
-        values = logits[...]
-        peak = jnp.max(values, axis=1, keepdims=True)
-        shifted = jnp.exp(values - peak)
-        columns = who[2] + lax.broadcasted_iota(jnp.int32, values.shape, 1)
-        hits = labels[...] == columns
-        total = jnp.sum(shifted, axis=1, keepdims=True)
-        target = jnp.sum(jnp.where(hits, values, 0.0), axis=1, keepdims=True)
-        powers[...] = shifted.astype(BF)
-        tokens = values.shape[0]
-        lanes = lax.broadcasted_iota(jnp.int32, (tokens, 128), 1)
-        both = jnp.where(lanes == 0, peak, jnp.where(lanes == 1, total, target))
-        stats[...] = both.T[:8]
+def far_kernel(who, states, labels, near, left, left_other, right, right_other, powers, stats, logits, rows, few, sems):
+    copies = [
+        pltpu.make_async_copy(states.at[who[0]], few.at[0], sems.at[0]),
+        pltpu.make_async_copy(states.at[who[1]], few.at[1], sems.at[1]),
+        pltpu.make_async_copy(left, rows.at[0], sems.at[2]),
+        pltpu.make_async_copy(left_other, rows.at[1], sems.at[3]),
+        pltpu.make_async_copy(near, logits, sems.at[4]),
+        pltpu.make_async_copy(right, rows.at[2], sems.at[5]),
+        pltpu.make_async_copy(right_other, rows.at[3], sems.at[6]),
+    ]
+    for copy in copies:
+        copy.start()
+    half = rows.shape[2]
+    for side, ready in ((0, copies[:5]), (1, copies[5:])):
+        for copy in ready:
+            copy.wait()
+        at = slice(side * half, (side + 1) * half)
+        logits[:, at] += dot(few[0], rows[2 * side]) + dot(few[1], rows[2 * side + 1])
+    values = logits[...]
+    peak = jnp.max(values, axis=1, keepdims=True)
+    shifted = jnp.exp(values - peak)
+    columns = who[2] + lax.broadcasted_iota(jnp.int32, values.shape, 1)
+    hits = labels[...] == columns
+    total = jnp.sum(shifted, axis=1, keepdims=True)
+    target = jnp.sum(jnp.where(hits, values, 0.0), axis=1, keepdims=True)
+    powers[...] = shifted.astype(BF)
+    lanes = lax.broadcasted_iota(jnp.int32, (values.shape[0], 128), 1)
+    both = jnp.where(lanes == 0, peak, jnp.where(lanes == 1, total, target))
+    stats[...] = both.T[:8]
 
 
 def far_logits(states, labels, near, left, right, who):
     tokens, width = near.shape
-    wide = width // STEPS
-    rows = left[0].shape[0]
-    args = [states, states, labels, near, *left, *right]
-    specs = [pl.BlockSpec((1, tokens, rows), lambda j, s, k=k: (s[k], 0, 0)) for k in (0, 1)]
-    specs += [whole(labels), pl.BlockSpec((tokens, wide), lambda j, s: (0, j))]
-    specs += [pl.BlockSpec((rows, wide), lambda j, s: (0, early(j)))] * 2
-    specs += [pl.BlockSpec((rows, wide), lambda j, s: (0, late(j)))] * 2
+    rows, half = left[0].shape
+    args = [states, labels, near, *left, *right]
+    far = pl.BlockSpec(memory_space=pltpu.HBM)
     powers = jax.ShapeDtypeStruct((tokens, width), BF)
     stats = jax.ShapeDtypeStruct((8, 128), F32)
     return call(
         far_kernel,
         who,
         args,
-        specs,
+        [far, whole(labels)] + [far] * 5,
         [whole(powers), whole(stats)],
         [powers, stats],
         4 * tokens * rows * width,
-        [pltpu.VMEM((tokens, width), F32)],
+        [
+            pltpu.VMEM((tokens, width), F32),
+            pltpu.VMEM((4, rows, half), BF),
+            pltpu.VMEM((2, tokens, rows), BF),
+            pltpu.SemaphoreType.DMA((7,)),
+        ],
+        steps=1,
+        room=ROOM,
     )
 
 
 def terms_kernel(starts, powers, labels, parts, stats, *refs):
-    *arrays, out, rows_out, errors = refs
+    *arrays, out, scales, losses, errors = refs
     step = pl.program_id(0)
     width, tokens = errors.shape
 
@@ -191,7 +199,8 @@
         target = jnp.sum(parts[:, 2, :], axis=0, keepdims=True)
         scale = jnp.exp(stats[0:1, :] - peak) / total
         loss = jnp.log(total) + peak - target
-        rows_out[...] = jnp.concatenate([scale, loss] + [scale] * 6, axis=0)
+        scales[...] = scale
+        losses[...] = loss
         columns = starts[8] + lax.broadcasted_iota(jnp.int32, (width, tokens), 0)
         hit = jnp.where(columns == labels[...], 1.0, 0.0)
         errors[...] = (powers[...].T.astype(F32) * scale - hit).astype(BF)
@@ -214,21 +223,22 @@
     specs = [whole(a) for a in args[:4]]
     specs += [pl.BlockSpec((rows, a.shape[1]), lambda j, s: (j, 0)) for a in args[4:]]
     terms = jax.ShapeDtypeStruct((depth, tokens), BF)
-    rows_out = jax.ShapeDtypeStruct((8, tokens), F32)
+    line = jax.ShapeDtypeStruct((1, tokens), F32)
     return call(
         terms_kernel,
         starts,
         args,
         specs,
-        [whole(terms), whole(rows_out)],
-        [terms, rows_out],
+        [whole(terms), whole(line), whole(line)],
+        [terms, line, line],
         2 * tokens * width * depth,
         [pltpu.VMEM((width, tokens), BF)],
     )
 
 
-def grad_kernel(who, p0, p1, p2, p3, scales, *refs):
+def grad_kernel(who, p0, p1, p2, p3, *refs):
     *arrays, out, states, turned = refs
+    scales, arrays = arrays[:4], arrays[4:]
     step = pl.program_id(0)
     groups, padded, tokens = p0.shape
     part = padded - 16
@@ -243,7 +253,8 @@
         for k in range(groups):
             digits = p0[who[k], part:, :].astype(F32)
             number = digits[0:1] * 256.0 + digits[1:2]
-            both = jnp.concatenate([number, scales[k : k + 1, :], digits[:6]], axis=0)
+            scale = scales[k // 2][k % 2 : k % 2 + 1, :]
+            both = jnp.concatenate([number, scale, digits[:6]], axis=0)
             turned[k] = both.T
 
     columns = who[8] + step * wide + lax.broadcasted_iota(jnp.int32, (tokens, wide), 1)
@@ -268,8 +279,8 @@
     rows = NY * (padded - 16)
     width = near[0].shape[1]
     wide = width // STEPS
-    args = [*parts, scales, *near, *left, *right]
-    specs = [whole(a) for a in args[:5]]
+    args = [*parts, *scales, *near, *left, *right]
+    specs = [whole(a) for a in args[:8]]
     specs += [pl.BlockSpec((tokens, wide), lambda j, s: (0, j))] * 6
     specs += [pl.BlockSpec((tokens, wide), lambda j, s: (0, early(j)))] * 2
     specs += [pl.BlockSpec((tokens, wide), lambda j, s: (0, late(j)))] * 2
@@ -298,10 +309,12 @@
         chip = ((x + offset) % NX) * 2
         return [chip + core, chip + 1 - core]
 
-    up_left = shift(head[:, :half], "x", NX, 1)
-    down_right = shift(head[:, half:], "x", NX, -1)
-    up_right = shift(head[:, half:], "x", NX, 1)
-    down_left = shift(head[:, :half], "x", NX, -1)
+    left_half = head[:, :half]
+    right_half = lax.optimization_barrier(head)[:, half:]
+    up_left = shift(left_half, "x", NX, 1)
+    down_right = shift(right_half, "x", NX, -1)
+    up_right = shift(right_half, "x", NX, 1)
+    down_left = shift(left_half, "x", NX, -1)
     own = [head, swap(head)]
     far_left = shift(up_left, "x", NX, 1)
     far_right = shift(down_right, "x", NX, -1)
@@ -344,19 +357,18 @@
     starts = [w * rows for w in who(0) + who(3) + who(1) + who(2)]
     all_left = [up_left, up_left_other, *left, *away_left]
     all_right = [*right, down_right, down_right_other, *away_right]
-    terms, lines = state_terms(
+    terms, scale, token_loss = state_terms(
         powers, labels[None], parts, stats, own, all_left, all_right, starts + [base], depth
     )
-    scale, token_loss = lines[0], lines[1]
+    token_loss = token_loss.reshape(tokens)
 
     arrived = lax.all_to_all(
         terms.reshape(NY * NZ, part, tokens), ("y", "z"), 0, 0, tiled=True
     )
     state_grad = arrived.astype(F32).sum(axis=0).astype(BF).T
 
-    scale = jnp.stack([scale, swap(scale)])
-    scales = [scale] + [shift(scale, "x", NX, s) for s in (1, -1, 2)]
-    scales = jnp.concatenate(scales)
+    pair = jnp.concatenate([scale, swap(scale)])
+    scales = [pair] + [shift(pair, "x", NX, s) for s in (1, -1, 2)]
     head_grad = head_grad_of(
         slices,
         scales,

time: 189 us -> 185 us (0.979)
  Pallas kernels: 38 us -> 34.1 us
    pallas_call x6, Pallas kernels: 38 us -> 34.1 us  [call(): pl.pallas_call(kernel, grid_spec=pltpu.PrefetchScalarGridSpec(num_scalar_...]
  transfers between devices with their start and end apart: 36 -> 36, of which waited for: 15 -> 16; matrix products, arithmetic and copies ran while one was open for 5% -> 4% of each run, Pallas kernels for 12% -> 11%
where the time goes in v4:
time: 185 us; the launch traced here: 182 us
  waiting for transfers between devices  75.2 us (41%)
  starting transfers between devices  57.3 us (31%)
  Pallas kernels  34.1 us (18%)
  local copies, waits for them, and re-layouts  11.1 us (6%)
  other arithmetic  3.11 us (2%)
    ppermute x19, waiting for transfers between devices, shift(): return lax.ppermute(a, axis, [(i, (i + s) % n) for i in range(n)])  59.4 us
    pallas_call x6, Pallas kernels, call(): pl.pallas_call(kernel, grid_spec=pltpu.PrefetchScalarGridSpec(num_scalar_...  34.1 us
    ppermute x19, starting transfers between devices, shift(): return lax.ppermute(a, axis, [(i, (i + s) % n) for i in range(n)])  27.9 us
    all_to_all x2, starting transfers between devices, from_everyone(): lax.all_to_all(jnp.broadcast_to(a[None], (n, *a.shape)), axis, 0, 0, tile...  18.5 us
    all_to_all x2, waiting for transfers between devices, from_everyone(): lax.all_to_all(jnp.broadcast_to(a[None], (n, *a.shape)), axis, 0, 0, tile...  8.47 us
    all_to_all x1, waiting for transfers between devices, step(): wanted = lax.all_to_all(wanted, ('x', 'core'), 0, 0, tiled=True)  5.72 us
    all_to_all x1, starting transfers between devices, step(): lax.all_to_all(terms.reshape(NY * NZ, part, tokens), ('y', 'z'), 0, 0, ti...  4.86 us
  transfers between devices with their start and end apart: 36, of which 16 were waited for; matrix products, arithmetic and copies ran while one was open for 4% of the time, Pallas kernels for 11%

profile of v4, /device:TPU:32, one launch (start us, length us, event | category | flops | bytes accessed | tf_op | source)
XLA Modules:
  0.0 181.7 jit_solution(16956023537153571850)
XLA Ops:
  0.6 1.5 broadcast_in_dim.8
  2.2 8.6 %all-to-all-start = ((bf16[8,96,128]{2,1,0:T(8,128)(2,1)}), bf16[8,96,128]{2,1,0:T(8,128)(2,1)S(1)}, u32[]{:S(2)}, u32[]{:S(2)}) async-start(bf16[8,96,128]{2,1,0:T(8,128)(2,1)} %broadcast_in_dim.8), calls=%async_computation | async-start | bytes 393216 | tf_op jit(solution)/shard_map/all_to_all | solution.py:27
  10.8 2.1 %slice.20 = bf16[384,1024]{1,0:T(8,128)(2,1)} slice(bf16[384,2048]{1,0:T(8,128)(2,1)} %refs_0_.3), slice={[0:384], [1024:2048]} | slice | bytes 1572864 | tf_op jit(solution)/shard_map/slice | solution.py:313
  12.9 2.8 %collective-permute-start.10 = (bf16[384,1024]{1,0:T(8,128)(2,1)}, bf16[384,1024]{1,0:T(8,128)(2,1)}, u32[]{:S(2)}, u32[]{:S(2)}) collective-permute-start(bf16[384,1024]{1,0:T(8,128)(2,1)} %slice.20), channel_id=1, source_target_pairs={{0,192},{64,0},{128,64},{192,128},{1,193},{65,1},{129,65},{193,129... | collective-permute-start | bytes 2359304 | tf_op jit(solution)/shard_map/ppermute | solution.py:19
  15.6 1.0 slice.15
  16.6 3.2 %collective-permute-start.3 = (bf16[384,1024]{1,0:T(8,128)(2,1)}, bf16[384,1024]{1,0:T(8,128)(2,1)}, u32[]{:S(2)}, u32[]{:S(2)}) collective-permute-start(bf16[384,1024]{1,0:T(8,128)(2,1)} %slice.15), channel_id=1, source_target_pairs={{0,192},{64,0},{128,64},{192,128},{1,193},{65,1},{129,65},{193,129... | collective-permute-start | bytes 2359304 | tf_op jit(solution)/shard_map/ppermute | solution.py:19
  19.8 3.1 %collective-permute-start = (bf16[8,96,128]{2,1,0:T(8,128)(2,1)S(1)}, bf16[8,96,128]{2,1,0:T(8,128)(2,1)S(1)}, u32[]{:S(2)}, u32[]{:S(2)}) collective-permute-start(bf16[8,96,128]{2,1,0:T(8,128)(2,1)S(1)} %all-to-all-done.p0), channel_id=1, source_target_pairs={{0,24},{8,0},{16,8},{24,16},{1,25},{9,1},{17,9},{25,17},{2,26},{10... | collective-permute-start | bytes 589832 | tf_op jit(solution)/shard_map/ppermute | solution.py:19
  22.9 3.2 %collective-permute-done.p1 = bf16[8,96,128]{2,1,0:T(8,128)(2,1)S(1)} collective-permute-done((bf16[8,96,128]{2,1,0:T(8,128)(2,1)S(1)}, bf16[8,96,128]{2,1,0:T(8,128)(2,1)S(1)}, u32[]{:S(2)}, u32[]{:S(2)}) %collective-permute-start) | collective-permute-done | bytes 196640 | tf_op jit(solution)/shard_map/ppermute | solution.py:19
  26.1 2.7 %collective-permute-start.1 = (bf16[8,96,128]{2,1,0:T(8,128)(2,1)S(1)}, bf16[8,96,128]{2,1,0:T(8,128)(2,1)S(1)}, u32[]{:S(2)}, u32[]{:S(2)}) collective-permute-start(bf16[8,96,128]{2,1,0:T(8,128)(2,1)S(1)} %all-to-all-done.p0), channel_id=1, source_target_pairs={{0,16},{8,24},{16,0},{24,8},{1,17},{9,25},{17,1},{25,9},{2,18},{10... | collective-permute-start | bytes 589832 | tf_op jit(solution)/shard_map/ppermute | solution.py:19
  28.8 4.5 %collective-permute-done.1.p2 = bf16[8,96,128]{2,1,0:T(8,128)(2,1)S(1)} collective-permute-done((bf16[8,96,128]{2,1,0:T(8,128)(2,1)S(1)}, bf16[8,96,128]{2,1,0:T(8,128)(2,1)S(1)}, u32[]{:S(2)}, u32[]{:S(2)}) %collective-permute-start.1) | collective-permute-done | bytes 196640 | tf_op jit(solution)/shard_map/ppermute | solution.py:19
  33.3 1.0 collective-permute-start.2
  34.3 6.4 %collective-permute-done.2.p3 = bf16[8,96,128]{2,1,0:T(8,128)(2,1)} collective-permute-done((bf16[8,96,128]{2,1,0:T(8,128)(2,1)S(1)}, bf16[8,96,128]{2,1,0:T(8,128)(2,1)}, u32[]{:S(2)}, u32[]{:S(2)}) %collective-permute-start.2) | collective-permute-done | bytes 196640 | tf_op jit(solution)/shard_map/ppermute | solution.py:19
  41.4 7.7 %collective-permute-done.3.refs_0_.refs_4_ = bf16[384,1024]{1,0:T(8,128)(2,1)} collective-permute-done((bf16[384,1024]{1,0:T(8,128)(2,1)}, bf16[384,1024]{1,0:T(8,128)(2,1)}, u32[]{:S(2)}, u32[]{:S(2)}) %collective-permute-start.3) | collective-permute-done | bytes 786464 | tf_op jit(solution)/shard_map/ppermute | solution.py:19
  49.0 1.2 collective-permute-start.12
  50.3 4.2 %collective-permute-done.5.refs_2_.refs_8_ = bf16[384,1024]{1,0:T(8,128)(2,1)} collective-permute-done((bf16[384,1024]{1,0:T(8,128)(2,1)}, bf16[384,1024]{1,0:T(8,128)(2,1)}, u32[]{:S(2)}, u32[]{:S(2)}) %collective-permute-start.5) | collective-permute-done | bytes 786464 | tf_op jit(solution)/shard_map/ppermute | solution.py:19
  55.0 0.7 copy.6.labels
  55.8 0.6 stack.125.who
  56.4 13.9 %collective-permute-done.12.left.refs_6_ = bf16[384,1024]{1,0:T(8,128)(2,1)} collective-permute-done((bf16[384,1024]{1,0:T(8,128)(2,1)}, bf16[384,1024]{1,0:T(8,128)(2,1)}, u32[]{:S(2)}, u32[]{:S(2)}) %collective-permute-start.12) | collective-permute-done | bytes 786464 | tf_op jit(solution)/shard_map/ppermute | solution.py:19
  70.3 1.0 collective-permute-done.14.right.refs_12_
  71.9 0.6 fusion.2.digits
  72.5 3.1 %shard_map.58 = (bf16[8,128,384]{2,1,0:T(8,128)(2,1)}, bf16[8,112,128]{2,1,0:T(8,128)(2,1)}) custom-call(s32[2]{0:T(128)} %pad_add_fusion.1.who, bf16[8,96,128]{2,1,0:T(8,128)(2,1)} %copy-done.6, bf16[8,96,128]{2,1,0:T(8,128)(2,1)} %copy-done.12, bf16[8,96,128]{2,1,0:T(8,128)(2,1)} %copy-done.13, bf16[8,96,128]{2,1,0:T(8,128)(2,1)} %collective-permute-done.2.p3, ...), custom_call_target="tpu_custom_call" | custom-call | flops 1048576 | bytes 4096 | tf_op jit(solution)/shard_map/pallas_call | solution.py:48
  75.6 3.6 %all-to-all-start.1 = ((bf16[8,112,128]{2,1,0:T(8,128)(2,1)}), bf16[8,112,128]{2,1,0:T(8,128)(2,1)S(1)}, u32[]{:S(2)}, u32[]{:S(2)}) async-start(bf16[8,112,128]{2,1,0:T(8,128)(2,1)} %get-tuple-element.13), calls=%async_computation.1 | async-start | bytes 458752 | tf_op jit(solution)/shard_map/all_to_all | solution.py:332
  80.4 5.7 %all-to-all-done.1.p0 = bf16[8,112,128]{2,1,0:T(8,128)(2,1)S(1)} async-done(((bf16[8,112,128]{2,1,0:T(8,128)(2,1)}), bf16[8,112,128]{2,1,0:T(8,128)(2,1)S(1)}, u32[]{:S(2)}, u32[]{:S(2)}) %all-to-all-start.1) | async-done | bytes 229408 | tf_op jit(solution)/shard_map/all_to_all | solution.py:332
  86.1 1.2 copy-done.1
  87.3 5.8 %shard_map.59.refs_4_ = f32[128,2048]{1,0:T(8,128)} custom-call(s32[6]{0:T(128)} %stack.125.who, bf16[8,128,384]{2,1,0:T(8,128)(2,1)} %get-tuple-element.14.states, bf16[384,2048]{1,0:T(8,128)(2,1)} %refs_0_.3, bf16[384,2048]{1,0:T(8,128)(2,1)} %copy-done.1, bf16[384,1024]{1,0:T(8,128)(2,1)} %collective-permute-done.8.refs_2_, ...), custom_call_target="tpu_custom_call" | custom-call | flops 805306368 | bytes 3145728 | tf_op jit(solution)/shard_map/pallas_call | solution.py:48
  93.1 4.7 %shard_map.60.near = f32[128,2048]{1,0:T(8,128)} custom-call(s32[4]{0:T(128)} %pad_add_fusion.2.who, bf16[8,128,384]{2,1,0:T(8,128)(2,1)} %get-tuple-element.14.states, bf16[384,1024]{1,0:T(8,128)(2,1)} %collective-permute-done.3.refs_0_.refs_4_, bf16[384,1024]{1,0:T(8,128)(2,1)} %collective-permute-done.4.refs_1_.refs_5_, ...), custom_call_target="tpu_custom_call" | custom-call | flops 402653184 | bytes 1572864 | tf_op jit(solution)/shard_map/pallas_call | solution.py:48
  97.8 5.3 %shard_map.61 = (bf16[128,2048]{1,0:T(8,128)(2,1)}, f32[8,128]{1,0:T(8,128)}) custom-call(s32[3]{0:T(128)} %pad_add_fusion.who, bf16[8,128,384]{2,1,0:T(8,128)(2,1)} %get-tuple-element.14.states, s32[128,1]{1,0:T(8,128)} %copy.6.labels, f32[128,2048]{1,0:T(8,128)} %shard_map.60.near, bf16[384,1024]{1,0:T(8,128)(2,1)} %collective-permute-done.12.left.refs_6_, ...), custom_call_target="tpu_custom_call" | custom-call | flops 402653184 | bytes 1572864 | tf_op jit(solution)/shard_map/pallas_call | solution.py:48
  103.1 0.7 slice.17
  103.8 0.6 broadcast_in_dim.21
  104.4 10.0 %all-to-all-start.2 = ((f32[32,3,128]{2,1,0:T(4,128)}), f32[32,3,128]{2,1,0:T(4,128)S(1)}, u32[]{:S(2)}, u32[]{:S(2)}) async-start(f32[32,3,128]{2,1,0:T(4,128)} %broadcast_in_dim.21), calls=%async_computation.2 | async-start | bytes 131072 | tf_op jit(solution)/shard_map/all_to_all | solution.py:27
  114.5 0.6 stack.109.starts
  115.1 8.5 %all-to-all-done.2.parts = f32[32,3,128]{2,1,0:T(4,128)S(1)} async-done(((f32[32,3,128]{2,1,0:T(4,128)}), f32[32,3,128]{2,1,0:T(4,128)S(1)}, u32[]{:S(2)}, u32[]{:S(2)}) %all-to-all-start.2) | async-done | bytes 49184 | tf_op jit(solution)/shard_map/all_to_all | solution.py:27
  123.5 0.6 copy-done.9
  124.1 8.5 %shard_map.62 = (bf16[3072,128]{1,0:T(8,128)(2,1)}, f32[1,128]{1,0:T(1,128)}, f32[1,128]{1,0:T(1,128)}) custom-call(s32[9]{0:T(128)} %stack.109.starts, bf16[128,2048]{1,0:T(8,128)(2,1)} %get-tuple-element.15.powers.refs_4_, s32[1,128]{1,0:T(1,128)} %bitcast.31, f32[32,3,128]{2,1,0:T(4,128)} %copy-done.9, f32[8,128]{1,0:T(8,128)} %get-tuple-element.16.stats, ...), custom_call_target="tpu_custom_call" | custom-call | flops 1610612736 | bytes 6291456 | tf_op jit(solution)/shard_map/pallas_call | solution.py:48
  132.7 4.9 %all-to-all-start.3 = ((bf16[32,96,128]{2,1,0:T(8,128)(2,1)}), bf16[32,96,128]{2,1,0:T(8,128)(2,1)S(1)}, u32[]{:S(2)}, u32[]{:S(2)}) async-start(bf16[32,96,128]{2,1,0:T(8,128)(2,1)} %bitcast.28), calls=%async_computation.3 | async-start | bytes 1572864 | tf_op jit(solution)/shard_map/all_to_all | solution.py:365
  137.6 0.6 collective-permute-start.24
  138.2 2.7 %collective-permute-start.26 = (bf16[128,2048]{1,0:T(8,128)(2,1)S(1)}, bf16[128,2048]{1,0:T(8,128)(2,1)S(1)}, u32[]{:S(2)}, u32[]{:S(2)}) collective-permute-start(bf16[128,2048]{1,0:T(8,128)(2,1)S(1)} %copy-done.2), channel_id=1, source_target_pairs={{0,192},{64,0},{128,64},{192,128},{1,193},{65,1},{129,65},{193,129... | collective-permute-start | bytes 1572872 | tf_op jit(solution)/shard_map/ppermute | solution.py:19
  140.9 2.8 %collective-permute-start.16 = (bf16[8,112,128]{2,1,0:T(8,128)(2,1)S(1)}, bf16[8,112,128]{2,1,0:T(8,128)(2,1)S(1)}, u32[]{:S(2)}, u32[]{:S(2)}) collective-permute-start(bf16[8,112,128]{2,1,0:T(8,128)(2,1)S(1)} %all-to-all-done.1.p0), channel_id=1, source_target_pairs={{0,24},{8,0},{16,8},{24,16},{1,25},{9,1},{17,9},{25,17},{2,26},{10... | collective-permute-start | bytes 688136 | tf_op jit(solution)/shard_map/ppermute | solution.py:19
  143.7 0.7 collective-permute-start.17
  145.4 11.3 %collective-permute-done.16.p1 = bf16[8,112,128]{2,1,0:T(8,128)(2,1)S(1)} collective-permute-done((bf16[8,112,128]{2,1,0:T(8,128)(2,1)S(1)}, bf16[8,112,128]{2,1,0:T(8,128)(2,1)S(1)}, u32[]{:S(2)}, u32[]{:S(2)}) %collective-permute-start.16) | collective-permute-done | bytes 229408 | tf_op jit(solution)/shard_map/ppermute | solution.py:19
  156.7 3.2 %collective-permute-start.21 = (f32[2,128]{1,0:T(2,128)S(1)}, f32[2,128]{1,0:T(2,128)S(1)}, u32[]{:S(2)}, u32[]{:S(2)}) collective-permute-start(f32[2,128]{1,0:T(2,128)S(1)} %pad_maximum_fusion.refs_0_), channel_id=1, source_target_pairs={{0,192},{64,0},{128,64},{192,128},{1,193},{65,1},{129,65},{193,129... | collective-permute-start | bytes 3080 | tf_op jit(solution)/shard_map/ppermute | solution.py:19
  160.4 1.3 collective-permute-done.18.p3
  161.9 2.9 %collective-permute-start.30 = (bf16[128,1024]{1,0:T(8,128)(2,1)S(1)}, bf16[128,1024]{1,0:T(8,128)(2,1)}, u32[]{:S(2)}, u32[]{:S(2)}) collective-permute-start(bf16[128,1024]{1,0:T(8,128)(2,1)S(1)} %slice.22), channel_id=1, source_target_pairs={{0,192},{64,0},{128,64},{192,128},{1,193},{65,1},{129,65},{193,129... | collective-permute-start | bytes 786440 | tf_op jit(solution)/shard_map/ppermute | solution.py:19
  165.5 5.8 %collective-permute-done.28.refs_10_ = bf16[128,1024]{1,0:T(8,128)(2,1)} collective-permute-done((bf16[128,1024]{1,0:T(8,128)(2,1)S(1)}, bf16[128,1024]{1,0:T(8,128)(2,1)}, u32[]{:S(2)}, u32[]{:S(2)}) %collective-permute-start.28) | collective-permute-done | bytes 262176 | tf_op jit(solution)/shard_map/ppermute | solution.py:19
  172.4 0.8 collective-permute-done.29.refs_11_
  173.6 0.7 copy-done.8
  174.3 6.6 %shard_map.63 = f32[384,2048]{1,0:T(8,128)} custom-call(s32[10]{0:T(128)} %stack.126.who, bf16[8,112,128]{2,1,0:T(8,128)(2,1)} %copy-done.5, bf16[8,112,128]{2,1,0:T(8,128)(2,1)} %copy-done.10, bf16[8,112,128]{2,1,0:T(8,128)(2,1)} %collective-permute-done.17.p2, bf16[8,112,128]{2,1,0:T(8,128)(2,1)} %copy-done.11, f32[2,128]{1,0:T(2,128)} %copy-done.14, ...), custom_call_target="tpu_custom_call" | custom-call | flops 1610612736 | bytes 6291456 | tf_op jit(solution)/shard_map/pallas_call | solution.py:48
  181.0 0.7 reduce_sum.12
  (88 shorter events, 6.7 us)
Async XLA Ops:
  0.6 15.0 %copy-start = (bf16[384,2048]{1,0:T(8,128)(2,1)S(1)}, bf16[384,2048]{1,0:T(8,128)(2,1)}, u32[]{:S(2)}) copy-start(bf16[384,2048]{1,0:T(8,128)(2,1)} %refs_0_.3) | copy-start | bytes 4718596
  2.2 17.6 %all-to-all-start = ((bf16[8,96,128]{2,1,0:T(8,128)(2,1)}), bf16[8,96,128]{2,1,0:T(8,128)(2,1)S(1)}, u32[]{:S(2)}, u32[]{:S(2)}) async-start(bf16[8,96,128]{2,1,0:T(8,128)(2,1)} %broadcast_in_dim.8), calls=%async_computation | async-start | bytes 393216 | tf_op jit(solution)/shard_map/all_to_all | solution.py:27
  10.8 44.3 %copy-start.15 = (s32[128]{0:T(128)S(1)}, s32[128]{0:T(128)}, u32[]{:S(2)}) copy-start(s32[128]{0:T(128)} %param.5) | copy-start | bytes 1540
  12.9 27.9 %collective-permute-start.10 = (bf16[384,1024]{1,0:T(8,128)(2,1)}, bf16[384,1024]{1,0:T(8,128)(2,1)}, u32[]{:S(2)}, u32[]{:S(2)}) collective-permute-start(bf16[384,1024]{1,0:T(8,128)(2,1)} %slice.20), channel_id=1, source_target_pairs={{0,192},{64,0},{128,64},{192,128},{1,193},{65,1},{129,65},{193,129... | collective-permute-start | bytes 2359304 | tf_op jit(solution)/shard_map/ppermute | solution.py:19
  16.6 24.7 %collective-permute-start.8 = (bf16[384,1024]{1,0:T(8,128)(2,1)}, bf16[384,1024]{1,0:T(8,128)(2,1)}, u32[]{:S(2)}, u32[]{:S(2)}) collective-permute-start(bf16[384,1024]{1,0:T(8,128)(2,1)} %slice.15), channel_id=1, source_target_pairs={{0,64},{64,128},{128,192},{192,0},{1,65},{65,129},{129,193},{193,1... | collective-permute-start | bytes 2359304 | tf_op jit(solution)/shard_map/ppermute | solution.py:19
  16.6 32.5 %collective-permute-start.3 = (bf16[384,1024]{1,0:T(8,128)(2,1)}, bf16[384,1024]{1,0:T(8,128)(2,1)}, u32[]{:S(2)}, u32[]{:S(2)}) collective-permute-start(bf16[384,1024]{1,0:T(8,128)(2,1)} %slice.15), channel_id=1, source_target_pairs={{0,192},{64,0},{128,64},{192,128},{1,193},{65,1},{129,65},{193,129... | collective-permute-start | bytes 2359304 | tf_op jit(solution)/shard_map/ppermute | solution.py:19
  19.8 34.7 %collective-permute-start.5 = (bf16[384,1024]{1,0:T(8,128)(2,1)}, bf16[384,1024]{1,0:T(8,128)(2,1)}, u32[]{:S(2)}, u32[]{:S(2)}) collective-permute-start(bf16[384,1024]{1,0:T(8,128)(2,1)} %slice.20), channel_id=1, source_target_pairs={{0,64},{64,128},{128,192},{192,0},{1,65},{65,129},{129,193},{193,1... | collective-permute-start | bytes 2359304 | tf_op jit(solution)/shard_map/ppermute | solution.py:19
  19.8 52.7 %copy-start.6 = (bf16[8,96,128]{2,1,0:T(8,128)(2,1)}, bf16[8,96,128]{2,1,0:T(8,128)(2,1)S(1)}, u32[]{:S(2)}) copy-start(bf16[8,96,128]{2,1,0:T(8,128)(2,1)S(1)} %all-to-all-done.p0) | copy-start | bytes 589828
  19.8 6.3 %collective-permute-start = (bf16[8,96,128]{2,1,0:T(8,128)(2,1)S(1)}, bf16[8,96,128]{2,1,0:T(8,128)(2,1)S(1)}, u32[]{:S(2)}, u32[]{:S(2)}) collective-permute-start(bf16[8,96,128]{2,1,0:T(8,128)(2,1)S(1)} %all-to-all-done.p0), channel_id=1, source_target_pairs={{0,24},{8,0},{16,8},{24,16},{1,25},{9,1},{17,9},{25,17},{2,26},{10... | collective-permute-start | bytes 589832 | tf_op jit(solution)/shard_map/ppermute | solution.py:19
  26.1 46.4 %copy-start.12 = (bf16[8,96,128]{2,1,0:T(8,128)(2,1)}, bf16[8,96,128]{2,1,0:T(8,128)(2,1)S(1)}, u32[]{:S(2)}) copy-start(bf16[8,96,128]{2,1,0:T(8,128)(2,1)S(1)} %collective-permute-done.p1) | copy-start | bytes 589828
  26.1 7.2 %collective-permute-start.1 = (bf16[8,96,128]{2,1,0:T(8,128)(2,1)S(1)}, bf16[8,96,128]{2,1,0:T(8,128)(2,1)S(1)}, u32[]{:S(2)}, u32[]{:S(2)}) collective-permute-start(bf16[8,96,128]{2,1,0:T(8,128)(2,1)S(1)} %all-to-all-done.p0), channel_id=1, source_target_pairs={{0,16},{8,24},{16,0},{24,8},{1,17},{9,25},{17,1},{25,9},{2,18},{10... | collective-permute-start | bytes 589832 | tf_op jit(solution)/shard_map/ppermute | solution.py:19
  33.3 7.4 %collective-permute-start.2 = (bf16[8,96,128]{2,1,0:T(8,128)(2,1)S(1)}, bf16[8,96,128]{2,1,0:T(8,128)(2,1)}, u32[]{:S(2)}, u32[]{:S(2)}) collective-permute-start(bf16[8,96,128]{2,1,0:T(8,128)(2,1)S(1)} %all-to-all-done.p0), channel_id=1, source_target_pairs={{0,8},{8,16},{16,24},{24,0},{1,9},{9,17},{17,25},{25,1},{2,10},{10... | collective-permute-start | bytes 589832 | tf_op jit(solution)/shard_map/ppermute | solution.py:19
  40.7 45.4 %collective-permute-start.7 = (bf16[384,2048]{1,0:T(8,128)(2,1)S(1)}, bf16[384,2048]{1,0:T(8,128)(2,1)S(1)}, u32[]{:S(2)}, u32[]{:S(2)}) collective-permute-start(bf16[384,2048]{1,0:T(8,128)(2,1)S(1)} %copy-done), channel_id=1, source_target_pairs={{0,32},{32,0},{1,33},{33,1},{2,34},{34,2},{3,35},{35,3},{4,36},{36... | collective-permute-start | bytes 4718600 | tf_op jit(solution)/shard_map/ppermute | solution.py:23
  40.7 13.8 %collective-permute-start.11 = (bf16[384,1024]{1,0:T(8,128)(2,1)}, bf16[384,1024]{1,0:T(8,128)(2,1)}, u32[]{:S(2)}, u32[]{:S(2)}) collective-permute-start(bf16[384,1024]{1,0:T(8,128)(2,1)} %collective-permute-done.10.refs_4_.refs_10_), channel_id=1, source_target_pairs={{0,32},{32,0},{1,33},{33,1},{2,34},{34,2},{3,35},{35,3},{4,36},{36... | collective-permute-start | bytes 2359304 | tf_op jit(solution)/shard_map/ppermute | solution.py:23
  41.3 13.3 %collective-permute-start.9 = (bf16[384,1024]{1,0:T(8,128)(2,1)}, bf16[384,1024]{1,0:T(8,128)(2,1)}, u32[]{:S(2)}, u32[]{:S(2)}) collective-permute-start(bf16[384,1024]{1,0:T(8,128)(2,1)} %collective-permute-done.8.refs_2_), channel_id=1, source_target_pairs={{0,32},{32,0},{1,33},{33,1},{2,34},{34,2},{3,35},{35,3},{4,36},{36... | collective-permute-start | bytes 2359304 | tf_op jit(solution)/shard_map/ppermute | solution.py:23
  49.0 21.2 %collective-permute-start.12 = (bf16[384,1024]{1,0:T(8,128)(2,1)}, bf16[384,1024]{1,0:T(8,128)(2,1)}, u32[]{:S(2)}, u32[]{:S(2)}) collective-permute-start(bf16[384,1024]{1,0:T(8,128)(2,1)} %collective-permute-done.8.refs_2_), channel_id=1, source_target_pairs={{0,64},{64,128},{128,192},{192,0},{1,65},{65,129},{129,193},{193,1... | collective-permute-start | bytes 2359304 | tf_op jit(solution)/shard_map/ppermute | solution.py:19
  54.5 16.8 %collective-permute-start.14 = (bf16[384,1024]{1,0:T(8,128)(2,1)}, bf16[384,1024]{1,0:T(8,128)(2,1)}, u32[]{:S(2)}, u32[]{:S(2)}) collective-permute-start(bf16[384,1024]{1,0:T(8,128)(2,1)} %collective-permute-done.10.refs_4_.refs_10_), channel_id=1, source_target_pairs={{0,192},{64,0},{128,64},{192,128},{1,193},{65,1},{129,65},{193,129... | collective-permute-start | bytes 2359304 | tf_op jit(solution)/shard_map/ppermute | solution.py:19
  54.5 38.5 %collective-permute-start.4 = (bf16[384,1024]{1,0:T(8,128)(2,1)}, bf16[384,1024]{1,0:T(8,128)(2,1)}, u32[]{:S(2)}, u32[]{:S(2)}) collective-permute-start(bf16[384,1024]{1,0:T(8,128)(2,1)} %collective-permute-done.3.refs_0_.refs_4_), channel_id=1, source_target_pairs={{0,32},{32,0},{1,33},{33,1},{2,34},{34,2},{3,35},{35,3},{4,36},{36... | collective-permute-start | bytes 2359304 | tf_op jit(solution)/shard_map/ppermute | solution.py:23
  54.5 38.5 %collective-permute-start.6 = (bf16[384,1024]{1,0:T(8,128)(2,1)}, bf16[384,1024]{1,0:T(8,128)(2,1)}, u32[]{:S(2)}, u32[]{:S(2)}) collective-permute-start(bf16[384,1024]{1,0:T(8,128)(2,1)} %collective-permute-done.5.refs_2_.refs_8_), channel_id=1, source_target_pairs={{0,32},{32,0},{1,33},{33,1},{2,34},{34,2},{3,35},{35,3},{4,36},{36... | collective-permute-start | bytes 2359304 | tf_op jit(solution)/shard_map/ppermute | solution.py:23
  70.3 27.5 %collective-permute-start.13 = (bf16[384,1024]{1,0:T(8,128)(2,1)}, bf16[384,1024]{1,0:T(8,128)(2,1)}, u32[]{:S(2)}, u32[]{:S(2)}) collective-permute-start(bf16[384,1024]{1,0:T(8,128)(2,1)} %collective-permute-done.12.left.refs_6_), channel_id=1, source_target_pairs={{0,32},{32,0},{1,33},{33,1},{2,34},{34,2},{3,35},{35,3},{4,36},{36... | collective-permute-start | bytes 2359304 | tf_op jit(solution)/shard_map/ppermute | solution.py:23
  71.3 26.5 %collective-permute-start.15 = (bf16[384,1024]{1,0:T(8,128)(2,1)}, bf16[384,1024]{1,0:T(8,128)(2,1)}, u32[]{:S(2)}, u32[]{:S(2)}) collective-permute-start(bf16[384,1024]{1,0:T(8,128)(2,1)} %collective-permute-done.14.right.refs_12_), channel_id=1, source_target_pairs={{0,32},{32,0},{1,33},{33,1},{2,34},{34,2},{3,35},{35,3},{4,36},{36... | collective-permute-start | bytes 2359304 | tf_op jit(solution)/shard_map/ppermute | solution.py:23
  75.6 10.5 %all-to-all-start.1 = ((bf16[8,112,128]{2,1,0:T(8,128)(2,1)}), bf16[8,112,128]{2,1,0:T(8,128)(2,1)S(1)}, u32[]{:S(2)}, u32[]{:S(2)}) async-start(bf16[8,112,128]{2,1,0:T(8,128)(2,1)} %get-tuple-element.13), calls=%async_computation.1 | async-start | bytes 458752 | tf_op jit(solution)/shard_map/all_to_all | solution.py:332
  86.1 58.8 %copy-start.5 = (bf16[8,112,128]{2,1,0:T(8,128)(2,1)}, bf16[8,112,128]{2,1,0:T(8,128)(2,1)S(1)}, u32[]{:S(2)}) copy-start(bf16[8,112,128]{2,1,0:T(8,128)(2,1)S(1)} %all-to-all-done.1.p0) | copy-start | bytes 688132
  104.4 19.1 %all-to-all-start.2 = ((f32[32,3,128]{2,1,0:T(4,128)}), f32[32,3,128]{2,1,0:T(4,128)S(1)}, u32[]{:S(2)}, u32[]{:S(2)}) async-start(f32[32,3,128]{2,1,0:T(4,128)} %broadcast_in_dim.21), calls=%async_computation.2 | async-start | bytes 131072 | tf_op jit(solution)/shard_map/all_to_all | solution.py:27
  132.7 11.0 %copy-start.19 = (f32[1,128]{1,0:T(1,128)S(1)}, f32[1,128]{1,0:T(1,128)}, u32[]{:S(2)}) copy-start(f32[1,128]{1,0:T(1,128)} %get-tuple-element.20) | copy-start | bytes 1540
  132.7 48.3 %all-to-all-start.3 = ((bf16[32,96,128]{2,1,0:T(8,128)(2,1)}), bf16[32,96,128]{2,1,0:T(8,128)(2,1)S(1)}, u32[]{:S(2)}, u32[]{:S(2)}) async-start(bf16[32,96,128]{2,1,0:T(8,128)(2,1)} %bitcast.28), calls=%async_computation.3 | async-start | bytes 1572864 | tf_op jit(solution)/shard_map/all_to_all | solution.py:365
  137.6 19.2 %collective-permute-start.24 = (bf16[128,2048]{1,0:T(8,128)(2,1)S(1)}, bf16[128,2048]{1,0:T(8,128)(2,1)S(1)}, u32[]{:S(2)}, u32[]{:S(2)}) collective-permute-start(bf16[128,2048]{1,0:T(8,128)(2,1)S(1)} %copy-done.2), channel_id=1, source_target_pairs={{0,64},{64,128},{128,192},{192,0},{1,65},{65,129},{129,193},{193,1... | collective-permute-start | bytes 1572872 | tf_op jit(solution)/shard_map/ppermute | solution.py:19
  138.2 21.7 %collective-permute-start.26 = (bf16[128,2048]{1,0:T(8,128)(2,1)S(1)}, bf16[128,2048]{1,0:T(8,128)(2,1)S(1)}, u32[]{:S(2)}, u32[]{:S(2)}) collective-permute-start(bf16[128,2048]{1,0:T(8,128)(2,1)S(1)} %copy-done.2), channel_id=1, source_target_pairs={{0,192},{64,0},{128,64},{192,128},{1,193},{65,1},{129,65},{193,129... | collective-permute-start | bytes 1572872 | tf_op jit(solution)/shard_map/ppermute | solution.py:19
  140.9 15.8 %collective-permute-start.16 = (bf16[8,112,128]{2,1,0:T(8,128)(2,1)S(1)}, bf16[8,112,128]{2,1,0:T(8,128)(2,1)S(1)}, u32[]{:S(2)}, u32[]{:S(2)}) collective-permute-start(bf16[8,112,128]{2,1,0:T(8,128)(2,1)S(1)} %all-to-all-done.1.p0), channel_id=1, source_target_pairs={{0,24},{8,0},{16,8},{24,16},{1,25},{9,1},{17,9},{25,17},{2,26},{10... | collective-permute-start | bytes 688136 | tf_op jit(solution)/shard_map/ppermute | solution.py:19
  143.7 1.2 collective-permute-start.19
  143.7 16.3 %collective-permute-start.17 = (bf16[8,112,128]{2,1,0:T(8,128)(2,1)S(1)}, bf16[8,112,128]{2,1,0:T(8,128)(2,1)}, u32[]{:S(2)}, u32[]{:S(2)}) collective-permute-start(bf16[8,112,128]{2,1,0:T(8,128)(2,1)S(1)} %all-to-all-done.1.p0), channel_id=1, source_target_pairs={{0,16},{8,24},{16,0},{24,8},{1,17},{9,25},{17,1},{25,9},{2,18},{10... | collective-permute-start | bytes 688136 | tf_op jit(solution)/shard_map/ppermute | solution.py:19
  144.9 16.7 %collective-permute-start.18 = (bf16[8,112,128]{2,1,0:T(8,128)(2,1)S(1)}, bf16[8,112,128]{2,1,0:T(8,128)(2,1)S(1)}, u32[]{:S(2)}, u32[]{:S(2)}) collective-permute-start(bf16[8,112,128]{2,1,0:T(8,128)(2,1)S(1)} %all-to-all-done.1.p0), channel_id=1, source_target_pairs={{0,8},{8,16},{16,24},{24,0},{1,9},{9,17},{17,25},{25,1},{2,10},{10... | collective-permute-start | bytes 688136 | tf_op jit(solution)/shard_map/ppermute | solution.py:19
  145.4 28.1 %copy-start.14 = (f32[2,128]{1,0:T(2,128)}, f32[2,128]{1,0:T(2,128)S(1)}, u32[]{:S(2)}) copy-start(f32[2,128]{1,0:T(2,128)S(1)} %pad_maximum_fusion.refs_0_) | copy-start | bytes 3076
  156.7 5.2 %collective-permute-start.20 = (f32[2,128]{1,0:T(2,128)S(1)}, f32[2,128]{1,0:T(2,128)S(1)}, u32[]{:S(2)}, u32[]{:S(2)}) collective-permute-start(f32[2,128]{1,0:T(2,128)S(1)} %pad_maximum_fusion.refs_0_), channel_id=1, source_target_pairs={{0,64},{64,128},{128,192},{192,0},{1,65},{65,129},{129,193},{193,1... | collective-permute-start | bytes 3080 | tf_op jit(solution)/shard_map/ppermute | solution.py:19
  156.7 16.8 %copy-start.3 = (bf16[128,2048]{1,0:T(8,128)(2,1)}, bf16[128,2048]{1,0:T(8,128)(2,1)S(1)}, u32[]{:S(2)}) copy-start(bf16[128,2048]{1,0:T(8,128)(2,1)S(1)} %collective-permute-done.24.refs_6_) | copy-start | bytes 1572868
  156.7 8.1 %collective-permute-start.21 = (f32[2,128]{1,0:T(2,128)S(1)}, f32[2,128]{1,0:T(2,128)S(1)}, u32[]{:S(2)}, u32[]{:S(2)}) collective-permute-start(f32[2,128]{1,0:T(2,128)S(1)} %pad_maximum_fusion.refs_0_), channel_id=1, source_target_pairs={{0,192},{64,0},{128,64},{192,128},{1,193},{65,1},{129,65},{193,129... | collective-permute-start | bytes 3080 | tf_op jit(solution)/shard_map/ppermute | solution.py:19
  160.0 13.6 %copy-start.4 = (bf16[128,2048]{1,0:T(8,128)(2,1)}, bf16[128,2048]{1,0:T(8,128)(2,1)S(1)}, u32[]{:S(2)}) copy-start(bf16[128,2048]{1,0:T(8,128)(2,1)S(1)} %collective-permute-done.26.refs_8_) | copy-start | bytes 1572868
  160.0 5.1 %collective-permute-start.22 = (f32[2,128]{1,0:T(2,128)S(1)}, f32[2,128]{1,0:T(2,128)S(1)}, u32[]{:S(2)}, u32[]{:S(2)}) collective-permute-start(f32[2,128]{1,0:T(2,128)S(1)} %pad_maximum_fusion.refs_0_), channel_id=1, source_target_pairs={{0,128},{64,192},{128,0},{192,64},{1,129},{65,193},{129,1},{193,65... | collective-permute-start | bytes 3080 | tf_op jit(solution)/shard_map/ppermute | solution.py:19
  160.0 12.3 %collective-permute-start.23 = (bf16[128,2048]{1,0:T(8,128)(2,1)S(1)}, bf16[128,2048]{1,0:T(8,128)(2,1)S(1)}, u32[]{:S(2)}, u32[]{:S(2)}) collective-permute-start(bf16[128,2048]{1,0:T(8,128)(2,1)S(1)} %copy-done.2), channel_id=1, source_target_pairs={{0,32},{32,0},{1,33},{33,1},{2,34},{34,2},{3,35},{35,3},{4,36},{36... | collective-permute-start | bytes 1572872 | tf_op jit(solution)/shard_map/ppermute | solution.py:23
  161.6 9.6 %collective-permute-start.28 = (bf16[128,1024]{1,0:T(8,128)(2,1)S(1)}, bf16[128,1024]{1,0:T(8,128)(2,1)}, u32[]{:S(2)}, u32[]{:S(2)}) collective-permute-start(bf16[128,1024]{1,0:T(8,128)(2,1)S(1)} %slice.21), channel_id=1, source_target_pairs={{0,64},{64,128},{128,192},{192,0},{1,65},{65,129},{129,193},{193,1... | collective-permute-start | bytes 786440 | tf_op jit(solution)/shard_map/ppermute | solution.py:19
  161.9 11.6 %copy-start.16 = (f32[2,128]{1,0:T(2,128)}, f32[2,128]{1,0:T(2,128)S(1)}, u32[]{:S(2)}) copy-start(f32[2,128]{1,0:T(2,128)S(1)} %collective-permute-done.20.refs_1_) | copy-start | bytes 3076
  161.9 9.3 %collective-permute-start.30 = (bf16[128,1024]{1,0:T(8,128)(2,1)S(1)}, bf16[128,1024]{1,0:T(8,128)(2,1)}, u32[]{:S(2)}, u32[]{:S(2)}) collective-permute-start(bf16[128,1024]{1,0:T(8,128)(2,1)S(1)} %slice.22), channel_id=1, source_target_pairs={{0,192},{64,0},{128,64},{192,128},{1,193},{65,1},{129,65},{193,129... | collective-permute-start | bytes 786440 | tf_op jit(solution)/shard_map/ppermute | solution.py:19
  164.9 8.7 %copy-start.17 = (f32[2,128]{1,0:T(2,128)}, f32[2,128]{1,0:T(2,128)S(1)}, u32[]{:S(2)}) copy-start(f32[2,128]{1,0:T(2,128)S(1)} %collective-permute-done.21.refs_2_) | copy-start | bytes 3076
  164.9 8.6 %collective-permute-start.25 = (bf16[128,2048]{1,0:T(8,128)(2,1)S(1)}, bf16[128,2048]{1,0:T(8,128)(2,1)S(1)}, u32[]{:S(2)}, u32[]{:S(2)}) collective-permute-start(bf16[128,2048]{1,0:T(8,128)(2,1)S(1)} %collective-permute-done.24.refs_6_), channel_id=1, source_target_pairs={{0,32},{32,0},{1,33},{33,1},{2,34},{34,2},{3,35},{35,3},{4,36},{36... | collective-permute-start | bytes 1572872 | tf_op jit(solution)/shard_map/ppermute | solution.py:23
  165.0 8.5 %copy-start.18 = (f32[2,128]{1,0:T(2,128)}, f32[2,128]{1,0:T(2,128)S(1)}, u32[]{:S(2)}) copy-start(f32[2,128]{1,0:T(2,128)S(1)} %collective-permute-done.22.refs_3_) | copy-start | bytes 3076
  165.0 8.5 %collective-permute-start.27 = (bf16[128,2048]{1,0:T(8,128)(2,1)S(1)}, bf16[128,2048]{1,0:T(8,128)(2,1)}, u32[]{:S(2)}, u32[]{:S(2)}) collective-permute-start(bf16[128,2048]{1,0:T(8,128)(2,1)S(1)} %collective-permute-done.26.refs_8_), channel_id=1, source_target_pairs={{0,32},{32,0},{1,33},{33,1},{2,34},{34,2},{3,35},{35,3},{4,36},{36... | collective-permute-start | bytes 1572872 | tf_op jit(solution)/shard_map/ppermute | solution.py:23
  171.3 1.9 %collective-permute-start.29 = (bf16[128,1024]{1,0:T(8,128)(2,1)}, bf16[128,1024]{1,0:T(8,128)(2,1)}, u32[]{:S(2)}, u32[]{:S(2)}) collective-permute-start(bf16[128,1024]{1,0:T(8,128)(2,1)} %collective-permute-done.28.refs_10_), channel_id=1, source_target_pairs={{0,32},{32,0},{1,33},{33,1},{2,34},{34,2},{3,35},{35,3},{4,36},{36... | collective-permute-start | bytes 786440 | tf_op jit(solution)/shard_map/ppermute | solution.py:23
  171.3 2.2 %collective-permute-start.31 = (bf16[128,1024]{1,0:T(8,128)(2,1)}, bf16[128,1024]{1,0:T(8,128)(2,1)}, u32[]{:S(2)}, u32[]{:S(2)}) collective-permute-start(bf16[128,1024]{1,0:T(8,128)(2,1)} %collective-permute-done.30.refs_12_), channel_id=1, source_target_pairs={{0,32},{32,0},{1,33},{33,1},{2,34},{34,2},{3,35},{35,3},{4,36},{36... | collective-permute-start | bytes 786440 | tf_op jit(solution)/shard_map/ppermute | solution.py:23
  (8 other events, 16.3 us)

commit v5 on v4

--- a/solution.py
+++ b/solution.py
@@ -44,7 +44,7 @@
     return jnp.maximum(j - STEPS // 2, 0)
 
 
-def call(kernel, scalars, args, in_specs, out_specs, out_shape, flops, scratch=(), steps=STEPS, room=None):
+def call(kernel, scalars, args, in_specs, out_specs, out_shape, flops, scratch=(), steps=STEPS, room=ROOM):
     return pl.pallas_call(
         kernel,
         grid_spec=pltpu.PrefetchScalarGridSpec(
@@ -129,7 +129,7 @@
     )
 
 
-def far_kernel(who, states, labels, near, left, left_other, right, right_other, powers, stats, logits, rows, few, sems):
+def far_kernel(who, states, labels, near, left, left_other, right, right_other, powers, stats, peaks, logits, rows, few, sems):
     copies = [
         pltpu.make_async_copy(states.at[who[0]], few.at[0], sems.at[0]),
         pltpu.make_async_copy(states.at[who[1]], few.at[1], sems.at[1]),
@@ -157,7 +157,9 @@
     powers[...] = shifted.astype(BF)
     lanes = lax.broadcasted_iota(jnp.int32, (values.shape[0], 128), 1)
     both = jnp.where(lanes == 0, peak, jnp.where(lanes == 1, total, target))
-    stats[...] = both.T[:8]
+    lines = both.T
+    stats[...] = jnp.broadcast_to(lines[None, :3], stats.shape)
+    peaks[...] = lines[:1]
 
 
 def far_logits(states, labels, near, left, right, who):
@@ -166,14 +168,15 @@
     args = [states, labels, near, *left, *right]
     far = pl.BlockSpec(memory_space=pltpu.HBM)
     powers = jax.ShapeDtypeStruct((tokens, width), BF)
-    stats = jax.ShapeDtypeStruct((8, 128), F32)
+    stats = jax.ShapeDtypeStruct((NY * NZ, 3, tokens), F32)
+    peaks = jax.ShapeDtypeStruct((1, tokens), F32)
     return call(
         far_kernel,
         who,
         args,
         [far, whole(labels)] + [far] * 5,
-        [whole(powers), whole(stats)],
-        [powers, stats],
+        [whole(powers), whole(stats), whole(peaks)],
+        [powers, stats, peaks],
         4 * tokens * rows * width,
         [
             pltpu.VMEM((tokens, width), F32),
@@ -186,18 +189,18 @@
     )
 
 
-def terms_kernel(starts, powers, labels, parts, stats, *refs):
-    *arrays, out, scales, losses, errors = refs
+def terms_kernel(starts, powers, labels, parts, peaks, *refs):
+    *arrays, out0, out1, out2, out3, scales, losses, errors, out = refs
     step = pl.program_id(0)
     width, tokens = errors.shape
 
     @pl.when(step == 0)
     def _():
-        peaks = parts[:, 0, :]
-        peak = jnp.max(peaks, axis=0, keepdims=True)
-        total = jnp.sum(parts[:, 1, :] * jnp.exp(peaks - peak), axis=0, keepdims=True)
+        theirs = parts[:, 0, :]
+        peak = jnp.max(theirs, axis=0, keepdims=True)
+        total = jnp.sum(parts[:, 1, :] * jnp.exp(theirs - peak), axis=0, keepdims=True)
         target = jnp.sum(parts[:, 2, :], axis=0, keepdims=True)
-        scale = jnp.exp(stats[0:1, :] - peak) / total
+        scale = jnp.exp(peaks[...] - peak) / total
         loss = jnp.log(total) + peak - target
         scales[...] = scale
         losses[...] = loss
@@ -215,24 +218,29 @@
         at = pl.ds(pl.multiple_of(starts[k] + step * rows, 32), rows)
         out[at, :] = term[k * rows : (k + 1) * rows].astype(BF)
 
-
-def state_terms(powers, labels, parts, stats, own, left, right, starts, depth):
+    @pl.when(step == STEPS - 1)
+    def _():
+        for j, ref in enumerate((out0, out1, out2, out3)):
+            ref[...] = out[pl.ds(j * ref.shape[0], ref.shape[0]), :]
+
+
+def state_terms(powers, labels, parts, peaks, own, left, right, starts, depth):
     tokens, width = powers.shape
     rows = own[0].shape[0] // STEPS
-    args = [powers, labels, parts, stats, *own, *left, *right]
+    args = [powers, labels, parts, peaks, *own, *left, *right]
     specs = [whole(a) for a in args[:4]]
     specs += [pl.BlockSpec((rows, a.shape[1]), lambda j, s: (j, 0)) for a in args[4:]]
-    terms = jax.ShapeDtypeStruct((depth, tokens), BF)
+    terms = jax.ShapeDtypeStruct((depth // NY, tokens), BF)
     line = jax.ShapeDtypeStruct((1, tokens), F32)
     return call(
         terms_kernel,
         starts,
         args,
         specs,
-        [whole(terms), whole(line), whole(line)],
-        [terms, line, line],
+        [whole(terms)] * NY + [whole(line)] * 2,
+        [terms] * NY + [line] * 2,
         2 * tokens * width * depth,
-        [pltpu.VMEM((width, tokens), BF)],
+        [pltpu.VMEM((width, tokens), BF), pltpu.VMEM((depth, tokens), BF)],
     )
 
 
@@ -341,7 +349,7 @@
         who(0) + who(3) + who(1),
     )
     logits = logits_part(states, [], left, right, who(1) + who(3), logits)
-    powers, stats = far_logits(
+    powers, stats, peaks = far_logits(
         far_states, labels[:, None], logits, away_left, away_right, who(2) + [base]
     )
 
@@ -353,18 +361,21 @@
     pow_left = [pow_left, swap(pow_left)]
     pow_right = [pow_right, swap(pow_right)]
 
-    parts = from_everyone(stats[:3], ("y", "z"), NY * NZ)
-    starts = [w * rows for w in who(0) + who(3) + who(1) + who(2)]
+    parts = lax.all_to_all(stats, ("y", "z"), 0, 0, tiled=True)
+    starts = []
+    for offset in (0, 3, 1, 2):
+        chip = ((x + offset - y) % NY) * 2
+        starts += [(chip + core) * rows, (chip + 1 - core) * rows]
     all_left = [up_left, up_left_other, *left, *away_left]
     all_right = [*right, down_right, down_right_other, *away_right]
-    terms, scale, token_loss = state_terms(
-        powers, labels[None], parts, stats, own, all_left, all_right, starts + [base], depth
+    *terms, scale, token_loss = state_terms(
+        powers, labels[None], parts, peaks, own, all_left, all_right, starts + [base], depth
     )
     token_loss = token_loss.reshape(tokens)
 
-    arrived = lax.all_to_all(
-        terms.reshape(NY * NZ, part, tokens), ("y", "z"), 0, 0, tiled=True
-    )
+    arrived = [terms[0]] + [shift(terms[j], "y", NY, j) for j in (1, 2, 3)]
+    row_sum = sum(a.astype(F32) for a in arrived).astype(BF)
+    arrived = lax.all_to_all(row_sum.reshape(NZ, part, tokens), "z", 0, 0, tiled=True)
     state_grad = arrived.astype(F32).sum(axis=0).astype(BF).T
 
     pair = jnp.concatenate([scale, swap(scale)])

time: 185 us -> 187 us (1.011)
  waiting for transfers between devices: 75.2 us -> 69.4 us
  starting transfers between devices: 57.3 us -> 62.4 us
  other arithmetic: 3.11 us -> 5.38 us
    all_to_all x1 -> x2, waiting for transfers between devices: 0.01 us -> 10.9 us  [the longest x1 8.45 us: step(): lax.all_to_all(row_sum.reshape(NZ, part, tokens), 'z', 0, 0, tiled=True)]
    all_to_all x2 -> x1, starting transfers between devices: 18.5 us -> 8.57 us  [from_everyone(): lax.all_to_all(jnp.broadcast_to(a[None], (n, *a.shape)), axis, 0, 0, tile...]
    all_to_all x1 -> x2, starting transfers between devices: 4.86 us -> 14.1 us  [the longest x1 9.35 us: step(): parts = lax.all_to_all(stats, ('y', 'z'), 0, 0, tiled=True)]
    ppermute x19 -> x22, waiting for transfers between devices: 59.4 us -> 50.8 us  [shift(): return lax.ppermute(a, axis, [(i, (i + s) % n) for i in range(n)])]
    all_to_all x2 -> x1, waiting for transfers between devices: 8.47 us -> 2 us  [from_everyone(): lax.all_to_all(jnp.broadcast_to(a[None], (n, *a.shape)), axis, 0, 0, tile...]
    ppermute x19 -> x22, starting transfers between devices: 27.9 us -> 34.2 us  [shift(): return lax.ppermute(a, axis, [(i, (i + s) % n) for i in range(n)])]
    slice x1, local copies, waits for them, and re-layouts: 2.11 us -> 0.06 us  [step(): right_half = lax.optimization_barrier(head)[:, half:]]
  transfers between devices with their start and end apart: 36 -> 39, of which waited for: 16 -> 14; matrix products, arithmetic and copies ran while one was open for 4% -> 7% of each run, Pallas kernels for 11% -> 12%
where the time goes in v5:
time: 187 us; the launch traced here: 184 us
  waiting for transfers between devices  69.4 us (37%)
  starting transfers between devices  62.4 us (33%)
  Pallas kernels  34.2 us (18%)
  local copies, waits for them, and re-layouts  11.3 us (6%)
  other arithmetic  5.38 us (3%)
    ppermute x22, waiting for transfers between devices, shift(): return lax.ppermute(a, axis, [(i, (i + s) % n) for i in range(n)])  50.8 us
    ppermute x22, starting transfers between devices, shift(): return lax.ppermute(a, axis, [(i, (i + s) % n) for i in range(n)])  34.2 us
    pallas_call x6, Pallas kernels, call(): pl.pallas_call(kernel, grid_spec=pltpu.PrefetchScalarGridSpec(num_scalar_...  34.2 us
    all_to_all x1, starting transfers between devices, step(): parts = lax.all_to_all(stats, ('y', 'z'), 0, 0, tiled=True)  9.35 us
    all_to_all x1, starting transfers between devices, from_everyone(): lax.all_to_all(jnp.broadcast_to(a[None], (n, *a.shape)), axis, 0, 0, tile...  8.57 us
    all_to_all x1, waiting for transfers between devices, step(): lax.all_to_all(row_sum.reshape(NZ, part, tokens), 'z', 0, 0, tiled=True)  8.45 us
    all_to_all x1, waiting for transfers between devices, step(): wanted = lax.all_to_all(wanted, ('x', 'core'), 0, 0, tiled=True)  5.72 us
    all_to_all x1, starting transfers between devices, step(): lax.all_to_all(row_sum.reshape(NZ, part, tokens), 'z', 0, 0, tiled=True)  4.77 us
  transfers between devices with their start and end apart: 39, of which 14 were waited for; matrix products, arithmetic and copies ran while one was open for 7% of the time, Pallas kernels for 12%

profile of v5, /device:TPU:32, one launch (start us, length us, event | category | flops | bytes accessed | tf_op | source)
XLA Modules:
  0.0 183.8 jit_solution(17408322750918988934)
XLA Ops:
  0.6 1.6 broadcast_in_dim.12
  2.2 8.6 %all-to-all-start = ((bf16[8,96,128]{2,1,0:T(8,128)(2,1)}), bf16[8,96,128]{2,1,0:T(8,128)(2,1)S(1)}, u32[]{:S(2)}, u32[]{:S(2)}) async-start(bf16[8,96,128]{2,1,0:T(8,128)(2,1)} %broadcast_in_dim.12), calls=%async_computation | async-start | bytes 393216 | tf_op jit(solution)/shard_map/all_to_all | solution.py:27
  10.8 2.1 %slice.12 = bf16[384,1024]{1,0:T(8,128)(2,1)} slice(bf16[384,2048]{1,0:T(8,128)(2,1)} %refs_0_.3), slice={[0:384], [0:1024]} | slice | bytes 1572864 | tf_op jit(solution)/shard_map/slice | solution.py:320
  12.8 1.5 collective-permute-start.8
  14.3 1.7 collective-permute-start.3
  16.1 1.6 collective-permute-start.10
  17.8 2.0 %all-to-all-done.p0 = bf16[8,96,128]{2,1,0:T(8,128)(2,1)S(1)} async-done(((bf16[8,96,128]{2,1,0:T(8,128)(2,1)}), bf16[8,96,128]{2,1,0:T(8,128)(2,1)S(1)}, u32[]{:S(2)}, u32[]{:S(2)}) %all-to-all-start) | async-done | bytes 196640 | tf_op jit(solution)/shard_map/all_to_all | solution.py:27
  19.8 3.0 %collective-permute-start = (bf16[8,96,128]{2,1,0:T(8,128)(2,1)S(1)}, bf16[8,96,128]{2,1,0:T(8,128)(2,1)S(1)}, u32[]{:S(2)}, u32[]{:S(2)}) collective-permute-start(bf16[8,96,128]{2,1,0:T(8,128)(2,1)S(1)} %all-to-all-done.p0), channel_id=1, source_target_pairs={{0,24},{8,0},{16,8},{24,16},{1,25},{9,1},{17,9},{25,17},{2,26},{10... | collective-permute-start | bytes 589832 | tf_op jit(solution)/shard_map/ppermute | solution.py:19
  22.8 3.2 %collective-permute-done.p1 = bf16[8,96,128]{2,1,0:T(8,128)(2,1)S(1)} collective-permute-done((bf16[8,96,128]{2,1,0:T(8,128)(2,1)S(1)}, bf16[8,96,128]{2,1,0:T(8,128)(2,1)S(1)}, u32[]{:S(2)}, u32[]{:S(2)}) %collective-permute-start) | collective-permute-done | bytes 196640 | tf_op jit(solution)/shard_map/ppermute | solution.py:19
  26.0 2.7 %collective-permute-start.1 = (bf16[8,96,128]{2,1,0:T(8,128)(2,1)S(1)}, bf16[8,96,128]{2,1,0:T(8,128)(2,1)S(1)}, u32[]{:S(2)}, u32[]{:S(2)}) collective-permute-start(bf16[8,96,128]{2,1,0:T(8,128)(2,1)S(1)} %all-to-all-done.p0), channel_id=1, source_target_pairs={{0,16},{8,24},{16,0},{24,8},{1,17},{9,25},{17,1},{25,9},{2,18},{10... | collective-permute-start | bytes 589832 | tf_op jit(solution)/shard_map/ppermute | solution.py:19
  28.6 4.5 %collective-permute-done.1.p2 = bf16[8,96,128]{2,1,0:T(8,128)(2,1)S(1)} collective-permute-done((bf16[8,96,128]{2,1,0:T(8,128)(2,1)S(1)}, bf16[8,96,128]{2,1,0:T(8,128)(2,1)S(1)}, u32[]{:S(2)}, u32[]{:S(2)}) %collective-permute-start.1) | collective-permute-done | bytes 196640 | tf_op jit(solution)/shard_map/ppermute | solution.py:19
  33.2 1.0 collective-permute-start.2
  34.2 6.3 %collective-permute-done.2.p3 = bf16[8,96,128]{2,1,0:T(8,128)(2,1)S(1)} collective-permute-done((bf16[8,96,128]{2,1,0:T(8,128)(2,1)S(1)}, bf16[8,96,128]{2,1,0:T(8,128)(2,1)S(1)}, u32[]{:S(2)}, u32[]{:S(2)}) %collective-permute-start.2) | collective-permute-done | bytes 196640 | tf_op jit(solution)/shard_map/ppermute | solution.py:19
  40.5 1.5 collective-permute-start.5
  42.0 0.9 copy-done.1
  42.9 1.5 collective-permute-start.12
  44.4 6.8 %collective-permute-done.10.refs_4_.refs_10_ = bf16[384,1024]{1,0:T(8,128)(2,1)} collective-permute-done((bf16[384,1024]{1,0:T(8,128)(2,1)S(1)}, bf16[384,1024]{1,0:T(8,128)(2,1)}, u32[]{:S(2)}, u32[]{:S(2)}) %collective-permute-start.10) | collective-permute-done | bytes 786464 | tf_op jit(solution)/shard_map/ppermute | solution.py:19
  51.2 3.0 %collective-permute-start.14 = (bf16[384,1024]{1,0:T(8,128)(2,1)}, bf16[384,1024]{1,0:T(8,128)(2,1)}, u32[]{:S(2)}, u32[]{:S(2)}) collective-permute-start(bf16[384,1024]{1,0:T(8,128)(2,1)} %collective-permute-done.10.refs_4_.refs_10_), channel_id=1, source_target_pairs={{0,192},{64,0},{128,64},{192,128},{1,193},{65,1},{129,65},{193,129... | collective-permute-start | bytes 2359304 | tf_op jit(solution)/shard_map/ppermute | solution.py:19
  54.1 8.1 %collective-permute-done.5.refs_2_.refs_8_ = bf16[384,1024]{1,0:T(8,128)(2,1)} collective-permute-done((bf16[384,1024]{1,0:T(8,128)(2,1)S(1)}, bf16[384,1024]{1,0:T(8,128)(2,1)}, u32[]{:S(2)}, u32[]{:S(2)}) %collective-permute-start.5) | collective-permute-done | bytes 786464 | tf_op jit(solution)/shard_map/ppermute | solution.py:19
  62.8 0.9 copy-done.2
  65.0 8.3 %collective-permute-done.12.left.refs_6_ = bf16[384,1024]{1,0:T(8,128)(2,1)} collective-permute-done((bf16[384,1024]{1,0:T(8,128)(2,1)S(1)}, bf16[384,1024]{1,0:T(8,128)(2,1)}, u32[]{:S(2)}, u32[]{:S(2)}) %collective-permute-start.12) | collective-permute-done | bytes 786464 | tf_op jit(solution)/shard_map/ppermute | solution.py:19
  75.0 3.1 %shard_map.58 = (bf16[8,128,384]{2,1,0:T(8,128)(2,1)}, bf16[8,112,128]{2,1,0:T(8,128)(2,1)}) custom-call(s32[2]{0:T(128)} %pad_add_fusion.1.who, bf16[8,96,128]{2,1,0:T(8,128)(2,1)} %copy-done.4, bf16[8,96,128]{2,1,0:T(8,128)(2,1)} %copy-done.11, bf16[8,96,128]{2,1,0:T(8,128)(2,1)} %copy-done.12, bf16[8,96,128]{2,1,0:T(8,128)(2,1)} %copy-done.13, ...), custom_call_target="tpu_custom_call" | custom-call | flops 1048576 | bytes 4096 | tf_op jit(solution)/shard_map/pallas_call | solution.py:48
  78.1 3.6 %all-to-all-start.1 = ((bf16[8,112,128]{2,1,0:T(8,128)(2,1)}), bf16[8,112,128]{2,1,0:T(8,128)(2,1)S(1)}, u32[]{:S(2)}, u32[]{:S(2)}) async-start(bf16[8,112,128]{2,1,0:T(8,128)(2,1)} %get-tuple-element.17), calls=%async_computation.1 | async-start | bytes 458752 | tf_op jit(solution)/shard_map/all_to_all | solution.py:340
  82.9 5.7 %all-to-all-done.1.p0 = bf16[8,112,128]{2,1,0:T(8,128)(2,1)S(1)} async-done(((bf16[8,112,128]{2,1,0:T(8,128)(2,1)}), bf16[8,112,128]{2,1,0:T(8,128)(2,1)S(1)}, u32[]{:S(2)}, u32[]{:S(2)}) %all-to-all-start.1) | async-done | bytes 229408 | tf_op jit(solution)/shard_map/all_to_all | solution.py:340
  88.6 5.8 %shard_map.59.refs_4_ = f32[128,2048]{1,0:T(8,128)} custom-call(s32[6]{0:T(128)} %stack.125.who, bf16[8,128,384]{2,1,0:T(8,128)(2,1)} %get-tuple-element.18.states, bf16[384,2048]{1,0:T(8,128)(2,1)} %refs_0_.3, bf16[384,2048]{1,0:T(8,128)(2,1)} %collective-permute-done.7.refs_1_, bf16[384,1024]{1,0:T(8,128)(2,1)} %copy-done.1, bf16[384,1024]{1,0:T(8,128)(2,1)} %copy-done.2, ...), custom_call_target="tpu_custom_call" | custom-call | flops 805306368 | bytes 3145728 | tf_op jit(solution)/shard_map/pallas_call | solution.py:48
  94.4 4.7 %shard_map.60.near = f32[128,2048]{1,0:T(8,128)} custom-call(s32[4]{0:T(128)} %pad_add_fusion.2.who, bf16[8,128,384]{2,1,0:T(8,128)(2,1)} %get-tuple-element.18.states, bf16[384,1024]{1,0:T(8,128)(2,1)} %collective-permute-done.3.refs_0_.refs_4_, bf16[384,1024]{1,0:T(8,128)(2,1)} %collective-permute-done.4.refs_1_.refs_5_, ...), custom_call_target="tpu_custom_call" | custom-call | flops 402653184 | bytes 1572864 | tf_op jit(solution)/shard_map/pallas_call | solution.py:48
  99.2 5.3 %shard_map.61 = (bf16[128,2048]{1,0:T(8,128)(2,1)}, f32[32,3,128]{2,1,0:T(4,128)}, f32[1,128]{1,0:T(1,128)}) custom-call(s32[3]{0:T(128)} %pad_add_fusion.who, bf16[8,128,384]{2,1,0:T(8,128)(2,1)} %get-tuple-element.18.states, s32[128,1]{1,0:T(8,128)} %copy.6.labels, f32[128,2048]{1,0:T(8,128)} %shard_map.60.near, ...), custom_call_target="tpu_custom_call" | custom-call | flops 402653184 | bytes 1572864 | tf_op jit(solution)/shard_map/pallas_call | solution.py:48
  104.5 9.3 %all-to-all-start.2 = ((f32[32,3,128]{2,1,0:T(4,128)}), f32[32,3,128]{2,1,0:T(4,128)S(1)}, u32[]{:S(2)}, u32[]{:S(2)}) async-start(f32[32,3,128]{2,1,0:T(4,128)} %get-tuple-element.20), calls=%async_computation.2 | async-start | bytes 131072 | tf_op jit(solution)/shard_map/all_to_all | solution.py:364
  114.5 2.7 %collective-permute-start.19 = (bf16[8,112,128]{2,1,0:T(8,128)(2,1)S(1)}, bf16[8,112,128]{2,1,0:T(8,128)(2,1)}, u32[]{:S(2)}, u32[]{:S(2)}) collective-permute-start(bf16[8,112,128]{2,1,0:T(8,128)(2,1)S(1)} %all-to-all-done.1.p0), channel_id=1, source_target_pairs={{0,24},{8,0},{16,8},{24,16},{1,25},{9,1},{17,9},{25,17},{2,26},{10... | collective-permute-start | bytes 688136 | tf_op jit(solution)/shard_map/ppermute | solution.py:19
  117.9 2.6 %collective-permute-start.29 = (bf16[128,2048]{1,0:T(8,128)(2,1)}, bf16[128,2048]{1,0:T(8,128)(2,1)}, u32[]{:S(2)}, u32[]{:S(2)}) collective-permute-start(bf16[128,2048]{1,0:T(8,128)(2,1)} %get-tuple-element.19.powers.refs_4_), channel_id=1, source_target_pairs={{0,192},{64,0},{128,64},{192,128},{1,193},{65,1},{129,65},{193,129... | collective-permute-start | bytes 1572872 | tf_op jit(solution)/shard_map/ppermute | solution.py:19
  120.5 2.5 %all-to-all-done.2.parts = f32[32,3,128]{2,1,0:T(4,128)S(1)} async-done(((f32[32,3,128]{2,1,0:T(4,128)}), f32[32,3,128]{2,1,0:T(4,128)S(1)}, u32[]{:S(2)}, u32[]{:S(2)}) %all-to-all-start.2) | async-done | bytes 49184 | tf_op jit(solution)/shard_map/all_to_all | solution.py:364
  123.6 8.6 %shard_map.62 = (bf16[768,128]{1,0:T(8,128)(2,1)}, bf16[768,128]{1,0:T(8,128)(2,1)}, bf16[768,128]{1,0:T(8,128)(2,1)}, bf16[768,128]{1,0:T(8,128)(2,1)}, f32[1,128]{1,0:T(1,128)}, /*index=5*/f32[1,128]{1,0:T(1,128)}) custom-call(s32[9]{0:T(128)} %stack.109.starts, bf16[128,2048]{1,0:T(8,128)(2,1)} %get-tuple-element.19.powers.refs_4_, s32[1,128]{1,0:T(1,128)} %bitcast.30, ...), custom_call_target="tpu_custom_call" | custom-call | flops 1610612736 | bytes 6291456 | tf_op jit(solution)/shard_map/pallas_call | solution.py:48
  132.2 1.4 collective-permute-start.20
  135.7 6.6 %collective-permute-done.20.p2 = bf16[8,112,128]{2,1,0:T(8,128)(2,1)S(1)} collective-permute-done((bf16[8,112,128]{2,1,0:T(8,128)(2,1)S(1)}, bf16[8,112,128]{2,1,0:T(8,128)(2,1)S(1)}, u32[]{:S(2)}, u32[]{:S(2)}) %collective-permute-start.20) | collective-permute-done | bytes 229408 | tf_op jit(solution)/shard_map/ppermute | solution.py:19
  142.9 3.7 %collective-permute-done.21.p3 = bf16[8,112,128]{2,1,0:T(8,128)(2,1)S(1)} collective-permute-done((bf16[8,112,128]{2,1,0:T(8,128)(2,1)S(1)}, bf16[8,112,128]{2,1,0:T(8,128)(2,1)S(1)}, u32[]{:S(2)}, u32[]{:S(2)}) %collective-permute-start.21) | collective-permute-done | bytes 229408 | tf_op jit(solution)/shard_map/ppermute | solution.py:19
  146.7 1.3 collective-permute-start.17
  148.1 1.1 collective-permute-start.24
  149.3 1.5 collective-permute-start.25
  150.8 1.0 slice.17
  151.8 1.0 slice.18
  152.9 1.5 collective-permute-done.25.refs_3_
  154.4 0.9 collective-permute-start.31
  155.3 2.4 %collective-permute-start.33 = (bf16[128,1024]{1,0:T(8,128)(2,1)S(1)}, bf16[128,1024]{1,0:T(8,128)(2,1)S(1)}, u32[]{:S(2)}, u32[]{:S(2)}) collective-permute-start(bf16[128,1024]{1,0:T(8,128)(2,1)S(1)} %slice.18), channel_id=1, source_target_pairs={{0,192},{64,0},{128,64},{192,128},{1,193},{65,1},{129,65},{193,129... | collective-permute-start | bytes 786440 | tf_op jit(solution)/shard_map/ppermute | solution.py:19
  157.7 1.7 collective-permute-done.16
  159.4 1.7 add_convert_fusion
  161.2 4.8 %all-to-all-start.3 = ((bf16[8,96,128]{2,1,0:T(8,128)(2,1)}), bf16[8,96,128]{2,1,0:T(8,128)(2,1)S(1)}, u32[]{:S(2)}, u32[]{:S(2)}) async-start(bf16[8,96,128]{2,1,0:T(8,128)(2,1)} %bitcast.24), calls=%async_computation.3 | async-start | bytes 393216 | tf_op jit(solution)/shard_map/all_to_all | solution.py:378
  167.2 8.5 %all-to-all-done.3 = bf16[8,96,128]{2,1,0:T(8,128)(2,1)S(1)} async-done(((bf16[8,96,128]{2,1,0:T(8,128)(2,1)}), bf16[8,96,128]{2,1,0:T(8,128)(2,1)S(1)}, u32[]{:S(2)}, u32[]{:S(2)}) %all-to-all-start.3) | async-done | bytes 196640 | tf_op jit(solution)/shard_map/all_to_all | solution.py:378
  177.0 6.7 %shard_map.63 = f32[384,2048]{1,0:T(8,128)} custom-call(s32[10]{0:T(128)} %stack.126.who, bf16[8,112,128]{2,1,0:T(8,128)(2,1)} %copy-done.3, bf16[8,112,128]{2,1,0:T(8,128)(2,1)} %collective-permute-done.19.p1, bf16[8,112,128]{2,1,0:T(8,128)(2,1)} %copy-done.9, bf16[8,112,128]{2,1,0:T(8,128)(2,1)} %copy-done.10, f32[2,128]{1,0:T(2,128)} %copy-done.14, ...), custom_call_target="tpu_custom_call" | custom-call | flops 1610612736 | bytes 6291456 | tf_op jit(solution)/shard_map/pallas_call | solution.py:48
  (91 shorter events, 12.3 us)
Async XLA Ops:
  2.2 17.6 %all-to-all-start = ((bf16[8,96,128]{2,1,0:T(8,128)(2,1)}), bf16[8,96,128]{2,1,0:T(8,128)(2,1)S(1)}, u32[]{:S(2)}, u32[]{:S(2)}) async-start(bf16[8,96,128]{2,1,0:T(8,128)(2,1)} %broadcast_in_dim.12), calls=%async_computation | async-start | bytes 393216 | tf_op jit(solution)/shard_map/all_to_all | solution.py:27
  10.8 52.9 %copy-start.15 = (s32[128]{0:T(128)S(1)}, s32[128]{0:T(128)}, u32[]{:S(2)}) copy-start(s32[128]{0:T(128)} %param.5) | copy-start | bytes 1540
  10.8 51.5 %collective-permute-start.7 = (bf16[384,2048]{1,0:T(8,128)(2,1)}, bf16[384,2048]{1,0:T(8,128)(2,1)}, u32[]{:S(2)}, u32[]{:S(2)}) collective-permute-start(bf16[384,2048]{1,0:T(8,128)(2,1)} %refs_0_.3), channel_id=1, source_target_pairs={{0,32},{32,0},{1,33},{33,1},{2,34},{34,2},{3,35},{35,3},{4,36},{36... | collective-permute-start | bytes 4718600 | tf_op jit(solution)/shard_map/ppermute | solution.py:23
  12.8 29.2 %collective-permute-start.8 = (bf16[384,1024]{1,0:T(8,128)(2,1)}, bf16[384,1024]{1,0:T(8,128)(2,1)S(1)}, u32[]{:S(2)}, u32[]{:S(2)}) collective-permute-start(bf16[384,1024]{1,0:T(8,128)(2,1)} %slice.12), channel_id=1, source_target_pairs={{0,64},{64,128},{128,192},{192,0},{1,65},{65,129},{129,193},{193,1... | collective-permute-start | bytes 2359304 | tf_op jit(solution)/shard_map/ppermute | solution.py:19
  14.3 27.7 %collective-permute-start.3 = (bf16[384,1024]{1,0:T(8,128)(2,1)}, bf16[384,1024]{1,0:T(8,128)(2,1)}, u32[]{:S(2)}, u32[]{:S(2)}) collective-permute-start(bf16[384,1024]{1,0:T(8,128)(2,1)} %slice.12), channel_id=1, source_target_pairs={{0,192},{64,0},{128,64},{192,128},{1,193},{65,1},{129,65},{193,129... | collective-permute-start | bytes 2359304 | tf_op jit(solution)/shard_map/ppermute | solution.py:19
  16.1 35.0 %collective-permute-start.10 = (bf16[384,1024]{1,0:T(8,128)(2,1)S(1)}, bf16[384,1024]{1,0:T(8,128)(2,1)}, u32[]{:S(2)}, u32[]{:S(2)}) collective-permute-start(bf16[384,1024]{1,0:T(8,128)(2,1)S(1)} %slice.16), channel_id=1, source_target_pairs={{0,192},{64,0},{128,64},{192,128},{1,193},{65,1},{129,65},{193,129... | collective-permute-start | bytes 2359304 | tf_op jit(solution)/shard_map/ppermute | solution.py:19
  19.8 55.2 %copy-start.4 = (bf16[8,96,128]{2,1,0:T(8,128)(2,1)}, bf16[8,96,128]{2,1,0:T(8,128)(2,1)S(1)}, u32[]{:S(2)}) copy-start(bf16[8,96,128]{2,1,0:T(8,128)(2,1)S(1)} %all-to-all-done.p0) | copy-start | bytes 589828
  19.8 6.2 %collective-permute-start = (bf16[8,96,128]{2,1,0:T(8,128)(2,1)S(1)}, bf16[8,96,128]{2,1,0:T(8,128)(2,1)S(1)}, u32[]{:S(2)}, u32[]{:S(2)}) collective-permute-start(bf16[8,96,128]{2,1,0:T(8,128)(2,1)S(1)} %all-to-all-done.p0), channel_id=1, source_target_pairs={{0,24},{8,0},{16,8},{24,16},{1,25},{9,1},{17,9},{25,17},{2,26},{10... | collective-permute-start | bytes 589832 | tf_op jit(solution)/shard_map/ppermute | solution.py:19
  26.0 49.0 %copy-start.11 = (bf16[8,96,128]{2,1,0:T(8,128)(2,1)}, bf16[8,96,128]{2,1,0:T(8,128)(2,1)S(1)}, u32[]{:S(2)}) copy-start(bf16[8,96,128]{2,1,0:T(8,128)(2,1)S(1)} %collective-permute-done.p1) | copy-start | bytes 589828
  26.0 7.2 %collective-permute-start.1 = (bf16[8,96,128]{2,1,0:T(8,128)(2,1)S(1)}, bf16[8,96,128]{2,1,0:T(8,128)(2,1)S(1)}, u32[]{:S(2)}, u32[]{:S(2)}) collective-permute-start(bf16[8,96,128]{2,1,0:T(8,128)(2,1)S(1)} %all-to-all-done.p0), channel_id=1, source_target_pairs={{0,16},{8,24},{16,0},{24,8},{1,17},{9,25},{17,1},{25,9},{2,18},{10... | collective-permute-start | bytes 589832 | tf_op jit(solution)/shard_map/ppermute | solution.py:19
  33.2 40.1 %copy-start.12 = (bf16[8,96,128]{2,1,0:T(8,128)(2,1)}, bf16[8,96,128]{2,1,0:T(8,128)(2,1)S(1)}, u32[]{:S(2)}) copy-start(bf16[8,96,128]{2,1,0:T(8,128)(2,1)S(1)} %collective-permute-done.1.p2) | copy-start | bytes 589828
  33.2 7.3 %collective-permute-start.2 = (bf16[8,96,128]{2,1,0:T(8,128)(2,1)S(1)}, bf16[8,96,128]{2,1,0:T(8,128)(2,1)S(1)}, u32[]{:S(2)}, u32[]{:S(2)}) collective-permute-start(bf16[8,96,128]{2,1,0:T(8,128)(2,1)S(1)} %all-to-all-done.p0), channel_id=1, source_target_pairs={{0,8},{8,16},{16,24},{24,0},{1,9},{9,17},{17,25},{25,1},{2,10},{10... | collective-permute-start | bytes 589832 | tf_op jit(solution)/shard_map/ppermute | solution.py:19
  40.5 32.8 %copy-start.13 = (bf16[8,96,128]{2,1,0:T(8,128)(2,1)}, bf16[8,96,128]{2,1,0:T(8,128)(2,1)S(1)}, u32[]{:S(2)}) copy-start(bf16[8,96,128]{2,1,0:T(8,128)(2,1)S(1)} %collective-permute-done.2.p3) | copy-start | bytes 589828
  40.5 21.7 %collective-permute-start.5 = (bf16[384,1024]{1,0:T(8,128)(2,1)S(1)}, bf16[384,1024]{1,0:T(8,128)(2,1)}, u32[]{:S(2)}, u32[]{:S(2)}) collective-permute-start(bf16[384,1024]{1,0:T(8,128)(2,1)S(1)} %slice.16), channel_id=1, source_target_pairs={{0,64},{64,128},{128,192},{192,0},{1,65},{65,129},{129,193},{193,1... | collective-permute-start | bytes 2359304 | tf_op jit(solution)/shard_map/ppermute | solution.py:19
  42.0 20.7 %collective-permute-start.9 = (bf16[384,1024]{1,0:T(8,128)(2,1)S(1)}, bf16[384,1024]{1,0:T(8,128)(2,1)S(1)}, u32[]{:S(2)}, u32[]{:S(2)}) collective-permute-start(bf16[384,1024]{1,0:T(8,128)(2,1)S(1)} %collective-permute-done.8.refs_2_), channel_id=1, source_target_pairs={{0,32},{32,0},{1,33},{33,1},{2,34},{34,2},{3,35},{35,3},{4,36},{36... | collective-permute-start | bytes 2359304 | tf_op jit(solution)/shard_map/ppermute | solution.py:23
  42.9 30.4 %collective-permute-start.12 = (bf16[384,1024]{1,0:T(8,128)(2,1)S(1)}, bf16[384,1024]{1,0:T(8,128)(2,1)}, u32[]{:S(2)}, u32[]{:S(2)}) collective-permute-start(bf16[384,1024]{1,0:T(8,128)(2,1)S(1)} %collective-permute-done.8.refs_2_), channel_id=1, source_target_pairs={{0,64},{64,128},{128,192},{192,0},{1,65},{65,129},{129,193},{193,1... | collective-permute-start | bytes 2359304 | tf_op jit(solution)/shard_map/ppermute | solution.py:19
  51.2 22.1 %collective-permute-start.14 = (bf16[384,1024]{1,0:T(8,128)(2,1)}, bf16[384,1024]{1,0:T(8,128)(2,1)}, u32[]{:S(2)}, u32[]{:S(2)}) collective-permute-start(bf16[384,1024]{1,0:T(8,128)(2,1)} %collective-permute-done.10.refs_4_.refs_10_), channel_id=1, source_target_pairs={{0,192},{64,0},{128,64},{192,128},{1,193},{65,1},{129,65},{193,129... | collective-permute-start | bytes 2359304 | tf_op jit(solution)/shard_map/ppermute | solution.py:19
  62.2 26.4 %collective-permute-start.11 = (bf16[384,1024]{1,0:T(8,128)(2,1)}, bf16[384,1024]{1,0:T(8,128)(2,1)}, u32[]{:S(2)}, u32[]{:S(2)}) collective-permute-start(bf16[384,1024]{1,0:T(8,128)(2,1)} %collective-permute-done.10.refs_4_.refs_10_), channel_id=1, source_target_pairs={{0,32},{32,0},{1,33},{33,1},{2,34},{34,2},{3,35},{35,3},{4,36},{36... | collective-permute-start | bytes 2359304 | tf_op jit(solution)/shard_map/ppermute | solution.py:23
  62.2 32.2 %collective-permute-start.4 = (bf16[384,1024]{1,0:T(8,128)(2,1)}, bf16[384,1024]{1,0:T(8,128)(2,1)}, u32[]{:S(2)}, u32[]{:S(2)}) collective-permute-start(bf16[384,1024]{1,0:T(8,128)(2,1)} %collective-permute-done.3.refs_0_.refs_4_), channel_id=1, source_target_pairs={{0,32},{32,0},{1,33},{33,1},{2,34},{34,2},{3,35},{35,3},{4,36},{36... | collective-permute-start | bytes 2359304 | tf_op jit(solution)/shard_map/ppermute | solution.py:23
  63.7 30.7 %collective-permute-start.6 = (bf16[384,1024]{1,0:T(8,128)(2,1)}, bf16[384,1024]{1,0:T(8,128)(2,1)}, u32[]{:S(2)}, u32[]{:S(2)}) collective-permute-start(bf16[384,1024]{1,0:T(8,128)(2,1)} %collective-permute-done.5.refs_2_.refs_8_), channel_id=1, source_target_pairs={{0,32},{32,0},{1,33},{33,1},{2,34},{34,2},{3,35},{35,3},{4,36},{36... | collective-permute-start | bytes 2359304 | tf_op jit(solution)/shard_map/ppermute | solution.py:23
  73.3 25.9 %collective-permute-start.13 = (bf16[384,1024]{1,0:T(8,128)(2,1)}, bf16[384,1024]{1,0:T(8,128)(2,1)}, u32[]{:S(2)}, u32[]{:S(2)}) collective-permute-start(bf16[384,1024]{1,0:T(8,128)(2,1)} %collective-permute-done.12.left.refs_6_), channel_id=1, source_target_pairs={{0,32},{32,0},{1,33},{33,1},{2,34},{34,2},{3,35},{35,3},{4,36},{36... | collective-permute-start | bytes 2359304 | tf_op jit(solution)/shard_map/ppermute | solution.py:23
  73.3 25.9 %collective-permute-start.15 = (bf16[384,1024]{1,0:T(8,128)(2,1)}, bf16[384,1024]{1,0:T(8,128)(2,1)}, u32[]{:S(2)}, u32[]{:S(2)}) collective-permute-start(bf16[384,1024]{1,0:T(8,128)(2,1)} %collective-permute-done.14.right.refs_12_), channel_id=1, source_target_pairs={{0,32},{32,0},{1,33},{33,1},{2,34},{34,2},{3,35},{35,3},{4,36},{36... | collective-permute-start | bytes 2359304 | tf_op jit(solution)/shard_map/ppermute | solution.py:23
  78.1 10.5 %all-to-all-start.1 = ((bf16[8,112,128]{2,1,0:T(8,128)(2,1)}), bf16[8,112,128]{2,1,0:T(8,128)(2,1)S(1)}, u32[]{:S(2)}, u32[]{:S(2)}) async-start(bf16[8,112,128]{2,1,0:T(8,128)(2,1)} %get-tuple-element.17), calls=%async_computation.1 | async-start | bytes 458752 | tf_op jit(solution)/shard_map/all_to_all | solution.py:340
  88.6 45.0 %copy-start.3 = (bf16[8,112,128]{2,1,0:T(8,128)(2,1)}, bf16[8,112,128]{2,1,0:T(8,128)(2,1)S(1)}, u32[]{:S(2)}) copy-start(bf16[8,112,128]{2,1,0:T(8,128)(2,1)S(1)} %all-to-all-done.1.p0) | copy-start | bytes 688132
  104.5 18.5 %all-to-all-start.2 = ((f32[32,3,128]{2,1,0:T(4,128)}), f32[32,3,128]{2,1,0:T(4,128)S(1)}, u32[]{:S(2)}, u32[]{:S(2)}) async-start(f32[32,3,128]{2,1,0:T(4,128)} %get-tuple-element.20), calls=%async_computation.2 | async-start | bytes 131072 | tf_op jit(solution)/shard_map/all_to_all | solution.py:364
  114.5 20.5 %collective-permute-start.19 = (bf16[8,112,128]{2,1,0:T(8,128)(2,1)S(1)}, bf16[8,112,128]{2,1,0:T(8,128)(2,1)}, u32[]{:S(2)}, u32[]{:S(2)}) collective-permute-start(bf16[8,112,128]{2,1,0:T(8,128)(2,1)S(1)} %all-to-all-done.1.p0), channel_id=1, source_target_pairs={{0,24},{8,0},{16,8},{24,16},{1,25},{9,1},{17,9},{25,17},{2,26},{10... | collective-permute-start | bytes 688136 | tf_op jit(solution)/shard_map/ppermute | solution.py:19
  117.3 30.9 %collective-permute-start.27 = (bf16[128,2048]{1,0:T(8,128)(2,1)}, bf16[128,2048]{1,0:T(8,128)(2,1)}, u32[]{:S(2)}, u32[]{:S(2)}) collective-permute-start(bf16[128,2048]{1,0:T(8,128)(2,1)} %get-tuple-element.19.powers.refs_4_), channel_id=1, source_target_pairs={{0,64},{64,128},{128,192},{192,0},{1,65},{65,129},{129,193},{193,1... | collective-permute-start | bytes 1572872 | tf_op jit(solution)/shard_map/ppermute | solution.py:19
  117.9 31.4 %collective-permute-start.29 = (bf16[128,2048]{1,0:T(8,128)(2,1)}, bf16[128,2048]{1,0:T(8,128)(2,1)}, u32[]{:S(2)}, u32[]{:S(2)}) collective-permute-start(bf16[128,2048]{1,0:T(8,128)(2,1)} %get-tuple-element.19.powers.refs_4_), channel_id=1, source_target_pairs={{0,192},{64,0},{128,64},{192,128},{1,193},{65,1},{129,65},{193,129... | collective-permute-start | bytes 1572872 | tf_op jit(solution)/shard_map/ppermute | solution.py:19
  132.1 1.5 collective-permute-start.22
  132.2 10.1 %collective-permute-start.20 = (bf16[8,112,128]{2,1,0:T(8,128)(2,1)S(1)}, bf16[8,112,128]{2,1,0:T(8,128)(2,1)S(1)}, u32[]{:S(2)}, u32[]{:S(2)}) collective-permute-start(bf16[8,112,128]{2,1,0:T(8,128)(2,1)S(1)} %all-to-all-done.1.p0), channel_id=1, source_target_pairs={{0,16},{8,24},{16,0},{24,8},{1,17},{9,25},{17,1},{25,9},{2,18},{10... | collective-permute-start | bytes 688136 | tf_op jit(solution)/shard_map/ppermute | solution.py:19
  133.7 13.0 %collective-permute-start.21 = (bf16[8,112,128]{2,1,0:T(8,128)(2,1)S(1)}, bf16[8,112,128]{2,1,0:T(8,128)(2,1)S(1)}, u32[]{:S(2)}, u32[]{:S(2)}) collective-permute-start(bf16[8,112,128]{2,1,0:T(8,128)(2,1)S(1)} %all-to-all-done.1.p0), channel_id=1, source_target_pairs={{0,8},{8,16},{16,24},{24,0},{1,9},{9,17},{17,25},{25,1},{2,10},{10... | collective-permute-start | bytes 688136 | tf_op jit(solution)/shard_map/ppermute | solution.py:19
  135.0 42.0 %copy-start.14 = (f32[2,128]{1,0:T(2,128)}, f32[2,128]{1,0:T(2,128)S(1)}, u32[]{:S(2)}) copy-start(f32[2,128]{1,0:T(2,128)S(1)} %pad_maximum_fusion.refs_0_) | copy-start | bytes 3076
  135.0 13.0 %collective-permute-start.23 = (f32[2,128]{1,0:T(2,128)S(1)}, f32[2,128]{1,0:T(2,128)S(1)}, u32[]{:S(2)}, u32[]{:S(2)}) collective-permute-start(f32[2,128]{1,0:T(2,128)S(1)} %pad_maximum_fusion.refs_0_), channel_id=1, source_target_pairs={{0,64},{64,128},{128,192},{192,0},{1,65},{65,129},{129,193},{193,1... | collective-permute-start | bytes 3080 | tf_op jit(solution)/shard_map/ppermute | solution.py:19
  142.3 12.9 %collective-permute-start.18 = (bf16[768,128]{1,0:T(8,128)(2,1)}, bf16[768,128]{1,0:T(8,128)(2,1)S(1)}, u32[]{:S(2)}, u32[]{:S(2)}) collective-permute-start(bf16[768,128]{1,0:T(8,128)(2,1)} %get-tuple-element.26), channel_id=1, source_target_pairs={{0,24},{8,0},{16,8},{24,16},{1,25},{9,1},{17,9},{25,17},{2,26},{10... | collective-permute-start | bytes 589832 | tf_op jit(solution)/shard_map/ppermute | solution.py:19
  146.7 10.9 %collective-permute-start.17 = (bf16[768,128]{1,0:T(8,128)(2,1)}, bf16[768,128]{1,0:T(8,128)(2,1)S(1)}, u32[]{:S(2)}, u32[]{:S(2)}) collective-permute-start(bf16[768,128]{1,0:T(8,128)(2,1)} %get-tuple-element.25), channel_id=1, source_target_pairs={{0,16},{8,24},{16,0},{24,8},{1,17},{9,25},{17,1},{25,9},{2,18},{10... | collective-permute-start | bytes 589832 | tf_op jit(solution)/shard_map/ppermute | solution.py:19
  148.0 29.0 %copy-start.16 = (f32[2,128]{1,0:T(2,128)}, f32[2,128]{1,0:T(2,128)S(1)}, u32[]{:S(2)}) copy-start(f32[2,128]{1,0:T(2,128)S(1)} %collective-permute-done.23.refs_1_) | copy-start | bytes 3076
  148.0 11.4 %collective-permute-start.16 = (bf16[768,128]{1,0:T(8,128)(2,1)}, bf16[768,128]{1,0:T(8,128)(2,1)S(1)}, u32[]{:S(2)}, u32[]{:S(2)}) collective-permute-start(bf16[768,128]{1,0:T(8,128)(2,1)} %get-tuple-element.24), channel_id=1, source_target_pairs={{0,8},{8,16},{16,24},{24,0},{1,9},{9,17},{17,25},{25,1},{2,10},{10... | collective-permute-start | bytes 589832 | tf_op jit(solution)/shard_map/ppermute | solution.py:19
  148.1 4.6 %collective-permute-start.24 = (f32[2,128]{1,0:T(2,128)S(1)}, f32[2,128]{1,0:T(2,128)S(1)}, u32[]{:S(2)}, u32[]{:S(2)}) collective-permute-start(f32[2,128]{1,0:T(2,128)S(1)} %pad_maximum_fusion.refs_0_), channel_id=1, source_target_pairs={{0,192},{64,0},{128,64},{192,128},{1,193},{65,1},{129,65},{193,129... | collective-permute-start | bytes 3080 | tf_op jit(solution)/shard_map/ppermute | solution.py:19
  149.3 5.1 %collective-permute-start.25 = (f32[2,128]{1,0:T(2,128)S(1)}, f32[2,128]{1,0:T(2,128)S(1)}, u32[]{:S(2)}, u32[]{:S(2)}) collective-permute-start(f32[2,128]{1,0:T(2,128)S(1)} %pad_maximum_fusion.refs_0_), channel_id=1, source_target_pairs={{0,128},{64,192},{128,0},{192,64},{1,129},{65,193},{129,1},{193,65... | collective-permute-start | bytes 3080 | tf_op jit(solution)/shard_map/ppermute | solution.py:19
  152.8 24.2 %copy-start.17 = (f32[2,128]{1,0:T(2,128)}, f32[2,128]{1,0:T(2,128)S(1)}, u32[]{:S(2)}) copy-start(f32[2,128]{1,0:T(2,128)S(1)} %collective-permute-done.24.refs_2_) | copy-start | bytes 3076
  152.8 23.5 %collective-permute-start.26 = (bf16[128,2048]{1,0:T(8,128)(2,1)}, bf16[128,2048]{1,0:T(8,128)(2,1)}, u32[]{:S(2)}, u32[]{:S(2)}) collective-permute-start(bf16[128,2048]{1,0:T(8,128)(2,1)} %get-tuple-element.19.powers.refs_4_), channel_id=1, source_target_pairs={{0,32},{32,0},{1,33},{33,1},{2,34},{34,2},{3,35},{35,3},{4,36},{36... | collective-permute-start | bytes 1572872 | tf_op jit(solution)/shard_map/ppermute | solution.py:23
  154.4 11.6 %collective-permute-start.31 = (bf16[128,1024]{1,0:T(8,128)(2,1)S(1)}, bf16[128,1024]{1,0:T(8,128)(2,1)S(1)}, u32[]{:S(2)}, u32[]{:S(2)}) collective-permute-start(bf16[128,1024]{1,0:T(8,128)(2,1)S(1)} %slice.17), channel_id=1, source_target_pairs={{0,64},{64,128},{128,192},{192,0},{1,65},{65,129},{129,193},{193,1... | collective-permute-start | bytes 786440 | tf_op jit(solution)/shard_map/ppermute | solution.py:19
  155.3 10.8 %collective-permute-start.33 = (bf16[128,1024]{1,0:T(8,128)(2,1)S(1)}, bf16[128,1024]{1,0:T(8,128)(2,1)S(1)}, u32[]{:S(2)}, u32[]{:S(2)}) collective-permute-start(bf16[128,1024]{1,0:T(8,128)(2,1)S(1)} %slice.18), channel_id=1, source_target_pairs={{0,192},{64,0},{128,64},{192,128},{1,193},{65,1},{129,65},{193,129... | collective-permute-start | bytes 786440 | tf_op jit(solution)/shard_map/ppermute | solution.py:19
  157.6 18.6 %collective-permute-start.28 = (bf16[128,2048]{1,0:T(8,128)(2,1)}, bf16[128,2048]{1,0:T(8,128)(2,1)}, u32[]{:S(2)}, u32[]{:S(2)}) collective-permute-start(bf16[128,2048]{1,0:T(8,128)(2,1)} %collective-permute-done.27.refs_6_), channel_id=1, source_target_pairs={{0,32},{32,0},{1,33},{33,1},{2,34},{34,2},{3,35},{35,3},{4,36},{36... | collective-permute-start | bytes 1572872 | tf_op jit(solution)/shard_map/ppermute | solution.py:23
  159.4 16.8 %collective-permute-start.30 = (bf16[128,2048]{1,0:T(8,128)(2,1)}, bf16[128,2048]{1,0:T(8,128)(2,1)}, u32[]{:S(2)}, u32[]{:S(2)}) collective-permute-start(bf16[128,2048]{1,0:T(8,128)(2,1)} %collective-permute-done.29.refs_8_), channel_id=1, source_target_pairs={{0,32},{32,0},{1,33},{33,1},{2,34},{34,2},{3,35},{35,3},{4,36},{36... | collective-permute-start | bytes 1572872 | tf_op jit(solution)/shard_map/ppermute | solution.py:23
  161.2 14.4 %all-to-all-start.3 = ((bf16[8,96,128]{2,1,0:T(8,128)(2,1)}), bf16[8,96,128]{2,1,0:T(8,128)(2,1)S(1)}, u32[]{:S(2)}, u32[]{:S(2)}) async-start(bf16[8,96,128]{2,1,0:T(8,128)(2,1)} %bitcast.24), calls=%async_computation.3 | async-start | bytes 393216 | tf_op jit(solution)/shard_map/all_to_all | solution.py:378
  165.9 10.3 %collective-permute-start.32 = (bf16[128,1024]{1,0:T(8,128)(2,1)S(1)}, bf16[128,1024]{1,0:T(8,128)(2,1)S(1)}, u32[]{:S(2)}, u32[]{:S(2)}) collective-permute-start(bf16[128,1024]{1,0:T(8,128)(2,1)S(1)} %collective-permute-done.31.refs_10_), channel_id=1, source_target_pairs={{0,32},{32,0},{1,33},{33,1},{2,34},{34,2},{3,35},{35,3},{4,36},{36... | collective-permute-start | bytes 786440 | tf_op jit(solution)/shard_map/ppermute | solution.py:23
  166.1 10.9 %collective-permute-start.34 = (bf16[128,1024]{1,0:T(8,128)(2,1)S(1)}, bf16[128,1024]{1,0:T(8,128)(2,1)}, u32[]{:S(2)}, u32[]{:S(2)}) collective-permute-start(bf16[128,1024]{1,0:T(8,128)(2,1)S(1)} %collective-permute-done.33.refs_12_), channel_id=1, source_target_pairs={{0,32},{32,0},{1,33},{33,1},{2,34},{34,2},{3,35},{35,3},{4,36},{36... | collective-permute-start | bytes 786440 | tf_op jit(solution)/shard_map/ppermute | solution.py:23
  (10 other events, 88.7 us)

commit v6 on v5

--- a/solution.py
+++ b/solution.py
@@ -44,7 +44,7 @@
     return jnp.maximum(j - STEPS // 2, 0)
 
 
-def call(kernel, scalars, args, in_specs, out_specs, out_shape, flops, scratch=(), steps=STEPS, room=ROOM):
+def call(kernel, scalars, args, in_specs, out_specs, out_shape, flops, scratch=(), steps=STEPS, room=None):
     return pl.pallas_call(
         kernel,
         grid_spec=pltpu.PrefetchScalarGridSpec(
@@ -130,23 +130,37 @@
 
 
 def far_kernel(who, states, labels, near, left, left_other, right, right_other, powers, stats, peaks, logits, rows, few, sems):
+    depth = states.shape[2]
+    wide = rows.shape[2]
+    per = left.shape[1] // wide
     copies = [
-        pltpu.make_async_copy(states.at[who[0]], few.at[0], sems.at[0]),
-        pltpu.make_async_copy(states.at[who[1]], few.at[1], sems.at[1]),
-        pltpu.make_async_copy(left, rows.at[0], sems.at[2]),
-        pltpu.make_async_copy(left_other, rows.at[1], sems.at[3]),
-        pltpu.make_async_copy(near, logits, sems.at[4]),
-        pltpu.make_async_copy(right, rows.at[2], sems.at[5]),
-        pltpu.make_async_copy(right_other, rows.at[3], sems.at[6]),
+        pltpu.make_async_copy(states.at[who[k]], few.at[:, k * depth : (k + 1) * depth], sems.at[k])
+        for k in (0, 1)
     ]
+    ready = []
+    for q in range(2 * per):
+        mine, theirs = ((left, left_other), (right, right_other))[q // per]
+        at = slice((q % per) * wide, (q % per + 1) * wide)
+        ready.append(
+            [
+                pltpu.make_async_copy(mine.at[:, at], rows.at[q, :depth], sems.at[2 + 3 * q]),
+                pltpu.make_async_copy(theirs.at[:, at], rows.at[q, depth:], sems.at[3 + 3 * q]),
+                pltpu.make_async_copy(
+                    near.at[:, q * wide : (q + 1) * wide],
+                    logits.at[:, q * wide : (q + 1) * wide],
+                    sems.at[4 + 3 * q],
+                ),
+            ]
+        )
+        copies += ready[-1]
     for copy in copies:
         copy.start()
-    half = rows.shape[2]
-    for side, ready in ((0, copies[:5]), (1, copies[5:])):
-        for copy in ready:
+    for copy in copies[:2]:
+        copy.wait()
+    for q in range(2 * per):
+        for copy in ready[q]:
             copy.wait()
-        at = slice(side * half, (side + 1) * half)
-        logits[:, at] += dot(few[0], rows[2 * side]) + dot(few[1], rows[2 * side + 1])
+        logits[:, q * wide : (q + 1) * wide] += dot(few[...], rows[q])
     values = logits[...]
     peak = jnp.max(values, axis=1, keepdims=True)
     shifted = jnp.exp(values - peak)
@@ -156,20 +170,20 @@
     target = jnp.sum(jnp.where(hits, values, 0.0), axis=1, keepdims=True)
     powers[...] = shifted.astype(BF)
     lanes = lax.broadcasted_iota(jnp.int32, (values.shape[0], 128), 1)
-    both = jnp.where(lanes == 0, peak, jnp.where(lanes == 1, total, target))
-    lines = both.T
+    lines = jnp.where(lanes == 0, peak, jnp.where(lanes == 1, total, target)).T
     stats[...] = jnp.broadcast_to(lines[None, :3], stats.shape)
     peaks[...] = lines[:1]
 
 
-def far_logits(states, labels, near, left, right, who):
+def far_logits(states, labels, near, left, right, who, wide=512):
     tokens, width = near.shape
-    rows, half = left[0].shape
+    rows, _ = left[0].shape
     args = [states, labels, near, *left, *right]
     far = pl.BlockSpec(memory_space=pltpu.HBM)
     powers = jax.ShapeDtypeStruct((tokens, width), BF)
     stats = jax.ShapeDtypeStruct((NY * NZ, 3, tokens), F32)
     peaks = jax.ShapeDtypeStruct((1, tokens), F32)
+    count = width // wide
     return call(
         far_kernel,
         who,
@@ -180,9 +194,9 @@
         4 * tokens * rows * width,
         [
             pltpu.VMEM((tokens, width), F32),
-            pltpu.VMEM((4, rows, half), BF),
-            pltpu.VMEM((2, tokens, rows), BF),
-            pltpu.SemaphoreType.DMA((7,)),
+            pltpu.VMEM((count, 2 * rows, wide), BF),
+            pltpu.VMEM((tokens, 2 * rows), BF),
+            pltpu.SemaphoreType.DMA((2 + 3 * count,)),
         ],
         steps=1,
         room=ROOM,
@@ -190,57 +204,72 @@
 
 
 def terms_kernel(starts, powers, labels, parts, peaks, *refs):
-    *arrays, out0, out1, out2, out3, scales, losses, errors, out = refs
-    step = pl.program_id(0)
+    arrays, (out, scales, losses, errors, full, cut, pieces, sems, done) = refs[:14], refs[14:]
     width, tokens = errors.shape
-
-    @pl.when(step == 0)
-    def _():
-        theirs = parts[:, 0, :]
-        peak = jnp.max(theirs, axis=0, keepdims=True)
-        total = jnp.sum(parts[:, 1, :] * jnp.exp(theirs - peak), axis=0, keepdims=True)
-        target = jnp.sum(parts[:, 2, :], axis=0, keepdims=True)
-        scale = jnp.exp(peaks[...] - peak) / total
-        loss = jnp.log(total) + peak - target
-        scales[...] = scale
-        losses[...] = loss
-        columns = starts[8] + lax.broadcasted_iota(jnp.int32, (width, tokens), 0)
-        hit = jnp.where(columns == labels[...], 1.0, 0.0)
-        errors[...] = (powers[...].T.astype(F32) * scale - hit).astype(BF)
-
     half = width // 2
-    own, left, right = arrays[:2], arrays[2:8], arrays[8:]
-    lefts = jnp.concatenate([a[:, :half] for a in own] + [a[...] for a in left], axis=0)
-    rights = jnp.concatenate([a[:, half:] for a in own] + [a[...] for a in right], axis=0)
-    term = dot(lefts, errors[:half, :]) + dot(rights, errors[half:, :])
-    rows = own[0].shape[0]
+    rows = cut.shape[1]
+
+    loads = [[pltpu.make_async_copy(arrays[k], full.at[k], sems.at[k])] for k in range(2)]
+    loads += [
+        [pltpu.make_async_copy(arrays[j + k], cut.at[j - 2 + k], sems.at[j + k]) for j in (2, 8)]
+        for k in range(6)
+    ]
+    for load in loads:
+        for copy in load:
+            copy.start()
+
+    theirs = parts[:, 0, :]
+    peak = jnp.max(theirs, axis=0, keepdims=True)
+    total = jnp.sum(parts[:, 1, :] * jnp.exp(theirs - peak), axis=0, keepdims=True)
+    target = jnp.sum(parts[:, 2, :], axis=0, keepdims=True)
+    scale = jnp.exp(peaks[...] - peak) / total
+    scales[...] = scale
+    losses[...] = jnp.log(total) + peak - target
+    columns = starts[8] + lax.broadcasted_iota(jnp.int32, (width, tokens), 0)
+    hit = jnp.where(columns == labels[...], 1.0, 0.0)
+    errors[...] = (powers[...].T.astype(F32) * scale - hit).astype(BF)
+
+    stores = []
     for k in range(8):
-        at = pl.ds(pl.multiple_of(starts[k] + step * rows, 32), rows)
-        out[at, :] = term[k * rows : (k + 1) * rows].astype(BF)
-
-    @pl.when(step == STEPS - 1)
-    def _():
-        for j, ref in enumerate((out0, out1, out2, out3)):
-            ref[...] = out[pl.ds(j * ref.shape[0], ref.shape[0]), :]
+        for copy in loads[k]:
+            copy.wait()
+        if k < 2:
+            term = dot(full[k], errors[...])
+        else:
+            term = dot(cut[k - 2], errors[:half, :]) + dot(cut[k + 4], errors[half:, :])
+        pieces[k] = term.astype(BF)
+        at = pl.ds(pl.multiple_of(starts[k], rows), rows)
+        stores.append(pltpu.make_async_copy(pieces.at[k], out.at[at], done.at[k]))
+        stores[-1].start()
+    for copy in stores:
+        copy.wait()
 
 
 def state_terms(powers, labels, parts, peaks, own, left, right, starts, depth):
     tokens, width = powers.shape
-    rows = own[0].shape[0] // STEPS
+    rows = own[0].shape[0]
     args = [powers, labels, parts, peaks, *own, *left, *right]
-    specs = [whole(a) for a in args[:4]]
-    specs += [pl.BlockSpec((rows, a.shape[1]), lambda j, s: (j, 0)) for a in args[4:]]
-    terms = jax.ShapeDtypeStruct((depth // NY, tokens), BF)
+    away = pl.BlockSpec(memory_space=pltpu.HBM)
+    terms = jax.ShapeDtypeStruct((depth, tokens), BF)
     line = jax.ShapeDtypeStruct((1, tokens), F32)
     return call(
         terms_kernel,
         starts,
         args,
-        specs,
-        [whole(terms)] * NY + [whole(line)] * 2,
-        [terms] * NY + [line] * 2,
+        [whole(a) for a in args[:4]] + [away] * 14,
+        [away, whole(line), whole(line)],
+        [terms, line, line],
         2 * tokens * width * depth,
-        [pltpu.VMEM((width, tokens), BF), pltpu.VMEM((depth, tokens), BF)],
+        [
+            pltpu.VMEM((width, tokens), BF),
+            pltpu.VMEM((2, rows, width), BF),
+            pltpu.VMEM((12, rows, width // 2), BF),
+            pltpu.VMEM((8, rows, tokens), BF),
+            pltpu.SemaphoreType.DMA((14,)),
+            pltpu.SemaphoreType.DMA((8,)),
+        ],
+        steps=1,
+        room=ROOM,
     )
 
 
@@ -267,9 +296,7 @@
 
     columns = who[8] + step * wide + lax.broadcasted_iota(jnp.int32, (tokens, wide), 1)
     columns = columns.astype(F32)
-    blocks = [a[...] for a in arrays[:6]]
-    first = step < STEPS // 2
-    blocks += [jnp.where(first, arrays[6 + k][...], arrays[8 + k][...]) for k in range(2)]
+    blocks = [a[...] for a in arrays]
     acc = None
     for pair in range(4):
         left, right = [], []
@@ -282,16 +309,14 @@
     out[...] = acc
 
 
-def head_grad_of(parts, scales, near, left, right, who):
+def head_grad_of(parts, scales, blocks, who):
     groups, padded, tokens = parts[0].shape
     rows = NY * (padded - 16)
-    width = near[0].shape[1]
+    width = blocks[0].shape[1]
     wide = width // STEPS
-    args = [*parts, *scales, *near, *left, *right]
+    args = [*parts, *scales, *blocks]
     specs = [whole(a) for a in args[:8]]
-    specs += [pl.BlockSpec((tokens, wide), lambda j, s: (0, j))] * 6
-    specs += [pl.BlockSpec((tokens, wide), lambda j, s: (0, early(j)))] * 2
-    specs += [pl.BlockSpec((tokens, wide), lambda j, s: (0, late(j)))] * 2
+    specs += [pl.BlockSpec((tokens, wide), lambda j, s: (0, j))] * 8
     return call(
         grad_kernel,
         who,
@@ -355,39 +380,29 @@
 
     pow_up = shift(powers, "x", NX, 1)
     pow_down = shift(powers, "x", NX, -1)
-    pow_left = shift(pow_up[:, :half], "x", NX, 1)
-    pow_right = shift(pow_down[:, half:], "x", NX, -1)
-    pow_near = [powers, swap(powers), pow_up, swap(pow_up), pow_down, swap(pow_down)]
-    pow_left = [pow_left, swap(pow_left)]
-    pow_right = [pow_right, swap(pow_right)]
+    pow_far = shift(powers, "x", NX, 2)
+    pow_own = swap(powers)
+    blocks = [powers, pow_own]
+    for block in (pow_up, pow_down, pow_far):
+        blocks += [block, swap(block)]
 
     parts = lax.all_to_all(stats, ("y", "z"), 0, 0, tiled=True)
-    starts = []
-    for offset in (0, 3, 1, 2):
-        chip = ((x + offset - y) % NY) * 2
-        starts += [(chip + core) * rows, (chip + 1 - core) * rows]
+    starts = [w * rows for w in who(0) + who(3) + who(1) + who(2)]
     all_left = [up_left, up_left_other, *left, *away_left]
     all_right = [*right, down_right, down_right_other, *away_right]
-    *terms, scale, token_loss = state_terms(
+    terms, scale, token_loss = state_terms(
         powers, labels[None], parts, peaks, own, all_left, all_right, starts + [base], depth
     )
     token_loss = token_loss.reshape(tokens)
 
-    arrived = [terms[0]] + [shift(terms[j], "y", NY, j) for j in (1, 2, 3)]
-    row_sum = sum(a.astype(F32) for a in arrived).astype(BF)
-    arrived = lax.all_to_all(row_sum.reshape(NZ, part, tokens), "z", 0, 0, tiled=True)
+    arrived = lax.all_to_all(
+        terms.reshape(NY * NZ, part, tokens), ("y", "z"), 0, 0, tiled=True
+    )
     state_grad = arrived.astype(F32).sum(axis=0).astype(BF).T
 
     pair = jnp.concatenate([scale, swap(scale)])
     scales = [pair] + [shift(pair, "x", NX, s) for s in (1, -1, 2)]
-    head_grad = head_grad_of(
-        slices,
-        scales,
-        pow_near,
-        pow_left,
-        pow_right,
-        who(0) + who(3) + who(1) + who(2) + [base, y],
-    )
+    head_grad = head_grad_of(slices, scales, blocks, who(0) + who(3) + who(1) + who(2) + [base, y])
     return (token_loss, state_grad, head_grad)
 
 

time: 187 us -> 207 us (1.11); the launches traced: 184 us -> 206 us
  waiting for transfers between devices: 69.4 us -> 97.4 us
  starting transfers between devices: 62.4 us -> 56.1 us
  Pallas kernels: 34.2 us -> 37.4 us
  other arithmetic: 5.38 us -> 3.11 us
    ppermute x22 -> x18, waiting for transfers between devices: 50.8 us -> 82.8 us  [shift(): return lax.ppermute(a, axis, [(i, (i + s) % n) for i in range(n)])]
    all_to_all x1, waiting for transfers between devices: 8.45 us -> 0.01 us  [step(): lax.all_to_all(terms.reshape(NY * NZ, part, tokens), ('y', 'z'), 0, 0, ti...]
    ppermute x22 -> x18, starting transfers between devices: 34.2 us -> 27.2 us  [shift(): return lax.ppermute(a, axis, [(i, (i + s) % n) for i in range(n)])]
    all_to_all x1, waiting for transfers between devices: 2.46 us -> 8.45 us  [step(): parts = lax.all_to_all(stats, ('y', 'z'), 0, 0, tiled=True)]
    pallas_call x6, Pallas kernels: 34.2 us -> 37.4 us  [call(): pl.pallas_call(kernel, grid_spec=pltpu.PrefetchScalarGridSpec(num_scalar_...]
  transfers between devices with their start and end apart: 39 -> 34, of which waited for: 14 -> 16; matrix products, arithmetic and copies ran while one was open for 7% -> 4% of each run, Pallas kernels for 12% -> 10%
where the time goes in v6:
time: 207 us; the launch traced here: 206 us
  waiting for transfers between devices  97.4 us (47%)
  starting transfers between devices  56.1 us (27%)
  Pallas kernels  37.4 us (18%)
  local copies, waits for them, and re-layouts  10.9 us (5%)
  other arithmetic  3.11 us (2%)
    ppermute x18, waiting for transfers between devices, shift(): return lax.ppermute(a, axis, [(i, (i + s) % n) for i in range(n)])  82.8 us
    pallas_call x6, Pallas kernels, call(): pl.pallas_call(kernel, grid_spec=pltpu.PrefetchScalarGridSpec(num_scalar_...  37.4 us
    ppermute x18, starting transfers between devices, shift(): return lax.ppermute(a, axis, [(i, (i + s) % n) for i in range(n)])  27.2 us
    all_to_all x1, starting transfers between devices, step(): parts = lax.all_to_all(stats, ('y', 'z'), 0, 0, tiled=True)  10 us
    all_to_all x1, starting transfers between devices, from_everyone(): lax.all_to_all(jnp.broadcast_to(a[None], (n, *a.shape)), axis, 0, 0, tile...  8.57 us
    all_to_all x1, waiting for transfers between devices, step(): parts = lax.all_to_all(stats, ('y', 'z'), 0, 0, tiled=True)  8.45 us
    all_to_all x1, waiting for transfers between devices, step(): wanted = lax.all_to_all(wanted, ('x', 'core'), 0, 0, tiled=True)  5.72 us
    all_to_all x1, starting transfers between devices, step(): lax.all_to_all(terms.reshape(NY * NZ, part, tokens), ('y', 'z'), 0, 0, ti...  4.85 us
  transfers between devices with their start and end apart: 34, of which 16 were waited for; matrix products, arithmetic and copies ran while one was open for 4% of the time, Pallas kernels for 10%

profile of v6, /device:TPU:32, one launch (start us, length us, event | category | flops | bytes accessed | tf_op | source)
XLA Modules:
  0.0 205.9 jit_solution(12472742197459861965)
XLA Ops:
  0.6 1.5 broadcast_in_dim.12
  2.2 8.6 %all-to-all-start = ((bf16[8,96,128]{2,1,0:T(8,128)(2,1)}), bf16[8,96,128]{2,1,0:T(8,128)(2,1)S(1)}, u32[]{:S(2)}, u32[]{:S(2)}) async-start(bf16[8,96,128]{2,1,0:T(8,128)(2,1)} %broadcast_in_dim.12), calls=%async_computation | async-start | bytes 393216 | tf_op jit(solution)/shard_map/all_to_all | solution.py:27
  10.8 2.1 %slice.8 = bf16[384,1024]{1,0:T(8,128)(2,1)} slice(bf16[384,2048]{1,0:T(8,128)(2,1)} %refs_0_.3), slice={[0:384], [1024:2048]} | slice | bytes 1572864 | tf_op jit(solution)/shard_map/slice | solution.py:346
  12.9 2.8 %collective-permute-start.10 = (bf16[384,1024]{1,0:T(8,128)(2,1)}, bf16[384,1024]{1,0:T(8,128)(2,1)}, u32[]{:S(2)}, u32[]{:S(2)}) collective-permute-start(bf16[384,1024]{1,0:T(8,128)(2,1)} %slice.8), channel_id=1, source_target_pairs={{0,192},{64,0},{128,64},{192,128},{1,193},{65,1},{129,65},{193,129... | collective-permute-start | bytes 2359304 | tf_op jit(solution)/shard_map/ppermute | solution.py:19
  15.6 1.0 slice.6
  16.6 3.2 %collective-permute-start.3 = (bf16[384,1024]{1,0:T(8,128)(2,1)}, bf16[384,1024]{1,0:T(8,128)(2,1)}, u32[]{:S(2)}, u32[]{:S(2)}) collective-permute-start(bf16[384,1024]{1,0:T(8,128)(2,1)} %slice.6), channel_id=1, source_target_pairs={{0,192},{64,0},{128,64},{192,128},{1,193},{65,1},{129,65},{193,129... | collective-permute-start | bytes 2359304 | tf_op jit(solution)/shard_map/ppermute | solution.py:19
  19.8 3.1 %collective-permute-start = (bf16[8,96,128]{2,1,0:T(8,128)(2,1)S(1)}, bf16[8,96,128]{2,1,0:T(8,128)(2,1)S(1)}, u32[]{:S(2)}, u32[]{:S(2)}) collective-permute-start(bf16[8,96,128]{2,1,0:T(8,128)(2,1)S(1)} %all-to-all-done.p0), channel_id=1, source_target_pairs={{0,24},{8,0},{16,8},{24,16},{1,25},{9,1},{17,9},{25,17},{2,26},{10... | collective-permute-start | bytes 589832 | tf_op jit(solution)/shard_map/ppermute | solution.py:19
  22.9 3.2 %collective-permute-done.p1 = bf16[8,96,128]{2,1,0:T(8,128)(2,1)S(1)} collective-permute-done((bf16[8,96,128]{2,1,0:T(8,128)(2,1)S(1)}, bf16[8,96,128]{2,1,0:T(8,128)(2,1)S(1)}, u32[]{:S(2)}, u32[]{:S(2)}) %collective-permute-start) | collective-permute-done | bytes 196640 | tf_op jit(solution)/shard_map/ppermute | solution.py:19
  26.1 2.7 %collective-permute-start.1 = (bf16[8,96,128]{2,1,0:T(8,128)(2,1)S(1)}, bf16[8,96,128]{2,1,0:T(8,128)(2,1)S(1)}, u32[]{:S(2)}, u32[]{:S(2)}) collective-permute-start(bf16[8,96,128]{2,1,0:T(8,128)(2,1)S(1)} %all-to-all-done.p0), channel_id=1, source_target_pairs={{0,16},{8,24},{16,0},{24,8},{1,17},{9,25},{17,1},{25,9},{2,18},{10... | collective-permute-start | bytes 589832 | tf_op jit(solution)/shard_map/ppermute | solution.py:19
  28.8 4.5 %collective-permute-done.1.p2 = bf16[8,96,128]{2,1,0:T(8,128)(2,1)S(1)} collective-permute-done((bf16[8,96,128]{2,1,0:T(8,128)(2,1)S(1)}, bf16[8,96,128]{2,1,0:T(8,128)(2,1)S(1)}, u32[]{:S(2)}, u32[]{:S(2)}) %collective-permute-start.1) | collective-permute-done | bytes 196640 | tf_op jit(solution)/shard_map/ppermute | solution.py:19
  33.3 1.0 collective-permute-start.2
  34.3 6.4 %collective-permute-done.2.p3 = bf16[8,96,128]{2,1,0:T(8,128)(2,1)} collective-permute-done((bf16[8,96,128]{2,1,0:T(8,128)(2,1)S(1)}, bf16[8,96,128]{2,1,0:T(8,128)(2,1)}, u32[]{:S(2)}, u32[]{:S(2)}) %collective-permute-start.2) | collective-permute-done | bytes 196640 | tf_op jit(solution)/shard_map/ppermute | solution.py:19
  41.3 7.7 %collective-permute-done.3.refs_0_.refs_4_ = bf16[384,1024]{1,0:T(8,128)(2,1)} collective-permute-done((bf16[384,1024]{1,0:T(8,128)(2,1)}, bf16[384,1024]{1,0:T(8,128)(2,1)}, u32[]{:S(2)}, u32[]{:S(2)}) %collective-permute-start.3) | collective-permute-done | bytes 786464 | tf_op jit(solution)/shard_map/ppermute | solution.py:19
  49.0 1.2 collective-permute-start.12
  50.2 4.2 %collective-permute-done.5.refs_2_.refs_8_ = bf16[384,1024]{1,0:T(8,128)(2,1)} collective-permute-done((bf16[384,1024]{1,0:T(8,128)(2,1)}, bf16[384,1024]{1,0:T(8,128)(2,1)}, u32[]{:S(2)}, u32[]{:S(2)}) %collective-permute-start.5) | collective-permute-done | bytes 786464 | tf_op jit(solution)/shard_map/ppermute | solution.py:19
  55.0 0.7 copy.6.labels
  55.8 0.7 stack.125.who
  56.4 13.8 %collective-permute-done.12.left.refs_6_ = bf16[384,1024]{1,0:T(8,128)(2,1)} collective-permute-done((bf16[384,1024]{1,0:T(8,128)(2,1)}, bf16[384,1024]{1,0:T(8,128)(2,1)}, u32[]{:S(2)}, u32[]{:S(2)}) %collective-permute-start.12) | collective-permute-done | bytes 786464 | tf_op jit(solution)/shard_map/ppermute | solution.py:19
  70.3 1.0 collective-permute-done.14.right.refs_12_
  72.5 3.1 %shard_map.58 = (bf16[8,128,384]{2,1,0:T(8,128)(2,1)}, bf16[8,112,128]{2,1,0:T(8,128)(2,1)}) custom-call(s32[2]{0:T(128)} %pad_add_fusion.1.who, bf16[8,96,128]{2,1,0:T(8,128)(2,1)} %copy-done.4, bf16[8,96,128]{2,1,0:T(8,128)(2,1)} %copy-done.12, bf16[8,96,128]{2,1,0:T(8,128)(2,1)} %copy-done.13, bf16[8,96,128]{2,1,0:T(8,128)(2,1)} %collective-permute-done.2.p3, ...), custom_call_target="tpu_custom_call" | custom-call | flops 1048576 | bytes 4096 | tf_op jit(solution)/shard_map/pallas_call | solution.py:48
  75.6 3.6 %all-to-all-start.1 = ((bf16[8,112,128]{2,1,0:T(8,128)(2,1)}), bf16[8,112,128]{2,1,0:T(8,128)(2,1)S(1)}, u32[]{:S(2)}, u32[]{:S(2)}) async-start(bf16[8,112,128]{2,1,0:T(8,128)(2,1)} %get-tuple-element.14), calls=%async_computation.1 | async-start | bytes 458752 | tf_op jit(solution)/shard_map/all_to_all | solution.py:365
  80.4 5.7 %all-to-all-done.1.p0 = bf16[8,112,128]{2,1,0:T(8,128)(2,1)S(1)} async-done(((bf16[8,112,128]{2,1,0:T(8,128)(2,1)}), bf16[8,112,128]{2,1,0:T(8,128)(2,1)S(1)}, u32[]{:S(2)}, u32[]{:S(2)}) %all-to-all-start.1) | async-done | bytes 229408 | tf_op jit(solution)/shard_map/all_to_all | solution.py:365
  86.1 1.2 copy-done.1
  87.3 5.8 %shard_map.59.refs_4_ = f32[128,2048]{1,0:T(8,128)} custom-call(s32[6]{0:T(128)} %stack.125.who, bf16[8,128,384]{2,1,0:T(8,128)(2,1)} %get-tuple-element.15.states, bf16[384,2048]{1,0:T(8,128)(2,1)} %refs_0_.3, bf16[384,2048]{1,0:T(8,128)(2,1)} %copy-done.1, bf16[384,1024]{1,0:T(8,128)(2,1)} %collective-permute-done.8.refs_2_, ...), custom_call_target="tpu_custom_call" | custom-call | flops 805306368 | bytes 3145728 | tf_op jit(solution)/shard_map/pallas_call | solution.py:48
  93.1 4.7 %shard_map.60.near = f32[128,2048]{1,0:T(8,128)} custom-call(s32[4]{0:T(128)} %pad_add_fusion.2.who, bf16[8,128,384]{2,1,0:T(8,128)(2,1)} %get-tuple-element.15.states, bf16[384,1024]{1,0:T(8,128)(2,1)} %collective-permute-done.3.refs_0_.refs_4_, bf16[384,1024]{1,0:T(8,128)(2,1)} %collective-permute-done.4.refs_1_.refs_5_, ...), custom_call_target="tpu_custom_call" | custom-call | flops 402653184 | bytes 1572864 | tf_op jit(solution)/shard_map/pallas_call | solution.py:48
  97.8 5.2 %shard_map.61 = (bf16[128,2048]{1,0:T(8,128)(2,1)}, f32[32,3,128]{2,1,0:T(4,128)}, f32[1,128]{1,0:T(1,128)}) custom-call(s32[3]{0:T(128)} %pad_add_fusion.who, bf16[8,128,384]{2,1,0:T(8,128)(2,1)} %get-tuple-element.15.states, s32[128,1]{1,0:T(8,128)} %copy.6.labels, f32[128,2048]{1,0:T(8,128)} %shard_map.60.near, ...), custom_call_target="tpu_custom_call" | custom-call | flops 402653184 | bytes 1572864 | tf_op jit(solution)/shard_map/pallas_call | solution.py:48
  103.0 10.0 %all-to-all-start.2 = ((f32[32,3,128]{2,1,0:T(4,128)}), f32[32,3,128]{2,1,0:T(4,128)S(1)}, u32[]{:S(2)}, u32[]{:S(2)}) async-start(f32[32,3,128]{2,1,0:T(4,128)} %get-tuple-element.17), calls=%async_computation.2 | async-start | bytes 131072 | tf_op jit(solution)/shard_map/all_to_all | solution.py:389
  113.7 8.5 %all-to-all-done.2.parts = f32[32,3,128]{2,1,0:T(4,128)S(1)} async-done(((f32[32,3,128]{2,1,0:T(4,128)}), f32[32,3,128]{2,1,0:T(4,128)S(1)}, u32[]{:S(2)}, u32[]{:S(2)}) %all-to-all-start.2) | async-done | bytes 49184 | tf_op jit(solution)/shard_map/all_to_all | solution.py:389
  122.1 0.6 copy-done.8
  122.7 12.2 %shard_map.62 = (bf16[3072,128]{1,0:T(8,128)(2,1)}, f32[1,128]{1,0:T(1,128)}, f32[1,128]{1,0:T(1,128)}) custom-call(s32[9]{0:T(128)} %stack.109.starts, bf16[128,2048]{1,0:T(8,128)(2,1)} %get-tuple-element.16.powers.refs_4_, s32[1,128]{1,0:T(1,128)} %bitcast.31, f32[32,3,128]{2,1,0:T(4,128)} %copy-done.8, f32[1,128]{1,0:T(1,128)} %get-tuple-element.18.peaks, ...), custom_call_target="tpu_custom_call" | custom-call | flops 1610612736 | bytes 6291456 | tf_op jit(solution)/shard_map/pallas_call | solution.py:48
  134.9 4.9 %all-to-all-start.3 = ((bf16[32,96,128]{2,1,0:T(8,128)(2,1)}), bf16[32,96,128]{2,1,0:T(8,128)(2,1)S(1)}, u32[]{:S(2)}, u32[]{:S(2)}) async-start(bf16[32,96,128]{2,1,0:T(8,128)(2,1)} %bitcast.28), calls=%async_computation.3 | async-start | bytes 1572864 | tf_op jit(solution)/shard_map/all_to_all | solution.py:398
  139.8 0.6 collective-permute-start.24
  140.4 2.7 %collective-permute-start.26 = (bf16[128,2048]{1,0:T(8,128)(2,1)S(1)}, bf16[128,2048]{1,0:T(8,128)(2,1)S(1)}, u32[]{:S(2)}, u32[]{:S(2)}) collective-permute-start(bf16[128,2048]{1,0:T(8,128)(2,1)S(1)} %copy-done.2), channel_id=1, source_target_pairs={{0,192},{64,0},{128,64},{192,128},{1,193},{65,1},{129,65},{193,129... | collective-permute-start | bytes 1572872 | tf_op jit(solution)/shard_map/ppermute | solution.py:19
  143.1 2.8 %collective-permute-start.16 = (bf16[8,112,128]{2,1,0:T(8,128)(2,1)S(1)}, bf16[8,112,128]{2,1,0:T(8,128)(2,1)S(1)}, u32[]{:S(2)}, u32[]{:S(2)}) collective-permute-start(bf16[8,112,128]{2,1,0:T(8,128)(2,1)S(1)} %all-to-all-done.1.p0), channel_id=1, source_target_pairs={{0,24},{8,0},{16,8},{24,16},{1,25},{9,1},{17,9},{25,17},{2,26},{10... | collective-permute-start | bytes 688136 | tf_op jit(solution)/shard_map/ppermute | solution.py:19
  145.9 18.0 %collective-permute-done.24.refs_6_ = bf16[128,2048]{1,0:T(8,128)(2,1)S(1)} collective-permute-done((bf16[128,2048]{1,0:T(8,128)(2,1)S(1)}, bf16[128,2048]{1,0:T(8,128)(2,1)S(1)}, u32[]{:S(2)}, u32[]{:S(2)}) %collective-permute-start.24) | collective-permute-done | bytes 524320 | tf_op jit(solution)/shard_map/ppermute | solution.py:19
  164.8 3.1 %collective-permute-start.17 = (bf16[8,112,128]{2,1,0:T(8,128)(2,1)S(1)}, bf16[8,112,128]{2,1,0:T(8,128)(2,1)S(1)}, u32[]{:S(2)}, u32[]{:S(2)}) collective-permute-start(bf16[8,112,128]{2,1,0:T(8,128)(2,1)S(1)} %all-to-all-done.1.p0), channel_id=1, source_target_pairs={{0,16},{8,24},{16,0},{24,8},{1,17},{9,25},{17,1},{25,9},{2,18},{10... | collective-permute-start | bytes 688136 | tf_op jit(solution)/shard_map/ppermute | solution.py:19
  167.9 6.1 %collective-permute-done.17.p2 = bf16[8,112,128]{2,1,0:T(8,128)(2,1)S(1)} collective-permute-done((bf16[8,112,128]{2,1,0:T(8,128)(2,1)S(1)}, bf16[8,112,128]{2,1,0:T(8,128)(2,1)S(1)}, u32[]{:S(2)}, u32[]{:S(2)}) %collective-permute-start.17) | collective-permute-done | bytes 229408 | tf_op jit(solution)/shard_map/ppermute | solution.py:19
  174.0 0.7 copy-done.10
  175.2 1.5 collective-permute-start.18
  176.7 7.4 %collective-permute-done.18.p3 = bf16[8,112,128]{2,1,0:T(8,128)(2,1)S(1)} collective-permute-done((bf16[8,112,128]{2,1,0:T(8,128)(2,1)S(1)}, bf16[8,112,128]{2,1,0:T(8,128)(2,1)S(1)}, u32[]{:S(2)}, u32[]{:S(2)}) %collective-permute-start.18) | collective-permute-done | bytes 229408 | tf_op jit(solution)/shard_map/ppermute | solution.py:19
  184.0 0.7 copy-done.11
  185.1 4.4 %collective-permute-done.20.refs_1_ = f32[2,128]{1,0:T(2,128)S(1)} collective-permute-done((f32[2,128]{1,0:T(2,128)S(1)}, f32[2,128]{1,0:T(2,128)S(1)}, u32[]{:S(2)}, u32[]{:S(2)}) %collective-permute-start.20) | collective-permute-done | bytes 1056 | tf_op jit(solution)/shard_map/ppermute | solution.py:19
  189.5 1.3 collective-permute-start.21
  190.8 2.2 %collective-permute-done.21.refs_2_ = f32[2,128]{1,0:T(2,128)S(1)} collective-permute-done((f32[2,128]{1,0:T(2,128)S(1)}, f32[2,128]{1,0:T(2,128)S(1)}, u32[]{:S(2)}, u32[]{:S(2)}) %collective-permute-start.21) | collective-permute-done | bytes 1056 | tf_op jit(solution)/shard_map/ppermute | solution.py:19
  193.1 0.8 collective-permute-start.22
  194.5 3.7 %collective-permute-done.22.refs_3_ = f32[2,128]{1,0:T(2,128)S(1)} collective-permute-done((f32[2,128]{1,0:T(2,128)S(1)}, f32[2,128]{1,0:T(2,128)S(1)}, u32[]{:S(2)}, u32[]{:S(2)}) %collective-permute-start.22) | collective-permute-done | bytes 1056 | tf_op jit(solution)/shard_map/ppermute | solution.py:19
  198.8 6.4 %shard_map.63 = f32[384,2048]{1,0:T(8,128)} custom-call(s32[10]{0:T(128)} %stack.126.who, bf16[8,112,128]{2,1,0:T(8,128)(2,1)} %copy-done.3, bf16[8,112,128]{2,1,0:T(8,128)(2,1)} %copy-done.9, bf16[8,112,128]{2,1,0:T(8,128)(2,1)} %copy-done.10, bf16[8,112,128]{2,1,0:T(8,128)(2,1)} %copy-done.11, f32[2,128]{1,0:T(2,128)} %copy-done.14, f32[2,128]{1,0:T(2,128)} %copy-done.16, ...), custom_call_target="tpu_custom_call" | custom-call | flops 1610612736 | bytes 6291456 | tf_op jit(solution)/shard_map/pallas_call | solution.py:48
  205.2 0.7 reduce_sum.12
  (80 shorter events, 7.0 us)
Async XLA Ops:
  0.6 15.0 %copy-start = (bf16[384,2048]{1,0:T(8,128)(2,1)S(1)}, bf16[384,2048]{1,0:T(8,128)(2,1)}, u32[]{:S(2)}) copy-start(bf16[384,2048]{1,0:T(8,128)(2,1)} %refs_0_.3) | copy-start | bytes 4718596
  2.2 17.6 %all-to-all-start = ((bf16[8,96,128]{2,1,0:T(8,128)(2,1)}), bf16[8,96,128]{2,1,0:T(8,128)(2,1)S(1)}, u32[]{:S(2)}, u32[]{:S(2)}) async-start(bf16[8,96,128]{2,1,0:T(8,128)(2,1)} %broadcast_in_dim.12), calls=%async_computation | async-start | bytes 393216 | tf_op jit(solution)/shard_map/all_to_all | solution.py:27
  10.8 44.3 %copy-start.15 = (s32[128]{0:T(128)S(1)}, s32[128]{0:T(128)}, u32[]{:S(2)}) copy-start(s32[128]{0:T(128)} %param.5) | copy-start | bytes 1540
  12.9 27.9 %collective-permute-start.10 = (bf16[384,1024]{1,0:T(8,128)(2,1)}, bf16[384,1024]{1,0:T(8,128)(2,1)}, u32[]{:S(2)}, u32[]{:S(2)}) collective-permute-start(bf16[384,1024]{1,0:T(8,128)(2,1)} %slice.8), channel_id=1, source_target_pairs={{0,192},{64,0},{128,64},{192,128},{1,193},{65,1},{129,65},{193,129... | collective-permute-start | bytes 2359304 | tf_op jit(solution)/shard_map/ppermute | solution.py:19
  16.6 24.7 %collective-permute-start.8 = (bf16[384,1024]{1,0:T(8,128)(2,1)}, bf16[384,1024]{1,0:T(8,128)(2,1)}, u32[]{:S(2)}, u32[]{:S(2)}) collective-permute-start(bf16[384,1024]{1,0:T(8,128)(2,1)} %slice.6), channel_id=1, source_target_pairs={{0,64},{64,128},{128,192},{192,0},{1,65},{65,129},{129,193},{193,1... | collective-permute-start | bytes 2359304 | tf_op jit(solution)/shard_map/ppermute | solution.py:19
  16.6 32.5 %collective-permute-start.3 = (bf16[384,1024]{1,0:T(8,128)(2,1)}, bf16[384,1024]{1,0:T(8,128)(2,1)}, u32[]{:S(2)}, u32[]{:S(2)}) collective-permute-start(bf16[384,1024]{1,0:T(8,128)(2,1)} %slice.6), channel_id=1, source_target_pairs={{0,192},{64,0},{128,64},{192,128},{1,193},{65,1},{129,65},{193,129... | collective-permute-start | bytes 2359304 | tf_op jit(solution)/shard_map/ppermute | solution.py:19
  19.8 34.7 %collective-permute-start.5 = (bf16[384,1024]{1,0:T(8,128)(2,1)}, bf16[384,1024]{1,0:T(8,128)(2,1)}, u32[]{:S(2)}, u32[]{:S(2)}) collective-permute-start(bf16[384,1024]{1,0:T(8,128)(2,1)} %slice.8), channel_id=1, source_target_pairs={{0,64},{64,128},{128,192},{192,0},{1,65},{65,129},{129,193},{193,1... | collective-permute-start | bytes 2359304 | tf_op jit(solution)/shard_map/ppermute | solution.py:19
  19.8 52.7 %copy-start.4 = (bf16[8,96,128]{2,1,0:T(8,128)(2,1)}, bf16[8,96,128]{2,1,0:T(8,128)(2,1)S(1)}, u32[]{:S(2)}) copy-start(bf16[8,96,128]{2,1,0:T(8,128)(2,1)S(1)} %all-to-all-done.p0) | copy-start | bytes 589828
  19.8 6.3 %collective-permute-start = (bf16[8,96,128]{2,1,0:T(8,128)(2,1)S(1)}, bf16[8,96,128]{2,1,0:T(8,128)(2,1)S(1)}, u32[]{:S(2)}, u32[]{:S(2)}) collective-permute-start(bf16[8,96,128]{2,1,0:T(8,128)(2,1)S(1)} %all-to-all-done.p0), channel_id=1, source_target_pairs={{0,24},{8,0},{16,8},{24,16},{1,25},{9,1},{17,9},{25,17},{2,26},{10... | collective-permute-start | bytes 589832 | tf_op jit(solution)/shard_map/ppermute | solution.py:19
  26.1 46.4 %copy-start.12 = (bf16[8,96,128]{2,1,0:T(8,128)(2,1)}, bf16[8,96,128]{2,1,0:T(8,128)(2,1)S(1)}, u32[]{:S(2)}) copy-start(bf16[8,96,128]{2,1,0:T(8,128)(2,1)S(1)} %collective-permute-done.p1) | copy-start | bytes 589828
  26.1 7.2 %collective-permute-start.1 = (bf16[8,96,128]{2,1,0:T(8,128)(2,1)S(1)}, bf16[8,96,128]{2,1,0:T(8,128)(2,1)S(1)}, u32[]{:S(2)}, u32[]{:S(2)}) collective-permute-start(bf16[8,96,128]{2,1,0:T(8,128)(2,1)S(1)} %all-to-all-done.p0), channel_id=1, source_target_pairs={{0,16},{8,24},{16,0},{24,8},{1,17},{9,25},{17,1},{25,9},{2,18},{10... | collective-permute-start | bytes 589832 | tf_op jit(solution)/shard_map/ppermute | solution.py:19
  33.3 7.4 %collective-permute-start.2 = (bf16[8,96,128]{2,1,0:T(8,128)(2,1)S(1)}, bf16[8,96,128]{2,1,0:T(8,128)(2,1)}, u32[]{:S(2)}, u32[]{:S(2)}) collective-permute-start(bf16[8,96,128]{2,1,0:T(8,128)(2,1)S(1)} %all-to-all-done.p0), channel_id=1, source_target_pairs={{0,8},{8,16},{16,24},{24,0},{1,9},{9,17},{17,25},{25,1},{2,10},{10... | collective-permute-start | bytes 589832 | tf_op jit(solution)/shard_map/ppermute | solution.py:19
  40.7 45.4 %collective-permute-start.7 = (bf16[384,2048]{1,0:T(8,128)(2,1)S(1)}, bf16[384,2048]{1,0:T(8,128)(2,1)S(1)}, u32[]{:S(2)}, u32[]{:S(2)}) collective-permute-start(bf16[384,2048]{1,0:T(8,128)(2,1)S(1)} %copy-done), channel_id=1, source_target_pairs={{0,32},{32,0},{1,33},{33,1},{2,34},{34,2},{3,35},{35,3},{4,36},{36... | collective-permute-start | bytes 4718600 | tf_op jit(solution)/shard_map/ppermute | solution.py:23
  40.7 13.8 %collective-permute-start.11 = (bf16[384,1024]{1,0:T(8,128)(2,1)}, bf16[384,1024]{1,0:T(8,128)(2,1)}, u32[]{:S(2)}, u32[]{:S(2)}) collective-permute-start(bf16[384,1024]{1,0:T(8,128)(2,1)} %collective-permute-done.10.refs_4_.refs_10_), channel_id=1, source_target_pairs={{0,32},{32,0},{1,33},{33,1},{2,34},{34,2},{3,35},{35,3},{4,36},{36... | collective-permute-start | bytes 2359304 | tf_op jit(solution)/shard_map/ppermute | solution.py:23
  41.3 13.3 %collective-permute-start.9 = (bf16[384,1024]{1,0:T(8,128)(2,1)}, bf16[384,1024]{1,0:T(8,128)(2,1)}, u32[]{:S(2)}, u32[]{:S(2)}) collective-permute-start(bf16[384,1024]{1,0:T(8,128)(2,1)} %collective-permute-done.8.refs_2_), channel_id=1, source_target_pairs={{0,32},{32,0},{1,33},{33,1},{2,34},{34,2},{3,35},{35,3},{4,36},{36... | collective-permute-start | bytes 2359304 | tf_op jit(solution)/shard_map/ppermute | solution.py:23
  49.0 21.2 %collective-permute-start.12 = (bf16[384,1024]{1,0:T(8,128)(2,1)}, bf16[384,1024]{1,0:T(8,128)(2,1)}, u32[]{:S(2)}, u32[]{:S(2)}) collective-permute-start(bf16[384,1024]{1,0:T(8,128)(2,1)} %collective-permute-done.8.refs_2_), channel_id=1, source_target_pairs={{0,64},{64,128},{128,192},{192,0},{1,65},{65,129},{129,193},{193,1... | collective-permute-start | bytes 2359304 | tf_op jit(solution)/shard_map/ppermute | solution.py:19
  54.5 16.8 %collective-permute-start.14 = (bf16[384,1024]{1,0:T(8,128)(2,1)}, bf16[384,1024]{1,0:T(8,128)(2,1)}, u32[]{:S(2)}, u32[]{:S(2)}) collective-permute-start(bf16[384,1024]{1,0:T(8,128)(2,1)} %collective-permute-done.10.refs_4_.refs_10_), channel_id=1, source_target_pairs={{0,192},{64,0},{128,64},{192,128},{1,193},{65,1},{129,65},{193,129... | collective-permute-start | bytes 2359304 | tf_op jit(solution)/shard_map/ppermute | solution.py:19
  54.5 38.6 %collective-permute-start.4 = (bf16[384,1024]{1,0:T(8,128)(2,1)}, bf16[384,1024]{1,0:T(8,128)(2,1)}, u32[]{:S(2)}, u32[]{:S(2)}) collective-permute-start(bf16[384,1024]{1,0:T(8,128)(2,1)} %collective-permute-done.3.refs_0_.refs_4_), channel_id=1, source_target_pairs={{0,32},{32,0},{1,33},{33,1},{2,34},{34,2},{3,35},{35,3},{4,36},{36... | collective-permute-start | bytes 2359304 | tf_op jit(solution)/shard_map/ppermute | solution.py:23
  54.5 38.5 %collective-permute-start.6 = (bf16[384,1024]{1,0:T(8,128)(2,1)}, bf16[384,1024]{1,0:T(8,128)(2,1)}, u32[]{:S(2)}, u32[]{:S(2)}) collective-permute-start(bf16[384,1024]{1,0:T(8,128)(2,1)} %collective-permute-done.5.refs_2_.refs_8_), channel_id=1, source_target_pairs={{0,32},{32,0},{1,33},{33,1},{2,34},{34,2},{3,35},{35,3},{4,36},{36... | collective-permute-start | bytes 2359304 | tf_op jit(solution)/shard_map/ppermute | solution.py:23
  70.3 27.5 %collective-permute-start.13 = (bf16[384,1024]{1,0:T(8,128)(2,1)}, bf16[384,1024]{1,0:T(8,128)(2,1)}, u32[]{:S(2)}, u32[]{:S(2)}) collective-permute-start(bf16[384,1024]{1,0:T(8,128)(2,1)} %collective-permute-done.12.left.refs_6_), channel_id=1, source_target_pairs={{0,32},{32,0},{1,33},{33,1},{2,34},{34,2},{3,35},{35,3},{4,36},{36... | collective-permute-start | bytes 2359304 | tf_op jit(solution)/shard_map/ppermute | solution.py:23
  71.3 26.5 %collective-permute-start.15 = (bf16[384,1024]{1,0:T(8,128)(2,1)}, bf16[384,1024]{1,0:T(8,128)(2,1)}, u32[]{:S(2)}, u32[]{:S(2)}) collective-permute-start(bf16[384,1024]{1,0:T(8,128)(2,1)} %collective-permute-done.14.right.refs_12_), channel_id=1, source_target_pairs={{0,32},{32,0},{1,33},{33,1},{2,34},{34,2},{3,35},{35,3},{4,36},{36... | collective-permute-start | bytes 2359304 | tf_op jit(solution)/shard_map/ppermute | solution.py:23
  75.6 10.5 %all-to-all-start.1 = ((bf16[8,112,128]{2,1,0:T(8,128)(2,1)}), bf16[8,112,128]{2,1,0:T(8,128)(2,1)S(1)}, u32[]{:S(2)}, u32[]{:S(2)}) async-start(bf16[8,112,128]{2,1,0:T(8,128)(2,1)} %get-tuple-element.14), calls=%async_computation.1 | async-start | bytes 458752 | tf_op jit(solution)/shard_map/all_to_all | solution.py:365
  86.1 89.1 %copy-start.3 = (bf16[8,112,128]{2,1,0:T(8,128)(2,1)}, bf16[8,112,128]{2,1,0:T(8,128)(2,1)S(1)}, u32[]{:S(2)}) copy-start(bf16[8,112,128]{2,1,0:T(8,128)(2,1)S(1)} %all-to-all-done.1.p0) | copy-start | bytes 688132
  103.0 19.1 %all-to-all-start.2 = ((f32[32,3,128]{2,1,0:T(4,128)}), f32[32,3,128]{2,1,0:T(4,128)S(1)}, u32[]{:S(2)}, u32[]{:S(2)}) async-start(f32[32,3,128]{2,1,0:T(4,128)} %get-tuple-element.17), calls=%async_computation.2 | async-start | bytes 131072 | tf_op jit(solution)/shard_map/all_to_all | solution.py:389
  134.9 4.9 %copy-start.2 = (bf16[128,2048]{1,0:T(8,128)(2,1)S(1)}, bf16[128,2048]{1,0:T(8,128)(2,1)}, u32[]{:S(2)}) copy-start(bf16[128,2048]{1,0:T(8,128)(2,1)} %get-tuple-element.16.powers.refs_4_) | copy-start | bytes 1572868
  134.9 39.1 %copy-start.19 = (f32[1,128]{1,0:T(1,128)S(1)}, f32[1,128]{1,0:T(1,128)}, u32[]{:S(2)}) copy-start(f32[1,128]{1,0:T(1,128)} %get-tuple-element.22) | copy-start | bytes 1540
  134.9 70.3 %all-to-all-start.3 = ((bf16[32,96,128]{2,1,0:T(8,128)(2,1)}), bf16[32,96,128]{2,1,0:T(8,128)(2,1)S(1)}, u32[]{:S(2)}, u32[]{:S(2)}) async-start(bf16[32,96,128]{2,1,0:T(8,128)(2,1)} %bitcast.28), calls=%async_computation.3 | async-start | bytes 1572864 | tf_op jit(solution)/shard_map/all_to_all | solution.py:398
  139.8 24.1 %collective-permute-start.24 = (bf16[128,2048]{1,0:T(8,128)(2,1)S(1)}, bf16[128,2048]{1,0:T(8,128)(2,1)S(1)}, u32[]{:S(2)}, u32[]{:S(2)}) collective-permute-start(bf16[128,2048]{1,0:T(8,128)(2,1)S(1)} %copy-done.2), channel_id=1, source_target_pairs={{0,64},{64,128},{128,192},{192,0},{1,65},{65,129},{129,193},{193,1... | collective-permute-start | bytes 1572872 | tf_op jit(solution)/shard_map/ppermute | solution.py:19
  140.4 23.5 %collective-permute-start.26 = (bf16[128,2048]{1,0:T(8,128)(2,1)S(1)}, bf16[128,2048]{1,0:T(8,128)(2,1)S(1)}, u32[]{:S(2)}, u32[]{:S(2)}) collective-permute-start(bf16[128,2048]{1,0:T(8,128)(2,1)S(1)} %copy-done.2), channel_id=1, source_target_pairs={{0,192},{64,0},{128,64},{192,128},{1,193},{65,1},{129,65},{193,129... | collective-permute-start | bytes 1572872 | tf_op jit(solution)/shard_map/ppermute | solution.py:19
  143.1 21.3 %collective-permute-start.28 = (bf16[128,2048]{1,0:T(8,128)(2,1)S(1)}, bf16[128,2048]{1,0:T(8,128)(2,1)S(1)}, u32[]{:S(2)}, u32[]{:S(2)}) collective-permute-start(bf16[128,2048]{1,0:T(8,128)(2,1)S(1)} %copy-done.2), channel_id=1, source_target_pairs={{0,128},{64,192},{128,0},{192,64},{1,129},{65,193},{129,1},{193,65... | collective-permute-start | bytes 1572872 | tf_op jit(solution)/shard_map/ppermute | solution.py:19
  143.1 21.7 %collective-permute-start.16 = (bf16[8,112,128]{2,1,0:T(8,128)(2,1)S(1)}, bf16[8,112,128]{2,1,0:T(8,128)(2,1)S(1)}, u32[]{:S(2)}, u32[]{:S(2)}) collective-permute-start(bf16[8,112,128]{2,1,0:T(8,128)(2,1)S(1)} %all-to-all-done.1.p0), channel_id=1, source_target_pairs={{0,24},{8,0},{16,8},{24,16},{1,25},{9,1},{17,9},{25,17},{2,26},{10... | collective-permute-start | bytes 688136 | tf_op jit(solution)/shard_map/ppermute | solution.py:19
  145.9 52.2 %collective-permute-start.23 = (bf16[128,2048]{1,0:T(8,128)(2,1)S(1)}, bf16[128,2048]{1,0:T(8,128)(2,1)}, u32[]{:S(2)}, u32[]{:S(2)}) collective-permute-start(bf16[128,2048]{1,0:T(8,128)(2,1)S(1)} %copy-done.2), channel_id=1, source_target_pairs={{0,32},{32,0},{1,33},{33,1},{2,34},{34,2},{3,35},{35,3},{4,36},{36... | collective-permute-start | bytes 1572872 | tf_op jit(solution)/shard_map/ppermute | solution.py:23
  163.9 34.3 %copy-start.5 = (bf16[128,2048]{1,0:T(8,128)(2,1)}, bf16[128,2048]{1,0:T(8,128)(2,1)S(1)}, u32[]{:S(2)}) copy-start(bf16[128,2048]{1,0:T(8,128)(2,1)S(1)} %collective-permute-done.24.refs_6_) | copy-start | bytes 1572868
  163.9 34.2 %collective-permute-start.25 = (bf16[128,2048]{1,0:T(8,128)(2,1)S(1)}, bf16[128,2048]{1,0:T(8,128)(2,1)}, u32[]{:S(2)}, u32[]{:S(2)}) collective-permute-start(bf16[128,2048]{1,0:T(8,128)(2,1)S(1)} %collective-permute-done.24.refs_6_), channel_id=1, source_target_pairs={{0,32},{32,0},{1,33},{33,1},{2,34},{34,2},{3,35},{35,3},{4,36},{36... | collective-permute-start | bytes 1572872 | tf_op jit(solution)/shard_map/ppermute | solution.py:23
  163.9 34.3 %copy-start.6 = (bf16[128,2048]{1,0:T(8,128)(2,1)}, bf16[128,2048]{1,0:T(8,128)(2,1)S(1)}, u32[]{:S(2)}) copy-start(bf16[128,2048]{1,0:T(8,128)(2,1)S(1)} %collective-permute-done.26.refs_8_) | copy-start | bytes 1572868
  163.9 34.2 %collective-permute-start.27 = (bf16[128,2048]{1,0:T(8,128)(2,1)S(1)}, bf16[128,2048]{1,0:T(8,128)(2,1)}, u32[]{:S(2)}, u32[]{:S(2)}) collective-permute-start(bf16[128,2048]{1,0:T(8,128)(2,1)S(1)} %collective-permute-done.26.refs_8_), channel_id=1, source_target_pairs={{0,32},{32,0},{1,33},{33,1},{2,34},{34,2},{3,35},{35,3},{4,36},{36... | collective-permute-start | bytes 1572872 | tf_op jit(solution)/shard_map/ppermute | solution.py:23
  164.4 33.8 %copy-start.7 = (bf16[128,2048]{1,0:T(8,128)(2,1)}, bf16[128,2048]{1,0:T(8,128)(2,1)S(1)}, u32[]{:S(2)}) copy-start(bf16[128,2048]{1,0:T(8,128)(2,1)S(1)} %collective-permute-done.28.refs_10_) | copy-start | bytes 1572868
  164.4 33.7 %collective-permute-start.29 = (bf16[128,2048]{1,0:T(8,128)(2,1)S(1)}, bf16[128,2048]{1,0:T(8,128)(2,1)}, u32[]{:S(2)}, u32[]{:S(2)}) collective-permute-start(bf16[128,2048]{1,0:T(8,128)(2,1)S(1)} %collective-permute-done.28.refs_10_), channel_id=1, source_target_pairs={{0,32},{32,0},{1,33},{33,1},{2,34},{34,2},{3,35},{35,3},{4,36},{36... | collective-permute-start | bytes 1572872 | tf_op jit(solution)/shard_map/ppermute | solution.py:23
  164.8 33.5 %copy-start.9 = (bf16[8,112,128]{2,1,0:T(8,128)(2,1)}, bf16[8,112,128]{2,1,0:T(8,128)(2,1)S(1)}, u32[]{:S(2)}) copy-start(bf16[8,112,128]{2,1,0:T(8,128)(2,1)S(1)} %collective-permute-done.16.p1) | copy-start | bytes 688132
  164.8 9.2 %collective-permute-start.17 = (bf16[8,112,128]{2,1,0:T(8,128)(2,1)S(1)}, bf16[8,112,128]{2,1,0:T(8,128)(2,1)S(1)}, u32[]{:S(2)}, u32[]{:S(2)}) collective-permute-start(bf16[8,112,128]{2,1,0:T(8,128)(2,1)S(1)} %all-to-all-done.1.p0), channel_id=1, source_target_pairs={{0,16},{8,24},{16,0},{24,8},{1,17},{9,25},{17,1},{25,9},{2,18},{10... | collective-permute-start | bytes 688136 | tf_op jit(solution)/shard_map/ppermute | solution.py:19
  174.0 1.2 collective-permute-start.19
  175.2 8.9 %collective-permute-start.18 = (bf16[8,112,128]{2,1,0:T(8,128)(2,1)S(1)}, bf16[8,112,128]{2,1,0:T(8,128)(2,1)S(1)}, u32[]{:S(2)}, u32[]{:S(2)}) collective-permute-start(bf16[8,112,128]{2,1,0:T(8,128)(2,1)S(1)} %all-to-all-done.1.p0), channel_id=1, source_target_pairs={{0,8},{8,16},{16,24},{24,0},{1,9},{9,17},{17,25},{25,1},{2,10},{10... | collective-permute-start | bytes 688136 | tf_op jit(solution)/shard_map/ppermute | solution.py:19
  176.7 21.6 %copy-start.14 = (f32[2,128]{1,0:T(2,128)}, f32[2,128]{1,0:T(2,128)S(1)}, u32[]{:S(2)}) copy-start(f32[2,128]{1,0:T(2,128)S(1)} %pad_maximum_fusion.refs_0_) | copy-start | bytes 3076
  184.7 4.8 %collective-permute-start.20 = (f32[2,128]{1,0:T(2,128)S(1)}, f32[2,128]{1,0:T(2,128)S(1)}, u32[]{:S(2)}, u32[]{:S(2)}) collective-permute-start(f32[2,128]{1,0:T(2,128)S(1)} %pad_maximum_fusion.refs_0_), channel_id=1, source_target_pairs={{0,64},{64,128},{128,192},{192,0},{1,65},{65,129},{129,193},{193,1... | collective-permute-start | bytes 3080 | tf_op jit(solution)/shard_map/ppermute | solution.py:19
  189.5 8.7 %copy-start.16 = (f32[2,128]{1,0:T(2,128)}, f32[2,128]{1,0:T(2,128)S(1)}, u32[]{:S(2)}) copy-start(f32[2,128]{1,0:T(2,128)S(1)} %collective-permute-done.20.refs_1_) | copy-start | bytes 3076
  189.5 3.6 %collective-permute-start.21 = (f32[2,128]{1,0:T(2,128)S(1)}, f32[2,128]{1,0:T(2,128)S(1)}, u32[]{:S(2)}, u32[]{:S(2)}) collective-permute-start(f32[2,128]{1,0:T(2,128)S(1)} %pad_maximum_fusion.refs_0_), channel_id=1, source_target_pairs={{0,192},{64,0},{128,64},{192,128},{1,193},{65,1},{129,65},{193,129... | collective-permute-start | bytes 3080 | tf_op jit(solution)/shard_map/ppermute | solution.py:19
  193.1 5.2 %copy-start.17 = (f32[2,128]{1,0:T(2,128)}, f32[2,128]{1,0:T(2,128)S(1)}, u32[]{:S(2)}) copy-start(f32[2,128]{1,0:T(2,128)S(1)} %collective-permute-done.21.refs_2_) | copy-start | bytes 3076
  193.1 5.1 %collective-permute-start.22 = (f32[2,128]{1,0:T(2,128)S(1)}, f32[2,128]{1,0:T(2,128)S(1)}, u32[]{:S(2)}, u32[]{:S(2)}) collective-permute-start(f32[2,128]{1,0:T(2,128)S(1)} %pad_maximum_fusion.refs_0_), channel_id=1, source_target_pairs={{0,128},{64,192},{128,0},{192,64},{1,129},{65,193},{129,1},{193,65... | collective-permute-start | bytes 3080 | tf_op jit(solution)/shard_map/ppermute | solution.py:19
  (6 other events, 4.8 us)

commit v7 on v6

--- a/solution.py
+++ b/solution.py
@@ -204,72 +204,52 @@
 
 
 def terms_kernel(starts, powers, labels, parts, peaks, *refs):
-    arrays, (out, scales, losses, errors, full, cut, pieces, sems, done) = refs[:14], refs[14:]
+    *arrays, out, scales, losses, errors = refs
+    step = pl.program_id(0)
     width, tokens = errors.shape
+
+    @pl.when(step == 0)
+    def _():
+        theirs = parts[:, 0, :]
+        peak = jnp.max(theirs, axis=0, keepdims=True)
+        total = jnp.sum(parts[:, 1, :] * jnp.exp(theirs - peak), axis=0, keepdims=True)
+        target = jnp.sum(parts[:, 2, :], axis=0, keepdims=True)
+        scale = jnp.exp(peaks[...] - peak) / total
+        loss = jnp.log(total) + peak - target
+        scales[...] = scale
+        losses[...] = loss
+        columns = starts[8] + lax.broadcasted_iota(jnp.int32, (width, tokens), 0)
+        hit = jnp.where(columns == labels[...], 1.0, 0.0)
+        errors[...] = (powers[...].T.astype(F32) * scale - hit).astype(BF)
+
     half = width // 2
-    rows = cut.shape[1]
-
-    loads = [[pltpu.make_async_copy(arrays[k], full.at[k], sems.at[k])] for k in range(2)]
-    loads += [
-        [pltpu.make_async_copy(arrays[j + k], cut.at[j - 2 + k], sems.at[j + k]) for j in (2, 8)]
-        for k in range(6)
-    ]
-    for load in loads:
-        for copy in load:
-            copy.start()
-
-    theirs = parts[:, 0, :]
-    peak = jnp.max(theirs, axis=0, keepdims=True)
-    total = jnp.sum(parts[:, 1, :] * jnp.exp(theirs - peak), axis=0, keepdims=True)
-    target = jnp.sum(parts[:, 2, :], axis=0, keepdims=True)
-    scale = jnp.exp(peaks[...] - peak) / total
-    scales[...] = scale
-    losses[...] = jnp.log(total) + peak - target
-    columns = starts[8] + lax.broadcasted_iota(jnp.int32, (width, tokens), 0)
-    hit = jnp.where(columns == labels[...], 1.0, 0.0)
-    errors[...] = (powers[...].T.astype(F32) * scale - hit).astype(BF)
-
-    stores = []
+    own, left, right = arrays[:2], arrays[2:8], arrays[8:]
+    lefts = jnp.concatenate([a[:, :half] for a in own] + [a[...] for a in left], axis=0)
+    rights = jnp.concatenate([a[:, half:] for a in own] + [a[...] for a in right], axis=0)
+    term = dot(lefts, errors[:half, :]) + dot(rights, errors[half:, :])
+    rows = own[0].shape[0]
     for k in range(8):
-        for copy in loads[k]:
-            copy.wait()
-        if k < 2:
-            term = dot(full[k], errors[...])
-        else:
-            term = dot(cut[k - 2], errors[:half, :]) + dot(cut[k + 4], errors[half:, :])
-        pieces[k] = term.astype(BF)
-        at = pl.ds(pl.multiple_of(starts[k], rows), rows)
-        stores.append(pltpu.make_async_copy(pieces.at[k], out.at[at], done.at[k]))
-        stores[-1].start()
-    for copy in stores:
-        copy.wait()
+        at = pl.ds(pl.multiple_of(starts[k] + step * rows, 32), rows)
+        out[at, :] = term[k * rows : (k + 1) * rows].astype(BF)
 
 
 def state_terms(powers, labels, parts, peaks, own, left, right, starts, depth):
     tokens, width = powers.shape
-    rows = own[0].shape[0]
+    rows = own[0].shape[0] // STEPS
     args = [powers, labels, parts, peaks, *own, *left, *right]
-    away = pl.BlockSpec(memory_space=pltpu.HBM)
+    specs = [whole(a) for a in args[:4]]
+    specs += [pl.BlockSpec((rows, a.shape[1]), lambda j, s: (j, 0)) for a in args[4:]]
     terms = jax.ShapeDtypeStruct((depth, tokens), BF)
     line = jax.ShapeDtypeStruct((1, tokens), F32)
     return call(
         terms_kernel,
         starts,
         args,
-        [whole(a) for a in args[:4]] + [away] * 14,
-        [away, whole(line), whole(line)],
+        specs,
+        [whole(terms), whole(line), whole(line)],
         [terms, line, line],
         2 * tokens * width * depth,
-        [
-            pltpu.VMEM((width, tokens), BF),
-            pltpu.VMEM((2, rows, width), BF),
-            pltpu.VMEM((12, rows, width // 2), BF),
-            pltpu.VMEM((8, rows, tokens), BF),
-            pltpu.SemaphoreType.DMA((14,)),
-            pltpu.SemaphoreType.DMA((8,)),
-        ],
-        steps=1,
-        room=ROOM,
+        [pltpu.VMEM((width, tokens), BF)],
     )
 
 

time: 207 us -> 203 us (0.981)
  Pallas kernels: 37.4 us -> 33.7 us
    pallas_call x6, Pallas kernels: 37.4 us -> 33.7 us  [call(): pl.pallas_call(kernel, grid_spec=pltpu.PrefetchScalarGridSpec(num_scalar_...]
where the time goes in v7:
time: 203 us; the launch traced here: 202 us
  waiting for transfers between devices  97.7 us (48%)
  starting transfers between devices  55.9 us (28%)
  Pallas kernels  33.7 us (17%)
  local copies, waits for them, and re-layouts  10.9 us (5%)
  other arithmetic  3.11 us (2%)
    ppermute x18, waiting for transfers between devices, shift(): return lax.ppermute(a, axis, [(i, (i + s) % n) for i in range(n)])  83 us
    pallas_call x6, Pallas kernels, call(): pl.pallas_call(kernel, grid_spec=pltpu.PrefetchScalarGridSpec(num_scalar_...  33.7 us
    ppermute x18, starting transfers between devices, shift(): return lax.ppermute(a, axis, [(i, (i + s) % n) for i in range(n)])  27.2 us
    all_to_all x1, starting transfers between devices, step(): parts = lax.all_to_all(stats, ('y', 'z'), 0, 0, tiled=True)  10 us
    all_to_all x1, starting transfers between devices, from_everyone(): lax.all_to_all(jnp.broadcast_to(a[None], (n, *a.shape)), axis, 0, 0, tile...  8.57 us
    all_to_all x1, waiting for transfers between devices, step(): parts = lax.all_to_all(stats, ('y', 'z'), 0, 0, tiled=True)  8.45 us
    all_to_all x1, waiting for transfers between devices, step(): wanted = lax.all_to_all(wanted, ('x', 'core'), 0, 0, tiled=True)  5.72 us
    all_to_all x1, starting transfers between devices, step(): lax.all_to_all(terms.reshape(NY * NZ, part, tokens), ('y', 'z'), 0, 0, ti...  4.85 us
  transfers between devices with their start and end apart: 34, of which 16 were waited for; matrix products, arithmetic and copies ran while one was open for 4% of the time, Pallas kernels for 10%

profile of v7, /device:TPU:32, one launch (start us, length us, event | category | flops | bytes accessed | tf_op | source)
XLA Modules:
  0.0 202.3 jit_solution(15331431578704827524)
XLA Ops:
  0.6 1.5 broadcast_in_dim.12
  2.2 8.6 %all-to-all-start = ((bf16[8,96,128]{2,1,0:T(8,128)(2,1)}), bf16[8,96,128]{2,1,0:T(8,128)(2,1)S(1)}, u32[]{:S(2)}, u32[]{:S(2)}) async-start(bf16[8,96,128]{2,1,0:T(8,128)(2,1)} %broadcast_in_dim.12), calls=%async_computation | async-start | bytes 393216 | tf_op jit(solution)/shard_map/all_to_all | solution.py:27
  10.8 2.1 %slice.8 = bf16[384,1024]{1,0:T(8,128)(2,1)} slice(bf16[384,2048]{1,0:T(8,128)(2,1)} %refs_0_.3), slice={[0:384], [1024:2048]} | slice | bytes 1572864 | tf_op jit(solution)/shard_map/slice | solution.py:326
  12.9 2.8 %collective-permute-start.10 = (bf16[384,1024]{1,0:T(8,128)(2,1)}, bf16[384,1024]{1,0:T(8,128)(2,1)}, u32[]{:S(2)}, u32[]{:S(2)}) collective-permute-start(bf16[384,1024]{1,0:T(8,128)(2,1)} %slice.8), channel_id=1, source_target_pairs={{0,192},{64,0},{128,64},{192,128},{1,193},{65,1},{129,65},{193,129... | collective-permute-start | bytes 2359304 | tf_op jit(solution)/shard_map/ppermute | solution.py:19
  15.6 1.0 slice.6
  16.6 3.2 %collective-permute-start.3 = (bf16[384,1024]{1,0:T(8,128)(2,1)}, bf16[384,1024]{1,0:T(8,128)(2,1)}, u32[]{:S(2)}, u32[]{:S(2)}) collective-permute-start(bf16[384,1024]{1,0:T(8,128)(2,1)} %slice.6), channel_id=1, source_target_pairs={{0,192},{64,0},{128,64},{192,128},{1,193},{65,1},{129,65},{193,129... | collective-permute-start | bytes 2359304 | tf_op jit(solution)/shard_map/ppermute | solution.py:19
  19.8 3.1 %collective-permute-start = (bf16[8,96,128]{2,1,0:T(8,128)(2,1)S(1)}, bf16[8,96,128]{2,1,0:T(8,128)(2,1)S(1)}, u32[]{:S(2)}, u32[]{:S(2)}) collective-permute-start(bf16[8,96,128]{2,1,0:T(8,128)(2,1)S(1)} %all-to-all-done.p0), channel_id=1, source_target_pairs={{0,24},{8,0},{16,8},{24,16},{1,25},{9,1},{17,9},{25,17},{2,26},{10... | collective-permute-start | bytes 589832 | tf_op jit(solution)/shard_map/ppermute | solution.py:19
  22.9 3.2 %collective-permute-done.p1 = bf16[8,96,128]{2,1,0:T(8,128)(2,1)S(1)} collective-permute-done((bf16[8,96,128]{2,1,0:T(8,128)(2,1)S(1)}, bf16[8,96,128]{2,1,0:T(8,128)(2,1)S(1)}, u32[]{:S(2)}, u32[]{:S(2)}) %collective-permute-start) | collective-permute-done | bytes 196640 | tf_op jit(solution)/shard_map/ppermute | solution.py:19
  26.1 2.7 %collective-permute-start.1 = (bf16[8,96,128]{2,1,0:T(8,128)(2,1)S(1)}, bf16[8,96,128]{2,1,0:T(8,128)(2,1)S(1)}, u32[]{:S(2)}, u32[]{:S(2)}) collective-permute-start(bf16[8,96,128]{2,1,0:T(8,128)(2,1)S(1)} %all-to-all-done.p0), channel_id=1, source_target_pairs={{0,16},{8,24},{16,0},{24,8},{1,17},{9,25},{17,1},{25,9},{2,18},{10... | collective-permute-start | bytes 589832 | tf_op jit(solution)/shard_map/ppermute | solution.py:19
  28.8 4.5 %collective-permute-done.1.p2 = bf16[8,96,128]{2,1,0:T(8,128)(2,1)S(1)} collective-permute-done((bf16[8,96,128]{2,1,0:T(8,128)(2,1)S(1)}, bf16[8,96,128]{2,1,0:T(8,128)(2,1)S(1)}, u32[]{:S(2)}, u32[]{:S(2)}) %collective-permute-start.1) | collective-permute-done | bytes 196640 | tf_op jit(solution)/shard_map/ppermute | solution.py:19
  33.3 1.0 collective-permute-start.2
  34.3 6.4 %collective-permute-done.2.p3 = bf16[8,96,128]{2,1,0:T(8,128)(2,1)} collective-permute-done((bf16[8,96,128]{2,1,0:T(8,128)(2,1)S(1)}, bf16[8,96,128]{2,1,0:T(8,128)(2,1)}, u32[]{:S(2)}, u32[]{:S(2)}) %collective-permute-start.2) | collective-permute-done | bytes 196640 | tf_op jit(solution)/shard_map/ppermute | solution.py:19
  41.3 7.7 %collective-permute-done.3.refs_0_.refs_4_ = bf16[384,1024]{1,0:T(8,128)(2,1)} collective-permute-done((bf16[384,1024]{1,0:T(8,128)(2,1)}, bf16[384,1024]{1,0:T(8,128)(2,1)}, u32[]{:S(2)}, u32[]{:S(2)}) %collective-permute-start.3) | collective-permute-done | bytes 786464 | tf_op jit(solution)/shard_map/ppermute | solution.py:19
  49.0 1.2 collective-permute-start.12
  50.2 4.2 %collective-permute-done.5.refs_2_.refs_8_ = bf16[384,1024]{1,0:T(8,128)(2,1)} collective-permute-done((bf16[384,1024]{1,0:T(8,128)(2,1)}, bf16[384,1024]{1,0:T(8,128)(2,1)}, u32[]{:S(2)}, u32[]{:S(2)}) %collective-permute-start.5) | collective-permute-done | bytes 786464 | tf_op jit(solution)/shard_map/ppermute | solution.py:19
  55.0 0.7 copy.6.labels
  55.8 0.7 stack.125.who
  56.4 13.8 %collective-permute-done.12.left.refs_6_ = bf16[384,1024]{1,0:T(8,128)(2,1)} collective-permute-done((bf16[384,1024]{1,0:T(8,128)(2,1)}, bf16[384,1024]{1,0:T(8,128)(2,1)}, u32[]{:S(2)}, u32[]{:S(2)}) %collective-permute-start.12) | collective-permute-done | bytes 786464 | tf_op jit(solution)/shard_map/ppermute | solution.py:19
  70.3 1.0 collective-permute-done.14.right.refs_12_
  72.5 3.1 %shard_map.58 = (bf16[8,128,384]{2,1,0:T(8,128)(2,1)}, bf16[8,112,128]{2,1,0:T(8,128)(2,1)}) custom-call(s32[2]{0:T(128)} %pad_add_fusion.1.who, bf16[8,96,128]{2,1,0:T(8,128)(2,1)} %copy-done.4, bf16[8,96,128]{2,1,0:T(8,128)(2,1)} %copy-done.12, bf16[8,96,128]{2,1,0:T(8,128)(2,1)} %copy-done.13, bf16[8,96,128]{2,1,0:T(8,128)(2,1)} %collective-permute-done.2.p3, ...), custom_call_target="tpu_custom_call" | custom-call | flops 1048576 | bytes 4096 | tf_op jit(solution)/shard_map/pallas_call | solution.py:48
  75.6 3.6 %all-to-all-start.1 = ((bf16[8,112,128]{2,1,0:T(8,128)(2,1)}), bf16[8,112,128]{2,1,0:T(8,128)(2,1)S(1)}, u32[]{:S(2)}, u32[]{:S(2)}) async-start(bf16[8,112,128]{2,1,0:T(8,128)(2,1)} %get-tuple-element.14), calls=%async_computation.1 | async-start | bytes 458752 | tf_op jit(solution)/shard_map/all_to_all | solution.py:345
  80.4 5.7 %all-to-all-done.1.p0 = bf16[8,112,128]{2,1,0:T(8,128)(2,1)S(1)} async-done(((bf16[8,112,128]{2,1,0:T(8,128)(2,1)}), bf16[8,112,128]{2,1,0:T(8,128)(2,1)S(1)}, u32[]{:S(2)}, u32[]{:S(2)}) %all-to-all-start.1) | async-done | bytes 229408 | tf_op jit(solution)/shard_map/all_to_all | solution.py:345
  86.1 1.2 copy-done.1
  87.3 5.8 %shard_map.59.refs_4_ = f32[128,2048]{1,0:T(8,128)} custom-call(s32[6]{0:T(128)} %stack.125.who, bf16[8,128,384]{2,1,0:T(8,128)(2,1)} %get-tuple-element.15.states, bf16[384,2048]{1,0:T(8,128)(2,1)} %refs_0_.3, bf16[384,2048]{1,0:T(8,128)(2,1)} %copy-done.1, bf16[384,1024]{1,0:T(8,128)(2,1)} %collective-permute-done.8.refs_2_, ...), custom_call_target="tpu_custom_call" | custom-call | flops 805306368 | bytes 3145728 | tf_op jit(solution)/shard_map/pallas_call | solution.py:48
  93.1 4.7 %shard_map.60.near = f32[128,2048]{1,0:T(8,128)} custom-call(s32[4]{0:T(128)} %pad_add_fusion.2.who, bf16[8,128,384]{2,1,0:T(8,128)(2,1)} %get-tuple-element.15.states, bf16[384,1024]{1,0:T(8,128)(2,1)} %collective-permute-done.3.refs_0_.refs_4_, bf16[384,1024]{1,0:T(8,128)(2,1)} %collective-permute-done.4.refs_1_.refs_5_, ...), custom_call_target="tpu_custom_call" | custom-call | flops 402653184 | bytes 1572864 | tf_op jit(solution)/shard_map/pallas_call | solution.py:48
  97.8 5.2 %shard_map.61 = (bf16[128,2048]{1,0:T(8,128)(2,1)}, f32[32,3,128]{2,1,0:T(4,128)}, f32[1,128]{1,0:T(1,128)}) custom-call(s32[3]{0:T(128)} %pad_add_fusion.who, bf16[8,128,384]{2,1,0:T(8,128)(2,1)} %get-tuple-element.15.states, s32[128,1]{1,0:T(8,128)} %copy.6.labels, f32[128,2048]{1,0:T(8,128)} %shard_map.60.near, ...), custom_call_target="tpu_custom_call" | custom-call | flops 402653184 | bytes 1572864 | tf_op jit(solution)/shard_map/pallas_call | solution.py:48
  103.0 10.0 %all-to-all-start.2 = ((f32[32,3,128]{2,1,0:T(4,128)}), f32[32,3,128]{2,1,0:T(4,128)S(1)}, u32[]{:S(2)}, u32[]{:S(2)}) async-start(f32[32,3,128]{2,1,0:T(4,128)} %get-tuple-element.17), calls=%async_computation.2 | async-start | bytes 131072 | tf_op jit(solution)/shard_map/all_to_all | solution.py:369
  113.7 8.5 %all-to-all-done.2.parts = f32[32,3,128]{2,1,0:T(4,128)S(1)} async-done(((f32[32,3,128]{2,1,0:T(4,128)}), f32[32,3,128]{2,1,0:T(4,128)S(1)}, u32[]{:S(2)}, u32[]{:S(2)}) %all-to-all-start.2) | async-done | bytes 49184 | tf_op jit(solution)/shard_map/all_to_all | solution.py:369
  122.1 0.6 copy-done.8
  122.7 8.5 %shard_map.62 = (bf16[3072,128]{1,0:T(8,128)(2,1)}, f32[1,128]{1,0:T(1,128)}, f32[1,128]{1,0:T(1,128)}) custom-call(s32[9]{0:T(128)} %stack.109.starts, bf16[128,2048]{1,0:T(8,128)(2,1)} %get-tuple-element.16.powers.refs_4_, s32[1,128]{1,0:T(1,128)} %bitcast.31, f32[32,3,128]{2,1,0:T(4,128)} %copy-done.8, f32[1,128]{1,0:T(1,128)} %get-tuple-element.18.peaks, ...), custom_call_target="tpu_custom_call" | custom-call | flops 1610612736 | bytes 6291456 | tf_op jit(solution)/shard_map/pallas_call | solution.py:48
  131.3 4.9 %all-to-all-start.3 = ((bf16[32,96,128]{2,1,0:T(8,128)(2,1)}), bf16[32,96,128]{2,1,0:T(8,128)(2,1)S(1)}, u32[]{:S(2)}, u32[]{:S(2)}) async-start(bf16[32,96,128]{2,1,0:T(8,128)(2,1)} %bitcast.28), calls=%async_computation.3 | async-start | bytes 1572864 | tf_op jit(solution)/shard_map/all_to_all | solution.py:378
  136.1 0.6 collective-permute-start.24
  136.8 2.7 %collective-permute-start.26 = (bf16[128,2048]{1,0:T(8,128)(2,1)S(1)}, bf16[128,2048]{1,0:T(8,128)(2,1)S(1)}, u32[]{:S(2)}, u32[]{:S(2)}) collective-permute-start(bf16[128,2048]{1,0:T(8,128)(2,1)S(1)} %copy-done.2), channel_id=1, source_target_pairs={{0,192},{64,0},{128,64},{192,128},{1,193},{65,1},{129,65},{193,129... | collective-permute-start | bytes 1572872 | tf_op jit(solution)/shard_map/ppermute | solution.py:19
  139.5 2.8 %collective-permute-start.16 = (bf16[8,112,128]{2,1,0:T(8,128)(2,1)S(1)}, bf16[8,112,128]{2,1,0:T(8,128)(2,1)S(1)}, u32[]{:S(2)}, u32[]{:S(2)}) collective-permute-start(bf16[8,112,128]{2,1,0:T(8,128)(2,1)S(1)} %all-to-all-done.1.p0), channel_id=1, source_target_pairs={{0,24},{8,0},{16,8},{24,16},{1,25},{9,1},{17,9},{25,17},{2,26},{10... | collective-permute-start | bytes 688136 | tf_op jit(solution)/shard_map/ppermute | solution.py:19
  142.3 18.0 %collective-permute-done.24.refs_6_ = bf16[128,2048]{1,0:T(8,128)(2,1)S(1)} collective-permute-done((bf16[128,2048]{1,0:T(8,128)(2,1)S(1)}, bf16[128,2048]{1,0:T(8,128)(2,1)S(1)}, u32[]{:S(2)}, u32[]{:S(2)}) %collective-permute-start.24) | collective-permute-done | bytes 524320 | tf_op jit(solution)/shard_map/ppermute | solution.py:19
  160.9 3.1 %collective-permute-start.17 = (bf16[8,112,128]{2,1,0:T(8,128)(2,1)S(1)}, bf16[8,112,128]{2,1,0:T(8,128)(2,1)S(1)}, u32[]{:S(2)}, u32[]{:S(2)}) collective-permute-start(bf16[8,112,128]{2,1,0:T(8,128)(2,1)S(1)} %all-to-all-done.1.p0), channel_id=1, source_target_pairs={{0,16},{8,24},{16,0},{24,8},{1,17},{9,25},{17,1},{25,9},{2,18},{10... | collective-permute-start | bytes 688136 | tf_op jit(solution)/shard_map/ppermute | solution.py:19
  164.0 6.3 %collective-permute-done.17.p2 = bf16[8,112,128]{2,1,0:T(8,128)(2,1)S(1)} collective-permute-done((bf16[8,112,128]{2,1,0:T(8,128)(2,1)S(1)}, bf16[8,112,128]{2,1,0:T(8,128)(2,1)S(1)}, u32[]{:S(2)}, u32[]{:S(2)}) %collective-permute-start.17) | collective-permute-done | bytes 229408 | tf_op jit(solution)/shard_map/ppermute | solution.py:19
  170.4 0.7 copy-done.10
  171.5 1.5 collective-permute-start.18
  173.0 7.4 %collective-permute-done.18.p3 = bf16[8,112,128]{2,1,0:T(8,128)(2,1)S(1)} collective-permute-done((bf16[8,112,128]{2,1,0:T(8,128)(2,1)S(1)}, bf16[8,112,128]{2,1,0:T(8,128)(2,1)S(1)}, u32[]{:S(2)}, u32[]{:S(2)}) %collective-permute-start.18) | collective-permute-done | bytes 229408 | tf_op jit(solution)/shard_map/ppermute | solution.py:19
  180.4 0.7 copy-done.11
  181.4 4.4 %collective-permute-done.20.refs_1_ = f32[2,128]{1,0:T(2,128)S(1)} collective-permute-done((f32[2,128]{1,0:T(2,128)S(1)}, f32[2,128]{1,0:T(2,128)S(1)}, u32[]{:S(2)}, u32[]{:S(2)}) %collective-permute-start.20) | collective-permute-done | bytes 1056 | tf_op jit(solution)/shard_map/ppermute | solution.py:19
  185.9 1.3 collective-permute-start.21
  187.2 2.2 %collective-permute-done.21.refs_2_ = f32[2,128]{1,0:T(2,128)S(1)} collective-permute-done((f32[2,128]{1,0:T(2,128)S(1)}, f32[2,128]{1,0:T(2,128)S(1)}, u32[]{:S(2)}, u32[]{:S(2)}) %collective-permute-start.21) | collective-permute-done | bytes 1056 | tf_op jit(solution)/shard_map/ppermute | solution.py:19
  189.5 0.8 collective-permute-start.22
  190.8 3.7 %collective-permute-done.22.refs_3_ = f32[2,128]{1,0:T(2,128)S(1)} collective-permute-done((f32[2,128]{1,0:T(2,128)S(1)}, f32[2,128]{1,0:T(2,128)S(1)}, u32[]{:S(2)}, u32[]{:S(2)}) %collective-permute-start.22) | collective-permute-done | bytes 1056 | tf_op jit(solution)/shard_map/ppermute | solution.py:19
  195.1 6.4 %shard_map.63 = f32[384,2048]{1,0:T(8,128)} custom-call(s32[10]{0:T(128)} %stack.126.who, bf16[8,112,128]{2,1,0:T(8,128)(2,1)} %copy-done.3, bf16[8,112,128]{2,1,0:T(8,128)(2,1)} %copy-done.9, bf16[8,112,128]{2,1,0:T(8,128)(2,1)} %copy-done.10, bf16[8,112,128]{2,1,0:T(8,128)(2,1)} %copy-done.11, f32[2,128]{1,0:T(2,128)} %copy-done.14, f32[2,128]{1,0:T(2,128)} %copy-done.16, ...), custom_call_target="tpu_custom_call" | custom-call | flops 1610612736 | bytes 6291456 | tf_op jit(solution)/shard_map/pallas_call | solution.py:48
  201.6 0.7 reduce_sum.12
  (80 shorter events, 6.8 us)
Async XLA Ops:
  0.6 15.0 %copy-start = (bf16[384,2048]{1,0:T(8,128)(2,1)S(1)}, bf16[384,2048]{1,0:T(8,128)(2,1)}, u32[]{:S(2)}) copy-start(bf16[384,2048]{1,0:T(8,128)(2,1)} %refs_0_.3) | copy-start | bytes 4718596
  2.2 17.6 %all-to-all-start = ((bf16[8,96,128]{2,1,0:T(8,128)(2,1)}), bf16[8,96,128]{2,1,0:T(8,128)(2,1)S(1)}, u32[]{:S(2)}, u32[]{:S(2)}) async-start(bf16[8,96,128]{2,1,0:T(8,128)(2,1)} %broadcast_in_dim.12), calls=%async_computation | async-start | bytes 393216 | tf_op jit(solution)/shard_map/all_to_all | solution.py:27
  10.8 44.3 %copy-start.15 = (s32[128]{0:T(128)S(1)}, s32[128]{0:T(128)}, u32[]{:S(2)}) copy-start(s32[128]{0:T(128)} %param.5) | copy-start | bytes 1540
  12.9 27.9 %collective-permute-start.10 = (bf16[384,1024]{1,0:T(8,128)(2,1)}, bf16[384,1024]{1,0:T(8,128)(2,1)}, u32[]{:S(2)}, u32[]{:S(2)}) collective-permute-start(bf16[384,1024]{1,0:T(8,128)(2,1)} %slice.8), channel_id=1, source_target_pairs={{0,192},{64,0},{128,64},{192,128},{1,193},{65,1},{129,65},{193,129... | collective-permute-start | bytes 2359304 | tf_op jit(solution)/shard_map/ppermute | solution.py:19
  16.6 24.7 %collective-permute-start.8 = (bf16[384,1024]{1,0:T(8,128)(2,1)}, bf16[384,1024]{1,0:T(8,128)(2,1)}, u32[]{:S(2)}, u32[]{:S(2)}) collective-permute-start(bf16[384,1024]{1,0:T(8,128)(2,1)} %slice.6), channel_id=1, source_target_pairs={{0,64},{64,128},{128,192},{192,0},{1,65},{65,129},{129,193},{193,1... | collective-permute-start | bytes 2359304 | tf_op jit(solution)/shard_map/ppermute | solution.py:19
  16.6 32.5 %collective-permute-start.3 = (bf16[384,1024]{1,0:T(8,128)(2,1)}, bf16[384,1024]{1,0:T(8,128)(2,1)}, u32[]{:S(2)}, u32[]{:S(2)}) collective-permute-start(bf16[384,1024]{1,0:T(8,128)(2,1)} %slice.6), channel_id=1, source_target_pairs={{0,192},{64,0},{128,64},{192,128},{1,193},{65,1},{129,65},{193,129... | collective-permute-start | bytes 2359304 | tf_op jit(solution)/shard_map/ppermute | solution.py:19
  19.8 34.7 %collective-permute-start.5 = (bf16[384,1024]{1,0:T(8,128)(2,1)}, bf16[384,1024]{1,0:T(8,128)(2,1)}, u32[]{:S(2)}, u32[]{:S(2)}) collective-permute-start(bf16[384,1024]{1,0:T(8,128)(2,1)} %slice.8), channel_id=1, source_target_pairs={{0,64},{64,128},{128,192},{192,0},{1,65},{65,129},{129,193},{193,1... | collective-permute-start | bytes 2359304 | tf_op jit(solution)/shard_map/ppermute | solution.py:19
  19.8 52.7 %copy-start.4 = (bf16[8,96,128]{2,1,0:T(8,128)(2,1)}, bf16[8,96,128]{2,1,0:T(8,128)(2,1)S(1)}, u32[]{:S(2)}) copy-start(bf16[8,96,128]{2,1,0:T(8,128)(2,1)S(1)} %all-to-all-done.p0) | copy-start | bytes 589828
  19.8 6.3 %collective-permute-start = (bf16[8,96,128]{2,1,0:T(8,128)(2,1)S(1)}, bf16[8,96,128]{2,1,0:T(8,128)(2,1)S(1)}, u32[]{:S(2)}, u32[]{:S(2)}) collective-permute-start(bf16[8,96,128]{2,1,0:T(8,128)(2,1)S(1)} %all-to-all-done.p0), channel_id=1, source_target_pairs={{0,24},{8,0},{16,8},{24,16},{1,25},{9,1},{17,9},{25,17},{2,26},{10... | collective-permute-start | bytes 589832 | tf_op jit(solution)/shard_map/ppermute | solution.py:19
  26.1 46.4 %copy-start.12 = (bf16[8,96,128]{2,1,0:T(8,128)(2,1)}, bf16[8,96,128]{2,1,0:T(8,128)(2,1)S(1)}, u32[]{:S(2)}) copy-start(bf16[8,96,128]{2,1,0:T(8,128)(2,1)S(1)} %collective-permute-done.p1) | copy-start | bytes 589828
  26.1 7.2 %collective-permute-start.1 = (bf16[8,96,128]{2,1,0:T(8,128)(2,1)S(1)}, bf16[8,96,128]{2,1,0:T(8,128)(2,1)S(1)}, u32[]{:S(2)}, u32[]{:S(2)}) collective-permute-start(bf16[8,96,128]{2,1,0:T(8,128)(2,1)S(1)} %all-to-all-done.p0), channel_id=1, source_target_pairs={{0,16},{8,24},{16,0},{24,8},{1,17},{9,25},{17,1},{25,9},{2,18},{10... | collective-permute-start | bytes 589832 | tf_op jit(solution)/shard_map/ppermute | solution.py:19
  33.3 7.4 %collective-permute-start.2 = (bf16[8,96,128]{2,1,0:T(8,128)(2,1)S(1)}, bf16[8,96,128]{2,1,0:T(8,128)(2,1)}, u32[]{:S(2)}, u32[]{:S(2)}) collective-permute-start(bf16[8,96,128]{2,1,0:T(8,128)(2,1)S(1)} %all-to-all-done.p0), channel_id=1, source_target_pairs={{0,8},{8,16},{16,24},{24,0},{1,9},{9,17},{17,25},{25,1},{2,10},{10... | collective-permute-start | bytes 589832 | tf_op jit(solution)/shard_map/ppermute | solution.py:19
  40.7 45.4 %collective-permute-start.7 = (bf16[384,2048]{1,0:T(8,128)(2,1)S(1)}, bf16[384,2048]{1,0:T(8,128)(2,1)S(1)}, u32[]{:S(2)}, u32[]{:S(2)}) collective-permute-start(bf16[384,2048]{1,0:T(8,128)(2,1)S(1)} %copy-done), channel_id=1, source_target_pairs={{0,32},{32,0},{1,33},{33,1},{2,34},{34,2},{3,35},{35,3},{4,36},{36... | collective-permute-start | bytes 4718600 | tf_op jit(solution)/shard_map/ppermute | solution.py:23
  40.7 13.8 %collective-permute-start.11 = (bf16[384,1024]{1,0:T(8,128)(2,1)}, bf16[384,1024]{1,0:T(8,128)(2,1)}, u32[]{:S(2)}, u32[]{:S(2)}) collective-permute-start(bf16[384,1024]{1,0:T(8,128)(2,1)} %collective-permute-done.10.refs_4_.refs_10_), channel_id=1, source_target_pairs={{0,32},{32,0},{1,33},{33,1},{2,34},{34,2},{3,35},{35,3},{4,36},{36... | collective-permute-start | bytes 2359304 | tf_op jit(solution)/shard_map/ppermute | solution.py:23
  41.3 13.3 %collective-permute-start.9 = (bf16[384,1024]{1,0:T(8,128)(2,1)}, bf16[384,1024]{1,0:T(8,128)(2,1)}, u32[]{:S(2)}, u32[]{:S(2)}) collective-permute-start(bf16[384,1024]{1,0:T(8,128)(2,1)} %collective-permute-done.8.refs_2_), channel_id=1, source_target_pairs={{0,32},{32,0},{1,33},{33,1},{2,34},{34,2},{3,35},{35,3},{4,36},{36... | collective-permute-start | bytes 2359304 | tf_op jit(solution)/shard_map/ppermute | solution.py:23
  49.0 21.2 %collective-permute-start.12 = (bf16[384,1024]{1,0:T(8,128)(2,1)}, bf16[384,1024]{1,0:T(8,128)(2,1)}, u32[]{:S(2)}, u32[]{:S(2)}) collective-permute-start(bf16[384,1024]{1,0:T(8,128)(2,1)} %collective-permute-done.8.refs_2_), channel_id=1, source_target_pairs={{0,64},{64,128},{128,192},{192,0},{1,65},{65,129},{129,193},{193,1... | collective-permute-start | bytes 2359304 | tf_op jit(solution)/shard_map/ppermute | solution.py:19
  54.5 16.8 %collective-permute-start.14 = (bf16[384,1024]{1,0:T(8,128)(2,1)}, bf16[384,1024]{1,0:T(8,128)(2,1)}, u32[]{:S(2)}, u32[]{:S(2)}) collective-permute-start(bf16[384,1024]{1,0:T(8,128)(2,1)} %collective-permute-done.10.refs_4_.refs_10_), channel_id=1, source_target_pairs={{0,192},{64,0},{128,64},{192,128},{1,193},{65,1},{129,65},{193,129... | collective-permute-start | bytes 2359304 | tf_op jit(solution)/shard_map/ppermute | solution.py:19
  54.5 38.6 %collective-permute-start.4 = (bf16[384,1024]{1,0:T(8,128)(2,1)}, bf16[384,1024]{1,0:T(8,128)(2,1)}, u32[]{:S(2)}, u32[]{:S(2)}) collective-permute-start(bf16[384,1024]{1,0:T(8,128)(2,1)} %collective-permute-done.3.refs_0_.refs_4_), channel_id=1, source_target_pairs={{0,32},{32,0},{1,33},{33,1},{2,34},{34,2},{3,35},{35,3},{4,36},{36... | collective-permute-start | bytes 2359304 | tf_op jit(solution)/shard_map/ppermute | solution.py:23
  54.5 38.5 %collective-permute-start.6 = (bf16[384,1024]{1,0:T(8,128)(2,1)}, bf16[384,1024]{1,0:T(8,128)(2,1)}, u32[]{:S(2)}, u32[]{:S(2)}) collective-permute-start(bf16[384,1024]{1,0:T(8,128)(2,1)} %collective-permute-done.5.refs_2_.refs_8_), channel_id=1, source_target_pairs={{0,32},{32,0},{1,33},{33,1},{2,34},{34,2},{3,35},{35,3},{4,36},{36... | collective-permute-start | bytes 2359304 | tf_op jit(solution)/shard_map/ppermute | solution.py:23
  70.3 27.5 %collective-permute-start.13 = (bf16[384,1024]{1,0:T(8,128)(2,1)}, bf16[384,1024]{1,0:T(8,128)(2,1)}, u32[]{:S(2)}, u32[]{:S(2)}) collective-permute-start(bf16[384,1024]{1,0:T(8,128)(2,1)} %collective-permute-done.12.left.refs_6_), channel_id=1, source_target_pairs={{0,32},{32,0},{1,33},{33,1},{2,34},{34,2},{3,35},{35,3},{4,36},{36... | collective-permute-start | bytes 2359304 | tf_op jit(solution)/shard_map/ppermute | solution.py:23
  71.3 26.5 %collective-permute-start.15 = (bf16[384,1024]{1,0:T(8,128)(2,1)}, bf16[384,1024]{1,0:T(8,128)(2,1)}, u32[]{:S(2)}, u32[]{:S(2)}) collective-permute-start(bf16[384,1024]{1,0:T(8,128)(2,1)} %collective-permute-done.14.right.refs_12_), channel_id=1, source_target_pairs={{0,32},{32,0},{1,33},{33,1},{2,34},{34,2},{3,35},{35,3},{4,36},{36... | collective-permute-start | bytes 2359304 | tf_op jit(solution)/shard_map/ppermute | solution.py:23
  75.6 10.5 %all-to-all-start.1 = ((bf16[8,112,128]{2,1,0:T(8,128)(2,1)}), bf16[8,112,128]{2,1,0:T(8,128)(2,1)S(1)}, u32[]{:S(2)}, u32[]{:S(2)}) async-start(bf16[8,112,128]{2,1,0:T(8,128)(2,1)} %get-tuple-element.14), calls=%async_computation.1 | async-start | bytes 458752 | tf_op jit(solution)/shard_map/all_to_all | solution.py:345
  86.1 85.4 %copy-start.3 = (bf16[8,112,128]{2,1,0:T(8,128)(2,1)}, bf16[8,112,128]{2,1,0:T(8,128)(2,1)S(1)}, u32[]{:S(2)}) copy-start(bf16[8,112,128]{2,1,0:T(8,128)(2,1)S(1)} %all-to-all-done.1.p0) | copy-start | bytes 688132
  103.0 19.1 %all-to-all-start.2 = ((f32[32,3,128]{2,1,0:T(4,128)}), f32[32,3,128]{2,1,0:T(4,128)S(1)}, u32[]{:S(2)}, u32[]{:S(2)}) async-start(f32[32,3,128]{2,1,0:T(4,128)} %get-tuple-element.17), calls=%async_computation.2 | async-start | bytes 131072 | tf_op jit(solution)/shard_map/all_to_all | solution.py:369
  131.3 4.9 %copy-start.2 = (bf16[128,2048]{1,0:T(8,128)(2,1)S(1)}, bf16[128,2048]{1,0:T(8,128)(2,1)}, u32[]{:S(2)}) copy-start(bf16[128,2048]{1,0:T(8,128)(2,1)} %get-tuple-element.16.powers.refs_4_) | copy-start | bytes 1572868
  131.3 39.1 %copy-start.19 = (f32[1,128]{1,0:T(1,128)S(1)}, f32[1,128]{1,0:T(1,128)}, u32[]{:S(2)}) copy-start(f32[1,128]{1,0:T(1,128)} %get-tuple-element.22) | copy-start | bytes 1540
  131.3 70.3 %all-to-all-start.3 = ((bf16[32,96,128]{2,1,0:T(8,128)(2,1)}), bf16[32,96,128]{2,1,0:T(8,128)(2,1)S(1)}, u32[]{:S(2)}, u32[]{:S(2)}) async-start(bf16[32,96,128]{2,1,0:T(8,128)(2,1)} %bitcast.28), calls=%async_computation.3 | async-start | bytes 1572864 | tf_op jit(solution)/shard_map/all_to_all | solution.py:378
  136.1 24.1 %collective-permute-start.24 = (bf16[128,2048]{1,0:T(8,128)(2,1)S(1)}, bf16[128,2048]{1,0:T(8,128)(2,1)S(1)}, u32[]{:S(2)}, u32[]{:S(2)}) collective-permute-start(bf16[128,2048]{1,0:T(8,128)(2,1)S(1)} %copy-done.2), channel_id=1, source_target_pairs={{0,64},{64,128},{128,192},{192,0},{1,65},{65,129},{129,193},{193,1... | collective-permute-start | bytes 1572872 | tf_op jit(solution)/shard_map/ppermute | solution.py:19
  136.8 23.5 %collective-permute-start.26 = (bf16[128,2048]{1,0:T(8,128)(2,1)S(1)}, bf16[128,2048]{1,0:T(8,128)(2,1)S(1)}, u32[]{:S(2)}, u32[]{:S(2)}) collective-permute-start(bf16[128,2048]{1,0:T(8,128)(2,1)S(1)} %copy-done.2), channel_id=1, source_target_pairs={{0,192},{64,0},{128,64},{192,128},{1,193},{65,1},{129,65},{193,129... | collective-permute-start | bytes 1572872 | tf_op jit(solution)/shard_map/ppermute | solution.py:19
  139.5 21.4 %collective-permute-start.28 = (bf16[128,2048]{1,0:T(8,128)(2,1)S(1)}, bf16[128,2048]{1,0:T(8,128)(2,1)S(1)}, u32[]{:S(2)}, u32[]{:S(2)}) collective-permute-start(bf16[128,2048]{1,0:T(8,128)(2,1)S(1)} %copy-done.2), channel_id=1, source_target_pairs={{0,128},{64,192},{128,0},{192,64},{1,129},{65,193},{129,1},{193,65... | collective-permute-start | bytes 1572872 | tf_op jit(solution)/shard_map/ppermute | solution.py:19
  139.5 21.5 %collective-permute-start.16 = (bf16[8,112,128]{2,1,0:T(8,128)(2,1)S(1)}, bf16[8,112,128]{2,1,0:T(8,128)(2,1)S(1)}, u32[]{:S(2)}, u32[]{:S(2)}) collective-permute-start(bf16[8,112,128]{2,1,0:T(8,128)(2,1)S(1)} %all-to-all-done.1.p0), channel_id=1, source_target_pairs={{0,24},{8,0},{16,8},{24,16},{1,25},{9,1},{17,9},{25,17},{2,26},{10... | collective-permute-start | bytes 688136 | tf_op jit(solution)/shard_map/ppermute | solution.py:19
  142.3 52.2 %collective-permute-start.23 = (bf16[128,2048]{1,0:T(8,128)(2,1)S(1)}, bf16[128,2048]{1,0:T(8,128)(2,1)}, u32[]{:S(2)}, u32[]{:S(2)}) collective-permute-start(bf16[128,2048]{1,0:T(8,128)(2,1)S(1)} %copy-done.2), channel_id=1, source_target_pairs={{0,32},{32,0},{1,33},{33,1},{2,34},{34,2},{3,35},{35,3},{4,36},{36... | collective-permute-start | bytes 1572872 | tf_op jit(solution)/shard_map/ppermute | solution.py:23
  160.3 34.3 %copy-start.5 = (bf16[128,2048]{1,0:T(8,128)(2,1)}, bf16[128,2048]{1,0:T(8,128)(2,1)S(1)}, u32[]{:S(2)}) copy-start(bf16[128,2048]{1,0:T(8,128)(2,1)S(1)} %collective-permute-done.24.refs_6_) | copy-start | bytes 1572868
  160.3 34.2 %collective-permute-start.25 = (bf16[128,2048]{1,0:T(8,128)(2,1)S(1)}, bf16[128,2048]{1,0:T(8,128)(2,1)}, u32[]{:S(2)}, u32[]{:S(2)}) collective-permute-start(bf16[128,2048]{1,0:T(8,128)(2,1)S(1)} %collective-permute-done.24.refs_6_), channel_id=1, source_target_pairs={{0,32},{32,0},{1,33},{33,1},{2,34},{34,2},{3,35},{35,3},{4,36},{36... | collective-permute-start | bytes 1572872 | tf_op jit(solution)/shard_map/ppermute | solution.py:23
  160.3 34.3 %copy-start.6 = (bf16[128,2048]{1,0:T(8,128)(2,1)}, bf16[128,2048]{1,0:T(8,128)(2,1)S(1)}, u32[]{:S(2)}) copy-start(bf16[128,2048]{1,0:T(8,128)(2,1)S(1)} %collective-permute-done.26.refs_8_) | copy-start | bytes 1572868
  160.3 34.2 %collective-permute-start.27 = (bf16[128,2048]{1,0:T(8,128)(2,1)S(1)}, bf16[128,2048]{1,0:T(8,128)(2,1)}, u32[]{:S(2)}, u32[]{:S(2)}) collective-permute-start(bf16[128,2048]{1,0:T(8,128)(2,1)S(1)} %collective-permute-done.26.refs_8_), channel_id=1, source_target_pairs={{0,32},{32,0},{1,33},{33,1},{2,34},{34,2},{3,35},{35,3},{4,36},{36... | collective-permute-start | bytes 1572872 | tf_op jit(solution)/shard_map/ppermute | solution.py:23
  160.8 33.8 %copy-start.7 = (bf16[128,2048]{1,0:T(8,128)(2,1)}, bf16[128,2048]{1,0:T(8,128)(2,1)S(1)}, u32[]{:S(2)}) copy-start(bf16[128,2048]{1,0:T(8,128)(2,1)S(1)} %collective-permute-done.28.refs_10_) | copy-start | bytes 1572868
  160.8 33.7 %collective-permute-start.29 = (bf16[128,2048]{1,0:T(8,128)(2,1)S(1)}, bf16[128,2048]{1,0:T(8,128)(2,1)}, u32[]{:S(2)}, u32[]{:S(2)}) collective-permute-start(bf16[128,2048]{1,0:T(8,128)(2,1)S(1)} %collective-permute-done.28.refs_10_), channel_id=1, source_target_pairs={{0,32},{32,0},{1,33},{33,1},{2,34},{34,2},{3,35},{35,3},{4,36},{36... | collective-permute-start | bytes 1572872 | tf_op jit(solution)/shard_map/ppermute | solution.py:23
  160.9 33.7 %copy-start.9 = (bf16[8,112,128]{2,1,0:T(8,128)(2,1)}, bf16[8,112,128]{2,1,0:T(8,128)(2,1)S(1)}, u32[]{:S(2)}) copy-start(bf16[8,112,128]{2,1,0:T(8,128)(2,1)S(1)} %collective-permute-done.16.p1) | copy-start | bytes 688132
  160.9 9.4 %collective-permute-start.17 = (bf16[8,112,128]{2,1,0:T(8,128)(2,1)S(1)}, bf16[8,112,128]{2,1,0:T(8,128)(2,1)S(1)}, u32[]{:S(2)}, u32[]{:S(2)}) collective-permute-start(bf16[8,112,128]{2,1,0:T(8,128)(2,1)S(1)} %all-to-all-done.1.p0), channel_id=1, source_target_pairs={{0,16},{8,24},{16,0},{24,8},{1,17},{9,25},{17,1},{25,9},{2,18},{10... | collective-permute-start | bytes 688136 | tf_op jit(solution)/shard_map/ppermute | solution.py:19
  170.4 1.2 collective-permute-start.19
  171.5 8.9 %collective-permute-start.18 = (bf16[8,112,128]{2,1,0:T(8,128)(2,1)S(1)}, bf16[8,112,128]{2,1,0:T(8,128)(2,1)S(1)}, u32[]{:S(2)}, u32[]{:S(2)}) collective-permute-start(bf16[8,112,128]{2,1,0:T(8,128)(2,1)S(1)} %all-to-all-done.1.p0), channel_id=1, source_target_pairs={{0,8},{8,16},{16,24},{24,0},{1,9},{9,17},{17,25},{25,1},{2,10},{10... | collective-permute-start | bytes 688136 | tf_op jit(solution)/shard_map/ppermute | solution.py:19
  173.0 21.6 %copy-start.14 = (f32[2,128]{1,0:T(2,128)}, f32[2,128]{1,0:T(2,128)S(1)}, u32[]{:S(2)}) copy-start(f32[2,128]{1,0:T(2,128)S(1)} %pad_maximum_fusion.refs_0_) | copy-start | bytes 3076
  181.1 4.8 %collective-permute-start.20 = (f32[2,128]{1,0:T(2,128)S(1)}, f32[2,128]{1,0:T(2,128)S(1)}, u32[]{:S(2)}, u32[]{:S(2)}) collective-permute-start(f32[2,128]{1,0:T(2,128)S(1)} %pad_maximum_fusion.refs_0_), channel_id=1, source_target_pairs={{0,64},{64,128},{128,192},{192,0},{1,65},{65,129},{129,193},{193,1... | collective-permute-start | bytes 3080 | tf_op jit(solution)/shard_map/ppermute | solution.py:19
  185.9 8.7 %copy-start.16 = (f32[2,128]{1,0:T(2,128)}, f32[2,128]{1,0:T(2,128)S(1)}, u32[]{:S(2)}) copy-start(f32[2,128]{1,0:T(2,128)S(1)} %collective-permute-done.20.refs_1_) | copy-start | bytes 3076
  185.9 3.6 %collective-permute-start.21 = (f32[2,128]{1,0:T(2,128)S(1)}, f32[2,128]{1,0:T(2,128)S(1)}, u32[]{:S(2)}, u32[]{:S(2)}) collective-permute-start(f32[2,128]{1,0:T(2,128)S(1)} %pad_maximum_fusion.refs_0_), channel_id=1, source_target_pairs={{0,192},{64,0},{128,64},{192,128},{1,193},{65,1},{129,65},{193,129... | collective-permute-start | bytes 3080 | tf_op jit(solution)/shard_map/ppermute | solution.py:19
  189.4 5.2 %copy-start.17 = (f32[2,128]{1,0:T(2,128)}, f32[2,128]{1,0:T(2,128)S(1)}, u32[]{:S(2)}) copy-start(f32[2,128]{1,0:T(2,128)S(1)} %collective-permute-done.21.refs_2_) | copy-start | bytes 3076
  189.5 5.1 %collective-permute-start.22 = (f32[2,128]{1,0:T(2,128)S(1)}, f32[2,128]{1,0:T(2,128)S(1)}, u32[]{:S(2)}, u32[]{:S(2)}) collective-permute-start(f32[2,128]{1,0:T(2,128)S(1)} %pad_maximum_fusion.refs_0_), channel_id=1, source_target_pairs={{0,128},{64,192},{128,0},{192,64},{1,129},{65,193},{129,1},{193,65... | collective-permute-start | bytes 3080 | tf_op jit(solution)/shard_map/ppermute | solution.py:19
  (6 other events, 4.8 us)

commit v8 on v7

--- a/solution.py
+++ b/solution.py
@@ -323,7 +323,7 @@
         return [chip + core, chip + 1 - core]
 
     left_half = head[:, :half]
-    right_half = lax.optimization_barrier(head)[:, half:]
+    right_half = head[:, half:]
     up_left = shift(left_half, "x", NX, 1)
     down_right = shift(right_half, "x", NX, -1)
     up_right = shift(right_half, "x", NX, 1)
@@ -345,7 +345,9 @@
     wanted = lax.all_to_all(wanted, ("x", "core"), 0, 0, tiled=True)
     far_states, wanted = lax.optimization_barrier((states, wanted))
 
-    slices = [wanted] + [shift(wanted, "y", NY, -j) for j in (1, 2, 3)]
+    slices = [shift(wanted, "y", NY, -j) for j in (1, 3)]
+    across = shift(wanted, "y", NY, -2)
+    slices = [wanted, slices[0], across, slices[1]]
     logits = logits_part(
         states,
         own,

time: 203 us -> 203 us (level)
  transfers between devices with their start and end apart: 34 -> 34, of which waited for: 16 -> 17; matrix products, arithmetic and copies ran while one was open for 4% -> 4% of each run, Pallas kernels for 10% -> 10%
where the time goes in v8:
time: 203 us; the launch traced here: 202 us
  waiting for transfers between devices  97.8 us (48%)
  starting transfers between devices  56 us (28%)
  Pallas kernels  33.8 us (17%)
  local copies, waits for them, and re-layouts  10.3 us (5%)
  other arithmetic  3.11 us (2%)
    ppermute x18, waiting for transfers between devices, shift(): return lax.ppermute(a, axis, [(i, (i + s) % n) for i in range(n)])  82.8 us
    pallas_call x6, Pallas kernels, call(): pl.pallas_call(kernel, grid_spec=pltpu.PrefetchScalarGridSpec(num_scalar_...  33.8 us
    ppermute x18, starting transfers between devices, shift(): return lax.ppermute(a, axis, [(i, (i + s) % n) for i in range(n)])  27.3 us
    all_to_all x1, starting transfers between devices, step(): parts = lax.all_to_all(stats, ('y', 'z'), 0, 0, tiled=True)  10 us
    all_to_all x1, starting transfers between devices, from_everyone(): lax.all_to_all(jnp.broadcast_to(a[None], (n, *a.shape)), axis, 0, 0, tile...  8.57 us
    all_to_all x1, waiting for transfers between devices, step(): parts = lax.all_to_all(stats, ('y', 'z'), 0, 0, tiled=True)  8.49 us
    all_to_all x1, waiting for transfers between devices, step(): wanted = lax.all_to_all(wanted, ('x', 'core'), 0, 0, tiled=True)  5.72 us
    all_to_all x1, starting transfers between devices, step(): lax.all_to_all(terms.reshape(NY * NZ, part, tokens), ('y', 'z'), 0, 0, ti...  4.86 us
  transfers between devices with their start and end apart: 34, of which 17 were waited for; matrix products, arithmetic and copies ran while one was open for 4% of the time, Pallas kernels for 10%

profile of v8, /device:TPU:32, one launch (start us, length us, event | category | flops | bytes accessed | tf_op | source)
XLA Modules:
  0.0 201.9 jit_solution(3333966070646640656)
XLA Ops:
  0.6 1.4 broadcast_in_dim.12
  2.1 8.6 %all-to-all-start = ((bf16[8,96,128]{2,1,0:T(8,128)(2,1)}), bf16[8,96,128]{2,1,0:T(8,128)(2,1)S(1)}, u32[]{:S(2)}, u32[]{:S(2)}) async-start(bf16[8,96,128]{2,1,0:T(8,128)(2,1)} %broadcast_in_dim.12), calls=%async_computation | async-start | bytes 393216 | tf_op jit(solution)/shard_map/all_to_all | solution.py:27
  10.6 2.8 %fusion.5 = (bf16[384,1024]{1,0:T(8,128)(2,1)}, bf16[384,1024]{1,0:T(8,128)(2,1)}) fusion(bf16[384,2048]{1,0:T(8,128)(2,1)} %refs_0_.3), kind=kLoop, calls=%fused_computation.16 | loop fusion | bytes 3145728 | tf_op jit(solution)/shard_map/slice | solution.py:326
  13.4 2.8 %collective-permute-start.10 = (bf16[384,1024]{1,0:T(8,128)(2,1)}, bf16[384,1024]{1,0:T(8,128)(2,1)}, u32[]{:S(2)}, u32[]{:S(2)}) collective-permute-start(bf16[384,1024]{1,0:T(8,128)(2,1)} %get-tuple-element.23), channel_id=1, source_target_pairs={{0,192},{64,0},{128,64},{192,128},{1,193},{65,1},{129,65},{193,129... | collective-permute-start | bytes 2359304 | tf_op jit(solution)/shard_map/ppermute | solution.py:19
  16.2 3.2 %collective-permute-start.3 = (bf16[384,1024]{1,0:T(8,128)(2,1)}, bf16[384,1024]{1,0:T(8,128)(2,1)}, u32[]{:S(2)}, u32[]{:S(2)}) collective-permute-start(bf16[384,1024]{1,0:T(8,128)(2,1)} %get-tuple-element.24), channel_id=1, source_target_pairs={{0,192},{64,0},{128,64},{192,128},{1,193},{65,1},{129,65},{193,129... | collective-permute-start | bytes 2359304 | tf_op jit(solution)/shard_map/ppermute | solution.py:19
  19.7 3.0 %collective-permute-start = (bf16[8,96,128]{2,1,0:T(8,128)(2,1)S(1)}, bf16[8,96,128]{2,1,0:T(8,128)(2,1)S(1)}, u32[]{:S(2)}, u32[]{:S(2)}) collective-permute-start(bf16[8,96,128]{2,1,0:T(8,128)(2,1)S(1)} %all-to-all-done.p0), channel_id=1, source_target_pairs={{0,24},{8,0},{16,8},{24,16},{1,25},{9,1},{17,9},{25,17},{2,26},{10... | collective-permute-start | bytes 589832 | tf_op jit(solution)/shard_map/ppermute | solution.py:19
  22.7 3.2 %collective-permute-done.p1 = bf16[8,96,128]{2,1,0:T(8,128)(2,1)S(1)} collective-permute-done((bf16[8,96,128]{2,1,0:T(8,128)(2,1)S(1)}, bf16[8,96,128]{2,1,0:T(8,128)(2,1)S(1)}, u32[]{:S(2)}, u32[]{:S(2)}) %collective-permute-start) | collective-permute-done | bytes 196640 | tf_op jit(solution)/shard_map/ppermute | solution.py:19
  25.9 2.7 %collective-permute-start.1 = (bf16[8,96,128]{2,1,0:T(8,128)(2,1)S(1)}, bf16[8,96,128]{2,1,0:T(8,128)(2,1)S(1)}, u32[]{:S(2)}, u32[]{:S(2)}) collective-permute-start(bf16[8,96,128]{2,1,0:T(8,128)(2,1)S(1)} %all-to-all-done.p0), channel_id=1, source_target_pairs={{0,16},{8,24},{16,0},{24,8},{1,17},{9,25},{17,1},{25,9},{2,18},{10... | collective-permute-start | bytes 589832 | tf_op jit(solution)/shard_map/ppermute | solution.py:19
  28.5 4.5 %collective-permute-done.1.p2 = bf16[8,96,128]{2,1,0:T(8,128)(2,1)S(1)} collective-permute-done((bf16[8,96,128]{2,1,0:T(8,128)(2,1)S(1)}, bf16[8,96,128]{2,1,0:T(8,128)(2,1)S(1)}, u32[]{:S(2)}, u32[]{:S(2)}) %collective-permute-start.1) | collective-permute-done | bytes 196640 | tf_op jit(solution)/shard_map/ppermute | solution.py:19
  33.0 1.0 collective-permute-start.2
  34.1 6.4 %collective-permute-done.2.p3 = bf16[8,96,128]{2,1,0:T(8,128)(2,1)} collective-permute-done((bf16[8,96,128]{2,1,0:T(8,128)(2,1)S(1)}, bf16[8,96,128]{2,1,0:T(8,128)(2,1)}, u32[]{:S(2)}, u32[]{:S(2)}) %collective-permute-start.2) | collective-permute-done | bytes 196640 | tf_op jit(solution)/shard_map/ppermute | solution.py:19
  41.1 8.5 %collective-permute-done.3.refs_0_.refs_4_ = bf16[384,1024]{1,0:T(8,128)(2,1)} collective-permute-done((bf16[384,1024]{1,0:T(8,128)(2,1)}, bf16[384,1024]{1,0:T(8,128)(2,1)}, u32[]{:S(2)}, u32[]{:S(2)}) %collective-permute-start.3) | collective-permute-done | bytes 786464 | tf_op jit(solution)/shard_map/ppermute | solution.py:19
  49.6 1.2 collective-permute-start.12
  50.8 2.3 %collective-permute-done.5.refs_2_.refs_8_ = bf16[384,1024]{1,0:T(8,128)(2,1)} collective-permute-done((bf16[384,1024]{1,0:T(8,128)(2,1)}, bf16[384,1024]{1,0:T(8,128)(2,1)}, u32[]{:S(2)}, u32[]{:S(2)}) %collective-permute-start.5) | collective-permute-done | bytes 786464 | tf_op jit(solution)/shard_map/ppermute | solution.py:19
  53.8 0.7 copy.6.labels
  55.1 14.7 %collective-permute-done.12.left.refs_6_ = bf16[384,1024]{1,0:T(8,128)(2,1)} collective-permute-done((bf16[384,1024]{1,0:T(8,128)(2,1)}, bf16[384,1024]{1,0:T(8,128)(2,1)}, u32[]{:S(2)}, u32[]{:S(2)}) %collective-permute-start.12) | collective-permute-done | bytes 786464 | tf_op jit(solution)/shard_map/ppermute | solution.py:19
  69.8 1.0 collective-permute-done.14.right.refs_12_
  71.5 0.6 fusion.2.digits
  72.1 3.1 %shard_map.58 = (bf16[8,128,384]{2,1,0:T(8,128)(2,1)}, bf16[8,112,128]{2,1,0:T(8,128)(2,1)}) custom-call(s32[2]{0:T(128)} %pad_add_fusion.1.who, bf16[8,96,128]{2,1,0:T(8,128)(2,1)} %copy-done.4, bf16[8,96,128]{2,1,0:T(8,128)(2,1)} %copy-done.12, bf16[8,96,128]{2,1,0:T(8,128)(2,1)} %copy-done.13, bf16[8,96,128]{2,1,0:T(8,128)(2,1)} %collective-permute-done.2.p3, ...), custom_call_target="tpu_custom_call" | custom-call | flops 1048576 | bytes 4096 | tf_op jit(solution)/shard_map/pallas_call | solution.py:48
  75.2 3.6 %all-to-all-start.1 = ((bf16[8,112,128]{2,1,0:T(8,128)(2,1)}), bf16[8,112,128]{2,1,0:T(8,128)(2,1)S(1)}, u32[]{:S(2)}, u32[]{:S(2)}) async-start(bf16[8,112,128]{2,1,0:T(8,128)(2,1)} %get-tuple-element.14), calls=%async_computation.1 | async-start | bytes 458752 | tf_op jit(solution)/shard_map/all_to_all | solution.py:345
  78.8 0.6 pad_add_fusion.2.who
  79.9 5.7 %all-to-all-done.1.p0 = bf16[8,112,128]{2,1,0:T(8,128)(2,1)S(1)} async-done(((bf16[8,112,128]{2,1,0:T(8,128)(2,1)}), bf16[8,112,128]{2,1,0:T(8,128)(2,1)S(1)}, u32[]{:S(2)}, u32[]{:S(2)}) %all-to-all-start.1) | async-done | bytes 229408 | tf_op jit(solution)/shard_map/all_to_all | solution.py:345
  85.7 1.2 copy-done.1
  86.8 5.8 %shard_map.59.refs_4_ = f32[128,2048]{1,0:T(8,128)} custom-call(s32[6]{0:T(128)} %stack.125.who, bf16[8,128,384]{2,1,0:T(8,128)(2,1)} %get-tuple-element.15.states, bf16[384,2048]{1,0:T(8,128)(2,1)} %refs_0_.3, bf16[384,2048]{1,0:T(8,128)(2,1)} %copy-done.1, bf16[384,1024]{1,0:T(8,128)(2,1)} %collective-permute-done.8.refs_2_, ...), custom_call_target="tpu_custom_call" | custom-call | flops 805306368 | bytes 3145728 | tf_op jit(solution)/shard_map/pallas_call | solution.py:48
  92.7 4.8 %shard_map.60.near = f32[128,2048]{1,0:T(8,128)} custom-call(s32[4]{0:T(128)} %pad_add_fusion.2.who, bf16[8,128,384]{2,1,0:T(8,128)(2,1)} %get-tuple-element.15.states, bf16[384,1024]{1,0:T(8,128)(2,1)} %collective-permute-done.3.refs_0_.refs_4_, bf16[384,1024]{1,0:T(8,128)(2,1)} %collective-permute-done.4.refs_1_.refs_5_, ...), custom_call_target="tpu_custom_call" | custom-call | flops 402653184 | bytes 1572864 | tf_op jit(solution)/shard_map/pallas_call | solution.py:48
  97.5 5.2 %shard_map.61 = (bf16[128,2048]{1,0:T(8,128)(2,1)}, f32[32,3,128]{2,1,0:T(4,128)}, f32[1,128]{1,0:T(1,128)}) custom-call(s32[3]{0:T(128)} %pad_add_fusion.who, bf16[8,128,384]{2,1,0:T(8,128)(2,1)} %get-tuple-element.15.states, s32[128,1]{1,0:T(8,128)} %copy.6.labels, f32[128,2048]{1,0:T(8,128)} %shard_map.60.near, ...), custom_call_target="tpu_custom_call" | custom-call | flops 402653184 | bytes 1572864 | tf_op jit(solution)/shard_map/pallas_call | solution.py:48
  102.7 10.0 %all-to-all-start.2 = ((f32[32,3,128]{2,1,0:T(4,128)}), f32[32,3,128]{2,1,0:T(4,128)S(1)}, u32[]{:S(2)}, u32[]{:S(2)}) async-start(f32[32,3,128]{2,1,0:T(4,128)} %get-tuple-element.17), calls=%async_computation.2 | async-start | bytes 131072 | tf_op jit(solution)/shard_map/all_to_all | solution.py:371
  113.3 8.5 %all-to-all-done.2.parts = f32[32,3,128]{2,1,0:T(4,128)S(1)} async-done(((f32[32,3,128]{2,1,0:T(4,128)}), f32[32,3,128]{2,1,0:T(4,128)S(1)}, u32[]{:S(2)}, u32[]{:S(2)}) %all-to-all-start.2) | async-done | bytes 49184 | tf_op jit(solution)/shard_map/all_to_all | solution.py:371
  121.8 0.6 copy-done.8
  122.4 8.5 %shard_map.62 = (bf16[3072,128]{1,0:T(8,128)(2,1)}, f32[1,128]{1,0:T(1,128)}, f32[1,128]{1,0:T(1,128)}) custom-call(s32[9]{0:T(128)} %stack.109.starts, bf16[128,2048]{1,0:T(8,128)(2,1)} %get-tuple-element.16.powers.refs_4_, s32[1,128]{1,0:T(1,128)} %bitcast.31, f32[32,3,128]{2,1,0:T(4,128)} %copy-done.8, f32[1,128]{1,0:T(1,128)} %get-tuple-element.18.peaks, ...), custom_call_target="tpu_custom_call" | custom-call | flops 1610612736 | bytes 6291456 | tf_op jit(solution)/shard_map/pallas_call | solution.py:48
  130.9 4.9 %all-to-all-start.3 = ((bf16[32,96,128]{2,1,0:T(8,128)(2,1)}), bf16[32,96,128]{2,1,0:T(8,128)(2,1)S(1)}, u32[]{:S(2)}, u32[]{:S(2)}) async-start(bf16[32,96,128]{2,1,0:T(8,128)(2,1)} %bitcast.28), calls=%async_computation.3 | async-start | bytes 1572864 | tf_op jit(solution)/shard_map/all_to_all | solution.py:380
  135.8 0.6 collective-permute-start.24
  136.4 2.7 %collective-permute-start.26 = (bf16[128,2048]{1,0:T(8,128)(2,1)S(1)}, bf16[128,2048]{1,0:T(8,128)(2,1)S(1)}, u32[]{:S(2)}, u32[]{:S(2)}) collective-permute-start(bf16[128,2048]{1,0:T(8,128)(2,1)S(1)} %copy-done.2), channel_id=1, source_target_pairs={{0,192},{64,0},{128,64},{192,128},{1,193},{65,1},{129,65},{193,129... | collective-permute-start | bytes 1572872 | tf_op jit(solution)/shard_map/ppermute | solution.py:19
  139.1 2.8 %collective-permute-start.16 = (bf16[8,112,128]{2,1,0:T(8,128)(2,1)S(1)}, bf16[8,112,128]{2,1,0:T(8,128)(2,1)S(1)}, u32[]{:S(2)}, u32[]{:S(2)}) collective-permute-start(bf16[8,112,128]{2,1,0:T(8,128)(2,1)S(1)} %all-to-all-done.1.p0), channel_id=1, source_target_pairs={{0,24},{8,0},{16,8},{24,16},{1,25},{9,1},{17,9},{25,17},{2,26},{10... | collective-permute-start | bytes 688136 | tf_op jit(solution)/shard_map/ppermute | solution.py:19
  142.0 18.0 %collective-permute-done.24.refs_6_ = bf16[128,2048]{1,0:T(8,128)(2,1)S(1)} collective-permute-done((bf16[128,2048]{1,0:T(8,128)(2,1)S(1)}, bf16[128,2048]{1,0:T(8,128)(2,1)S(1)}, u32[]{:S(2)}, u32[]{:S(2)}) %collective-permute-start.24) | collective-permute-done | bytes 524320 | tf_op jit(solution)/shard_map/ppermute | solution.py:19
  160.6 3.1 %collective-permute-start.17 = (bf16[8,112,128]{2,1,0:T(8,128)(2,1)S(1)}, bf16[8,112,128]{2,1,0:T(8,128)(2,1)S(1)}, u32[]{:S(2)}, u32[]{:S(2)}) collective-permute-start(bf16[8,112,128]{2,1,0:T(8,128)(2,1)S(1)} %all-to-all-done.1.p0), channel_id=1, source_target_pairs={{0,16},{8,24},{16,0},{24,8},{1,17},{9,25},{17,1},{25,9},{2,18},{10... | collective-permute-start | bytes 688136 | tf_op jit(solution)/shard_map/ppermute | solution.py:19
  163.7 6.3 %collective-permute-done.17.p2 = bf16[8,112,128]{2,1,0:T(8,128)(2,1)S(1)} collective-permute-done((bf16[8,112,128]{2,1,0:T(8,128)(2,1)S(1)}, bf16[8,112,128]{2,1,0:T(8,128)(2,1)S(1)}, u32[]{:S(2)}, u32[]{:S(2)}) %collective-permute-start.17) | collective-permute-done | bytes 229408 | tf_op jit(solution)/shard_map/ppermute | solution.py:19
  170.0 0.7 copy-done.10
  171.2 1.5 collective-permute-start.18
  172.7 7.4 %collective-permute-done.18.p3 = bf16[8,112,128]{2,1,0:T(8,128)(2,1)S(1)} collective-permute-done((bf16[8,112,128]{2,1,0:T(8,128)(2,1)S(1)}, bf16[8,112,128]{2,1,0:T(8,128)(2,1)S(1)}, u32[]{:S(2)}, u32[]{:S(2)}) %collective-permute-start.18) | collective-permute-done | bytes 229408 | tf_op jit(solution)/shard_map/ppermute | solution.py:19
  180.1 0.7 copy-done.11
  181.1 4.4 %collective-permute-done.20.refs_1_ = f32[2,128]{1,0:T(2,128)S(1)} collective-permute-done((f32[2,128]{1,0:T(2,128)S(1)}, f32[2,128]{1,0:T(2,128)S(1)}, u32[]{:S(2)}, u32[]{:S(2)}) %collective-permute-start.20) | collective-permute-done | bytes 1056 | tf_op jit(solution)/shard_map/ppermute | solution.py:19
  185.6 1.3 collective-permute-start.21
  186.9 2.2 %collective-permute-done.21.refs_2_ = f32[2,128]{1,0:T(2,128)S(1)} collective-permute-done((f32[2,128]{1,0:T(2,128)S(1)}, f32[2,128]{1,0:T(2,128)S(1)}, u32[]{:S(2)}, u32[]{:S(2)}) %collective-permute-start.21) | collective-permute-done | bytes 1056 | tf_op jit(solution)/shard_map/ppermute | solution.py:19
  189.1 0.8 collective-permute-start.22
  190.5 3.7 %collective-permute-done.22.refs_3_ = f32[2,128]{1,0:T(2,128)S(1)} collective-permute-done((f32[2,128]{1,0:T(2,128)S(1)}, f32[2,128]{1,0:T(2,128)S(1)}, u32[]{:S(2)}, u32[]{:S(2)}) %collective-permute-start.22) | collective-permute-done | bytes 1056 | tf_op jit(solution)/shard_map/ppermute | solution.py:19
  194.7 6.4 %shard_map.63 = f32[384,2048]{1,0:T(8,128)} custom-call(s32[10]{0:T(128)} %stack.126.who, bf16[8,112,128]{2,1,0:T(8,128)(2,1)} %copy-done.3, bf16[8,112,128]{2,1,0:T(8,128)(2,1)} %copy-done.9, bf16[8,112,128]{2,1,0:T(8,128)(2,1)} %copy-done.10, bf16[8,112,128]{2,1,0:T(8,128)(2,1)} %copy-done.11, f32[2,128]{1,0:T(2,128)} %copy-done.14, f32[2,128]{1,0:T(2,128)} %copy-done.16, ...), custom_call_target="tpu_custom_call" | custom-call | flops 1610612736 | bytes 6291456 | tf_op jit(solution)/shard_map/pallas_call | solution.py:48
  201.2 0.7 reduce_sum.12
  (79 shorter events, 6.4 us)
Async XLA Ops:
  2.1 17.6 %all-to-all-start = ((bf16[8,96,128]{2,1,0:T(8,128)(2,1)}), bf16[8,96,128]{2,1,0:T(8,128)(2,1)S(1)}, u32[]{:S(2)}, u32[]{:S(2)}) async-start(bf16[8,96,128]{2,1,0:T(8,128)(2,1)} %broadcast_in_dim.12), calls=%async_computation | async-start | bytes 393216 | tf_op jit(solution)/shard_map/all_to_all | solution.py:27
  10.6 29.8 %copy-start = (bf16[384,2048]{1,0:T(8,128)(2,1)S(1)}, bf16[384,2048]{1,0:T(8,128)(2,1)}, u32[]{:S(2)}) copy-start(bf16[384,2048]{1,0:T(8,128)(2,1)} %refs_0_.3) | copy-start | bytes 4718596
  10.6 43.2 %copy-start.15 = (s32[128]{0:T(128)S(1)}, s32[128]{0:T(128)}, u32[]{:S(2)}) copy-start(s32[128]{0:T(128)} %param.5) | copy-start | bytes 1540
  13.4 27.1 %collective-permute-start.10 = (bf16[384,1024]{1,0:T(8,128)(2,1)}, bf16[384,1024]{1,0:T(8,128)(2,1)}, u32[]{:S(2)}, u32[]{:S(2)}) collective-permute-start(bf16[384,1024]{1,0:T(8,128)(2,1)} %get-tuple-element.23), channel_id=1, source_target_pairs={{0,192},{64,0},{128,64},{192,128},{1,193},{65,1},{129,65},{193,129... | collective-permute-start | bytes 2359304 | tf_op jit(solution)/shard_map/ppermute | solution.py:19
  16.2 24.8 %collective-permute-start.8 = (bf16[384,1024]{1,0:T(8,128)(2,1)}, bf16[384,1024]{1,0:T(8,128)(2,1)}, u32[]{:S(2)}, u32[]{:S(2)}) collective-permute-start(bf16[384,1024]{1,0:T(8,128)(2,1)} %get-tuple-element.24), channel_id=1, source_target_pairs={{0,64},{64,128},{128,192},{192,0},{1,65},{65,129},{129,193},{193,1... | collective-permute-start | bytes 2359304 | tf_op jit(solution)/shard_map/ppermute | solution.py:19
  16.2 33.4 %collective-permute-start.3 = (bf16[384,1024]{1,0:T(8,128)(2,1)}, bf16[384,1024]{1,0:T(8,128)(2,1)}, u32[]{:S(2)}, u32[]{:S(2)}) collective-permute-start(bf16[384,1024]{1,0:T(8,128)(2,1)} %get-tuple-element.24), channel_id=1, source_target_pairs={{0,192},{64,0},{128,64},{192,128},{1,193},{65,1},{129,65},{193,129... | collective-permute-start | bytes 2359304 | tf_op jit(solution)/shard_map/ppermute | solution.py:19
  19.4 33.7 %collective-permute-start.5 = (bf16[384,1024]{1,0:T(8,128)(2,1)}, bf16[384,1024]{1,0:T(8,128)(2,1)}, u32[]{:S(2)}, u32[]{:S(2)}) collective-permute-start(bf16[384,1024]{1,0:T(8,128)(2,1)} %get-tuple-element.23), channel_id=1, source_target_pairs={{0,64},{64,128},{128,192},{192,0},{1,65},{65,129},{129,193},{193,1... | collective-permute-start | bytes 2359304 | tf_op jit(solution)/shard_map/ppermute | solution.py:19
  19.7 52.4 %copy-start.4 = (bf16[8,96,128]{2,1,0:T(8,128)(2,1)}, bf16[8,96,128]{2,1,0:T(8,128)(2,1)S(1)}, u32[]{:S(2)}) copy-start(bf16[8,96,128]{2,1,0:T(8,128)(2,1)S(1)} %all-to-all-done.p0) | copy-start | bytes 589828
  19.7 6.2 %collective-permute-start = (bf16[8,96,128]{2,1,0:T(8,128)(2,1)S(1)}, bf16[8,96,128]{2,1,0:T(8,128)(2,1)S(1)}, u32[]{:S(2)}, u32[]{:S(2)}) collective-permute-start(bf16[8,96,128]{2,1,0:T(8,128)(2,1)S(1)} %all-to-all-done.p0), channel_id=1, source_target_pairs={{0,24},{8,0},{16,8},{24,16},{1,25},{9,1},{17,9},{25,17},{2,26},{10... | collective-permute-start | bytes 589832 | tf_op jit(solution)/shard_map/ppermute | solution.py:19
  25.9 46.2 %copy-start.12 = (bf16[8,96,128]{2,1,0:T(8,128)(2,1)}, bf16[8,96,128]{2,1,0:T(8,128)(2,1)S(1)}, u32[]{:S(2)}) copy-start(bf16[8,96,128]{2,1,0:T(8,128)(2,1)S(1)} %collective-permute-done.p1) | copy-start | bytes 589828
  25.9 7.2 %collective-permute-start.1 = (bf16[8,96,128]{2,1,0:T(8,128)(2,1)S(1)}, bf16[8,96,128]{2,1,0:T(8,128)(2,1)S(1)}, u32[]{:S(2)}, u32[]{:S(2)}) collective-permute-start(bf16[8,96,128]{2,1,0:T(8,128)(2,1)S(1)} %all-to-all-done.p0), channel_id=1, source_target_pairs={{0,16},{8,24},{16,0},{24,8},{1,17},{9,25},{17,1},{25,9},{2,18},{10... | collective-permute-start | bytes 589832 | tf_op jit(solution)/shard_map/ppermute | solution.py:19
  33.0 7.4 %collective-permute-start.2 = (bf16[8,96,128]{2,1,0:T(8,128)(2,1)S(1)}, bf16[8,96,128]{2,1,0:T(8,128)(2,1)}, u32[]{:S(2)}, u32[]{:S(2)}) collective-permute-start(bf16[8,96,128]{2,1,0:T(8,128)(2,1)S(1)} %all-to-all-done.p0), channel_id=1, source_target_pairs={{0,8},{8,16},{16,24},{24,0},{1,9},{9,17},{17,25},{25,1},{2,10},{10... | collective-permute-start | bytes 589832 | tf_op jit(solution)/shard_map/ppermute | solution.py:19
  40.5 45.2 %collective-permute-start.7 = (bf16[384,2048]{1,0:T(8,128)(2,1)S(1)}, bf16[384,2048]{1,0:T(8,128)(2,1)S(1)}, u32[]{:S(2)}, u32[]{:S(2)}) collective-permute-start(bf16[384,2048]{1,0:T(8,128)(2,1)S(1)} %copy-done), channel_id=1, source_target_pairs={{0,32},{32,0},{1,33},{33,1},{2,34},{34,2},{3,35},{35,3},{4,36},{36... | collective-permute-start | bytes 4718600 | tf_op jit(solution)/shard_map/ppermute | solution.py:23
  40.5 12.8 %collective-permute-start.11 = (bf16[384,1024]{1,0:T(8,128)(2,1)}, bf16[384,1024]{1,0:T(8,128)(2,1)}, u32[]{:S(2)}, u32[]{:S(2)}) collective-permute-start(bf16[384,1024]{1,0:T(8,128)(2,1)} %collective-permute-done.10.refs_4_.refs_10_), channel_id=1, source_target_pairs={{0,32},{32,0},{1,33},{33,1},{2,34},{34,2},{3,35},{35,3},{4,36},{36... | collective-permute-start | bytes 2359304 | tf_op jit(solution)/shard_map/ppermute | solution.py:23
  41.0 12.3 %collective-permute-start.9 = (bf16[384,1024]{1,0:T(8,128)(2,1)}, bf16[384,1024]{1,0:T(8,128)(2,1)}, u32[]{:S(2)}, u32[]{:S(2)}) collective-permute-start(bf16[384,1024]{1,0:T(8,128)(2,1)} %collective-permute-done.8.refs_2_), channel_id=1, source_target_pairs={{0,32},{32,0},{1,33},{33,1},{2,34},{34,2},{3,35},{35,3},{4,36},{36... | collective-permute-start | bytes 2359304 | tf_op jit(solution)/shard_map/ppermute | solution.py:23
  49.6 20.3 %collective-permute-start.12 = (bf16[384,1024]{1,0:T(8,128)(2,1)}, bf16[384,1024]{1,0:T(8,128)(2,1)}, u32[]{:S(2)}, u32[]{:S(2)}) collective-permute-start(bf16[384,1024]{1,0:T(8,128)(2,1)} %collective-permute-done.8.refs_2_), channel_id=1, source_target_pairs={{0,64},{64,128},{128,192},{192,0},{1,65},{65,129},{129,193},{193,1... | collective-permute-start | bytes 2359304 | tf_op jit(solution)/shard_map/ppermute | solution.py:19
  53.1 17.8 %collective-permute-start.14 = (bf16[384,1024]{1,0:T(8,128)(2,1)}, bf16[384,1024]{1,0:T(8,128)(2,1)}, u32[]{:S(2)}, u32[]{:S(2)}) collective-permute-start(bf16[384,1024]{1,0:T(8,128)(2,1)} %collective-permute-done.10.refs_4_.refs_10_), channel_id=1, source_target_pairs={{0,192},{64,0},{128,64},{192,128},{1,193},{65,1},{129,65},{193,129... | collective-permute-start | bytes 2359304 | tf_op jit(solution)/shard_map/ppermute | solution.py:19
  53.3 39.4 %collective-permute-start.4 = (bf16[384,1024]{1,0:T(8,128)(2,1)}, bf16[384,1024]{1,0:T(8,128)(2,1)}, u32[]{:S(2)}, u32[]{:S(2)}) collective-permute-start(bf16[384,1024]{1,0:T(8,128)(2,1)} %collective-permute-done.3.refs_0_.refs_4_), channel_id=1, source_target_pairs={{0,32},{32,0},{1,33},{33,1},{2,34},{34,2},{3,35},{35,3},{4,36},{36... | collective-permute-start | bytes 2359304 | tf_op jit(solution)/shard_map/ppermute | solution.py:23
  53.3 39.4 %collective-permute-start.6 = (bf16[384,1024]{1,0:T(8,128)(2,1)}, bf16[384,1024]{1,0:T(8,128)(2,1)}, u32[]{:S(2)}, u32[]{:S(2)}) collective-permute-start(bf16[384,1024]{1,0:T(8,128)(2,1)} %collective-permute-done.5.refs_2_.refs_8_), channel_id=1, source_target_pairs={{0,32},{32,0},{1,33},{33,1},{2,34},{34,2},{3,35},{35,3},{4,36},{36... | collective-permute-start | bytes 2359304 | tf_op jit(solution)/shard_map/ppermute | solution.py:23
  69.8 27.6 %collective-permute-start.13 = (bf16[384,1024]{1,0:T(8,128)(2,1)}, bf16[384,1024]{1,0:T(8,128)(2,1)}, u32[]{:S(2)}, u32[]{:S(2)}) collective-permute-start(bf16[384,1024]{1,0:T(8,128)(2,1)} %collective-permute-done.12.left.refs_6_), channel_id=1, source_target_pairs={{0,32},{32,0},{1,33},{33,1},{2,34},{34,2},{3,35},{35,3},{4,36},{36... | collective-permute-start | bytes 2359304 | tf_op jit(solution)/shard_map/ppermute | solution.py:23
  70.9 26.6 %collective-permute-start.15 = (bf16[384,1024]{1,0:T(8,128)(2,1)}, bf16[384,1024]{1,0:T(8,128)(2,1)}, u32[]{:S(2)}, u32[]{:S(2)}) collective-permute-start(bf16[384,1024]{1,0:T(8,128)(2,1)} %collective-permute-done.14.right.refs_12_), channel_id=1, source_target_pairs={{0,32},{32,0},{1,33},{33,1},{2,34},{34,2},{3,35},{35,3},{4,36},{36... | collective-permute-start | bytes 2359304 | tf_op jit(solution)/shard_map/ppermute | solution.py:23
  75.2 10.5 %all-to-all-start.1 = ((bf16[8,112,128]{2,1,0:T(8,128)(2,1)}), bf16[8,112,128]{2,1,0:T(8,128)(2,1)S(1)}, u32[]{:S(2)}, u32[]{:S(2)}) async-start(bf16[8,112,128]{2,1,0:T(8,128)(2,1)} %get-tuple-element.14), calls=%async_computation.1 | async-start | bytes 458752 | tf_op jit(solution)/shard_map/all_to_all | solution.py:345
  85.7 85.5 %copy-start.3 = (bf16[8,112,128]{2,1,0:T(8,128)(2,1)}, bf16[8,112,128]{2,1,0:T(8,128)(2,1)S(1)}, u32[]{:S(2)}) copy-start(bf16[8,112,128]{2,1,0:T(8,128)(2,1)S(1)} %all-to-all-done.1.p0) | copy-start | bytes 688132
  102.7 19.1 %all-to-all-start.2 = ((f32[32,3,128]{2,1,0:T(4,128)}), f32[32,3,128]{2,1,0:T(4,128)S(1)}, u32[]{:S(2)}, u32[]{:S(2)}) async-start(f32[32,3,128]{2,1,0:T(4,128)} %get-tuple-element.17), calls=%async_computation.2 | async-start | bytes 131072 | tf_op jit(solution)/shard_map/all_to_all | solution.py:371
  130.9 4.9 %copy-start.2 = (bf16[128,2048]{1,0:T(8,128)(2,1)S(1)}, bf16[128,2048]{1,0:T(8,128)(2,1)}, u32[]{:S(2)}) copy-start(bf16[128,2048]{1,0:T(8,128)(2,1)} %get-tuple-element.16.powers.refs_4_) | copy-start | bytes 1572868
  130.9 39.1 %copy-start.19 = (f32[1,128]{1,0:T(1,128)S(1)}, f32[1,128]{1,0:T(1,128)}, u32[]{:S(2)}) copy-start(f32[1,128]{1,0:T(1,128)} %get-tuple-element.22) | copy-start | bytes 1540
  130.9 70.2 %all-to-all-start.3 = ((bf16[32,96,128]{2,1,0:T(8,128)(2,1)}), bf16[32,96,128]{2,1,0:T(8,128)(2,1)S(1)}, u32[]{:S(2)}, u32[]{:S(2)}) async-start(bf16[32,96,128]{2,1,0:T(8,128)(2,1)} %bitcast.28), calls=%async_computation.3 | async-start | bytes 1572864 | tf_op jit(solution)/shard_map/all_to_all | solution.py:380
  135.8 24.2 %collective-permute-start.24 = (bf16[128,2048]{1,0:T(8,128)(2,1)S(1)}, bf16[128,2048]{1,0:T(8,128)(2,1)S(1)}, u32[]{:S(2)}, u32[]{:S(2)}) collective-permute-start(bf16[128,2048]{1,0:T(8,128)(2,1)S(1)} %copy-done.2), channel_id=1, source_target_pairs={{0,64},{64,128},{128,192},{192,0},{1,65},{65,129},{129,193},{193,1... | collective-permute-start | bytes 1572872 | tf_op jit(solution)/shard_map/ppermute | solution.py:19
  136.4 23.5 %collective-permute-start.26 = (bf16[128,2048]{1,0:T(8,128)(2,1)S(1)}, bf16[128,2048]{1,0:T(8,128)(2,1)S(1)}, u32[]{:S(2)}, u32[]{:S(2)}) collective-permute-start(bf16[128,2048]{1,0:T(8,128)(2,1)S(1)} %copy-done.2), channel_id=1, source_target_pairs={{0,192},{64,0},{128,64},{192,128},{1,193},{65,1},{129,65},{193,129... | collective-permute-start | bytes 1572872 | tf_op jit(solution)/shard_map/ppermute | solution.py:19
  139.1 21.4 %collective-permute-start.28 = (bf16[128,2048]{1,0:T(8,128)(2,1)S(1)}, bf16[128,2048]{1,0:T(8,128)(2,1)S(1)}, u32[]{:S(2)}, u32[]{:S(2)}) collective-permute-start(bf16[128,2048]{1,0:T(8,128)(2,1)S(1)} %copy-done.2), channel_id=1, source_target_pairs={{0,128},{64,192},{128,0},{192,64},{1,129},{65,193},{129,1},{193,65... | collective-permute-start | bytes 1572872 | tf_op jit(solution)/shard_map/ppermute | solution.py:19
  139.1 21.5 %collective-permute-start.16 = (bf16[8,112,128]{2,1,0:T(8,128)(2,1)S(1)}, bf16[8,112,128]{2,1,0:T(8,128)(2,1)S(1)}, u32[]{:S(2)}, u32[]{:S(2)}) collective-permute-start(bf16[8,112,128]{2,1,0:T(8,128)(2,1)S(1)} %all-to-all-done.1.p0), channel_id=1, source_target_pairs={{0,24},{8,0},{16,8},{24,16},{1,25},{9,1},{17,9},{25,17},{2,26},{10... | collective-permute-start | bytes 688136 | tf_op jit(solution)/shard_map/ppermute | solution.py:19
  142.0 52.2 %collective-permute-start.23 = (bf16[128,2048]{1,0:T(8,128)(2,1)S(1)}, bf16[128,2048]{1,0:T(8,128)(2,1)}, u32[]{:S(2)}, u32[]{:S(2)}) collective-permute-start(bf16[128,2048]{1,0:T(8,128)(2,1)S(1)} %copy-done.2), channel_id=1, source_target_pairs={{0,32},{32,0},{1,33},{33,1},{2,34},{34,2},{3,35},{35,3},{4,36},{36... | collective-permute-start | bytes 1572872 | tf_op jit(solution)/shard_map/ppermute | solution.py:23
  160.0 34.3 %copy-start.5 = (bf16[128,2048]{1,0:T(8,128)(2,1)}, bf16[128,2048]{1,0:T(8,128)(2,1)S(1)}, u32[]{:S(2)}) copy-start(bf16[128,2048]{1,0:T(8,128)(2,1)S(1)} %collective-permute-done.24.refs_6_) | copy-start | bytes 1572868
  160.0 34.3 %collective-permute-start.25 = (bf16[128,2048]{1,0:T(8,128)(2,1)S(1)}, bf16[128,2048]{1,0:T(8,128)(2,1)}, u32[]{:S(2)}, u32[]{:S(2)}) collective-permute-start(bf16[128,2048]{1,0:T(8,128)(2,1)S(1)} %collective-permute-done.24.refs_6_), channel_id=1, source_target_pairs={{0,32},{32,0},{1,33},{33,1},{2,34},{34,2},{3,35},{35,3},{4,36},{36... | collective-permute-start | bytes 1572872 | tf_op jit(solution)/shard_map/ppermute | solution.py:23
  160.0 34.3 %copy-start.6 = (bf16[128,2048]{1,0:T(8,128)(2,1)}, bf16[128,2048]{1,0:T(8,128)(2,1)S(1)}, u32[]{:S(2)}) copy-start(bf16[128,2048]{1,0:T(8,128)(2,1)S(1)} %collective-permute-done.26.refs_8_) | copy-start | bytes 1572868
  160.0 34.2 %collective-permute-start.27 = (bf16[128,2048]{1,0:T(8,128)(2,1)S(1)}, bf16[128,2048]{1,0:T(8,128)(2,1)}, u32[]{:S(2)}, u32[]{:S(2)}) collective-permute-start(bf16[128,2048]{1,0:T(8,128)(2,1)S(1)} %collective-permute-done.26.refs_8_), channel_id=1, source_target_pairs={{0,32},{32,0},{1,33},{33,1},{2,34},{34,2},{3,35},{35,3},{4,36},{36... | collective-permute-start | bytes 1572872 | tf_op jit(solution)/shard_map/ppermute | solution.py:23
  160.5 33.8 %copy-start.7 = (bf16[128,2048]{1,0:T(8,128)(2,1)}, bf16[128,2048]{1,0:T(8,128)(2,1)S(1)}, u32[]{:S(2)}) copy-start(bf16[128,2048]{1,0:T(8,128)(2,1)S(1)} %collective-permute-done.28.refs_10_) | copy-start | bytes 1572868
  160.5 33.7 %collective-permute-start.29 = (bf16[128,2048]{1,0:T(8,128)(2,1)S(1)}, bf16[128,2048]{1,0:T(8,128)(2,1)}, u32[]{:S(2)}, u32[]{:S(2)}) collective-permute-start(bf16[128,2048]{1,0:T(8,128)(2,1)S(1)} %collective-permute-done.28.refs_10_), channel_id=1, source_target_pairs={{0,32},{32,0},{1,33},{33,1},{2,34},{34,2},{3,35},{35,3},{4,36},{36... | collective-permute-start | bytes 1572872 | tf_op jit(solution)/shard_map/ppermute | solution.py:23
  160.6 33.7 %copy-start.9 = (bf16[8,112,128]{2,1,0:T(8,128)(2,1)}, bf16[8,112,128]{2,1,0:T(8,128)(2,1)S(1)}, u32[]{:S(2)}) copy-start(bf16[8,112,128]{2,1,0:T(8,128)(2,1)S(1)} %collective-permute-done.16.p1) | copy-start | bytes 688132
  160.6 9.4 %collective-permute-start.17 = (bf16[8,112,128]{2,1,0:T(8,128)(2,1)S(1)}, bf16[8,112,128]{2,1,0:T(8,128)(2,1)S(1)}, u32[]{:S(2)}, u32[]{:S(2)}) collective-permute-start(bf16[8,112,128]{2,1,0:T(8,128)(2,1)S(1)} %all-to-all-done.1.p0), channel_id=1, source_target_pairs={{0,16},{8,24},{16,0},{24,8},{1,17},{9,25},{17,1},{25,9},{2,18},{10... | collective-permute-start | bytes 688136 | tf_op jit(solution)/shard_map/ppermute | solution.py:19
  170.0 1.2 collective-permute-start.19
  171.2 8.9 %collective-permute-start.18 = (bf16[8,112,128]{2,1,0:T(8,128)(2,1)S(1)}, bf16[8,112,128]{2,1,0:T(8,128)(2,1)S(1)}, u32[]{:S(2)}, u32[]{:S(2)}) collective-permute-start(bf16[8,112,128]{2,1,0:T(8,128)(2,1)S(1)} %all-to-all-done.1.p0), channel_id=1, source_target_pairs={{0,8},{8,16},{16,24},{24,0},{1,9},{9,17},{17,25},{25,1},{2,10},{10... | collective-permute-start | bytes 688136 | tf_op jit(solution)/shard_map/ppermute | solution.py:19
  172.7 21.6 %copy-start.14 = (f32[2,128]{1,0:T(2,128)}, f32[2,128]{1,0:T(2,128)S(1)}, u32[]{:S(2)}) copy-start(f32[2,128]{1,0:T(2,128)S(1)} %pad_maximum_fusion.refs_0_) | copy-start | bytes 3076
  180.8 4.8 %collective-permute-start.20 = (f32[2,128]{1,0:T(2,128)S(1)}, f32[2,128]{1,0:T(2,128)S(1)}, u32[]{:S(2)}, u32[]{:S(2)}) collective-permute-start(f32[2,128]{1,0:T(2,128)S(1)} %pad_maximum_fusion.refs_0_), channel_id=1, source_target_pairs={{0,64},{64,128},{128,192},{192,0},{1,65},{65,129},{129,193},{193,1... | collective-permute-start | bytes 3080 | tf_op jit(solution)/shard_map/ppermute | solution.py:19
  185.6 8.7 %copy-start.16 = (f32[2,128]{1,0:T(2,128)}, f32[2,128]{1,0:T(2,128)S(1)}, u32[]{:S(2)}) copy-start(f32[2,128]{1,0:T(2,128)S(1)} %collective-permute-done.20.refs_1_) | copy-start | bytes 3076
  185.6 3.6 %collective-permute-start.21 = (f32[2,128]{1,0:T(2,128)S(1)}, f32[2,128]{1,0:T(2,128)S(1)}, u32[]{:S(2)}, u32[]{:S(2)}) collective-permute-start(f32[2,128]{1,0:T(2,128)S(1)} %pad_maximum_fusion.refs_0_), channel_id=1, source_target_pairs={{0,192},{64,0},{128,64},{192,128},{1,193},{65,1},{129,65},{193,129... | collective-permute-start | bytes 3080 | tf_op jit(solution)/shard_map/ppermute | solution.py:19
  189.1 5.2 %copy-start.17 = (f32[2,128]{1,0:T(2,128)}, f32[2,128]{1,0:T(2,128)S(1)}, u32[]{:S(2)}) copy-start(f32[2,128]{1,0:T(2,128)S(1)} %collective-permute-done.21.refs_2_) | copy-start | bytes 3076
  189.1 5.1 %collective-permute-start.22 = (f32[2,128]{1,0:T(2,128)S(1)}, f32[2,128]{1,0:T(2,128)S(1)}, u32[]{:S(2)}, u32[]{:S(2)}) collective-permute-start(f32[2,128]{1,0:T(2,128)S(1)} %pad_maximum_fusion.refs_0_), channel_id=1, source_target_pairs={{0,128},{64,192},{128,0},{192,64},{1,129},{65,193},{129,1},{193,65... | collective-permute-start | bytes 3080 | tf_op jit(solution)/shard_map/ppermute | solution.py:19
  (6 other events, 4.7 us)
